TPU v7x, 32 devices: a whole 2x2x4 slice. The times are simulated.
32 devices in a mesh: tp: 8 (over z, y), dp: 4 (over x, core).
Axes of the slice: x: 2, y: 2, z: 4, core: 2. Of those that a mesh axis runs over, the one named last changes fastest.
Arguments:
- tokens: int32 [16, 1024], P('dp')
- labels: int32 [16, 1024], P('dp')
- embed: float32 [50304, 512], P('tp')
- ln_scales: float32 [2, 512], replicated
- w_q: float32 [512, 512], P(None, 'tp')
- w_kv: float32 [2, 512, 64], replicated
- w_o: float32 [512, 512], P('tp')
- w_gu: float32 [2, 512, 2048], P(None, None, 'tp')
- w_down: float32 [2048, 512], P('tp')
- m_embed: float32 [50304, 512], P('tp')
- m_ln_scales: float32 [2, 512], replicated
- m_w_q: float32 [512, 512], P(None, 'tp')
- m_w_kv: float32 [2, 512, 64], replicated
- m_w_o: float32 [512, 512], P('tp')
- m_w_gu: float32 [2, 512, 2048], P(None, None, 'tp')
- m_w_down: float32 [2048, 512], P('tp')
- v_embed: float32 [50304, 512], P('tp')
- v_ln_scales: float32 [2, 512], replicated
- v_w_q: float32 [512, 512], P(None, 'tp')
- v_w_kv: float32 [2, 512, 64], replicated
- v_w_o: float32 [512, 512], P('tp')
- v_w_gu: float32 [2, 512, 2048], P(None, None, 'tp')
- v_w_down: float32 [2048, 512], P('tp')
Outputs:
- output 1: float32 [50304, 512], P('tp')
- output 2: float32 [2, 512], replicated
- output 3: float32 [512, 512], P(None, 'tp')
- output 4: float32 [2, 512, 64], replicated
- output 5: float32 [512, 512], P('tp')
- output 6: float32 [2, 512, 2048], P(None, None, 'tp')
- output 7: float32 [2048, 512], P('tp')
- output 8: float32 [50304, 512], P('tp')
- output 9: float32 [2, 512], replicated
- output 10: float32 [512, 512], P(None, 'tp')
- output 11: float32 [2, 512, 64], replicated
- output 12: float32 [512, 512], P('tp')
- output 13: float32 [2, 512, 2048], P(None, None, 'tp')
- output 14: float32 [2048, 512], P('tp')
- output 15: float32 [50304, 512], P('tp')
- output 16: float32 [2, 512], replicated
- output 17: float32 [512, 512], P(None, 'tp')
- output 18: float32 [2, 512, 64], replicated
- output 19: float32 [512, 512], P('tp')
- output 20: float32 [2, 512, 2048], P(None, None, 'tp')
- output 21: float32 [2048, 512], P('tp')
- output 22: float32 [], replicated
All inputs are finite; a program needn't handle non-finite values.
Results may differ from a plain program's by a relative error of at most 0.00961239.
Values sent between devices are 32-bit elements.
A program may use at most 1 GiB of HBM per device.

v0:
```python
import jax
import jax.numpy as jnp
from jax import lax
from jax.sharding import PartitionSpec as P

LN_EPS = 1e-5
LOGIT_ZLOSS = 1e-4
LEARN_RATE = 1e-2
BETA_ONE = 0.9
BETA_TWO = 0.95
ADAM_EPS = 1e-8
ROPE_BASE = 10000.0


def norm_fwd(x_in, scale):
    x_f32 = x_in.astype(jnp.float32)
    centered = x_f32 - jnp.mean(x_f32, axis=-1, keepdims=True)
    inv_std = lax.rsqrt(jnp.mean(centered * centered, axis=-1, keepdims=True) + LN_EPS)
    x_hat = centered * inv_std
    return (x_hat * scale).astype(jnp.bfloat16), x_hat, inv_std


def norm_bwd(d_out, x_hat, inv_std, scale):
    d_scale = jnp.sum(d_out * x_hat, axis=(0, 1))
    d_hat = d_out * scale
    d_in = inv_std * (d_hat - jnp.mean(d_hat, axis=-1, keepdims=True) - x_hat * jnp.mean(d_hat * x_hat, axis=-1, keepdims=True))
    return d_in, d_scale


def rope_tables(seq_len, head_dim):
    positions = jnp.arange(seq_len).astype(jnp.float32)
    inv_freq = ROPE_BASE ** (-jnp.arange(0, head_dim, 2).astype(jnp.float32) / head_dim)
    angles = positions[:, None] * inv_freq[None, :]
    return jnp.cos(angles), jnp.sin(angles)


def rotate(x_in, cos_t, sin_t):
    half_dim = x_in.shape[-1] // 2
    x_lo = x_in[..., :half_dim]
    x_hi = x_in[..., half_dim:]
    return jnp.concatenate([x_lo * cos_t - x_hi * sin_t, x_hi * cos_t + x_lo * sin_t], axis=-1)


def adam_update(param_in, grad_in, mom_in, vel_in):
    mom_new = BETA_ONE * mom_in + (1.0 - BETA_ONE) * grad_in
    vel_new = BETA_TWO * vel_in + (1.0 - BETA_TWO) * grad_in * grad_in
    return param_in - LEARN_RATE * mom_new / (jnp.sqrt(vel_new) + ADAM_EPS), mom_new, vel_new


def solution(mesh):
    dp_size = mesh.shape['dp']
    param_specs = (P('tp', None), P(None, None), P(None, 'tp'), P(None, None, None), P('tp', None), P(None, None, 'tp'), P('tp', None))

    def local_step(tokens, labels, *state_arrays):
        embed, ln_scales, w_q, w_kv, w_o, w_gu, w_down = state_arrays[0:7]
        batch_loc, seq_len = tokens.shape
        vocab_loc, d_model = embed.shape
        head_dim = w_kv.shape[2]
        heads_loc = w_q.shape[1] // head_dim
        tok_total = batch_loc * seq_len * dp_size
        tp_rank = lax.axis_index('tp')
        emb_b = embed.astype(jnp.bfloat16)
        wq_b = w_q.astype(jnp.bfloat16)
        wkv_b = w_kv.astype(jnp.bfloat16)
        wo_b = w_o.astype(jnp.bfloat16).reshape(heads_loc, head_dim, d_model)
        wgu_b = w_gu.astype(jnp.bfloat16)
        wdown_b = w_down.astype(jnp.bfloat16)

        local_ids = tokens - tp_rank * vocab_loc
        in_shard = (local_ids >= 0) & (local_ids < vocab_loc)
        safe_ids = jnp.where(in_shard, local_ids, 0)
        picked = jnp.take(emb_b, safe_ids, axis=0).astype(jnp.float32)
        x_zero = lax.psum(jnp.where(in_shard[..., None], picked, 0.0), 'tp')
        u_norm, u_hat, u_inv = norm_fwd(x_zero, ln_scales[0])

        cos_t, sin_t = rope_tables(seq_len, head_dim)
        q_raw = jnp.einsum('bsd,dn->bsn', u_norm, wq_b, preferred_element_type=jnp.float32).reshape(batch_loc, seq_len, heads_loc, head_dim)
        queries = rotate(q_raw, cos_t[:, None, :], sin_t[:, None, :]).astype(jnp.bfloat16)
        kv_raw = jnp.einsum('bsd,cde->cbse', u_norm, wkv_b, preferred_element_type=jnp.float32)
        key_rot = rotate(kv_raw[0], cos_t, sin_t).astype(jnp.bfloat16)
        values = kv_raw[1].astype(jnp.bfloat16)
        causal = jnp.arange(seq_len)[:, None] >= jnp.arange(seq_len)[None, :]
        scores = jnp.einsum('bqhe,bke->bhqk', queries, key_rot, preferred_element_type=jnp.float32) * head_dim ** -0.5
        prob_f32 = jax.nn.softmax(jnp.where(causal, scores, -1e30), axis=-1)
        prob_b16 = prob_f32.astype(jnp.bfloat16)
        context = jnp.einsum('bhqk,bke->bqhe', prob_b16, values, preferred_element_type=jnp.float32).astype(jnp.bfloat16)
        att_part = jnp.einsum('crif,ife->cre', context, wo_b, preferred_element_type=jnp.float32)
        gate_up = jnp.einsum('bsd,cdf->cbsf', u_norm, wgu_b, preferred_element_type=jnp.float32)
        gate_sig = jax.nn.sigmoid(gate_up[0])
        hidden = (gate_up[0] * gate_sig * gate_up[1]).astype(jnp.bfloat16)
        mlp_part = jnp.einsum('bsf,fd->bsd', hidden, wdown_b, preferred_element_type=jnp.float32)
        x_one = x_zero + lax.psum(att_part + mlp_part, 'tp')
        f_norm, f_hat, f_inv = norm_fwd(x_one, ln_scales[1])

        logit_scale = d_model ** -0.5
        logits = jnp.einsum('bsd,vd->bsv', f_norm, emb_b, preferred_element_type=jnp.float32) * logit_scale
        row_max = lax.pmax(jnp.max(logits, axis=-1), 'tp')
        exp_shift = jnp.exp(logits - row_max[..., None])
        lab_hit = jnp.arange(vocab_loc)[None, None, :] == (labels - tp_rank * vocab_loc)[..., None]
        shard_stats = lax.psum(jnp.stack([jnp.sum(exp_shift, axis=-1), jnp.sum(jnp.where(lab_hit, logits, 0.0), axis=-1)]), 'tp')
        log_norm = row_max + jnp.log(shard_stats[0])
        tok_loss = log_norm - shard_stats[1] + LOGIT_ZLOSS * log_norm * log_norm
        loss = lax.psum(jnp.sum(tok_loss), 'dp') / tok_total

        prob_coef = (1.0 + 2.0 * LOGIT_ZLOSS * log_norm) / shard_stats[0]
        d_logits = ((exp_shift * prob_coef[..., None] - lab_hit.astype(jnp.float32)) * (logit_scale / tok_total)).astype(jnp.bfloat16)
        d_fin = lax.psum(jnp.einsum('bsv,vd->bsd', d_logits, emb_b, preferred_element_type=jnp.float32), 'tp')
        g_embed_head = jnp.einsum('bsv,bsd->vd', d_logits, f_norm, preferred_element_type=jnp.float32)
        d_one, g_ln_fin = norm_bwd(d_fin, f_hat, f_inv, ln_scales[1])
        d_one_b = d_one.astype(jnp.bfloat16)

        d_hidden = jnp.einsum('bsd,fd->bsf', d_one_b, wdown_b, preferred_element_type=jnp.float32)
        g_down = jnp.einsum('bsf,bsd->fd', hidden, d_one_b, preferred_element_type=jnp.float32)
        d_gate = d_hidden * gate_up[1] * gate_sig * (1.0 + gate_up[0] * (1.0 - gate_sig))
        d_up = d_hidden * gate_up[0] * gate_sig
        d_gate_up = jnp.stack([d_gate, d_up]).astype(jnp.bfloat16)
        g_gu = jnp.einsum('cbsf,bsd->cdf', d_gate_up, u_norm, preferred_element_type=jnp.float32)
        d_u_mlp = jnp.einsum('cbsf,cdf->bsd', d_gate_up, wgu_b, preferred_element_type=jnp.float32)

        d_context = jnp.einsum('cre,ife->crif', d_one_b, wo_b, preferred_element_type=jnp.float32).astype(jnp.bfloat16)
        g_o = jnp.einsum('crif,cre->ife', context, d_one_b, preferred_element_type=jnp.float32).reshape(heads_loc * head_dim, d_model)
        d_probs = jnp.einsum('bqhe,bke->bhqk', d_context, values, preferred_element_type=jnp.float32)
        d_values = jnp.einsum('bhqk,bqhe->bke', prob_b16, d_context, preferred_element_type=jnp.float32)
        d_scores = (prob_f32 * (d_probs - jnp.sum(d_probs * prob_f32, axis=-1, keepdims=True)) * head_dim ** -0.5).astype(jnp.bfloat16)
        d_queries = jnp.einsum('bhqk,bke->bqhe', d_scores, key_rot, preferred_element_type=jnp.float32)
        d_keys = jnp.einsum('bhqk,bqhe->bke', d_scores, queries, preferred_element_type=jnp.float32)
        d_q_raw = rotate(d_queries, cos_t[:, None, :], -sin_t[:, None, :]).astype(jnp.bfloat16).reshape(batch_loc, seq_len, heads_loc * head_dim)
        d_kv = jnp.stack([rotate(d_keys, cos_t, -sin_t), d_values]).astype(jnp.bfloat16)
        g_q = jnp.einsum('bsd,bsn->dn', u_norm, d_q_raw, preferred_element_type=jnp.float32)
        g_kv_part = jnp.einsum('cbse,bsd->cde', d_kv, u_norm, preferred_element_type=jnp.float32)
        d_u_att = (jnp.einsum('bsn,dn->bsd', d_q_raw, wq_b, preferred_element_type=jnp.float32)
                   + jnp.einsum('cbse,cde->bsd', d_kv, wkv_b, preferred_element_type=jnp.float32))
        d_u = lax.psum(d_u_att + d_u_mlp, 'tp')
        d_zero_norm, g_ln_in = norm_bwd(d_u, u_hat, u_inv, ln_scales[0])
        d_zero = jnp.where(in_shard[..., None], d_one + d_zero_norm, 0.0)
        g_embed_look = jax.ops.segment_sum(d_zero.reshape(-1, d_model), safe_ids.reshape(-1), num_segments=vocab_loc)

        g_kv = lax.psum(g_kv_part, ('tp', 'dp'))
        summed = lax.psum((g_embed_head + g_embed_look, jnp.stack([g_ln_in, g_ln_fin]), g_q, g_o, g_gu, g_down), 'dp')
        gradients = tuple(summed[0:3]) + (g_kv,) + tuple(summed[3:6])

        outs_p = []
        outs_m = []
        outs_v = []
        for index in range(7):
            new_p, new_m, new_v = adam_update(state_arrays[index], gradients[index], state_arrays[7 + index], state_arrays[14 + index])
            outs_p.append(new_p)
            outs_m.append(new_m)
            outs_v.append(new_v)
        return tuple(outs_p) + tuple(outs_m) + tuple(outs_v) + (loss,)

    return jax.shard_map(local_step, mesh=mesh, in_specs=(P('dp', None), P('dp', None)) + param_specs * 3,
                         out_specs=param_specs * 3 + (P(),), check_vma=False)
```

profile of v0, /device:TPU:0, one launch (start us, length us, event | category | flops | bytes accessed | tf_op | source)
XLA Modules:
  0.0 1877.5 jit_solution(3333191637095113557)
XLA Ops:
  9.3 8.1 convert_element_type.148
  17.5 21.1 %gather_fusion = bf16[4096,512]{1,0:T(8,128)(2,1)} fusion(bf16[6288,512]{1,0:T(8,128)(2,1)} %convert_element_type.148, s32[4096]{0:T(1024)S(1)} %bitcast_clamp_fusion), kind=kCustom, calls=%fused_computation | custom fusion | bytes 8404992 | tf_op jit(solution)/shard_map/jit(_take)/gather | solution.py:72
  38.6 6.9 convert_select_fusion
  47.1 269.7 %all-reduce.9.cloned.1.call-done = f32[4,1024,512]{2,1,0:T(8,128)} async-done(((f32[4,1024,512]{2,1,0:T(8,128)}), f32[4,1024,512]{2,1,0:T(8,128)}) %all-reduce.9.cloned.1.call-update) | async-done | bytes 8388624 | tf_op jit(solution)/shard_map/psum | solution.py:73
  316.9 4.0 reduce_sum.135
  320.9 4.8 multiply_reduce_fusion.6
  331.6 2.3 fusion.27
  335.2 2.1 copy-done.6
  337.4 3.0 fusion.8
  340.4 3.7 fusion.6
  344.1 2.1 copy-done.5
  346.3 5.2 fusion.47
  352.8 4.7 convolution_add_fusion
  358.2 267.0 %all-reduce.11.cloned.1.call-done = f32[4,1024,512]{2,1,0:T(8,128)} async-done(((f32[4,1024,512]{2,1,0:T(8,128)}), f32[4,1024,512]{2,1,0:T(8,128)}) %all-reduce.11.cloned.1.call-update) | async-done | bytes 8388624 | tf_op jit(solution)/shard_map/psum | solution.py:92
  625.2 10.1 fusion.118
  635.3 4.1 multiply_reduce_fusion.5
  639.5 43.9 %multiply_reduce_fusion = (f32[4,1024]{1,0:T(4,128)S(1)}, f32[4,1024,6288]{1,2,0:T(8,128)}) fusion(bf16[6288,512]{1,0:T(8,128)(2,1)} %convert_element_type.148, f32[4,1024,512]{2,1,0:T(8,128)} %get-tuple-element.59, f32[512]{0:T(512)S(1)} %bitcast.254, f32[4,1024]{1,0:T(4,128)S(1)} %add_rsqrt_fusion, f32[4,1024]{1,0:T(4,128)S(1)} %broadcast_multiply_fusion.4), kind=kOutput, calls=%fused_computation.7 | convolution fusion | flops 26433679360 | bytes 117901312 | tf_op jit(solution)/shard_map/bsd,vd->bsv/dot_general | solution.py:96
  683.4 34.8 %pmax.7 = f32[4,1024]{1,0:T(4,128)S(1)} all-reduce(f32[4,1024]{1,0:T(4,128)S(1)} %get-tuple-element.83), channel_id=1, replica_groups=mesh['tp'=8,'dp'=4] {'tp'}, use_global_device_ids=true, to_apply=%region_9.10 | all-reduce | flops 4096 | bytes 32768 | tf_op jit(solution)/shard_map/pmax | solution.py:97
  718.2 32.2 %fusion = (f32[4,1024]{1,0:T(4,128)S(1)}, f32[4,1024]{1,0:T(4,128)S(1)}) fusion(f32[4,1024,6288]{1,2,0:T(8,128)} %get-tuple-element.84, f32[4,1024]{1,0:T(4,128)S(1)} %pmax.7, s32[4,1024]{1,0:T(4,128)S(1)} %broadcast_subtract_fusion), kind=kLoop, calls=%fused_computation.6 | loop fusion | flops 154525696 | bytes 103088128 | tf_op jit(solution)/shard_map/reduce_sum | solution.py:100
  750.4 33.2 %psum.93 = f32[2,4,1024]{2,1,0:T(4,128)S(1)} all-reduce(f32[2,4,1024]{2,1,0:T(4,128)S(1)} %pad_maximum_fusion.17), channel_id=1, replica_groups=mesh['tp'=8,'dp'=4] {'tp'}, use_global_device_ids=true, to_apply=%region_12.13 | all-reduce | flops 8192 | bytes 65536 | tf_op jit(solution)/shard_map/psum | solution.py:100
  784.3 47.6 %fusion.14 = f32[4,1024,512]{2,1,0:T(8,128)} fusion(bf16[6288,512]{1,0:T(8,128)(2,1)} %convert_element_type.148, f32[4,1024,6288]{1,2,0:T(8,128)} %get-tuple-element.84, f32[4,1024]{1,0:T(4,128)S(1)} %get-tuple-element.71, s32[4,1024]{1,0:T(4,128)S(1)} %broadcast_subtract_fusion, f32[4,1024]{1,0:T(4,128)S(1)} %pmax.7), kind=kOutput, calls=%fused_computation.46 | convolution fusion | flops 26579828736 | bytes 117899264 | tf_op jit(solution)/shard_map/bsv,vd->bsd/dot_general | solution.py:107
  833.2 5.5 multiply_convert_fusion.16
  838.7 259.1 %all-reduce.13.cloned.1.call-done = f32[4,1024,512]{2,1,0:T(8,128)} async-done(((f32[4,1024,512]{2,1,0:T(8,128)}), f32[4,1024,512]{2,1,0:T(8,128)}) %all-reduce.13.cloned.1.call-update) | async-done | bytes 8388624 | tf_op jit(solution)/shard_map/psum | solution.py:107
  1097.8 8.3 multiply_reduce_fusion.1
  1106.7 7.5 fusion.54
  1114.3 7.5 fusion.31
  1124.0 5.8 fusion.44
  1129.8 11.2 fusion.1
  1141.0 13.0 fusion.9
  1154.1 2.7 fusion.61
  1161.4 8.5 bitcast_add_fusion
  1170.7 48.2 %convolution_bitcast_fusion = f32[6288,512]{1,0:T(8,128)} fusion(f32[4,1024,6288]{1,2,0:T(8,128)} %get-tuple-element.84, f32[4,1024]{1,0:T(4,128)S(1)} %copy-done.79, s32[4,1024]{1,0:T(4,128)S(1)} %copy-done.68, f32[4,1024]{1,0:T(4,128)S(1)} %copy-done.59, bf16[4,1024,512]{2,1,0:T(8,128)(2,1)} %multiply_convert_fusion.16), kind=kOutput, calls=%fused_computation.23 | convolution fusion | flops 26579828736 | bytes 120143872 | tf_op jit(solution)/shard_map/bsv,bsd->vd/dot_general | solution.py:108
  1218.8 3.8 convolution_bitcast_fusion.4
  1222.7 3.8 convolution_bitcast_fusion.5
  1227.9 4.2 convolution_bitcast_fusion.3
  1232.2 6.8 fusion.35
  1239.1 198.5 %all-reduce.15.cloned.1.call-done = f32[4,1024,512]{2,1,0:T(8,128)} async-done(((f32[4,1024,512]{2,1,0:T(8,128)}), f32[4,1024,512]{2,1,0:T(8,128)}) %all-reduce.15.cloned.1.call-update) | async-done | bytes 8388624 | tf_op jit(solution)/shard_map/psum | solution.py:133
  1437.7 8.0 multiply_reduce_fusion.2
  1445.9 12.8 add_select_fusion
  1458.6 36.0 %scatter_fusion = f32[6288,512]{1,0:T(8,128)} fusion(f32[6288,512]{1,0:T(8,128)} %convolution_bitcast_fusion, s32[4096]{0:T(1024)S(1)} %bitcast.251, f32[4096,512]{1,0:T(8,128)} %bitcast.249), kind=kCustom, calls=%fused_computation.1 | custom fusion | flops 2097152 | bytes 25182208 | tf_op jit(solution)/shard_map/scatter-add | solution.py:136
  1494.8 75.6 %all-reduce.17.cloned.1.call-done = f32[2,512,64]{1,2,0:T(8,128)} async-done(((f32[2,512,64]{1,2,0:T(8,128)}), f32[2,512,64]{1,2,0:T(8,128)}) %all-reduce.17.cloned.1.call-update) | async-done | bytes 262160 | tf_op jit(solution)/shard_map/psum | solution.py:138
  1570.4 2.0 divide_subtract_fusion.3
  1572.4 6.5 all-reduce
  1580.9 247.7 %all-reduce.19.cloned.1.call-done = (f32[6288,512]{1,0:T(8,128)}, f32[512,64]{0,1:T(8,128)}, f32[64,512]{1,0:T(8,128)}, f32[2,512,256]{2,1,0:T(8,128)}, f32[256,512]{1,0:T(8,128)}) async-done(((f32[6288,512]{1,0:T(8,128)}, f32[512,64]{0,1:T(8,128)}, f32[64,512]{1,0:T(8,128)}, f32[2,512,256]{2,1,0:T(8,128)}, f32[256,512]{1,0:T(8,128)}), (f32[6288,512]{1,0:T(8,128)}, f32[512,64]{0,1:T(8,128)}, ...) | async-done | bytes 14712848 | tf_op jit(solution)/shard_map/psum | solution.py:139
  1830.4 1.8 divide_subtract_fusion.4
  1832.2 2.7 divide_subtract_fusion.2
  1834.9 3.5 divide_subtract_fusion.1
  1838.4 30.8 %divide_subtract_fusion = (f32[6288,512]{1,0:T(8,128)}, f32[6288,512]{1,0:T(8,128)}, f32[6288,512]{1,0:T(8,128)}) fusion(f32[6288,512]{1,0:T(8,128)} %param.25, f32[6288,512]{1,0:T(8,128)} %get-tuple-element.32, f32[6288,512]{1,0:T(8,128)} %param.32, f32[6288,512]{1,0:T(8,128)} %param.39), kind=kLoop, calls=%fused_computation.20 | loop fusion | flops 35414016 | bytes 90144768 | tf_op jit(solution)/shard_map/sub | solution.py:47
  (221 shorter events, 27.6 us)
Async XLA Ops:
  7.2 309.7 %all-reduce.9.cloned.1.call-start = ((), (), s32[]{:S(2)}) async-start(), calls=%async_computation | async-start | bytes 16777216 | tf_op jit(solution)/shard_map/psum | solution.py:73
  8.0 30.6 %copy-start.71 = (pred[4,1024]{1,0:T(4,128)(4,1)}, pred[4,1024]{1,0:T(4,128)(4,1)S(1)}, u32[]{:S(2)}) copy-start(pred[4,1024]{1,0:T(4,128)(4,1)S(1)} %get-tuple-element.74) | copy-start | bytes 12292
  45.5 579.8 %all-reduce.11.cloned.1.call-start = ((), (), s32[]{:S(2)}) async-start(), calls=%async_computation.1 | async-start | bytes 16777216 | tf_op jit(solution)/shard_map/psum | solution.py:92
  45.9 298.3 %copy-start.10 = (pred[1024,1024]{0,1:T(8,128)(4,1)}, pred[1024,1024]{0,1:T(8,128)(4,1)S(1)}, u32[]{:S(2)}) copy-start(pred[1024,1024]{0,1:T(8,128)(4,1)S(1)} %iota_compare_fusion.1) | copy-start | bytes 3145732
  45.9 279.9 %copy-start.73 = (f32[1,512]{1,0:T(1,128)}, f32[1,512]{1,0:T(1,128)S(1)}, u32[]{:S(2)}) copy-start(f32[1,512]{1,0:T(1,128)S(1)} %get-tuple-element.80) | copy-start | bytes 6148
  45.9 1060.2 %copy-start.69 = (f32[1,512]{1,0:T(1,128)}, f32[1,512]{1,0:T(1,128)S(1)}, u32[]{:S(2)}) copy-start(f32[1,512]{1,0:T(1,128)S(1)} %get-tuple-element.79) | copy-start | bytes 6148
  47.1 284.3 %copy-start.16 = (f32[1024,32]{0,1:T(8,128)}, f32[1024,32]{0,1:T(8,128)S(1)}, u32[]{:S(2)}) copy-start(f32[1024,32]{0,1:T(8,128)S(1)} %get-tuple-element.78) | copy-start | bytes 393220
  331.1 13.0 copy-start.15
  335.2 16.2 copy-start.8
  357.5 740.3 %all-reduce.13.cloned.1.call-start = ((), (), s32[]{:S(2)}) async-start(), calls=%async_computation.2 | async-start | bytes 16777216 | tf_op jit(solution)/shard_map/psum | solution.py:107
  358.2 426.1 %copy-start.67 = (s32[4,1024]{1,0:T(4,128)}, s32[4,1024]{1,0:T(4,128)S(1)}, u32[]{:S(2)}) copy-start(s32[4,1024]{1,0:T(4,128)S(1)} %broadcast_subtract_fusion) | copy-start | bytes 49156
  635.3 470.8 %copy-start.43 = (f32[4,1024]{1,0:T(4,128)}, f32[4,1024]{1,0:T(4,128)S(1)}, u32[]{:S(2)}) copy-start(f32[4,1024]{1,0:T(4,128)S(1)} %broadcast_multiply_fusion.4) | copy-start | bytes 49156
  639.5 466.7 %copy-start.49 = (f32[4,1024]{1,0:T(4,128)}, f32[4,1024]{1,0:T(4,128)S(1)}, u32[]{:S(2)}) copy-start(f32[4,1024]{1,0:T(4,128)S(1)} %add_rsqrt_fusion) | copy-start | bytes 49156
  718.2 66.1 %copy-start.58 = (f32[4,1024]{1,0:T(4,128)}, f32[4,1024]{1,0:T(4,128)S(1)}, u32[]{:S(2)}) copy-start(f32[4,1024]{1,0:T(4,128)S(1)} %pmax.7) | copy-start | bytes 49156
  784.3 47.6 %copy-start.78 = (f32[4,1024]{1,0:T(4,128)}, f32[4,1024]{1,0:T(4,128)S(1)}, u32[]{:S(2)}) copy-start(f32[4,1024]{1,0:T(4,128)S(1)} %get-tuple-element.71) | copy-start | bytes 49156
  831.9 605.8 %all-reduce.15.cloned.1.call-start = ((), (), s32[]{:S(2)}) async-start(), calls=%async_computation.3 | async-start | bytes 16777216 | tf_op jit(solution)/shard_map/psum | solution.py:133
  1106.7 17.3 slice-start
  1106.7 17.3 slice-start.1
  1114.3 9.7 slice-start.2
  1114.3 9.7 slice-start.3
  1114.3 9.7 copy-start.11
  1114.3 9.7 copy-start.64
  1141.0 13.0 copy-start.36
  1141.0 13.0 copy-start.38
  1169.9 52.7 %copy-start.19 = (bf16[4,1024,64]{1,2,0:T(8,128)(2,1)S(1)}, bf16[4,1024,64]{1,2,0:T(8,128)(2,1)}, u32[]{:S(2)}) copy-start(bf16[4,1024,64]{1,2,0:T(8,128)(2,1)} %copy-done.18) | copy-start | bytes 1572868
  1170.0 400.5 %all-reduce.17.cloned.1.call-start = ((), (), s32[]{:S(2)}) async-start(), calls=%async_computation.4 | async-start | bytes 524288 | tf_op jit(solution)/shard_map/psum | solution.py:138
  1232.2 205.5 %copy-start.48 = (f32[4,1024]{1,0:T(4,128)S(1)}, f32[4,1024]{1,0:T(4,128)}, u32[]{:S(2)}) copy-start(f32[4,1024]{1,0:T(4,128)} %copy-done.47) | copy-start | bytes 49156
  1232.2 205.5 %copy-start.52 = (f32[4,1024]{1,0:T(4,128)S(1)}, f32[4,1024]{1,0:T(4,128)}, u32[]{:S(2)}) copy-start(f32[4,1024]{1,0:T(4,128)} %copy-done.51) | copy-start | bytes 49156
  1232.2 205.5 %copy-start.74 = (f32[1,512]{1,0:T(1,128)S(1)}, f32[1,512]{1,0:T(1,128)}, u32[]{:S(2)}) copy-start(f32[1,512]{1,0:T(1,128)} %copy-done.73) | copy-start | bytes 6148
  1239.0 206.7 %copy-start.44 = (f32[4,1024]{1,0:T(4,128)S(1)}, f32[4,1024]{1,0:T(4,128)}, u32[]{:S(2)}) copy-start(f32[4,1024]{1,0:T(4,128)} %copy-done.43) | copy-start | bytes 49156
  1239.0 206.7 %copy-start.50 = (f32[4,1024]{1,0:T(4,128)S(1)}, f32[4,1024]{1,0:T(4,128)}, u32[]{:S(2)}) copy-start(f32[4,1024]{1,0:T(4,128)} %copy-done.49) | copy-start | bytes 49156
  1239.0 206.7 %copy-start.55 = (f32[4,1024]{1,0:T(4,128)S(1)}, f32[4,1024]{1,0:T(4,128)}, u32[]{:S(2)}) copy-start(f32[4,1024]{1,0:T(4,128)} %copy-done.54) | copy-start | bytes 49156
  1239.0 206.7 %copy-start.57 = (f32[4,1024]{1,0:T(4,128)S(1)}, f32[4,1024]{1,0:T(4,128)}, u32[]{:S(2)}) copy-start(f32[4,1024]{1,0:T(4,128)} %copy-done.56) | copy-start | bytes 49156
  1239.1 206.7 %copy-start.70 = (f32[1,512]{1,0:T(1,128)S(1)}, f32[1,512]{1,0:T(1,128)}, u32[]{:S(2)}) copy-start(f32[1,512]{1,0:T(1,128)} %copy-done.69) | copy-start | bytes 6148
  1239.1 206.7 %copy-start.72 = (pred[4,1024]{1,0:T(4,128)(4,1)S(1)}, pred[4,1024]{1,0:T(4,128)(4,1)}, u32[]{:S(2)}) copy-start(pred[4,1024]{1,0:T(4,128)(4,1)} %copy-done.71) | copy-start | bytes 12292
  1239.1 589.6 %all-reduce.19.cloned.1.call-start = ((), (), s32[]{:S(2)}) async-start(), calls=%async_computation.5 | async-start | bytes 29425664 | tf_op jit(solution)/shard_map/psum | solution.py:139
  1445.9 12.8 copy-start.61
  1494.7 75.8 %copy-start.22 = (f32[2,512,64]{1,2,0:T(8,128)S(1)}, f32[2,512,64]{1,2,0:T(8,128)}, u32[]{:S(2)}) copy-start(f32[2,512,64]{1,2,0:T(8,128)} %param.28) | copy-start | bytes 786436
  1494.7 75.8 %copy-start.53 = (f32[2,512,64]{1,2,0:T(8,128)S(1)}, f32[2,512,64]{1,2,0:T(8,128)}, u32[]{:S(2)}) copy-start(f32[2,512,64]{1,2,0:T(8,128)} %param.35) | copy-start | bytes 786436
  1494.7 77.7 %copy-start.80 = (f32[512]{0:T(512)S(1)}, f32[512]{0:T(512)}, u32[]{:S(2)}) copy-start(f32[512]{0:T(512)} %get-tuple-element.26) | copy-start | bytes 6148
  1494.7 84.9 %copy-start.76 = (f32[2,512]{1,0:T(2,128)S(1)}, f32[2,512]{1,0:T(2,128)}, u32[]{:S(2)}) copy-start(f32[2,512]{1,0:T(2,128)} %param.26) | copy-start | bytes 12292
  1494.7 84.9 %copy-start.81 = (f32[2,512]{1,0:T(2,128)S(1)}, f32[2,512]{1,0:T(2,128)}, u32[]{:S(2)}) copy-start(f32[2,512]{1,0:T(2,128)} %param.33) | copy-start | bytes 12292
  1494.7 333.9 %copy-start.28 = (f32[512,64]{0,1:T(8,128)S(1)}, f32[512,64]{0,1:T(8,128)}, u32[]{:S(2)}) copy-start(f32[512,64]{0,1:T(8,128)} %param.27) | copy-start | bytes 393220
  1494.7 333.9 %copy-start.60 = (f32[512,64]{0,1:T(8,128)S(1)}, f32[512,64]{0,1:T(8,128)}, u32[]{:S(2)}) copy-start(f32[512,64]{0,1:T(8,128)} %param.34) | copy-start | bytes 393220
  1494.7 335.7 %copy-start.31 = (f32[64,512]{1,0:T(8,128)S(1)}, f32[64,512]{1,0:T(8,128)}, u32[]{:S(2)}) copy-start(f32[64,512]{1,0:T(8,128)} %param.29) | copy-start | bytes 393220
  1494.7 337.5 %copy-start.25 = (f32[256,512]{1,0:T(8,128)S(1)}, f32[256,512]{1,0:T(8,128)}, u32[]{:S(2)}) copy-start(f32[256,512]{1,0:T(8,128)} %param.31) | copy-start | bytes 1572868
  1494.7 340.2 %copy-start.14 = (f32[2,512,256]{2,1,0:T(8,128)S(1)}, f32[2,512,256]{2,1,0:T(8,128)}, u32[]{:S(2)}) copy-start(f32[2,512,256]{2,1,0:T(8,128)} %param.30) | copy-start | bytes 3145732
  1494.8 340.1 %copy-start.34 = (f32[2,512,256]{2,1,0:T(8,128)S(1)}, f32[2,512,256]{2,1,0:T(8,128)}, u32[]{:S(2)}) copy-start(f32[2,512,256]{2,1,0:T(8,128)} %param.37) | copy-start | bytes 3145732
  (44 other events, 185.8 us)
Sparse Core Ops, SparseCore 0:
  45.6 271.2 all-reduce.8
  357.6 267.5 all-reduce.10
  832.0 265.7 all-reduce.12
  1170.1 267.5 all-reduce.14
  1443.6 126.8 all-reduce.16
  1574.3 254.2 all-reduce.18
where the time goes:
time: 1880 us
  waiting for transfers between devices  1320 us (70%)
  matrix products  220 us (12%)
  other arithmetic  217 us (12%)
  blocking collectives  74.6 us (4%)
  local copies, waits for them, and re-layouts  30.9 us (2%)
    psum x1, waiting for transfers between devices, local_step(): x_zero = lax.psum(jnp.where(in_shard[..., None], picked, 0.0), 'tp')  270 us
    psum x1, waiting for transfers between devices, local_step(): x_one = x_zero + lax.psum(att_part + mlp_part, 'tp')  267 us
    psum x1, waiting for transfers between devices, local_step(): lax.psum(jnp.einsum('bsv,vd->bsd', d_logits, emb_b, preferred_element_typ...  259 us
    psum x1, waiting for transfers between devices, local_step(): lax.psum((g_embed_head + g_embed_look, jnp.stack([g_ln_in, g_ln_fin]), g_...  248 us
    psum x1, waiting for transfers between devices, local_step(): d_u = lax.psum(d_u_att + d_u_mlp, 'tp')  199 us
    psum x1, waiting for transfers between devices, local_step(): g_kv = lax.psum(g_kv_part, ('tp', 'dp'))  75.6 us
    dot_general x1, matrix products, local_step(): jnp.einsum('bsv,bsd->vd', d_logits, f_norm, preferred_element_type=jnp.fl...  48.2 us
    dot_general x1, matrix products, local_step(): jnp.einsum('bsv,vd->bsd', d_logits, emb_b, preferred_element_type=jnp.flo...  47.6 us
  transfers between devices with their start and end apart: 6, of which 6 were waited for; matrix products, arithmetic and copies ran while one was open for 7% of the time, Pallas kernels for 0%

commit v1 on v0

v1 whole, which is shorter than its diff:
```python
import functools

import jax
import jax.numpy as jnp
from jax import lax
from jax.experimental import pallas as pl
from jax.experimental.pallas import tpu as pltpu
from jax.sharding import PartitionSpec as P

LN_EPS = 1e-5
LOGIT_ZLOSS = 1e-4
LEARN_RATE = 1e-2
BETA_ONE = 0.9
BETA_TWO = 0.95
ADAM_EPS = 1e-8
ROPE_BASE = 10000.0
NZ = 4
CAP = 96
F32 = jnp.float32
BF16 = jnp.bfloat16
ANY = pl.BlockSpec(memory_space=pl.ANY)
VMEM = pl.BlockSpec(memory_space=pltpu.VMEM)

ARRIVALS = {
    0: (("R", 1), ("R", 2), ("R", 3)),
    1: (("L", 0), ("R", 2), ("R", 3)),
    2: (("R", 3), ("L", 1), ("L", 0)),
    3: (("L", 2), ("L", 1), ("L", 0)),
}
REDUCE_ORDER = {0: (3, 2, 1, 0), 1: (3, 0, 2, 1), 2: (0, 3, 1, 2), 3: (0, 1, 2, 3)}


def remote(src, dst, send_sem, recv_sem, tp, dp):
    return pltpu.make_async_remote_copy(src_ref=src, dst_ref=dst, send_sem=send_sem, recv_sem=recv_sem,
                                        device_id=(tp, dp), device_id_type=pl.DeviceIdType.MESH)


def place():
    tp = lax.axis_index("tp")
    dp = lax.axis_index("dp")
    return tp, dp, tp // 2, tp % 2


def signal(tp, dp):
    pl.semaphore_signal(pltpu.get_barrier_semaphore(), inc=1, device_id=(tp, dp), device_id_type=pl.DeviceIdType.MESH)


def line_barrier(k, tp, dp, others):
    peers = [(tp + 1 - 2 * (tp % 2), dp)] + others
    if k > 0:
        peers.append((tp - 2, dp))
    if k < NZ - 1:
        peers.append((tp + 2, dp))
    for peer in peers:
        signal(*peer)
    pl.semaphore_wait(pltpu.get_barrier_semaphore(), len(peers))


def gather_kernel(x_ref, out_ref, own_sem, send_y, send_l, send_r, recv):
    tp, dp, z, y = place()
    partner = tp + 1 - 2 * y

    def program(k):
        line_barrier(k, tp, dp, [])

        def send(src, slot, sems, to):
            copy = remote(src, out_ref.at[slot], sems.at[slot], recv.at[slot], to, dp)
            copy.start()
            return copy

        def arrived(slot):
            remote(x_ref, out_ref.at[slot], send_y.at[slot], recv.at[slot], partner, dp).wait_recv()

        sends = []
        if k > 0:
            sends.append(send(x_ref, tp, send_l, tp - 2))
        if k < NZ - 1:
            sends.append(send(x_ref, tp, send_r, tp + 2))
        sends.append(send(x_ref, tp, send_y, partner))
        own = pltpu.make_async_copy(x_ref, out_ref.at[tp], own_sem)
        own.start()
        for side, zz in ARRIVALS[k]:
            slot = 2 * zz + y
            arrived(slot)
            if side == "L" and k < NZ - 1:
                sends.append(send(out_ref.at[slot], slot, send_r, tp + 2))
            if side == "R" and k > 0:
                sends.append(send(out_ref.at[slot], slot, send_l, tp - 2))
            sends.append(send(out_ref.at[slot], slot, send_y, partner))
        for zz in range(NZ):
            arrived(2 * zz + 1 - y)
        own.wait()
        for copy in sends:
            copy.wait_send()

    for k in range(NZ):
        pl.when(z == k)(functools.partial(program, k))


def plane_gather(x, collective_id):
    return pl.pallas_call(
        gather_kernel,
        out_shape=jax.ShapeDtypeStruct((2 * NZ,) + x.shape, x.dtype),
        in_specs=[ANY],
        out_specs=ANY,
        scratch_shapes=[pltpu.SemaphoreType.DMA] + [pltpu.SemaphoreType.DMA((2 * NZ,))] * 4,
        compiler_params=pltpu.CompilerParams(collective_id=collective_id, has_side_effects=True),
        name="plane_gather",
    )(x)


def weight_gather_kernel(x_ref, out_ref, own_sem, send_y, send_l, send_r, send_c, recv):
    tp, dp, z, y = place()
    partner = tp + 1 - 2 * y
    core = dp % 2
    twin = dp + 1 - 2 * core

    def program(k):
        line_barrier(k, tp, dp, [(tp, twin)])

        def send(src, slot, sems, to, to_dp):
            copy = remote(src, out_ref.at[slot, core], sems.at[slot], recv.at[slot, core], to, to_dp)
            copy.start()
            return copy

        def arrived(slot, half):
            remote(x_ref.at[0], out_ref.at[slot, half], send_y.at[slot], recv.at[slot, half], partner, dp).wait_recv()

        mine = x_ref.at[core]
        sends = []
        if k > 0:
            sends.append(send(mine, tp, send_l, tp - 2, dp))
        if k < NZ - 1:
            sends.append(send(mine, tp, send_r, tp + 2, dp))
        sends.append(send(mine, tp, send_y, partner, dp))
        own = pltpu.make_async_copy(x_ref, out_ref.at[tp], own_sem)
        own.start()
        across = [k] + [zz for _, zz in ARRIVALS[k]]
        for n, (side, zz) in enumerate(ARRIVALS[k]):
            slot = 2 * zz + y
            arrived(slot, core)
            if side == "L" and k < NZ - 1:
                sends.append(send(out_ref.at[slot, core], slot, send_r, tp + 2, dp))
            if side == "R" and k > 0:
                sends.append(send(out_ref.at[slot, core], slot, send_l, tp - 2, dp))
            sends.append(send(out_ref.at[slot, core], slot, send_y, partner, dp))
            sends.append(send(out_ref.at[slot, core], slot, send_c, tp, twin))
            slot = 2 * across[n] + 1 - y
            arrived(slot, core)
            sends.append(send(out_ref.at[slot, core], slot, send_c, tp, twin))
        slot = 2 * across[-1] + 1 - y
        arrived(slot, core)
        sends.append(send(out_ref.at[slot, core], slot, send_c, tp, twin))
        for zz in range(NZ):
            if zz != k:
                arrived(2 * zz + y, 1 - core)
            arrived(2 * zz + 1 - y, 1 - core)
        own.wait()
        for copy in sends:
            copy.wait_send()

    for k in range(NZ):
        pl.when(z == k)(functools.partial(program, k))


def weight_gather(x, collective_id):
    rows, width = x.shape
    halves = x.reshape(2, rows // 2, width)
    out = pl.pallas_call(
        weight_gather_kernel,
        out_shape=jax.ShapeDtypeStruct((2 * NZ,) + halves.shape, x.dtype),
        in_specs=[ANY],
        out_specs=ANY,
        scratch_shapes=[pltpu.SemaphoreType.DMA] + [pltpu.SemaphoreType.DMA((2 * NZ,))] * 4
        + [pltpu.SemaphoreType.DMA((2 * NZ, 2))],
        compiler_params=pltpu.CompilerParams(collective_id=collective_id, has_side_effects=True),
        name="weight_gather",
    )(halves)
    return out.reshape(2 * NZ, rows, width)


def add_into(acc, other):
    rows = acc.shape[0]
    step = 64 if rows % 64 == 0 else rows

    def body(n, carry):
        at = pl.ds(pl.multiple_of(n * step, step), step)
        acc[at, :] = acc[at, :] + other[at, :]
        return carry

    lax.fori_loop(0, rows // step, body, 0)


def scatter_kernel(p_ref, out_ref, acc, from_y, from_l, from_r, load_sem, out_sem, send_y, send_l, send_r, recv_y, recv_l, recv_r):
    tp, dp, z, y = place()
    partner = tp + 1 - 2 * y

    def program(k):
        line_barrier(k, tp, dp, [])
        sends = []
        loads = []
        for zz in REDUCE_ORDER[k]:
            copy = remote(p_ref.at[2 * zz + 1 - y], from_y.at[zz], send_y.at[zz], recv_y.at[zz], partner, dp)
            copy.start()
            sends.append(copy)
        for zz in REDUCE_ORDER[k]:
            load = pltpu.make_async_copy(p_ref.at[2 * zz + y], acc.at[zz], load_sem.at[zz])
            load.start()
            loads.append(load)
        for n, zz in enumerate(REDUCE_ORDER[k]):
            loads[n].wait()
            remote(acc.at[zz], from_y.at[zz], send_y.at[zz], recv_y.at[zz], partner, dp).wait_recv()
            add_into(acc.at[zz], from_y.at[zz])
            if zz >= k and k > 0:
                remote(acc.at[zz], from_l.at[zz], send_l.at[zz], recv_l.at[zz], partner, dp).wait_recv()
                add_into(acc.at[zz], from_l.at[zz])
            if zz <= k and k < NZ - 1:
                remote(acc.at[zz], from_r.at[zz], send_r.at[zz], recv_r.at[zz], partner, dp).wait_recv()
                add_into(acc.at[zz], from_r.at[zz])
            if zz > k:
                copy = remote(acc.at[zz], from_l.at[zz], send_r.at[zz], recv_l.at[zz], tp + 2, dp)
                copy.start()
                sends.append(copy)
            if zz < k:
                copy = remote(acc.at[zz], from_r.at[zz], send_l.at[zz], recv_r.at[zz], tp - 2, dp)
                copy.start()
                sends.append(copy)
        out = pltpu.make_async_copy(acc.at[k], out_ref, out_sem)
        out.start()
        out.wait()
        for copy in sends:
            copy.wait_send()

    for k in range(NZ):
        pl.when(z == k)(functools.partial(program, k))


def plane_scatter(p, collective_id):
    _, rows, width = p.shape
    line = (NZ, rows, width)
    return pl.pallas_call(
        scatter_kernel,
        out_shape=jax.ShapeDtypeStruct((rows, width), p.dtype),
        in_specs=[ANY],
        out_specs=ANY,
        scratch_shapes=[pltpu.VMEM(line, p.dtype)] * 4
        + [pltpu.SemaphoreType.DMA((NZ,)), pltpu.SemaphoreType.DMA]
        + [pltpu.SemaphoreType.DMA((NZ,))] * 6,
        compiler_params=pltpu.CompilerParams(collective_id=collective_id, has_side_effects=True),
        name="plane_scatter",
    )(p)


def weight_scatter_kernel(p_ref, out_ref, acc, from_c, from_y, from_l, from_r, from_x, load_sem, out_sem, send_c, send_y, send_l, send_r,
                          last_send, recv_c, recv_y, recv_l, recv_r, last_recv):
    tp, dp, z, y = place()
    partner = tp + 1 - 2 * y
    core = dp % 2
    twin = dp + 1 - 2 * core
    facing = lax.rem(dp + 2, 4)

    def program(k):
        line_barrier(k, tp, dp, [(tp, twin), (tp, facing)])
        sends = []
        for zz in REDUCE_ORDER[k]:
            for slot in (2 * zz + 1 - y, 2 * zz + y):
                copy = remote(p_ref.at[slot, 1 - core], from_c.at[slot], send_c.at[slot], recv_c.at[slot], tp, twin)
                copy.start()
                sends.append(copy)
                pltpu.make_async_copy(p_ref.at[slot, core], acc.at[slot], load_sem.at[slot]).start()

        def chip_sum(slot):
            pltpu.make_async_copy(p_ref.at[slot, core], acc.at[slot], load_sem.at[slot]).wait()
            remote(acc.at[slot], from_c.at[slot], send_c.at[slot], recv_c.at[slot], tp, twin).wait_recv()
            add_into(acc.at[slot], from_c.at[slot])

        for zz in REDUCE_ORDER[k]:
            slot = 2 * zz + 1 - y
            chip_sum(slot)
            copy = remote(acc.at[slot], from_y.at[zz], send_y.at[zz], recv_y.at[zz], partner, dp)
            copy.start()
            sends.append(copy)
        for zz in REDUCE_ORDER[k]:
            chip_sum(2 * zz + y)
        for zz in REDUCE_ORDER[k]:
            slot = 2 * zz + y
            line = acc.at[slot]
            remote(line, from_y.at[zz], send_y.at[zz], recv_y.at[zz], partner, dp).wait_recv()
            add_into(line, from_y.at[zz])
            if zz >= k and k > 0:
                remote(line, from_l.at[zz], send_l.at[zz], recv_l.at[zz], partner, dp).wait_recv()
                add_into(line, from_l.at[zz])
            if zz <= k and k < NZ - 1:
                remote(line, from_r.at[zz], send_r.at[zz], recv_r.at[zz], partner, dp).wait_recv()
                add_into(line, from_r.at[zz])
            if zz > k:
                copy = remote(line, from_l.at[zz], send_r.at[zz], recv_l.at[zz], tp + 2, dp)
                copy.start()
                sends.append(copy)
            if zz < k:
                copy = remote(line, from_r.at[zz], send_l.at[zz], recv_r.at[zz], tp - 2, dp)
                copy.start()
                sends.append(copy)
        total = acc.at[2 * k + y]
        copy = remote(total, from_x, last_send.at[0], last_recv.at[0], tp, facing)
        copy.start()
        copy.wait()
        add_into(total, from_x)
        copy = remote(total, out_ref.at[core], last_send.at[1], last_recv.at[1], tp, twin)
        copy.start()
        out = pltpu.make_async_copy(total, out_ref.at[core], out_sem)
        out.start()
        copy.wait_send()
        remote(total, out_ref.at[1 - core], last_send.at[1], last_recv.at[1], tp, twin).wait_recv()
        out.wait()
        for copy in sends:
            copy.wait_send()

    for k in range(NZ):
        pl.when(z == k)(functools.partial(program, k))


def weight_scatter(p, collective_id):
    _, rows, width = p.shape
    half = (rows // 2, width)
    out = pl.pallas_call(
        weight_scatter_kernel,
        out_shape=jax.ShapeDtypeStruct((2,) + half, p.dtype),
        in_specs=[ANY],
        out_specs=ANY,
        scratch_shapes=[pltpu.VMEM((2 * NZ,) + half, p.dtype)] * 2 + [pltpu.VMEM((NZ,) + half, p.dtype)] * 3
        + [pltpu.VMEM(half, p.dtype)]
        + [pltpu.SemaphoreType.DMA((2 * NZ,)), pltpu.SemaphoreType.DMA]
        + ([pltpu.SemaphoreType.DMA((2 * NZ,))] + [pltpu.SemaphoreType.DMA((NZ,))] * 3 + [pltpu.SemaphoreType.DMA((2,))]) * 2,
        compiler_params=pltpu.CompilerParams(collective_id=collective_id, has_side_effects=True),
        name="weight_scatter",
    )(p.reshape((2 * NZ, 2) + half))
    return out.reshape(rows, width)


def plane_barrier(tp, dp, others):
    peers = [(lax.rem(tp + n, 2 * NZ), dp) for n in range(1, 2 * NZ)] + others
    for peer in peers:
        signal(*peer)
    pl.semaphore_wait(pltpu.get_barrier_semaphore(), len(peers))


def swap_kernel(spread, x_ref, out_ref, own_sem, send, recv):
    tp, dp, _, _ = place()
    plane_barrier(tp, dp, [])
    copies = []
    for n in range(1, 2 * NZ):
        to = lax.rem(tp + n, 2 * NZ)
        copy = remote(x_ref if spread else x_ref.at[to], out_ref.at[tp], send.at[to], recv.at[tp], to, dp)
        copy.start()
        copies.append(copy)
    own = pltpu.make_async_copy(x_ref if spread else x_ref.at[tp], out_ref.at[tp], own_sem)
    own.start()
    for n in range(1, 2 * NZ):
        source = lax.rem(tp + n, 2 * NZ)
        remote(out_ref.at[source], out_ref.at[source], send.at[source], recv.at[source], source, dp).wait_recv()
    own.wait()
    for copy in copies:
        copy.wait_send()


def plane_swap(x, spread, collective_id):
    return pl.pallas_call(
        functools.partial(swap_kernel, spread),
        out_shape=jax.ShapeDtypeStruct((2 * NZ,) + x.shape if spread else x.shape, x.dtype),
        in_specs=[ANY],
        out_specs=ANY,
        scratch_shapes=[pltpu.SemaphoreType.DMA] + [pltpu.SemaphoreType.DMA((2 * NZ,))] * 2,
        compiler_params=pltpu.CompilerParams(collective_id=collective_id, has_side_effects=True),
        name="plane_spread" if spread else "plane_swap",
    )(x)


def row_return_kernel(x_ref, out_ref, own_sem, send, send_c, send_x, recv):
    tp, dp, _, _ = place()
    core = dp % 2
    twin = dp + 1 - 2 * core
    facing = lax.rem(dp + 2, 4)
    plane_barrier(tp, dp, [(tp, twin), (tp, facing)])
    copies = []

    def forward(group, source, sems, to_dp):
        copy = remote(out_ref.at[group, source], out_ref.at[group, source], sems.at[source], recv.at[group, source], tp, to_dp)
        copy.start()
        copies.append(copy)

    def arrived(group, source):
        remote(out_ref.at[group, source], out_ref.at[group, source], send.at[source], recv.at[group, source], tp, twin).wait_recv()

    for n in range(1, 2 * NZ):
        to = lax.rem(tp + n, 2 * NZ)
        copy = remote(x_ref.at[to], out_ref.at[dp, tp], send.at[to], recv.at[dp, tp], to, dp)
        copy.start()
        copies.append(copy)
    own = pltpu.make_async_copy(x_ref.at[tp], out_ref.at[dp, tp], own_sem)
    own.start()
    own.wait()
    forward(dp, tp, send_x, facing)
    forward(dp, tp, send_c.at[0], twin)
    for n in range(1, 2 * NZ):
        source = lax.rem(tp + 2 * NZ - n, 2 * NZ)
        arrived(dp, source)
        forward(dp, source, send_x, facing)
        forward(dp, source, send_c.at[0], twin)
    for n in range(2 * NZ):
        source = lax.rem(tp + 2 * NZ - n, 2 * NZ)
        arrived(facing, source)
        forward(facing, source, send_c.at[1], twin)
    for n in range(2 * NZ):
        source = lax.rem(tp + 2 * NZ - n, 2 * NZ)
        arrived(twin, source)
        arrived(lax.rem(twin + 2, 4), source)
    for copy in copies:
        copy.wait_send()


def row_return(x, collective_id):
    return pl.pallas_call(
        row_return_kernel,
        out_shape=jax.ShapeDtypeStruct((4,) + x.shape, x.dtype),
        in_specs=[ANY],
        out_specs=ANY,
        scratch_shapes=[pltpu.SemaphoreType.DMA, pltpu.SemaphoreType.DMA((2 * NZ,)), pltpu.SemaphoreType.DMA((2, 2 * NZ)),
                        pltpu.SemaphoreType.DMA((2 * NZ,)), pltpu.SemaphoreType.DMA((4, 2 * NZ))],
        compiler_params=pltpu.CompilerParams(collective_id=collective_id, has_side_effects=True),
        name="row_return",
    )(x)


def pair_kernel(x_ref, out_ref, send, recv):
    tp, dp, _, y = place()
    partner = tp + 1 - 2 * y
    signal(partner, dp)
    pl.semaphore_wait(pltpu.get_barrier_semaphore(), 1)
    copy = remote(x_ref, out_ref, send, recv, partner, dp)
    copy.start()
    copy.wait()


def pair_swap(x, collective_id):
    return pl.pallas_call(
        pair_kernel,
        out_shape=jax.ShapeDtypeStruct(x.shape, x.dtype),
        in_specs=[VMEM],
        out_specs=VMEM,
        scratch_shapes=[pltpu.SemaphoreType.DMA, pltpu.SemaphoreType.DMA],
        compiler_params=pltpu.CompilerParams(collective_id=collective_id, has_side_effects=True),
        name="pair_swap",
    )(x)


def norm_fwd(x_f32, scale):
    centered = x_f32 - jnp.mean(x_f32, axis=-1, keepdims=True)
    inv_std = lax.rsqrt(jnp.mean(centered * centered, axis=-1, keepdims=True) + LN_EPS)
    x_hat = centered * inv_std
    return (x_hat * scale).astype(BF16), x_hat, inv_std


def norm_bwd(d_out, x_hat, inv_std, scale):
    d_scale = jnp.sum(d_out * x_hat, axis=0)
    d_hat = d_out * scale
    d_in = inv_std * (d_hat - jnp.mean(d_hat, axis=-1, keepdims=True) - x_hat * jnp.mean(d_hat * x_hat, axis=-1, keepdims=True))
    return d_in, d_scale


def rope_tables(positions, head_dim):
    inv_freq = ROPE_BASE ** (-jnp.arange(0, head_dim, 2).astype(F32) / head_dim)
    angles = positions.astype(F32)[:, None] * inv_freq[None, :]
    return jnp.cos(angles), jnp.sin(angles)


def rotate(x_in, cos_t, sin_t):
    half_dim = x_in.shape[-1] // 2
    x_lo = x_in[..., :half_dim]
    x_hi = x_in[..., half_dim:]
    return jnp.concatenate([x_lo * cos_t - x_hi * sin_t, x_hi * cos_t + x_lo * sin_t], axis=-1)


def adam_update(param_in, grad_in, mom_in, vel_in):
    mom_new = BETA_ONE * mom_in + (1.0 - BETA_ONE) * grad_in
    vel_new = BETA_TWO * vel_in + (1.0 - BETA_TWO) * grad_in * grad_in
    return param_in - LEARN_RATE * mom_new / (jnp.sqrt(vel_new) + ADAM_EPS), mom_new, vel_new


def dot(spec, a, b):
    return jnp.einsum(spec, a, b, preferred_element_type=F32)


def solution(mesh):
    param_specs = (P('tp', None), P(None, None), P(None, 'tp'), P(None, None, None), P('tp', None), P(None, None, 'tp'), P('tp', None))
    n_tp = mesh.shape['tp']
    n_dp = mesh.shape['dp']

    def local_step(tokens, labels, *state_arrays):
        embed, ln_scales, w_q, w_kv, w_o, w_gu, w_down = state_arrays[0:7]
        batch_loc, seq_len = tokens.shape
        vocab_loc, d_model = embed.shape
        head_dim = w_kv.shape[2]
        q_loc = w_q.shape[1]
        f_loc = w_down.shape[0]
        heads = n_tp * q_loc // head_dim
        tok_loc = batch_loc * seq_len
        tok_total = tok_loc * n_dp
        own = tok_loc // n_tp
        tp_rank = lax.axis_index('tp')
        half = tp_rank % 2
        emb_b = embed.astype(BF16)

        all_tokens = lax.all_gather(tokens, 'dp').reshape(n_dp * n_tp, own)
        strict = (jnp.arange(own)[:, None] > jnp.arange(own)[None, :]).astype(BF16)

        def routing(chunks):
            shard = chunks // vocab_loc
            row = chunks - shard * vocab_loc
            hot = (shard[:, :, None] == jnp.arange(n_tp)[None, None, :])
            before = dot('rs,nsj->nrj', strict, hot.astype(BF16))
            rank = jnp.sum(jnp.where(hot, before, 0.0), axis=-1).astype(jnp.int32)
            most = jnp.max(jnp.sum(hot.astype(jnp.int32), axis=1))
            return shard, row, rank, (most + CAP - 1) // CAP

        chunks = tokens.reshape(n_tp, own)
        shard, row, rank, _ = routing(chunks)
        shard_all, row_all, rank_all, rounds_all = routing(all_tokens)
        slots = jnp.arange(CAP)
        my_shard = lax.dynamic_index_in_dim(shard, tp_rank, 0, keepdims=False)
        my_rank = lax.dynamic_index_in_dim(rank, tp_rank, 0, keepdims=False)

        def fetch(step, x_sum, collective_id):
            here = (shard[:, None, :] == tp_rank) & (rank[:, None, :] == slots[None, :, None] + step * CAP)
            ids = jnp.sum(jnp.where(here, row[:, None, :], 0), axis=-1).reshape(-1)
            rows_out = jnp.take(embed, ids, axis=0).astype(BF16).astype(F32).reshape(n_tp, CAP, d_model)
            rows_in = plane_swap(rows_out, False, collective_id).reshape(n_tp * CAP, d_model).astype(BF16)
            pick = (my_shard[:, None, None] == jnp.arange(n_tp)[None, :, None]) & (my_rank[:, None, None] == slots[None, None, :] + step * CAP)
            return x_sum + dot('rc,cd->rd', pick.reshape(own, n_tp * CAP).astype(BF16), rows_in)

        x_zero = fetch(0, jnp.zeros((own, d_model), F32), 0)
        x_zero = lax.while_loop(lambda s: s[0] < rounds_all, lambda s: (s[0] + 1, fetch(s[0], s[1], 1)), (jnp.int32(1), x_zero))[1]

        w_rows = jnp.concatenate([w_q.T, w_o, w_gu.transpose(0, 2, 1).reshape(2 * f_loc, d_model), w_down], axis=0)
        w_all = weight_gather(w_rows, 2).astype(BF16)
        cuts = (q_loc, 2 * q_loc, 2 * q_loc + f_loc, 2 * q_loc + 2 * f_loc)
        wq_t = w_all[:, :cuts[0]].reshape(-1, d_model)
        wo_b = w_all[:, cuts[0]:cuts[1]].reshape(-1, d_model)
        wg_t = w_all[:, cuts[1]:cuts[2]].reshape(-1, d_model)
        wu_t = w_all[:, cuts[2]:cuts[3]].reshape(-1, d_model)
        wd_b = w_all[:, cuts[3]:].reshape(-1, d_model)
        wkv_b = w_kv.astype(BF16)

        u_norm, u_hat, u_inv = norm_fwd(x_zero, ln_scales[0])
        q_pos = half * own + jnp.arange(own)
        cos_t, sin_t = rope_tables(q_pos, head_dim)
        q_raw = dot('rd,nd->rn', u_norm, wq_t).reshape(own, heads, head_dim)
        queries = rotate(q_raw, cos_t[:, None, :], sin_t[:, None, :]).astype(BF16)
        kv_raw = dot('rd,cde->cre', u_norm, wkv_b)
        kv_own = jnp.concatenate([rotate(kv_raw[0], cos_t, sin_t), kv_raw[1]], axis=-1)
        kv_other = pair_swap(kv_own, 3)
        kv_seq = jnp.concatenate([jnp.where(half == 0, kv_own, kv_other), jnp.where(half == 0, kv_other, kv_own)], axis=0).astype(BF16)
        keys = kv_seq[:, :head_dim]
        values = kv_seq[:, head_dim:]
        causal = q_pos[:, None] >= jnp.arange(2 * own)[None, :]
        scores = dot('qhe,ke->hqk', queries, keys) * head_dim ** -0.5
        prob_f32 = jax.nn.softmax(jnp.where(causal, scores, -1e30), axis=-1)
        prob_b16 = prob_f32.astype(BF16)
        context = dot('hqk,ke->qhe', prob_b16, values).astype(BF16).reshape(own, heads * head_dim)
        att_out = dot('rf,fe->re', context, wo_b)
        gate = dot('rd,fd->rf', u_norm, wg_t)
        up = dot('rd,fd->rf', u_norm, wu_t)
        gate_sig = jax.nn.sigmoid(gate)
        hidden = (gate * gate_sig * up).astype(BF16)
        x_one = x_zero + att_out + dot('rf,fd->rd', hidden, wd_b)
        f_own, f_hat, f_inv = norm_fwd(x_one, ln_scales[1])

        f_norm = plane_gather(f_own.astype(F32), 4).reshape(tok_loc, d_model).astype(BF16)
        logit_scale = d_model ** -0.5
        logits = dot('rd,vd->rv', f_norm, emb_b) * logit_scale
        lab_loc = labels.reshape(tok_loc) - tp_rank * vocab_loc
        lab_hit = jnp.arange(vocab_loc)[None, :] == lab_loc[:, None]
        row_max = jnp.max(logits, axis=-1)
        exp_sum = jnp.sum(jnp.exp(logits - row_max[:, None]), axis=-1)
        lab_val = jnp.sum(jnp.where(lab_hit, logits, 0.0), axis=-1)
        stats = plane_swap(jnp.stack([row_max, exp_sum, lab_val]).reshape(3 * tok_loc // 128, 128), True, 5).reshape(n_tp, 3, tok_loc)
        top = jnp.max(stats[:, 0], axis=0)
        log_norm = top + jnp.log(jnp.sum(stats[:, 1] * jnp.exp(stats[:, 0] - top), axis=0))
        tok_loss = log_norm - jnp.sum(stats[:, 2], axis=0) + LOGIT_ZLOSS * log_norm * log_norm
        loss_part = jnp.sum(tok_loss) / (n_tp * tok_total)

        coef = 1.0 + 2.0 * LOGIT_ZLOSS * log_norm
        d_logits = ((jnp.exp(logits - log_norm[:, None]) * coef[:, None] - lab_hit.astype(F32)) * (logit_scale / tok_total)).astype(BF16)
        d_fin_part = dot('rv,vd->rd', d_logits, emb_b).reshape(n_tp, own, d_model)
        g_head = lax.psum(dot('rv,rd->vd', d_logits, f_norm), 'dp')
        d_fin = plane_scatter(d_fin_part, 6)
        d_one, g_ln_fin = norm_bwd(d_fin, f_hat, f_inv, ln_scales[1])
        d_one_b = d_one.astype(BF16)

        d_hidden = dot('rd,fd->rf', d_one_b, wd_b)
        g_down = dot('rf,rd->fd', hidden, d_one_b)
        d_gate = (d_hidden * up * gate_sig * (1.0 + gate * (1.0 - gate_sig))).astype(BF16)
        d_up = (d_hidden * gate * gate_sig).astype(BF16)
        g_gate = dot('rf,rd->fd', d_gate, u_norm)
        g_up = dot('rf,rd->fd', d_up, u_norm)
        d_u_mlp = dot('rf,fd->rd', d_gate, wg_t) + dot('rf,fd->rd', d_up, wu_t)

        d_context = dot('re,fe->rf', d_one_b, wo_b).astype(BF16).reshape(own, heads, head_dim)
        g_o = dot('rf,re->fe', context, d_one_b)
        d_probs = dot('qhe,ke->hqk', d_context, values)
        d_values = dot('hqk,qhe->ke', prob_b16, d_context)
        d_scores = (prob_f32 * (d_probs - jnp.sum(d_probs * prob_f32, axis=-1, keepdims=True)) * head_dim ** -0.5).astype(BF16)
        d_queries = dot('hqk,ke->qhe', d_scores, keys)
        d_keys = dot('hqk,qhe->ke', d_scores, queries)
        d_kv_seq = jnp.concatenate([d_keys, d_values], axis=-1)
        d_kv_lo = d_kv_seq[:own]
        d_kv_hi = d_kv_seq[own:]
        d_kv_own = jnp.where(half == 0, d_kv_lo, d_kv_hi) + pair_swap(jnp.where(half == 0, d_kv_hi, d_kv_lo), 7)
        d_q_raw = rotate(d_queries, cos_t[:, None, :], -sin_t[:, None, :]).astype(BF16).reshape(own, heads * head_dim)
        d_kv = jnp.stack([rotate(d_kv_own[:, :head_dim], cos_t, -sin_t), d_kv_own[:, head_dim:]]).astype(BF16)
        g_q_t = dot('rn,rd->nd', d_q_raw, u_norm)
        g_kv_part = dot('cre,rd->cde', d_kv, u_norm)
        d_u = dot('rn,nd->rd', d_q_raw, wq_t) + dot('cre,cde->rd', d_kv, wkv_b) + d_u_mlp
        d_zero_norm, g_ln_in = norm_bwd(d_u, u_hat, u_inv, ln_scales[0])
        d_zero = d_one + d_zero_norm

        my_row_shard = my_shard

        def give_back(step, g_look, collective_id):
            mine = (my_row_shard[None, None, :] == jnp.arange(n_tp)[:, None, None]) & (my_rank[None, None, :] == slots[None, :, None] + step * CAP)
            ids = jnp.sum(jnp.where(mine, jnp.arange(own)[None, None, :], 0), axis=-1).reshape(-1)
            rows_out = jnp.take(d_zero, ids, axis=0).reshape(n_tp, CAP, d_model)
            rows_in = row_return(rows_out, collective_id).reshape(-1, d_model)
            here = (shard_all[:, None, :] == tp_rank) & (rank_all[:, None, :] == slots[None, :, None] + step * CAP)
            row_id = jnp.where(jnp.any(here, axis=-1), jnp.sum(jnp.where(here, row_all[:, None, :], 0), axis=-1), vocab_loc).reshape(-1)
            return g_look.at[row_id].add(rows_in, mode='drop')

        g_look = give_back(0, jnp.zeros((vocab_loc, d_model), F32), 8)
        g_look = lax.while_loop(lambda s: s[0] < rounds_all, lambda s: (s[0] + 1, give_back(s[0], s[1], 9)), (jnp.int32(1), g_look))[1]

        g_gu_t = jnp.stack([g_gate.reshape(n_tp, f_loc, d_model), g_up.reshape(n_tp, f_loc, d_model)], axis=1)
        g_rows = jnp.concatenate([g_q_t.reshape(n_tp, q_loc, d_model), g_o.reshape(n_tp, q_loc, d_model),
                                  g_gu_t.reshape(n_tp, 2 * f_loc, d_model), g_down.reshape(n_tp, f_loc, d_model)], axis=1)
        g_shard = weight_scatter(g_rows, 10)
        g_kv, g_ln, loss = lax.psum((g_kv_part, jnp.stack([g_ln_in, g_ln_fin]), loss_part), ('tp', 'dp'))
        gradients = (g_head + g_look, g_ln, g_shard[:cuts[0]].T, g_kv, g_shard[cuts[0]:cuts[1]],
                     g_shard[cuts[1]:cuts[3]].reshape(2, f_loc, d_model).transpose(0, 2, 1), g_shard[cuts[3]:])

        outs_p = []
        outs_m = []
        outs_v = []
        for index in range(7):
            new_p, new_m, new_v = adam_update(state_arrays[index], gradients[index], state_arrays[7 + index], state_arrays[14 + index])
            outs_p.append(new_p)
            outs_m.append(new_m)
            outs_v.append(new_v)
        return tuple(outs_p) + tuple(outs_m) + tuple(outs_v) + (loss,)

    return jax.shard_map(local_step, mesh=mesh, in_specs=(P('dp', None), P('dp', None)) + param_specs * 3,
                         out_specs=param_specs * 3 + (P(),), check_vma=False)
```

time: 1880 us -> 1120 us (0.60)
  waiting for transfers between devices: 1320 us -> 18.7 us
  Pallas kernels: 0 us -> 530 us
  blocking collectives: 74.6 us -> 45.9 us
    psum x6 -> x2, waiting for transfers between devices: 1320 us -> 18.7 us  [the longest x1 18.7 us: local_step(): g_head = lax.psum(dot('rv,rd->vd', d_logits, f_norm), 'dp')]
    pallas_call x0 -> x9, Pallas kernels: none -> 530 us  [the longest x1 141 us: weight_scatter(): pl.pallas_call(weight_scatter_kernel, out_shape=jax.ShapeDtypeStruct((2,)...]
    convert_element_type x5 -> x10, other arithmetic: 18.3 us -> 71.4 us  [the longest x1 50.9 us: local_step(): ((jnp.exp(logits - log_norm[:, None]) * coef[:, None] - lab_hit.astype(F3...]
    pmax x1 -> x0, blocking collectives: 34.8 us -> none  [local_step(): row_max = lax.pmax(jnp.max(logits, axis=-1), 'tp')]
    reduce_sum x5 -> x9, other arithmetic: 52.8 us -> 39.1 us  [the longest x1 32.8 us: local_step(): exp_sum = jnp.sum(jnp.exp(logits - row_max[:, None]), axis=-1)]
    dot_general x24 -> x28, matrix products: 220 us -> 226 us  [dot(): return jnp.einsum(spec, a, b, preferred_element_type=F32)]
    psum x2 -> x1, blocking collectives: 39.7 us -> 39.7 us  [local_step(): lax.psum((g_kv_part, jnp.stack([g_ln_in, g_ln_fin]), loss_part), ('tp', '...]
  transfers between devices with their start and end apart: 6 -> 2, of which waited for: 6 -> 1; matrix products, arithmetic and copies ran while one was open for 7% -> 12% of each run, Pallas kernels for 0% -> 17%
where the time goes in v1:
time: 1120 us; the launch traced here: 1110 us
  Pallas kernels  530 us (47%)
  other arithmetic  234 us (21%)
  matrix products  228 us (20%)
  blocking collectives  45.9 us (4%)
  local copies, waits for them, and re-layouts  34.2 us (3%)
  waiting for transfers between devices  18.7 us (2%)
  between operations  17.5 us (2%)
    dot_general x28, matrix products, dot(): return jnp.einsum(spec, a, b, preferred_element_type=F32)  226 us
    pallas_call x1, Pallas kernels, weight_scatter(): pl.pallas_call(weight_scatter_kernel, out_shape=jax.ShapeDtypeStruct((2,)...  141 us
    pallas_call x1, Pallas kernels, plane_gather(): pl.pallas_call(gather_kernel, out_shape=jax.ShapeDtypeStruct((2 * NZ,) +...  100 us
    pallas_call x1, Pallas kernels, plane_scatter(): pl.pallas_call(scatter_kernel, out_shape=jax.ShapeDtypeStruct((rows, widt...  94.7 us
    pallas_call x1, Pallas kernels, weight_gather(): pl.pallas_call(weight_gather_kernel, out_shape=jax.ShapeDtypeStruct((2 *...  89.3 us
    convert_element_type x1, other arithmetic, local_step(): ((jnp.exp(logits - log_norm[:, None]) * coef[:, None] - lab_hit.astype(F3...  50.9 us
    pallas_call x1, Pallas kernels, row_return(): pl.pallas_call(row_return_kernel, out_shape=jax.ShapeDtypeStruct((4,) + x...  48 us
    sub x7, other arithmetic, adam_update(): param_in - LEARN_RATE * mom_new / (jnp.sqrt(vel_new) + ADAM_EPS)  47.8 us
  transfers between devices with their start and end apart: 2, of which 1 were waited for; matrix products, arithmetic and copies ran while one was open for 12% of the time, Pallas kernels for 17%

profile of v1, /device:TPU:0, one launch (start us, length us, event | category | flops | bytes accessed | tf_op | source)
XLA Modules:
  0.0 1107.7 jit_solution(12967609131845333872)
XLA Ops:
  8.8 6.2 all-gather.1
  19.9 2.5 pad_maximum_fusion.2
  22.4 89.3 %weight_gather.1 = f32[8,2,448,512]{3,2,1,0:T(8,128)} custom-call(f32[2,448,512]{2,1,0:T(8,128)} %bitcast.269), custom_call_target="tpu_custom_call" | custom-call | tf_op jit(solution)/shard_map/weight_gather/pallas_call | solution.py:169
  111.7 9.2 convert_element_type.139
  121.0 5.6 fusion.148
  126.6 1.9 slice.140
  128.6 8.2 convert.48
  136.8 7.4 gather_fusion.2
  145.5 29.1 %plane_swap.2 = f32[8,96,512]{2,1,0:T(8,128)} custom-call(f32[8,96,512]{2,1,0:T(8,128)} %fusion.71.x_ref), custom_call_target="tpu_custom_call" | custom-call | tf_op jit(solution)/shard_map/plane_swap/pallas_call | solution.py:368
  174.7 2.0 fusion.48
  182.5 1.9 multiply_cosine_fusion
  187.8 1.9 pad_maximum_fusion.8.x_ref
  189.7 10.1 pair_swap.2
  201.0 4.9 fusion.153
  207.9 8.1 fusion.92
  215.9 17.9 %fusion.150 = (f32[8,512]{1,0:T(8,128)S(1)}, f32[8,512,1024]{1,2,0:T(8,128)}) fusion(f32[1024,512,8]{1,0,2:T(8,128)} %fusion.92, pred[512,1024]{0,1:T(8,128)(4,1)S(1)} %copy-done.49), kind=kOutput, calls=%fused_computation.297 | output fusion | flops 25166848 | bytes 34095104 | tf_op jit(solution)/shard_map/sub | solution.py:567
  233.9 7.6 fusion.55
  241.5 3.5 multiply_convert_fusion.3
  250.0 100.0 %plane_gather.1 = f32[8,512,512]{2,1,0:T(8,128)} custom-call(f32[512,512]{1,0:T(8,128)} %fusion.76.x_ref), custom_call_target="tpu_custom_call" | custom-call | tf_op jit(solution)/shard_map/plane_gather/pallas_call | solution.py:101
  350.1 5.9 convert_element_type.147
  355.9 44.8 %multiply_reduce_fusion = (f32[4096]{0:T(1024)S(1)}, f32[4096,6288]{0,1:T(8,128)}) fusion(bf16[4096,512]{1,0:T(8,128)(2,1)} %bitcast.272, f32[6288,512]{1,0:T(8,128)} %param.29), kind=kOutput, calls=%fused_computation.49 | convolution fusion | flops 26428510208 | bytes 120111104 | tf_op jit(solution)/shard_map/rd,vd->rv/dot_general | solution.py:491
  400.7 32.8 %exponential_reduce_fusion = (f32[4096]{0:T(1024)S(1)}, f32[4096]{0:T(1024)S(1)}) fusion(f32[4096,6288]{0,1:T(8,128)} %get-tuple-element.302, f32[4096]{0:T(1024)S(1)} %get-tuple-element.301, s32[4096]{0:T(1024)S(1)} %bitcast.295), kind=kLoop, calls=%fused_computation.48 | loop fusion | flops 154525696 | bytes 103088128 | tf_op jit(solution)/shard_map/reduce_sum | solution.py:584
  434.2 9.0 plane_spread.1
  445.6 50.9 %multiply_convert_fusion = bf16[4096,6288]{0,1:T(8,128)(2,1)} fusion(f32[4096,6288]{0,1:T(8,128)} %get-tuple-element.302, f32[4096]{0:T(1024)S(1)} %multiply_add_fusion.7, f32[4096]{0:T(1024)S(1)} %get-tuple-element.257, s32[4096]{0:T(1024)S(1)} %bitcast.296), kind=kLoop, calls=%fused_computation.45 | loop fusion | flops 206045184 | bytes 154583040 | tf_op jit(solution)/shard_map/convert_element_type | solution.py:593
  496.5 37.6 %fusion.40 = f32[4096,512]{1,0:T(8,128)} fusion(bf16[4096,6288]{0,1:T(8,128)(2,1)} %multiply_convert_fusion, f32[6288,512]{1,0:T(8,128)} %param.29), kind=kOutput, calls=%fused_computation.85 | convolution fusion | flops 26377003008 | bytes 72777728 | tf_op jit(solution)/shard_map/rv,vd->rd/dot_general | solution.py:491
  534.2 94.7 %plane_scatter.1 = f32[512,512]{1,0:T(8,128)} custom-call(f32[8,512,512]{2,1,0:T(8,128)} %bitcast.262), custom_call_target="tpu_custom_call" | custom-call | tf_op jit(solution)/shard_map/plane_scatter/pallas_call | solution.py:241
  629.0 2.3 multiply_reduce_fusion.1
  631.3 2.7 fusion.147
  634.5 9.4 fusion.117
  644.0 2.3 fusion.58
  646.3 22.3 %fusion.61 = f32[1024,64]{1,0:T(8,128)S(1)} fusion(f32[1024,512,8]{1,0,2:T(8,128)} %fusion.117, bf16[512,8,32]{0,2,1:T(8,128)(2,1)S(1)} %copy-done.36, bf16[512,8,32]{0,2,1:T(8,128)(2,1)S(1)} %copy-done.34, f32[8,512,1024]{1,2,0:T(8,128)} %get-tuple-element.298, f32[8,512]{1,0:T(8,128)S(1)} %copy-done.83), kind=kOutput, calls=%fused_computation.112 | convolution fusion | flops 567284736 | bytes 34357248 | tf_op jit(solution)/shard_map/hqk,qhe->ke/dot_general | solution.py:491
  669.6 8.1 pair_swap.3
  681.5 34.4 %fusion.155 = f32[6288,512]{1,0:T(8,128)} fusion(bf16[4096,6288]{0,1:T(8,128)(2,1)} %multiply_convert_fusion, bf16[4096,512]{1,0:T(8,128)(2,1)} %bitcast.273), kind=kOutput, calls=%fused_computation.302 | convolution fusion | flops 26373783552 | bytes 68583424 | tf_op jit(solution)/shard_map/rv,rd->vd/dot_general | solution.py:491
  715.9 25.4 %fusion.47 = f32[512,8,64]{0,2,1:T(8,128)S(1)} fusion(f32[1024,512,8]{1,0,2:T(8,128)} %fusion.117, bf16[512,128]{1,0:T(8,128)(2,1)S(1)} %copy-done.30, bf16[512,128]{1,0:T(8,128)(2,1)S(1)} %copy-done.27, f32[8,512,1024]{1,2,0:T(8,128)} %get-tuple-element.298, f32[8,512]{1,0:T(8,128)S(1)} %copy-done.83), kind=kOutput, calls=%fused_computation.100 | convolution fusion | flops 566498304 | bytes 34881536 | tf_op jit(solution)/shard_map/hqk,ke->qhe/dot_general | solution.py:491
  742.5 5.5 multiply_convert_fusion.1
  749.5 2.7 convolution_bitcast_fusion.1
  755.3 2.3 gather_fusion.3
  759.0 48.0 %row_return.2 = f32[4,8,96,512]{3,2,1,0:T(8,128)} custom-call(f32[8,96,512]{2,1,0:T(8,128)} %broadcast_select_fusion.2.x_ref), custom_call_target="tpu_custom_call" | custom-call | tf_op jit(solution)/shard_map/row_return/pallas_call | solution.py:423
  809.6 24.9 %scatter_custom_fusion.1 = f32[6288,512]{1,0:T(8,128)} fusion(s32[3072]{0:T(1024)S(1)} %bitcast.307, f32[3072,512]{1,0:T(8,128)} %bitcast.270, f32[]{:T(128)} %constant.90.clone.1), kind=kCustom, calls=%fused_computation.69 | custom fusion | flops 1572864 | bytes 12878336 | tf_op jit(solution)/shard_map/scatter-add | solution.py:636
  835.5 3.0 fusion.157
  844.8 5.7 pad_maximum_fusion
  850.5 141.2 %weight_scatter.1 = f32[2,448,512]{2,1,0:T(8,128)} custom-call(f32[8,2,448,512]{3,2,1,0:T(8,128)} %bitcast.252), custom_call_target="tpu_custom_call" | custom-call | tf_op jit(solution)/shard_map/weight_scatter/pallas_call | solution.py:326
  994.2 39.7 %all-reduce = (f32[2,512]{1,0:T(2,128)S(1)}, f32[]{:T(128)}) all-reduce(f32[2,512]{1,0:T(2,128)S(1)} %pad_maximum_fusion.11, f32[]{:T(128)S(6)} %div.126), channel_id=1, replica_groups=mesh['tp'=8,'dp'=4] {'tp','dp'}, use_global_device_ids=true, to_apply=%region_37.38 | all-reduce | flops 1025 | bytes 8200 | tf_op jit(solution)/shard_map/psum | solution.py:645
  1038.7 2.9 divide_subtract_fusion.2
  1041.6 3.5 divide_subtract_fusion.1
  1045.2 1.9 divide_subtract_fusion.3
  1047.1 18.7 %all-reduce.4.cloned.1.call-done = f32[6288,512]{1,0:T(8,128)} async-done(((f32[6288,512]{1,0:T(8,128)}), f32[6288,512]{1,0:T(8,128)}) %all-reduce.4.cloned.1.call-update) | async-done | bytes 12877840 | tf_op jit(solution)/shard_map/psum | solution.py:595
  1065.8 34.6 %divide_subtract_fusion = (f32[6288,512]{1,0:T(8,128)}, f32[6288,512]{1,0:T(8,128)}, f32[6288,512]{1,0:T(8,128)}) fusion(f32[6288,512]{1,0:T(8,128)} %param.29, f32[6288,512]{1,0:T(8,128)} %all-reduce.4.cloned.1.call-done, f32[6288,512]{1,0:T(8,128)} %get-tuple-element.139, f32[6288,512]{1,0:T(8,128)} %param.36, f32[6288,512]{1,0:T(8,128)} %param.43), kind=kLoop, calls=%fused_computation.60 | loop fusion | flops 38633472 | bytes 103022592 | tf_op jit(solution)/shard_map/sub | solution.py:487
  (283 shorter events, 55.7 us)
Async XLA Ops:
  7.2 1038.0 %all-reduce.6.cloned.1.call-start = ((), (), s32[]{:S(2)}) async-start(), calls=%async_computation.1 | async-start | bytes 524288 | tf_op jit(solution)/shard_map/psum | solution.py:645
  18.4 164.1 %copy-start.80 = (f32[32]{0:T(128)}, f32[32]{0:T(128)S(1)}, u32[]{:S(2)}) copy-start(f32[32]{0:T(128)S(1)} %multiply_power_fusion) | copy-start | bytes 388
  177.0 69.3 %copy-start.3 = (f32[512,512]{1,0:T(8,128)}, f32[512,512]{1,0:T(8,128)S(1)}, u32[]{:S(2)}) copy-start(f32[512,512]{1,0:T(8,128)S(1)} %get-tuple-element.138) | copy-start | bytes 3145732
  177.5 70.7 %copy-start.68 = (f32[1,512]{1,0:T(1,128)}, f32[1,512]{1,0:T(1,128)S(1)}, u32[]{:S(2)}) copy-start(f32[1,512]{1,0:T(1,128)S(1)} %get-tuple-element.288) | copy-start | bytes 6148
  178.3 63.2 %copy-start = (bf16[512,512]{1,0:T(8,128)(2,1)}, bf16[512,512]{1,0:T(8,128)(2,1)S(1)}, u32[]{:S(2)}) copy-start(bf16[512,512]{1,0:T(8,128)(2,1)S(1)} %multiply_convert_fusion.5) | copy-start | bytes 1572868
  182.4 18.5 %copy-start.72 = (f32[512]{0:T(512)}, f32[512]{0:T(512)S(1)}, u32[]{:S(2)}) copy-start(f32[512]{0:T(512)S(1)} %get-tuple-element.307) | copy-start | bytes 6148
  184.4 21.5 %copy-start.21 = (f32[512,32]{1,0:T(8,128)S(1)}, f32[512,32]{1,0:T(8,128)}, u32[]{:S(2)}) copy-start(f32[512,32]{1,0:T(8,128)} %get-tuple-element.294) | copy-start | bytes 196612
  206.1 27.8 %copy-start.26 = (bf16[512,128]{1,0:T(8,128)(2,1)}, bf16[512,128]{1,0:T(8,128)(2,1)S(1)}, u32[]{:S(2)}) copy-start(bf16[512,128]{1,0:T(8,128)(2,1)S(1)} %get-tuple-element.276) | copy-start | bytes 393220
  207.2 8.7 copy-start.35
  207.9 8.1 copy-start.49
  215.9 17.9 %copy-start.29 = (bf16[512,128]{1,0:T(8,128)(2,1)S(1)}, bf16[512,128]{1,0:T(8,128)(2,1)}, u32[]{:S(2)}) copy-start(bf16[512,128]{1,0:T(8,128)(2,1)} %copy-done.28) | copy-start | bytes 393220
  233.8 7.7 copy-start.82
  233.8 7.7 copy-start.7
  233.9 7.7 copy-start.23
  355.9 44.8 %copy-start.76 = (s32[4,1024]{1,0:T(4,128)S(1)}, s32[4,1024]{1,0:T(4,128)}, u32[]{:S(2)}) copy-start(s32[4,1024]{1,0:T(4,128)} %param.28) | copy-start | bytes 49156
  534.2 94.8 %copy-start.6 = (f32[512,512]{1,0:T(8,128)S(1)}, f32[512,512]{1,0:T(8,128)}, u32[]{:S(2)}) copy-start(f32[512,512]{1,0:T(8,128)} %copy-done.5) | copy-start | bytes 3145732
  534.2 94.8 %copy-start.63 = (f32[512]{0:T(512)S(1)}, f32[512]{0:T(512)}, u32[]{:S(2)}) copy-start(f32[512]{0:T(512)} %copy-done.62) | copy-start | bytes 6148
  534.2 94.8 %copy-start.69 = (f32[1,512]{1,0:T(1,128)S(1)}, f32[1,512]{1,0:T(1,128)}, u32[]{:S(2)}) copy-start(f32[1,512]{1,0:T(1,128)} %copy-done.68) | copy-start | bytes 6148
  534.2 94.8 %copy-start.71 = (f32[512]{0:T(512)S(1)}, f32[512]{0:T(512)}, u32[]{:S(2)}) copy-start(f32[512]{0:T(512)} %copy-done.70) | copy-start | bytes 6148
  534.2 99.8 %copy-start.22 = (bf16[8,64,512]{2,1,0:T(8,128)(2,1)S(1)}, bf16[8,64,512]{2,1,0:T(8,128)(2,1)}, u32[]{:S(2)}) copy-start(bf16[8,64,512]{2,1,0:T(8,128)(2,1)} %slice.140) | copy-start | bytes 1572868
  534.2 100.3 %copy-start.27 = (bf16[512,128]{1,0:T(8,128)(2,1)S(1)}, bf16[512,128]{1,0:T(8,128)(2,1)}, u32[]{:S(2)}) copy-start(bf16[512,128]{1,0:T(8,128)(2,1)} %copy-done.26) | copy-start | bytes 393220
  534.2 100.3 %copy-start.30 = (bf16[512,128]{1,0:T(8,128)(2,1)S(1)}, bf16[512,128]{1,0:T(8,128)(2,1)}, u32[]{:S(2)}) copy-start(bf16[512,128]{1,0:T(8,128)(2,1)} %copy-done.28) | copy-start | bytes 393220
  631.3 12.7 %slice-start = ((s8[16777216]{0:T(1024)(128)(4,1)}), s8[4194304]{0:T(1024)(128)(4,1)S(1)}, s32[]{:S(2)}) async-start(s8[16777216]{0:T(1024)(128)(4,1)} %bitcast.310), calls=%async_computation.2 | async-start | bytes 8388608
  634.0 108.5 %copy-start.8 = (bf16[512,512]{1,0:T(8,128)(2,1)}, bf16[512,512]{1,0:T(8,128)(2,1)S(1)}, u32[]{:S(2)}) copy-start(bf16[512,512]{1,0:T(8,128)(2,1)S(1)} %get-tuple-element.263) | copy-start | bytes 1572868
  634.5 9.5 slice-start.1
  634.5 9.5 slice-start.2
  634.5 9.4 slice-start.3
  634.5 9.4 copy-start.83
  646.3 32.5 %copy-start.73 = (f32[512]{0:T(512)S(1)}, f32[512]{0:T(512)}, u32[]{:S(2)}) copy-start(f32[512]{0:T(512)} %copy-done.72) | copy-start | bytes 6148
  646.3 32.5 %copy-start.81 = (f32[32]{0:T(128)S(1)}, f32[32]{0:T(128)}, u32[]{:S(2)}) copy-start(f32[32]{0:T(128)} %copy-done.80) | copy-start | bytes 388
  668.7 11.8 %copy-start.1 = (bf16[512,512]{1,0:T(8,128)(2,1)S(1)}, bf16[512,512]{1,0:T(8,128)(2,1)}, u32[]{:S(2)}) copy-start(bf16[512,512]{1,0:T(8,128)(2,1)} %copy-done) | copy-start | bytes 1572868
  681.4 384.3 %all-reduce.4.cloned.1.call-start = ((), (), s32[]{:S(2)}) async-start(), calls=%async_computation | async-start | bytes 25755648 | tf_op jit(solution)/shard_map/psum | solution.py:595
  715.9 25.4 %copy-start.53 = (s32[512]{0:T(512)S(1)}, s32[512]{0:T(512)}, u32[]{:S(2)}) copy-start(s32[512]{0:T(512)} %copy-done.52) | copy-start | bytes 6148
  715.9 25.5 %copy-start.55 = (s32[512]{0:T(512)S(1)}, s32[512]{0:T(512)}, u32[]{:S(2)}) copy-start(s32[512]{0:T(512)} %copy-done.54) | copy-start | bytes 6148
  715.9 25.9 %copy-start.45 = (s32[32,512]{1,0:T(8,128)S(1)}, s32[32,512]{1,0:T(8,128)}, u32[]{:S(2)}) copy-start(s32[32,512]{1,0:T(8,128)} %copy-done.44) | copy-start | bytes 196612
  715.9 26.0 %copy-start.19 = (s32[32,512]{1,0:T(8,128)S(1)}, s32[32,512]{1,0:T(8,128)}, u32[]{:S(2)}) copy-start(s32[32,512]{1,0:T(8,128)} %copy-done.18) | copy-start | bytes 196612
  757.6 50.4 %copy-start.20 = (s32[32,512]{1,0:T(8,128)S(1)}, s32[32,512]{1,0:T(8,128)}, u32[]{:S(2)}) copy-start(s32[32,512]{1,0:T(8,128)} %get-tuple-element.474) | copy-start | bytes 196612
  850.5 143.6 %copy-start.77 = (f32[512]{0:T(512)S(1)}, f32[512]{0:T(512)}, u32[]{:S(2)}) copy-start(f32[512]{0:T(512)} %get-tuple-element.188) | copy-start | bytes 6148
  850.5 143.7 %copy-start.78 = (f32[512]{0:T(512)S(1)}, f32[512]{0:T(512)}, u32[]{:S(2)}) copy-start(f32[512]{0:T(512)} %get-tuple-element.190) | copy-start | bytes 6148
  850.5 183.4 %copy-start.75 = (f32[2,512]{1,0:T(2,128)S(1)}, f32[2,512]{1,0:T(2,128)}, u32[]{:S(2)}) copy-start(f32[2,512]{1,0:T(2,128)} %param.30) | copy-start | bytes 12292
  850.5 183.4 %copy-start.79 = (f32[2,512]{1,0:T(2,128)S(1)}, f32[2,512]{1,0:T(2,128)}, u32[]{:S(2)}) copy-start(f32[2,512]{1,0:T(2,128)} %param.37) | copy-start | bytes 12292
  850.5 184.7 %copy-start.47 = (f32[64,512]{1,0:T(8,128)S(1)}, f32[64,512]{1,0:T(8,128)}, u32[]{:S(2)}) copy-start(f32[64,512]{1,0:T(8,128)} %param.33) | copy-start | bytes 393220
  850.5 184.7 %copy-start.59 = (f32[64,512]{1,0:T(8,128)S(1)}, f32[64,512]{1,0:T(8,128)}, u32[]{:S(2)}) copy-start(f32[64,512]{1,0:T(8,128)} %param.40) | copy-start | bytes 393220
  850.5 186.4 %copy-start.48 = (f32[512,64]{0,1:T(8,128)S(1)}, f32[512,64]{0,1:T(8,128)}, u32[]{:S(2)}) copy-start(f32[512,64]{0,1:T(8,128)} %param.31) | copy-start | bytes 393220
  991.7 49.9 %copy-start.11 = (f32[2,512,256]{2,1,0:T(8,128)S(1)}, f32[2,512,256]{2,1,0:T(8,128)}, u32[]{:S(2)}) copy-start(f32[2,512,256]{2,1,0:T(8,128)} %param.34) | copy-start | bytes 3145732
  994.2 51.0 %copy-start.38 = (f32[2,512,64]{1,2,0:T(8,128)S(1)}, f32[2,512,64]{1,2,0:T(8,128)}, u32[]{:S(2)}) copy-start(f32[2,512,64]{1,2,0:T(8,128)} %param.32) | copy-start | bytes 786436
  994.2 51.0 %copy-start.56 = (f32[2,512,64]{1,2,0:T(8,128)S(1)}, f32[2,512,64]{1,2,0:T(8,128)}, u32[]{:S(2)}) copy-start(f32[2,512,64]{1,2,0:T(8,128)} %param.39) | copy-start | bytes 786436
  994.2 51.0 %copy-start.57 = (f32[2,512,64]{1,2,0:T(8,128)S(1)}, f32[2,512,64]{1,2,0:T(8,128)}, u32[]{:S(2)}) copy-start(f32[2,512,64]{1,2,0:T(8,128)} %param.46) | copy-start | bytes 786436
  (42 other events, 114.8 us)
Sparse Core Ops, SparseCore 0:
  681.6 135.4 all-reduce.5
  820.1 245.6 all-reduce.3

commit v2 on v1

--- a/solution.py
+++ b/solution.py
@@ -454,6 +454,264 @@
     )(x)
 
 
+FORWARD = {
+    0: {1: (("R", 1),), 3: (("R", 2),), 5: (("R", 3),)},
+    1: {1: (("L", 0), ("R", 2)), 3: (("R", 3),)},
+    2: {1: (("R", 3), ("L", 1)), 3: (("L", 0),)},
+    3: {1: (("L", 2),), 3: (("L", 1),), 5: (("L", 0),)},
+}
+REDUCE = {
+    0: {2: (3,), 4: (2,), 6: (1,), 7: (0,)},
+    1: {4: (3,), 6: (2, 0), 7: (1,)},
+    2: {4: (0,), 6: (1, 3), 7: (2,)},
+    3: {2: (0,), 4: (1,), 6: (2,), 7: (3,)},
+}
+SUB = 256
+GROUP = 6
+
+
+def lookup(table, z, step):
+    value = jnp.int32(0)
+    for k in range(NZ):
+        for s in range(2 * NZ):
+            value = value + jnp.where((z == k) & (step == s), table[k][s], 0)
+    return value
+
+
+def head_kernel(scale, token_scale, f_ref, lab_ref, e_ref, dfin_ref, ghead_ref, norm_ref, labsum_ref,
+                e_b, e_t, fbuf, f_b, g_acc, from_y, from_l, from_r, dl, lse_all, load_sem, ag_y, ag_l, ag_r, ag_recv,
+                rs_y, rs_l, rs_r, recv_y, recv_l, recv_r, st_send, st_recv):
+    tp, dp, z, y = place()
+    partner = tp + 1 - 2 * y
+    vocab, width = e_ref.shape
+    own = f_ref.shape[0]
+    whole = vocab // (SUB * GROUP)
+    rest = vocab - whole * SUB * GROUP
+    log2e = 1.4426950408889634
+    slope = scale * log2e
+    blocks = [(j * SUB, SUB) for j in range(GROUP)]
+    tail = [(n, min(SUB, rest - n)) for n in range(0, rest, SUB)]
+
+    plane_barrier(tp, dp, [])
+
+    def send(src, slot, sems, to):
+        remote(src, fbuf.at[slot], sems.at[slot], ag_recv.at[slot], to, dp).start()
+
+    def arrived(slot):
+        remote(f_ref, fbuf.at[slot], ag_y.at[slot], ag_recv.at[slot], partner, dp).wait_recv()
+
+    def first_sends(k):
+        if k > 0:
+            send(f_ref, tp, ag_l, tp - 2)
+        if k < NZ - 1:
+            send(f_ref, tp, ag_r, tp + 2)
+        send(f_ref, tp, ag_y, partner)
+
+    for k in range(NZ):
+        pl.when(z == k)(functools.partial(first_sends, k))
+    load = pltpu.make_async_copy(e_ref, g_acc, load_sem.at[0])
+    load.start()
+    own_copy = pltpu.make_async_copy(f_ref, fbuf.at[tp], load_sem.at[1])
+    own_copy.start()
+    load.wait()
+
+    def prepare(at, size):
+        part = g_acc[at, :]
+        e_b[at, :] = part.astype(BF16)
+        e_t[:, at] = part.T.astype(BF16)
+
+    def prepare_body(n, carry):
+        prepare(pl.ds(pl.multiple_of(n * SUB, SUB), SUB), SUB)
+        return carry
+
+    lax.fori_loop(0, vocab // SUB, prepare_body, 0)
+    if vocab % SUB:
+        prepare(pl.ds(vocab // SUB * SUB, vocab % SUB), vocab % SUB)
+    own_copy.wait()
+
+    def over_blocks(group, carry):
+        def body(n, c):
+            return group(pl.multiple_of(n * SUB * GROUP, SUB * GROUP), blocks, c)
+        carry = lax.fori_loop(0, whole, body, carry)
+        return group(whole * SUB * GROUP, tail, carry) if tail else carry
+
+    order1 = {k: (k,) + tuple(v for pair in zip([a[1] for a in ARRIVALS[k]], [k] + [a[1] for a in ARRIVALS[k]]) for v in pair) + (ARRIVALS[k][-1][1],) for k in range(NZ)}
+    order1 = {k: [2 * zz + (s % 2 == 0 and s > 0 or s == 7) for s, zz in enumerate(order1[k])] for k in range(NZ)}
+
+    def chunk_of(table, step):
+        code = lookup(table, z, step)
+        other = code % 2
+        return code // 2 * 2 + y + other - 2 * y * other
+
+    def gather_step(step, carry):
+        slot = chunk_of(order1, step)
+        for k in range(NZ):
+            for s, shards in FORWARD[k].items():
+                def pass_on(k=k, shards=shards):
+                    for side, zz in shards:
+                        at = 2 * zz + y
+                        arrived(at)
+                        if side == "L" and k < NZ - 1:
+                            send(fbuf.at[at], at, ag_r, tp + 2)
+                        if side == "R" and k > 0:
+                            send(fbuf.at[at], at, ag_l, tp - 2)
+                        send(fbuf.at[at], at, ag_y, partner)
+                pl.when((z == k) & (step == s))(pass_on)
+        pl.when(slot % 2 != y)(lambda: arrived(slot))
+        f_b[slot] = fbuf[slot].astype(BF16)
+        f_now = f_b[slot]
+
+        def group(base, parts, c):
+            top, total = c
+            for first, size in parts:
+                logit = lax.dot_general(e_b[pl.ds(base + first, size), :], f_now, (((1,), (1,)), ((), ())), preferred_element_type=F32)
+                logit = logit.reshape(size // 8, 8, own)
+                new = jnp.maximum(top, jnp.max(logit, axis=0))
+                total = total * jnp.exp2((top - new) * slope) + jnp.sum(jnp.exp2((logit - new[None]) * slope), axis=0)
+                top = new
+            return top, total
+
+        top, total = over_blocks(group, (jnp.full((8, own), -3e38, F32), jnp.zeros((8, own), F32)))
+        most = jnp.max(top, axis=0, keepdims=True)
+        total = jnp.sum(total * jnp.exp2((top - most) * slope), axis=0, keepdims=True)
+        lse_all[tp, pl.ds(slot, 1), :] = most * scale + jnp.log(total)
+        return carry
+
+    lax.fori_loop(0, 2 * NZ, gather_step, 0)
+
+    for n in range(1, 2 * NZ):
+        to = lax.rem(tp + n, 2 * NZ)
+        remote(lse_all.at[tp], lse_all.at[tp], st_send.at[to], st_recv.at[tp], to, dp).start()
+
+    def gathers_done(k):
+        def done(sems, slot):
+            remote(f_ref, fbuf.at[slot], sems.at[slot], ag_recv.at[slot], partner, dp).wait_send()
+        if k > 0:
+            done(ag_l, tp)
+        if k < NZ - 1:
+            done(ag_r, tp)
+        done(ag_y, tp)
+        for side, zz in ARRIVALS[k]:
+            at = 2 * zz + y
+            if side == "L" and k < NZ - 1:
+                done(ag_r, at)
+            if side == "R" and k > 0:
+                done(ag_l, at)
+            done(ag_y, at)
+
+    for k in range(NZ):
+        pl.when(z == k)(functools.partial(gathers_done, k))
+
+    def clear(n, carry):
+        g_acc[pl.ds(pl.multiple_of(n * 16, 16), 16), :] = jnp.zeros((16, width), F32)
+        return carry
+
+    lax.fori_loop(0, vocab // 16, clear, 0)
+    for n in range(1, 2 * NZ):
+        source = lax.rem(tp + n, 2 * NZ)
+        remote(lse_all.at[source], lse_all.at[source], st_send.at[source], st_recv.at[source], source, dp).wait_recv()
+    peak = jnp.max(lse_all[...], axis=0)
+    log_norm = peak + jnp.log(jnp.sum(jnp.exp(lse_all[...] - peak[None]), axis=0))
+    norm_ref[...] = log_norm
+
+    order2 = {k: [2 * zz + 1 - s for zz in REDUCE_ORDER[k] for s in range(2)] for k in range(NZ)}
+
+    def scatter_step(step, lab_sum):
+        slot = chunk_of(order2, step)
+        f_now = f_b[slot]
+        acc = fbuf.at[slot]
+        norm = norm_ref[pl.ds(slot, 1), :]
+        shift = norm * log2e
+        coef = (1.0 + 2.0 * LOGIT_ZLOSS * norm) * token_scale
+        lab = lab_ref[pl.ds(slot, 1), :]
+        acc[...] = jnp.zeros((width, own), F32)
+
+        def group(base, parts, hits):
+            for first, size in parts:
+                at = pl.ds(base + first, size)
+                logit = lax.dot_general(e_b[at, :], f_now, (((1,), (1,)), ((), ())), preferred_element_type=F32)
+                hit = lax.broadcasted_iota(jnp.int32, (size, own), 0) == lab - (base + first)
+                prob = jnp.exp2(logit * slope - shift) * coef
+                grad = jnp.where(hit, prob - token_scale, prob).astype(BF16)
+                hits = hits + jnp.sum(jnp.where(hit, logit, 0.0).reshape(size // 8, 8, own), axis=0)
+                dl[pl.ds(first, size), :] = grad
+                g_acc[at, :] += jnp.dot(grad, f_now, preferred_element_type=F32)
+            size = parts[-1][0] + parts[-1][1]
+            acc[...] += jnp.dot(e_t[:, pl.ds(base, size)], dl[pl.ds(0, size), :], preferred_element_type=F32)
+            return hits
+
+        lab_sum = over_blocks(group, lab_sum)
+
+        def hand_over():
+            remote(acc, from_y.at[slot // 2], rs_y.at[slot // 2], recv_y.at[slot // 2], partner, dp).start()
+        pl.when(slot % 2 != y)(hand_over)
+
+        for k in range(NZ):
+            for s, shards in REDUCE[k].items():
+                def reduce(k=k, shards=shards):
+                    for zz in shards:
+                        line = fbuf.at[2 * zz + y]
+                        remote(line, from_y.at[zz], rs_y.at[zz], recv_y.at[zz], partner, dp).wait_recv()
+                        add_into(line, from_y.at[zz])
+                        if zz >= k and k > 0:
+                            remote(line, from_l.at[zz - 1], rs_l.at[zz], recv_l.at[zz], partner, dp).wait_recv()
+                            add_into(line, from_l.at[zz - 1])
+                        if zz <= k and k < NZ - 1:
+                            remote(line, from_r.at[zz], rs_r.at[zz], recv_r.at[zz], partner, dp).wait_recv()
+                            add_into(line, from_r.at[zz])
+                        if zz > k:
+                            remote(line, from_l.at[zz - 1], rs_r.at[zz], recv_l.at[zz], tp + 2, dp).start()
+                        if zz < k:
+                            remote(line, from_r.at[zz], rs_l.at[zz], recv_r.at[zz], tp - 2, dp).start()
+                pl.when((z == k) & (step == s))(reduce)
+        return lab_sum
+
+    lab_sum = lax.fori_loop(0, 2 * NZ, scatter_step, jnp.zeros((8, own), F32))
+    labsum_ref[...] = lab_sum
+    store = pltpu.make_async_copy(g_acc, ghead_ref, load_sem.at[0])
+    store.start()
+    dfin_ref[...] = fbuf[tp].T
+
+    def scatters_done(k):
+        for zz in range(NZ):
+            line = fbuf.at[2 * zz + y]
+            remote(line, from_y.at[zz], rs_y.at[zz], recv_y.at[zz], partner, dp).wait_send()
+            if zz > k:
+                remote(line, from_l.at[zz - 1], rs_r.at[zz], recv_l.at[zz], partner, dp).wait_send()
+            if zz < k:
+                remote(line, from_r.at[zz], rs_l.at[zz], recv_r.at[zz], partner, dp).wait_send()
+
+    for k in range(NZ):
+        pl.when(z == k)(functools.partial(scatters_done, k))
+    for n in range(1, 2 * NZ):
+        to = lax.rem(tp + n, 2 * NZ)
+        remote(lse_all.at[tp], lse_all.at[tp], st_send.at[to], st_recv.at[tp], to, dp).wait_send()
+    store.wait()
+
+
+def head(f_own, labels, embed, scale, token_scale, collective_id):
+    own, width = f_own.shape
+    vocab = embed.shape[0]
+    chunk = (own, width)
+    dma8 = pltpu.SemaphoreType.DMA((2 * NZ,))
+    dma4 = pltpu.SemaphoreType.DMA((NZ,))
+    return pl.pallas_call(
+        functools.partial(head_kernel, scale, token_scale),
+        out_shape=(jax.ShapeDtypeStruct((own, width), F32), jax.ShapeDtypeStruct((vocab, width), F32),
+                   jax.ShapeDtypeStruct((2 * NZ, own), F32), jax.ShapeDtypeStruct((8, own), F32)),
+        in_specs=[VMEM, VMEM, ANY],
+        out_specs=(VMEM, ANY, VMEM, VMEM),
+        scratch_shapes=[pltpu.VMEM((vocab, width), BF16), pltpu.VMEM((width, vocab), BF16),
+                        pltpu.VMEM((2 * NZ,) + chunk, F32), pltpu.VMEM((2 * NZ,) + chunk, BF16), pltpu.VMEM((vocab, width), F32),
+                        pltpu.VMEM((NZ,) + chunk, F32), pltpu.VMEM((NZ - 1,) + chunk, F32), pltpu.VMEM((NZ - 1,) + chunk, F32),
+                        pltpu.VMEM((SUB * GROUP, own), BF16), pltpu.VMEM((2 * NZ, 2 * NZ, own), F32),
+                        pltpu.SemaphoreType.DMA((2,)), dma8, dma8, dma8, dma8, dma4, dma4, dma4, dma4, dma4, dma4, dma8, dma8],
+        compiler_params=pltpu.CompilerParams(collective_id=collective_id, has_side_effects=True, vmem_limit_bytes=67000000),
+        cost_estimate=pl.CostEstimate(flops=8 * vocab * width * own * 8, bytes_accessed=3 * 4 * vocab * width, transcendentals=2 * vocab * own * 8),
+        name="head",
+    )(f_own, labels, embed)
+
+
 def norm_fwd(x_f32, scale):
     centered = x_f32 - jnp.mean(x_f32, axis=-1, keepdims=True)
     inv_std = lax.rsqrt(jnp.mean(centered * centered, axis=-1, keepdims=True) + LN_EPS)
@@ -509,7 +767,6 @@
         own = tok_loc // n_tp
         tp_rank = lax.axis_index('tp')
         half = tp_rank % 2
-        emb_b = embed.astype(BF16)
 
         all_tokens = lax.all_gather(tokens, 'dp').reshape(n_dp * n_tp, own)
         strict = (jnp.arange(own)[:, None] > jnp.arange(own)[None, :]).astype(BF16)
@@ -575,25 +832,12 @@
         x_one = x_zero + att_out + dot('rf,fd->rd', hidden, wd_b)
         f_own, f_hat, f_inv = norm_fwd(x_one, ln_scales[1])
 
-        f_norm = plane_gather(f_own.astype(F32), 4).reshape(tok_loc, d_model).astype(BF16)
         logit_scale = d_model ** -0.5
-        logits = dot('rd,vd->rv', f_norm, emb_b) * logit_scale
-        lab_loc = labels.reshape(tok_loc) - tp_rank * vocab_loc
-        lab_hit = jnp.arange(vocab_loc)[None, :] == lab_loc[:, None]
-        row_max = jnp.max(logits, axis=-1)
-        exp_sum = jnp.sum(jnp.exp(logits - row_max[:, None]), axis=-1)
-        lab_val = jnp.sum(jnp.where(lab_hit, logits, 0.0), axis=-1)
-        stats = plane_swap(jnp.stack([row_max, exp_sum, lab_val]).reshape(3 * tok_loc // 128, 128), True, 5).reshape(n_tp, 3, tok_loc)
-        top = jnp.max(stats[:, 0], axis=0)
-        log_norm = top + jnp.log(jnp.sum(stats[:, 1] * jnp.exp(stats[:, 0] - top), axis=0))
-        tok_loss = log_norm - jnp.sum(stats[:, 2], axis=0) + LOGIT_ZLOSS * log_norm * log_norm
-        loss_part = jnp.sum(tok_loss) / (n_tp * tok_total)
-
-        coef = 1.0 + 2.0 * LOGIT_ZLOSS * log_norm
-        d_logits = ((jnp.exp(logits - log_norm[:, None]) * coef[:, None] - lab_hit.astype(F32)) * (logit_scale / tok_total)).astype(BF16)
-        d_fin_part = dot('rv,vd->rd', d_logits, emb_b).reshape(n_tp, own, d_model)
-        g_head = lax.psum(dot('rv,rd->vd', d_logits, f_norm), 'dp')
-        d_fin = plane_scatter(d_fin_part, 6)
+        lab_loc = labels.reshape(n_tp, own) - tp_rank * vocab_loc
+        d_fin, g_head_part, log_norm, lab_sum = head(f_own.astype(F32), lab_loc, embed, logit_scale, logit_scale / tok_total, 4)
+        log_norm = lax.dynamic_index_in_dim(log_norm, tp_rank, 0, keepdims=False)
+        loss_part = (jnp.sum(log_norm + LOGIT_ZLOSS * log_norm * log_norm) - jnp.sum(lab_sum) * logit_scale) / tok_total
+        g_head = lax.psum(g_head_part, 'dp')
         d_one, g_ln_fin = norm_bwd(d_fin, f_hat, f_inv, ln_scales[1])
         d_one_b = d_one.astype(BF16)
 

time: 1120 us -> 975 us (0.87)
  matrix products: 228 us -> 122 us
  other arithmetic: 234 us -> 143 us
  waiting for transfers between devices: 18.7 us -> 46.5 us
  Pallas kernels: 530 us -> 557 us
    dot_general x28 -> x25, matrix products: 226 us -> 120 us  [dot(): return jnp.einsum(spec, a, b, preferred_element_type=F32)]
    convert_element_type x2 -> x0, other arithmetic: 56.7 us -> none  [the longest x1 50.9 us: local_step(): ((jnp.exp(logits - log_norm[:, None]) * coef[:, None] - lab_hit.astype(F3...]
    pallas_call x2 -> x1, Pallas kernels: 195 us -> 245 us  [head(): pl.pallas_call(functools.partial(head_kernel, scale, token_scale), out_sh...]
    reduce_sum x4 -> x2, other arithmetic: 34 us -> 1.2 us  [the longest x1 0.6 us: local_step(): jnp.sum(log_norm + LOGIT_ZLOSS * log_norm * log_norm)]
    psum x1, waiting for transfers between devices: 18.7 us -> 45.9 us  [local_step(): g_head = lax.psum(g_head_part, 'dp')]
    pallas_call x1, Pallas kernels: 141 us -> 124 us  [weight_scatter(): pl.pallas_call(weight_scatter_kernel, out_shape=jax.ShapeDtypeStruct((2,)...]
    pallas_call x2 -> x1, Pallas kernels: 38.1 us -> 29.1 us  [plane_swap(): pl.pallas_call(functools.partial(swap_kernel, spread), out_shape=jax.Shap...]
  transfers between devices with their start and end apart: 2 -> 2, of which waited for: 1 -> 1; matrix products, arithmetic and copies ran while one was open for 12% -> 11% of each run, Pallas kernels for 17% -> 18%
where the time goes in v2:
time: 975 us; the launch traced here: 965 us
  Pallas kernels  557 us (57%)
  other arithmetic  143 us (15%)
  matrix products  122 us (13%)
  blocking collectives  46.6 us (5%)
  waiting for transfers between devices  46.5 us (5%)
  local copies, waits for them, and re-layouts  32.7 us (3%)
  between operations  17.9 us (2%)
    pallas_call x1, Pallas kernels, head(): pl.pallas_call(functools.partial(head_kernel, scale, token_scale), out_sh...  245 us
    pallas_call x1, Pallas kernels, weight_scatter(): pl.pallas_call(weight_scatter_kernel, out_shape=jax.ShapeDtypeStruct((2,)...  124 us
    dot_general x25, matrix products, dot(): return jnp.einsum(spec, a, b, preferred_element_type=F32)  120 us
    pallas_call x1, Pallas kernels, weight_gather(): pl.pallas_call(weight_gather_kernel, out_shape=jax.ShapeDtypeStruct((2 *...  89.3 us
    pallas_call x1, Pallas kernels, row_return(): pl.pallas_call(row_return_kernel, out_shape=jax.ShapeDtypeStruct((4,) + x...  50.2 us
    sub x7, other arithmetic, adam_update(): param_in - LEARN_RATE * mom_new / (jnp.sqrt(vel_new) + ADAM_EPS)  47.1 us
    psum x1, waiting for transfers between devices, local_step(): g_head = lax.psum(g_head_part, 'dp')  45.9 us
    psum x1, blocking collectives, local_step(): lax.psum((g_kv_part, jnp.stack([g_ln_in, g_ln_fin]), loss_part), ('tp', '...  40.4 us
  transfers between devices with their start and end apart: 2, of which 1 were waited for; matrix products, arithmetic and copies ran while one was open for 11% of the time, Pallas kernels for 18%

profile of v2, /device:TPU:0, one launch (start us, length us, event | category | flops | bytes accessed | tf_op | source)
XLA Modules:
  0.0 964.7 jit_solution(11273724580225401850)
XLA Ops:
  8.8 6.2 all-gather.1
  19.9 2.5 pad_maximum_fusion.2
  22.4 89.3 %weight_gather.1 = f32[8,2,448,512]{3,2,1,0:T(8,128)} custom-call(f32[2,448,512]{2,1,0:T(8,128)} %bitcast.243), custom_call_target="tpu_custom_call" | custom-call | tf_op jit(solution)/shard_map/weight_gather/pallas_call | solution.py:169
  111.7 9.2 convert_element_type.124
  121.0 5.6 fusion.139
  126.6 1.9 slice.127
  128.5 8.2 convert.48
  136.7 7.4 gather_fusion.2
  145.4 29.1 %plane_swap.2 = f32[8,96,512]{2,1,0:T(8,128)} custom-call(f32[8,96,512]{2,1,0:T(8,128)} %fusion.67.x_ref), custom_call_target="tpu_custom_call" | custom-call | tf_op jit(solution)/shard_map/plane_swap/pallas_call | solution.py:368
  174.6 2.0 fusion.44
  178.7 1.7 fusion.80
  180.4 4.9 fusion.144
  187.7 2.2 multiply_cosine_fusion
  191.5 10.1 %pair_swap.2 = f32[512,128]{1,0:T(8,128)} custom-call(f32[512,128]{1,0:T(8,128)} %pad_maximum_fusion.8.x_ref), custom_call_target="tpu_custom_call" | custom-call | tf_op jit(solution)/shard_map/pair_swap/pallas_call | solution.py:446
  204.9 6.3 multiply_convert_fusion.2
  211.3 2.2 fusion.145
  213.9 8.0 fusion.88
  221.9 17.4 %fusion.141 = (f32[8,512]{1,0:T(8,128)S(1)}, f32[8,512,1024]{1,2,0:T(8,128)}) fusion(f32[1024,512,8]{1,0,2:T(8,128)} %fusion.88, pred[512,1024]{0,1:T(8,128)(4,1)S(1)} %copy-done.48), kind=kOutput, calls=%fused_computation.277 | output fusion | flops 25166848 | bytes 34095104 | tf_op jit(solution)/shard_map/sub | solution.py:824
  240.0 7.5 fusion.51
  247.6 1.8 fusion.142
  251.5 245.5 %head.1 = (f32[512,512]{1,0:T(8,128)}, f32[6288,512]{1,0:T(8,128)}, f32[8,512]{1,0:T(8,128)}, f32[8,512]{1,0:T(8,128)}) custom-call(f32[512,512]{1,0:T(8,128)} %fusion.72.f_ref, s32[8,512]{1,0:T(8,128)} %sub.149.lab_ref, f32[6288,512]{1,0:T(8,128)} %e_ref.1), custom_call_target="tpu_custom_call" | custom-call | flops 105495134208 | bytes 38633472 | tf_op jit(solution)/shard_map/head/pallas_call | solution.py:698
  497.0 2.6 multiply_reduce_fusion
  499.7 3.0 fusion.138
  502.7 1.7 convolution_convert_fusion
  504.5 9.4 fusion.109
  513.9 2.3 fusion.54
  516.3 21.9 %fusion.57 = f32[1024,64]{1,0:T(8,128)S(1)} fusion(f32[1024,512,8]{1,0,2:T(8,128)} %fusion.109, bf16[512,8,32]{0,2,1:T(8,128)(2,1)S(1)} %copy-done.32, bf16[512,8,32]{0,2,1:T(8,128)(2,1)S(1)} %copy-done.30, f32[8,512,1024]{1,2,0:T(8,128)} %get-tuple-element.298, f32[8,512]{1,0:T(8,128)S(1)} %copy-done.75), kind=kOutput, calls=%fused_computation.103 | convolution fusion | flops 567284736 | bytes 34357248 | tf_op jit(solution)/shard_map/hqk,qhe->ke/dot_general | solution.py:749
  539.1 8.1 pair_swap.3
  548.3 1.9 fusion.95
  553.0 27.5 %fusion.43 = f32[512,8,64]{0,2,1:T(8,128)} fusion(f32[1024,512,8]{1,0,2:T(8,128)} %fusion.109, bf16[512,128]{1,0:T(8,128)(2,1)S(1)} %copy-done.24, bf16[512,128]{1,0:T(8,128)(2,1)S(1)} %copy-done.22, f32[8,512,1024]{1,2,0:T(8,128)} %get-tuple-element.298, f32[8,512]{1,0:T(8,128)S(1)} %copy-done.75), kind=kOutput, calls=%fused_computation.91 | convolution fusion | flops 566498304 | bytes 34881536 | tf_op jit(solution)/shard_map/hqk,ke->qhe/dot_general | solution.py:749
  583.6 6.5 multiply_convert_fusion
  590.2 2.2 fusion.146
  592.6 3.9 convolution_add_fusion
  596.7 1.8 convolution_bitcast_fusion.1
  600.2 2.2 gather_fusion.3
  603.7 50.2 %row_return.2 = f32[4,8,96,512]{3,2,1,0:T(8,128)} custom-call(f32[8,96,512]{2,1,0:T(8,128)} %broadcast_select_fusion.2.x_ref), custom_call_target="tpu_custom_call" | custom-call | tf_op jit(solution)/shard_map/row_return/pallas_call | solution.py:423
  653.9 25.0 %scatter_custom_fusion.1 = f32[6288,512]{1,0:T(8,128)} fusion(s32[3072]{0:T(1024)S(1)} %bitcast.274, f32[3072,512]{1,0:T(8,128)} %bitcast.244, f32[]{:T(128)} %constant.94.clone.1), kind=kCustom, calls=%fused_computation.64 | custom fusion | flops 1572864 | bytes 12878336 | tf_op jit(solution)/shard_map/scatter-add | solution.py:880
  680.3 3.0 fusion.148
  689.6 5.6 pad_maximum_fusion
  695.3 124.3 %weight_scatter.1 = f32[2,448,512]{2,1,0:T(8,128)} custom-call(f32[8,2,448,512]{3,2,1,0:T(8,128)} %bitcast.227), custom_call_target="tpu_custom_call" | custom-call | tf_op jit(solution)/shard_map/weight_scatter/pallas_call | solution.py:326
  824.1 40.4 %all-reduce = (f32[2,512]{1,0:T(2,128)S(1)}, f32[]{:T(128)}) all-reduce(f32[2,512]{1,0:T(2,128)S(1)} %pad_maximum_fusion.10, f32[]{:T(128)S(6)} %div.126), channel_id=1, replica_groups=mesh['tp'=8,'dp'=4] {'tp','dp'}, use_global_device_ids=true, to_apply=%region_32.33 | all-reduce | flops 1025 | bytes 8200 | tf_op jit(solution)/shard_map/psum | solution.py:889
  865.1 1.9 divide_subtract_fusion.5
  866.9 1.9 divide_subtract_fusion.4
  868.8 2.9 divide_subtract_fusion.2
  871.7 3.2 divide_subtract_fusion.1
  874.9 2.1 divide_subtract_fusion.3
  877.0 45.9 %all-reduce.4.cloned.1.call-done = f32[6288,512]{1,0:T(8,128)} async-done(((f32[6288,512]{1,0:T(8,128)}), f32[6288,512]{1,0:T(8,128)}) %all-reduce.4.cloned.1.call-update) | async-done | bytes 12877840 | tf_op jit(solution)/shard_map/psum | solution.py:840
  922.8 34.6 %divide_subtract_fusion = (f32[6288,512]{1,0:T(8,128)}, f32[6288,512]{1,0:T(8,128)}, f32[6288,512]{1,0:T(8,128)}) fusion(f32[6288,512]{1,0:T(8,128)} %e_ref.1, f32[6288,512]{1,0:T(8,128)} %all-reduce.4.cloned.1.call-done, f32[6288,512]{1,0:T(8,128)} %get-tuple-element.145, f32[6288,512]{1,0:T(8,128)} %param.36, f32[6288,512]{1,0:T(8,128)} %param.43), kind=kLoop, calls=%fused_computation.55 | loop fusion | flops 38633472 | bytes 103022592 | tf_op jit(solution)/shard_map/sub | solution.py:745
  (255 shorter events, 41.8 us)
Async XLA Ops:
  7.2 867.7 %all-reduce.6.cloned.1.call-start = ((), (), s32[]{:S(2)}) async-start(), calls=%async_computation.1 | async-start | bytes 524288 | tf_op jit(solution)/shard_map/psum | solution.py:889
  18.4 169.3 %copy-start.71 = (f32[32]{0:T(128)}, f32[32]{0:T(128)S(1)}, u32[]{:S(2)}) copy-start(f32[32]{0:T(128)S(1)} %multiply_power_fusion) | copy-start | bytes 388
  177.4 70.2 %copy-start.3 = (f32[512,512]{1,0:T(8,128)}, f32[512,512]{1,0:T(8,128)S(1)}, u32[]{:S(2)}) copy-start(f32[512,512]{1,0:T(8,128)S(1)} %get-tuple-element.142) | copy-start | bytes 3145732
  178.4 6.8 copy-start.34
  178.6 26.3 %copy-start = (bf16[512,512]{1,0:T(8,128)(2,1)}, bf16[512,512]{1,0:T(8,128)(2,1)S(1)}, u32[]{:S(2)}) copy-start(bf16[512,512]{1,0:T(8,128)(2,1)S(1)} %multiply_convert_fusion.4) | copy-start | bytes 1572868
  187.7 15.0 %copy-start.61 = (f32[512]{0:T(512)}, f32[512]{0:T(512)S(1)}, u32[]{:S(2)}) copy-start(f32[512]{0:T(512)S(1)} %get-tuple-element.305) | copy-start | bytes 6148
  203.7 9.9 %copy-start.45 = (f32[512,32]{0,1:T(8,128)}, f32[512,32]{0,1:T(8,128)S(1)}, u32[]{:S(2)}) copy-start(f32[512,32]{0,1:T(8,128)S(1)} %copy.174) | copy-start | bytes 196612
  204.9 6.3 copy-start.20
  213.7 25.7 %copy-start.21 = (bf16[512,128]{1,0:T(8,128)(2,1)}, bf16[512,128]{1,0:T(8,128)(2,1)S(1)}, u32[]{:S(2)}) copy-start(bf16[512,128]{1,0:T(8,128)(2,1)S(1)} %get-tuple-element.276) | copy-start | bytes 393220
  213.7 25.7 %copy-start.23 = (bf16[512,128]{1,0:T(8,128)(2,1)}, bf16[512,128]{1,0:T(8,128)(2,1)S(1)}, u32[]{:S(2)}) copy-start(bf16[512,128]{1,0:T(8,128)(2,1)S(1)} %get-tuple-element.277) | copy-start | bytes 393220
  213.9 8.1 copy-start.29
  213.9 8.1 copy-start.31
  213.9 8.1 copy-start.48
  240.0 7.6 copy-start.73
  240.0 9.7 %copy-start.65 = (s32[4,1024]{1,0:T(4,128)S(1)}, s32[4,1024]{1,0:T(4,128)}, u32[]{:S(2)}) copy-start(s32[4,1024]{1,0:T(4,128)} %param.28) | copy-start | bytes 49156
  497.0 7.4 copy-start.22
  497.0 7.4 copy-start.24
  499.7 14.2 %slice-start = ((s8[16777216]{0:T(1024)(128)(4,1)}), s8[4194304]{0:T(1024)(128)(4,1)S(1)}, s32[]{:S(2)}) async-start(s8[16777216]{0:T(1024)(128)(4,1)} %bitcast.278), calls=%async_computation.2 | async-start | bytes 8388608
  502.7 80.9 %copy-start.6 = (bf16[512,512]{1,0:T(8,128)(2,1)}, bf16[512,512]{1,0:T(8,128)(2,1)S(1)}, u32[]{:S(2)}) copy-start(bf16[512,512]{1,0:T(8,128)(2,1)S(1)} %get-tuple-element.265) | copy-start | bytes 1572868
  504.4 9.5 slice-start.1
  504.4 9.5 slice-start.2
  504.4 9.4 slice-start.3
  504.4 9.4 copy-start.75
  516.3 32.0 %copy-start.62 = (f32[512]{0:T(512)S(1)}, f32[512]{0:T(512)}, u32[]{:S(2)}) copy-start(f32[512]{0:T(512)} %copy-done.61) | copy-start | bytes 6148
  516.3 32.0 %copy-start.72 = (f32[32]{0:T(128)S(1)}, f32[32]{0:T(128)}, u32[]{:S(2)}) copy-start(f32[32]{0:T(128)} %copy-done.71) | copy-start | bytes 388
  538.2 12.4 %copy-start.1 = (bf16[512,512]{1,0:T(8,128)(2,1)S(1)}, bf16[512,512]{1,0:T(8,128)(2,1)}, u32[]{:S(2)}) copy-start(bf16[512,512]{1,0:T(8,128)(2,1)} %copy-done) | copy-start | bytes 1572868
  551.6 371.3 %all-reduce.4.cloned.1.call-start = ((), (), s32[]{:S(2)}) async-start(), calls=%async_computation | async-start | bytes 25755648 | tf_op jit(solution)/shard_map/psum | solution.py:840
  553.0 27.6 %copy-start.52 = (s32[512]{0:T(512)S(1)}, s32[512]{0:T(512)}, u32[]{:S(2)}) copy-start(s32[512]{0:T(512)} %copy-done.51) | copy-start | bytes 6148
  553.0 27.6 %copy-start.54 = (s32[512]{0:T(512)S(1)}, s32[512]{0:T(512)}, u32[]{:S(2)}) copy-start(s32[512]{0:T(512)} %copy-done.53) | copy-start | bytes 6148
  553.0 29.0 %copy-start.17 = (s32[32,512]{1,0:T(8,128)S(1)}, s32[32,512]{1,0:T(8,128)}, u32[]{:S(2)}) copy-start(s32[32,512]{1,0:T(8,128)} %get-tuple-element.472) | copy-start | bytes 196612
  583.6 6.5 copy-start.8
  590.2 6.3 copy-start.46
  592.4 4.1 copy-start.38
  592.5 6.0 copy-start.4
  592.5 6.0 copy-start.26
  592.5 6.0 copy-start.28
  592.5 6.0 copy-start.56
  592.6 6.0 copy-start.58
  592.6 6.0 copy-start.60
  695.2 128.8 %copy-start.67 = (f32[512]{0:T(512)S(1)}, f32[512]{0:T(512)}, u32[]{:S(2)}) copy-start(f32[512]{0:T(512)} %get-tuple-element.194) | copy-start | bytes 6148
  695.2 128.8 %copy-start.68 = (f32[512]{0:T(512)S(1)}, f32[512]{0:T(512)}, u32[]{:S(2)}) copy-start(f32[512]{0:T(512)} %get-tuple-element.196) | copy-start | bytes 6148
  695.3 169.2 %copy-start.64 = (f32[2,512]{1,0:T(2,128)S(1)}, f32[2,512]{1,0:T(2,128)}, u32[]{:S(2)}) copy-start(f32[2,512]{1,0:T(2,128)} %param.30) | copy-start | bytes 12292
  695.3 169.2 %copy-start.69 = (f32[2,512]{1,0:T(2,128)S(1)}, f32[2,512]{1,0:T(2,128)}, u32[]{:S(2)}) copy-start(f32[2,512]{1,0:T(2,128)} %param.37) | copy-start | bytes 12292
  695.3 169.2 %copy-start.70 = (f32[2,512]{1,0:T(2,128)S(1)}, f32[2,512]{1,0:T(2,128)}, u32[]{:S(2)}) copy-start(f32[2,512]{1,0:T(2,128)} %param.44) | copy-start | bytes 12292
  695.3 169.8 %copy-start.47 = (f32[512,64]{0,1:T(8,128)S(1)}, f32[512,64]{0,1:T(8,128)}, u32[]{:S(2)}) copy-start(f32[512,64]{0,1:T(8,128)} %param.31) | copy-start | bytes 393220
  819.6 52.1 %copy-start.9 = (f32[2,512,256]{2,1,0:T(8,128)S(1)}, f32[2,512,256]{2,1,0:T(8,128)}, u32[]{:S(2)}) copy-start(f32[2,512,256]{2,1,0:T(8,128)} %param.34) | copy-start | bytes 3145732
  821.3 50.4 %copy-start.33 = (f32[2,512,256]{2,1,0:T(8,128)S(1)}, f32[2,512,256]{2,1,0:T(8,128)}, u32[]{:S(2)}) copy-start(f32[2,512,256]{2,1,0:T(8,128)} %param.41) | copy-start | bytes 3145732
  865.1 9.8 %copy-start.35 = (f32[2,512,64]{1,2,0:T(8,128)S(1)}, f32[2,512,64]{1,2,0:T(8,128)}, u32[]{:S(2)}) copy-start(f32[2,512,64]{1,2,0:T(8,128)} %param.32) | copy-start | bytes 786436
  (34 other events, 57.2 us)
Sparse Core Ops, SparseCore 0:
  551.7 132.4 all-reduce.5
  686.7 236.1 all-reduce.3

commit v3 on v2

--- a/solution.py
+++ b/solution.py
@@ -251,8 +251,8 @@
     )(p)
 
 
-def weight_scatter_kernel(p_ref, out_ref, acc, from_c, from_y, from_l, from_r, from_x, load_sem, out_sem, send_c, send_y, send_l, send_r,
-                          last_send, recv_c, recv_y, recv_l, recv_r, last_recv):
+def weight_scatter_kernel(p_ref, out_ref, small_ref, acc, from_c, from_y, from_l, from_r, from_x, load_sem, out_sem, send_c, send_y, send_l, send_r,
+                          last_send, recv_c, recv_y, recv_l, recv_r, last_recv, small_send, small_recv):
     tp, dp, z, y = place()
     partner = tp + 1 - 2 * y
     core = dp % 2
@@ -260,7 +260,7 @@
     facing = lax.rem(dp + 2, 4)
 
     def program(k):
-        line_barrier(k, tp, dp, [(tp, twin), (tp, facing)])
+        plane_barrier(tp, dp, [(tp, twin), (tp, facing)])
         sends = []
         for zz in REDUCE_ORDER[k]:
             for slot in (2 * zz + 1 - y, 2 * zz + y):
@@ -313,6 +313,20 @@
         copy.wait_send()
         remote(total, out_ref.at[1 - core], last_send.at[1], last_recv.at[1], tp, twin).wait_recv()
         out.wait()
+
+        n_small, n_rows = small_ref.shape[1], out_ref.shape[1]
+        mine = out_ref.at[1, pl.ds(n_rows - 32, n_small), :]
+        for n in range(1, 2 * NZ):
+            to = lax.rem(tp + n, 2 * NZ)
+            copy = remote(mine, small_ref.at[tp], small_send.at[to], small_recv.at[tp], to, dp)
+            copy.start()
+            sends.append(copy)
+        here = pltpu.make_async_copy(mine, small_ref.at[tp], out_sem)
+        here.start()
+        for n in range(1, 2 * NZ):
+            source = lax.rem(tp + n, 2 * NZ)
+            remote(small_ref.at[source], small_ref.at[source], small_send.at[source], small_recv.at[source], source, dp).wait_recv()
+        here.wait()
         for copy in sends:
             copy.wait_send()
 
@@ -323,19 +337,20 @@
 def weight_scatter(p, collective_id):
     _, rows, width = p.shape
     half = (rows // 2, width)
-    out = pl.pallas_call(
+    out, small = pl.pallas_call(
         weight_scatter_kernel,
-        out_shape=jax.ShapeDtypeStruct((2,) + half, p.dtype),
+        out_shape=(jax.ShapeDtypeStruct((2,) + half, p.dtype), jax.ShapeDtypeStruct((2 * NZ, 24, width), p.dtype)),
         in_specs=[ANY],
-        out_specs=ANY,
+        out_specs=(ANY, ANY),
         scratch_shapes=[pltpu.VMEM((2 * NZ,) + half, p.dtype)] * 2 + [pltpu.VMEM((NZ,) + half, p.dtype)] * 3
         + [pltpu.VMEM(half, p.dtype)]
         + [pltpu.SemaphoreType.DMA((2 * NZ,)), pltpu.SemaphoreType.DMA]
-        + ([pltpu.SemaphoreType.DMA((2 * NZ,))] + [pltpu.SemaphoreType.DMA((NZ,))] * 3 + [pltpu.SemaphoreType.DMA((2,))]) * 2,
+        + ([pltpu.SemaphoreType.DMA((2 * NZ,))] + [pltpu.SemaphoreType.DMA((NZ,))] * 3 + [pltpu.SemaphoreType.DMA((2,))]) * 2
+        + [pltpu.SemaphoreType.DMA((2 * NZ,))] * 2,
         compiler_params=pltpu.CompilerParams(collective_id=collective_id, has_side_effects=True),
         name="weight_scatter",
     )(p.reshape((2 * NZ, 2) + half))
-    return out.reshape(rows, width)
+    return out.reshape(rows, width), small
 
 
 def plane_barrier(tp, dp, others):
@@ -712,6 +727,228 @@
     )(f_own, labels, embed)
 
 
+TB = (((1,), (1,)), ((), ()))
+TA = (((0,), (0,)), ((), ()))
+LOG2E = 1.4426950408889634
+
+
+def mm(a, b, dims=(((1,), (0,)), ((), ()))):
+    return lax.dot_general(a, b, dims, preferred_element_type=F32)
+
+
+def turn(lo, hi, cos_t, sin_t):
+    return lo * cos_t - hi * sin_t, hi * cos_t + lo * sin_t
+
+
+def layer_fwd_kernel(x0_ref, ln_ref, cos_ref, sin_ref, wq_ref, wkv_ref, wo_ref, wg_ref, wu_ref, wd_ref,
+                     f_ref, x1_ref, q_ref, kv_ref, kvt_ref, lse_ref, ctx_ref, u_b, kv_out, kv_in, send_sem, recv_sem):
+    tp, dp, _, y = place()
+    partner = tp + 1 - 2 * y
+    own, width = x0_ref.shape
+    hd = kv_out.shape[0] // 2
+    quarter = hd // 2
+    heads = q_ref.shape[0] // hd
+    signal(partner, dp)
+    u_b[...] = norm_fwd(x0_ref[...], ln_ref[0:1, :])[0]
+    u = u_b[...]
+    cos_t = cos_ref[...]
+    sin_t = sin_ref[...]
+    kv = mm(wkv_ref[...], u, TB)
+    lo, hi = turn(kv[:quarter], kv[quarter:hd], cos_t, sin_t)
+    kv_out[0:quarter, :] = lo
+    kv_out[quarter:hd, :] = hi
+    kv_out[hd:, :] = kv[hd:]
+    pl.semaphore_wait(pltpu.get_barrier_semaphore(), 1)
+    copy = remote(kv_out, kv_in, send_sem, recv_sem, partner, dp)
+    copy.start()
+
+    q_all = mm(wq_ref[...], u, TB)
+    for h in range(heads):
+        lo, hi = turn(q_all[h * hd:h * hd + quarter], q_all[h * hd + quarter:(h + 1) * hd], cos_t, sin_t)
+        q_ref[h * hd:h * hd + quarter, :] = lo.astype(BF16)
+        q_ref[h * hd + quarter:(h + 1) * hd, :] = hi.astype(BF16)
+
+    x1_ref[...] = x0_ref[...]
+    step = min(512, wg_ref.shape[0])
+
+    def mlp(n, carry):
+        at = pl.ds(pl.multiple_of(n * step, step), step)
+        gate = mm(u_b[...], wg_ref[at, :], TB)
+        up = mm(u_b[...], wu_ref[at, :], TB)
+        hidden = (gate * jax.nn.sigmoid(gate) * up).astype(BF16)
+        x1_ref[...] += mm(hidden, wd_ref[at, :])
+        return carry
+
+    lax.fori_loop(0, wg_ref.shape[0] // step, mlp, 0)
+
+    copy.wait()
+
+    def fill(mine, other):
+        kv_ref[mine * own:(mine + 1) * own, :] = kv_out[...].T.astype(BF16)
+        kv_ref[other * own:(other + 1) * own, :] = kv_in[...].T.astype(BF16)
+        kvt_ref[:, mine * own:(mine + 1) * own] = kv_out[...].astype(BF16)
+        kvt_ref[:, other * own:(other + 1) * own] = kv_in[...].astype(BF16)
+
+    pl.when(y == 0)(lambda: fill(0, 1))
+    pl.when(y == 1)(lambda: fill(1, 0))
+    blank = jnp.zeros((hd, own), BF16)
+    slope = hd ** -0.5 * LOG2E
+
+    def attend(h, carry):
+        at = pl.ds(pl.multiple_of(h * hd, hd), hd)
+        scores = mm(kv_ref[...], jnp.concatenate([q_ref[at, :], blank], axis=0))
+        allowed = lax.broadcasted_iota(jnp.int32, scores.shape, 0) <= lax.broadcasted_iota(jnp.int32, scores.shape, 1) + y * own
+        scores = jnp.where(allowed, scores * slope, -1e30)
+        top = jnp.max(scores, axis=0, keepdims=True)
+        prob = jnp.exp2(scores - top)
+        total = jnp.sum(prob, axis=0, keepdims=True)
+        lse_ref[pl.ds(h, 1), :] = top + jnp.log2(total)
+        ctx_ref[at, :] = mm(kvt_ref[hd:, :], (prob * (1.0 / total)).astype(BF16)).astype(BF16)
+        return carry
+
+    lax.fori_loop(0, heads, attend, 0)
+    x1_ref[...] += mm(ctx_ref[...], wo_ref[...], TA)
+    f_ref[...] = norm_fwd(x1_ref[...], ln_ref[1:2, :])[0].astype(F32)
+
+
+def layer_fwd(x0, ln, cos_t, sin_t, weights, collective_id):
+    own, width = x0.shape
+    two_hd = weights[1].shape[0]
+    nq = weights[0].shape[0]
+    return pl.pallas_call(
+        layer_fwd_kernel,
+        out_shape=(jax.ShapeDtypeStruct((own, width), F32), jax.ShapeDtypeStruct((own, width), F32),
+                   jax.ShapeDtypeStruct((nq, own), BF16), jax.ShapeDtypeStruct((2 * own, two_hd), BF16),
+                   jax.ShapeDtypeStruct((two_hd, 2 * own), BF16), jax.ShapeDtypeStruct((2 * nq // two_hd, own), F32),
+                   jax.ShapeDtypeStruct((nq, own), BF16)),
+        in_specs=[VMEM] * 10,
+        out_specs=(VMEM,) * 7,
+        scratch_shapes=[pltpu.VMEM((own, width), BF16), pltpu.VMEM((two_hd, own), F32), pltpu.VMEM((two_hd, own), F32),
+                        pltpu.SemaphoreType.DMA, pltpu.SemaphoreType.DMA],
+        compiler_params=pltpu.CompilerParams(collective_id=collective_id, has_side_effects=True, vmem_limit_bytes=60000000),
+        name="layer_fwd",
+    )(x0, ln, cos_t, sin_t, *weights)
+
+
+def layer_bwd_kernel(dfin_ref, x0_ref, x1_ref, loss_ref, ln_ref, cos_ref, sin_ref, wq_ref, wkv_ref, wo_ref, wg_ref, wu_ref, wd_ref,
+                     q_ref, kv_ref, kvt_ref, lse_ref, ctx_ref, rows_ref, d0_ref, d_one, d_b, u_b, dctx, dq, dkv, dkv_in,
+                     g_q, g_o, g_g, g_u, g_d, small, out_sem, send_sem, recv_sem):
+    tp, dp, _, y = place()
+    partner = tp + 1 - 2 * y
+    own, width = x0_ref.shape
+    hd = kv_ref.shape[1] // 2
+    quarter = hd // 2
+    nq = q_ref.shape[0]
+    heads = nq // hd
+    ff = wg_ref.shape[0]
+    signal(partner, dp)
+    _, f_hat, f_inv = norm_fwd(x1_ref[...], ln_ref[1:2, :])
+    d_in, g_fin = norm_bwd(dfin_ref[...], f_hat, f_inv, ln_ref[1:2, :])
+    d_one[...] = d_in
+    d_b[...] = d_in.astype(BF16)
+    u_b[...] = norm_fwd(x0_ref[...], ln_ref[0:1, :])[0]
+    dctx[...] = mm(wo_ref[...], d_b[...], TB).astype(BF16)
+    g_o[...] = mm(ctx_ref[...], d_b[...])
+    cos_t = cos_ref[...]
+    sin_t = sin_ref[...]
+    blank = jnp.zeros((hd, own), BF16)
+    slope = hd ** -0.5 * LOG2E
+    dkv[...] = jnp.zeros_like(dkv)
+
+    def attend(h, carry):
+        at = pl.ds(pl.multiple_of(h * hd, hd), hd)
+        q_pad = jnp.concatenate([q_ref[at, :], blank], axis=0)
+        d_pad = jnp.concatenate([blank, dctx[at, :]], axis=0)
+        scores = mm(kv_ref[...], q_pad)
+        allowed = lax.broadcasted_iota(jnp.int32, scores.shape, 0) <= lax.broadcasted_iota(jnp.int32, scores.shape, 1) + y * own
+        prob = jnp.where(allowed, jnp.exp2(scores * slope - lse_ref[pl.ds(h, 1), :]), 0.0)
+        d_prob = mm(kv_ref[...], d_pad)
+        mean = jnp.sum(d_prob * prob, axis=0, keepdims=True)
+        d_score = (prob * (d_prob - mean) * hd ** -0.5).astype(BF16)
+        dkv[...] += mm(d_score, q_pad, TB) + mm(prob.astype(BF16), d_pad, TB)
+        d_q = mm(kvt_ref[0:hd, :], d_score)
+        lo, hi = turn(d_q[:quarter], d_q[quarter:], cos_t, -sin_t)
+        dq[at, :] = jnp.concatenate([lo, hi], axis=0).astype(BF16)
+        return carry
+
+    lax.fori_loop(0, heads, attend, 0)
+    pl.semaphore_wait(pltpu.get_barrier_semaphore(), 1)
+    copy = remote(dkv.at[pl.ds(pl.multiple_of((1 - y) * own, own), own), :], dkv_in, send_sem, recv_sem, partner, dp)
+    copy.start()
+
+    d0_ref[...] = mm(dq[...], wq_ref[...], TA)
+    g_q[...] = mm(dq[...], u_b[...])
+    step = min(512, ff)
+
+    def mlp(n, carry):
+        at = pl.ds(pl.multiple_of(n * step, step), step)
+        gate = mm(wg_ref[at, :], u_b[...], TB)
+        up = mm(wu_ref[at, :], u_b[...], TB)
+        d_hidden = mm(wd_ref[at, :], d_b[...], TB)
+        sig = jax.nn.sigmoid(gate)
+        g_d[at, :] = mm((gate * sig * up).astype(BF16), d_b[...])
+        d_gate = (d_hidden * up * sig * (1.0 + gate * (1.0 - sig))).astype(BF16)
+        d_up = (d_hidden * gate * sig).astype(BF16)
+        g_g[at, :] = mm(d_gate, u_b[...])
+        g_u[at, :] = mm(d_up, u_b[...])
+        d0_ref[...] += mm(d_gate, wg_ref[at, :], TA) + mm(d_up, wu_ref[at, :], TA)
+        return carry
+
+    lax.fori_loop(0, ff // step, mlp, 0)
+    copy.wait()
+    d_kv = (dkv[pl.ds(pl.multiple_of(y * own, own), own), :] + dkv_in[...]).T
+    lo, hi = turn(d_kv[:quarter], d_kv[quarter:hd], cos_t, -sin_t)
+    d_kv = jnp.concatenate([lo, hi, d_kv[hd:]], axis=0).astype(BF16)
+    small[0:2 * hd, :] = mm(d_kv, u_b[...])
+    d_u = d0_ref[...] + mm(d_kv, wkv_ref[...], TA)
+    _, u_hat, u_inv = norm_fwd(x0_ref[...], ln_ref[0:1, :])
+    d_in, g_in = norm_bwd(d_u, u_hat, u_inv, ln_ref[0:1, :])
+    d0_ref[...] = d_one[...] + d_in
+    small[2 * hd:, :] = jnp.zeros_like(small[2 * hd:, :])
+    small[2 * hd:2 * hd + 1, :] = g_in.reshape(1, width)
+    small[2 * hd + 1:2 * hd + 2, :] = g_fin.reshape(1, width)
+    small[2 * hd + 2:2 * hd + 3, :] = loss_ref[...]
+    shards = rows_ref.shape[0]
+    copies = []
+
+    def put(src, first, size, s):
+        copies.append(pltpu.make_async_copy(src, rows_ref.at[s, pl.ds(first, size), :], out_sem.at[len(copies)]))
+
+    n_kv = 2 * hd // shards
+    for s in range(shards):
+        at = 0
+        for g, size in ((g_q, nq // shards), (g_o, nq // shards), (g_g, ff // shards), (g_u, ff // shards), (g_d, ff // shards)):
+            put(g.at[pl.ds(s * size, size), :], at, size, s)
+            at += size
+        put(small.at[pl.ds(s * n_kv, n_kv), :], at, n_kv, s)
+        put(small.at[pl.ds(2 * hd + (0 if s == 0 else 16), 16), :], at + n_kv, 16, s)
+    for c in copies:
+        c.start()
+    for c in copies:
+        c.wait()
+
+
+def layer_bwd(d_fin, x0, x1, loss_row, ln, cos_t, sin_t, weights, saved, collective_id):
+    own, width = x0.shape
+    nq = weights[0].shape[0]
+    two_hd = weights[1].shape[0]
+    ff = weights[3].shape[0]
+    rows = (2 * nq + 3 * ff + two_hd) // (2 * NZ) + 16
+    chunk = (own, width)
+    return pl.pallas_call(
+        layer_bwd_kernel,
+        out_shape=(jax.ShapeDtypeStruct((2 * NZ, rows, width), F32), jax.ShapeDtypeStruct(chunk, F32)),
+        in_specs=[VMEM] * 18,
+        out_specs=(ANY, VMEM),
+        scratch_shapes=[pltpu.VMEM(chunk, F32), pltpu.VMEM(chunk, BF16), pltpu.VMEM(chunk, BF16), pltpu.VMEM((nq, own), BF16),
+                        pltpu.VMEM((nq, own), BF16), pltpu.VMEM((2 * own, two_hd), F32), pltpu.VMEM((own, two_hd), F32),
+                        pltpu.VMEM((nq, width), F32), pltpu.VMEM((nq, width), F32)] + [pltpu.VMEM((ff, width), F32)] * 3
+        + [pltpu.VMEM((two_hd + 32, width), F32), pltpu.SemaphoreType.DMA((14 * NZ,)), pltpu.SemaphoreType.DMA, pltpu.SemaphoreType.DMA],
+        compiler_params=pltpu.CompilerParams(collective_id=collective_id, has_side_effects=True, vmem_limit_bytes=60000000),
+        name="layer_bwd",
+    )(d_fin, x0, x1, loss_row, ln, cos_t, sin_t, *weights, *saved)
+
+
 def norm_fwd(x_f32, scale):
     centered = x_f32 - jnp.mean(x_f32, axis=-1, keepdims=True)
     inv_std = lax.rsqrt(jnp.mean(centered * centered, axis=-1, keepdims=True) + LN_EPS)
@@ -790,7 +1027,7 @@
         def fetch(step, x_sum, collective_id):
             here = (shard[:, None, :] == tp_rank) & (rank[:, None, :] == slots[None, :, None] + step * CAP)
             ids = jnp.sum(jnp.where(here, row[:, None, :], 0), axis=-1).reshape(-1)
-            rows_out = jnp.take(embed, ids, axis=0).astype(BF16).astype(F32).reshape(n_tp, CAP, d_model)
+            rows_out = lax.optimization_barrier(jnp.take(embed, ids, axis=0)).astype(BF16).astype(F32).reshape(n_tp, CAP, d_model)
             rows_in = plane_swap(rows_out, False, collective_id).reshape(n_tp * CAP, d_model).astype(BF16)
             pick = (my_shard[:, None, None] == jnp.arange(n_tp)[None, :, None]) & (my_rank[:, None, None] == slots[None, None, :] + step * CAP)
             return x_sum + dot('rc,cd->rd', pick.reshape(own, n_tp * CAP).astype(BF16), rows_in)
@@ -806,67 +1043,20 @@
         wg_t = w_all[:, cuts[1]:cuts[2]].reshape(-1, d_model)
         wu_t = w_all[:, cuts[2]:cuts[3]].reshape(-1, d_model)
         wd_b = w_all[:, cuts[3]:].reshape(-1, d_model)
-        wkv_b = w_kv.astype(BF16)
-
-        u_norm, u_hat, u_inv = norm_fwd(x_zero, ln_scales[0])
-        q_pos = half * own + jnp.arange(own)
-        cos_t, sin_t = rope_tables(q_pos, head_dim)
-        q_raw = dot('rd,nd->rn', u_norm, wq_t).reshape(own, heads, head_dim)
-        queries = rotate(q_raw, cos_t[:, None, :], sin_t[:, None, :]).astype(BF16)
-        kv_raw = dot('rd,cde->cre', u_norm, wkv_b)
-        kv_own = jnp.concatenate([rotate(kv_raw[0], cos_t, sin_t), kv_raw[1]], axis=-1)
-        kv_other = pair_swap(kv_own, 3)
-        kv_seq = jnp.concatenate([jnp.where(half == 0, kv_own, kv_other), jnp.where(half == 0, kv_other, kv_own)], axis=0).astype(BF16)
-        keys = kv_seq[:, :head_dim]
-        values = kv_seq[:, head_dim:]
-        causal = q_pos[:, None] >= jnp.arange(2 * own)[None, :]
-        scores = dot('qhe,ke->hqk', queries, keys) * head_dim ** -0.5
-        prob_f32 = jax.nn.softmax(jnp.where(causal, scores, -1e30), axis=-1)
-        prob_b16 = prob_f32.astype(BF16)
-        context = dot('hqk,ke->qhe', prob_b16, values).astype(BF16).reshape(own, heads * head_dim)
-        att_out = dot('rf,fe->re', context, wo_b)
-        gate = dot('rd,fd->rf', u_norm, wg_t)
-        up = dot('rd,fd->rf', u_norm, wu_t)
-        gate_sig = jax.nn.sigmoid(gate)
-        hidden = (gate * gate_sig * up).astype(BF16)
-        x_one = x_zero + att_out + dot('rf,fd->rd', hidden, wd_b)
-        f_own, f_hat, f_inv = norm_fwd(x_one, ln_scales[1])
+        wkv_t = w_kv.transpose(0, 2, 1).reshape(2 * head_dim, d_model).astype(BF16)
+        weights = (wq_t, wkv_t, wo_b, wg_t, wu_t, wd_b)
+        inv_freq = ROPE_BASE ** (-jnp.arange(0, head_dim, 2).astype(F32) / head_dim)
+        angles = inv_freq[:, None] * (half * own + jnp.arange(own)).astype(F32)[None, :]
+        cos_t, sin_t = jnp.cos(angles), jnp.sin(angles)
+        f_own, x_one, *saved = layer_fwd(x_zero, ln_scales, cos_t, sin_t, weights, 3)
 
         logit_scale = d_model ** -0.5
         lab_loc = labels.reshape(n_tp, own) - tp_rank * vocab_loc
-        d_fin, g_head_part, log_norm, lab_sum = head(f_own.astype(F32), lab_loc, embed, logit_scale, logit_scale / tok_total, 4)
+        d_fin, g_head_part, log_norm, lab_sum = head(f_own, lab_loc, embed, logit_scale, logit_scale / tok_total, 4)
         log_norm = lax.dynamic_index_in_dim(log_norm, tp_rank, 0, keepdims=False)
-        loss_part = (jnp.sum(log_norm + LOGIT_ZLOSS * log_norm * log_norm) - jnp.sum(lab_sum) * logit_scale) / tok_total
+        loss_row = (log_norm + LOGIT_ZLOSS * log_norm * log_norm - jnp.sum(lab_sum, axis=0) * logit_scale) / tok_total
         g_head = lax.psum(g_head_part, 'dp')
-        d_one, g_ln_fin = norm_bwd(d_fin, f_hat, f_inv, ln_scales[1])
-        d_one_b = d_one.astype(BF16)
-
-        d_hidden = dot('rd,fd->rf', d_one_b, wd_b)
-        g_down = dot('rf,rd->fd', hidden, d_one_b)
-        d_gate = (d_hidden * up * gate_sig * (1.0 + gate * (1.0 - gate_sig))).astype(BF16)
-        d_up = (d_hidden * gate * gate_sig).astype(BF16)
-        g_gate = dot('rf,rd->fd', d_gate, u_norm)
-        g_up = dot('rf,rd->fd', d_up, u_norm)
-        d_u_mlp = dot('rf,fd->rd', d_gate, wg_t) + dot('rf,fd->rd', d_up, wu_t)
-
-        d_context = dot('re,fe->rf', d_one_b, wo_b).astype(BF16).reshape(own, heads, head_dim)
-        g_o = dot('rf,re->fe', context, d_one_b)
-        d_probs = dot('qhe,ke->hqk', d_context, values)
-        d_values = dot('hqk,qhe->ke', prob_b16, d_context)
-        d_scores = (prob_f32 * (d_probs - jnp.sum(d_probs * prob_f32, axis=-1, keepdims=True)) * head_dim ** -0.5).astype(BF16)
-        d_queries = dot('hqk,ke->qhe', d_scores, keys)
-        d_keys = dot('hqk,qhe->ke', d_scores, queries)
-        d_kv_seq = jnp.concatenate([d_keys, d_values], axis=-1)
-        d_kv_lo = d_kv_seq[:own]
-        d_kv_hi = d_kv_seq[own:]
-        d_kv_own = jnp.where(half == 0, d_kv_lo, d_kv_hi) + pair_swap(jnp.where(half == 0, d_kv_hi, d_kv_lo), 7)
-        d_q_raw = rotate(d_queries, cos_t[:, None, :], -sin_t[:, None, :]).astype(BF16).reshape(own, heads * head_dim)
-        d_kv = jnp.stack([rotate(d_kv_own[:, :head_dim], cos_t, -sin_t), d_kv_own[:, head_dim:]]).astype(BF16)
-        g_q_t = dot('rn,rd->nd', d_q_raw, u_norm)
-        g_kv_part = dot('cre,rd->cde', d_kv, u_norm)
-        d_u = dot('rn,nd->rd', d_q_raw, wq_t) + dot('cre,cde->rd', d_kv, wkv_b) + d_u_mlp
-        d_zero_norm, g_ln_in = norm_bwd(d_u, u_hat, u_inv, ln_scales[0])
-        d_zero = d_one + d_zero_norm
+        g_rows, d_zero = layer_bwd(d_fin, x_zero, x_one, loss_row[None, :], ln_scales, cos_t, sin_t, weights, saved, 7)
 
         my_row_shard = my_shard
 
@@ -882,13 +1072,12 @@
         g_look = give_back(0, jnp.zeros((vocab_loc, d_model), F32), 8)
         g_look = lax.while_loop(lambda s: s[0] < rounds_all, lambda s: (s[0] + 1, give_back(s[0], s[1], 9)), (jnp.int32(1), g_look))[1]
 
-        g_gu_t = jnp.stack([g_gate.reshape(n_tp, f_loc, d_model), g_up.reshape(n_tp, f_loc, d_model)], axis=1)
-        g_rows = jnp.concatenate([g_q_t.reshape(n_tp, q_loc, d_model), g_o.reshape(n_tp, q_loc, d_model),
-                                  g_gu_t.reshape(n_tp, 2 * f_loc, d_model), g_down.reshape(n_tp, f_loc, d_model)], axis=1)
-        g_shard = weight_scatter(g_rows, 10)
-        g_kv, g_ln, loss = lax.psum((g_kv_part, jnp.stack([g_ln_in, g_ln_fin]), loss_part), ('tp', 'dp'))
-        gradients = (g_head + g_look, g_ln, g_shard[:cuts[0]].T, g_kv, g_shard[cuts[0]:cuts[1]],
-                     g_shard[cuts[1]:cuts[3]].reshape(2, f_loc, d_model).transpose(0, 2, 1), g_shard[cuts[3]:])
+        g_shard, g_small = weight_scatter(g_rows, 10)
+        n_kv = 2 * head_dim // n_tp
+        g_kv = g_small[:, :n_kv].reshape(2, head_dim, d_model).transpose(0, 2, 1)
+        loss = jnp.sum(g_small[0, n_kv + 2])
+        gradients = (g_head + g_look, g_small[0, n_kv:n_kv + 2], g_shard[:cuts[0]].T, g_kv, g_shard[cuts[0]:cuts[1]],
+                     g_shard[cuts[1]:cuts[3]].reshape(2, f_loc, d_model).transpose(0, 2, 1), g_shard[cuts[3]:cuts[3] + f_loc])
 
         outs_p = []
         outs_m = []

time: 975 us -> 808 us (0.83)
  matrix products: 122 us -> 2.75 us
  Pallas kernels: 557 us -> 644 us
  waiting for transfers between devices: 46.5 us -> 0.02 us
  blocking collectives: 46.6 us -> 6.21 us
  other arithmetic: 143 us -> 104 us
    dot_general x25 -> x3, matrix products: 120 us -> 2.75 us  [dot(): return jnp.einsum(spec, a, b, preferred_element_type=F32)]
    pallas_call x3, Pallas kernels: 142 us -> 200 us  [the longest x1 138 us: weight_scatter(): pl.pallas_call(weight_scatter_kernel, out_shape=(jax.ShapeDtypeStruct((2,...]
    psum x1, waiting for transfers between devices: 45.9 us -> 0.01 us  [local_step(): g_head = lax.psum(g_head_part, 'dp')]
    psum x1 -> x0, blocking collectives: 40.4 us -> none  [local_step(): lax.psum((g_kv_part, jnp.stack([g_ln_in, g_ln_fin]), loss_part), ('tp', '...]
    pallas_call x1, Pallas kernels: 50.2 us -> 81.4 us  [row_return(): pl.pallas_call(row_return_kernel, out_shape=jax.ShapeDtypeStruct((4,) + x...]
    sub x2 -> x0, other arithmetic: 17.6 us -> none  [the longest x1 17.4 us: local_step(): prob_f32 = jax.nn.softmax(jnp.where(causal, scores, -1e+30), axis=-1)]
  transfers between devices with their start and end apart: 2 -> 1, of which waited for: 1 -> 0; matrix products, arithmetic and copies ran while one was open for 11% -> 6% of each run, Pallas kernels for 18% -> 32%
where the time goes in v3:
time: 808 us; the launch traced here: 799 us
  Pallas kernels  644 us (80%)
  other arithmetic  104 us (13%)
  local copies, waits for them, and re-layouts  25.4 us (3%)
  between operations  15.7 us (2%)
    pallas_call x1, Pallas kernels, head(): pl.pallas_call(functools.partial(head_kernel, scale, token_scale), out_sh...  244 us
    pallas_call x1, Pallas kernels, weight_scatter(): pl.pallas_call(weight_scatter_kernel, out_shape=(jax.ShapeDtypeStruct((2,...  138 us
    pallas_call x1, Pallas kernels, weight_gather(): pl.pallas_call(weight_gather_kernel, out_shape=jax.ShapeDtypeStruct((2 *...  89.3 us
    pallas_call x1, Pallas kernels, row_return(): pl.pallas_call(row_return_kernel, out_shape=jax.ShapeDtypeStruct((4,) + x...  81.4 us
    sub x7, other arithmetic, adam_update(): param_in - LEARN_RATE * mom_new / (jnp.sqrt(vel_new) + ADAM_EPS)  46.5 us
    pallas_call x1, Pallas kernels, layer_bwd(): pl.pallas_call(layer_bwd_kernel, out_shape=(jax.ShapeDtypeStruct((2 * NZ,...  38.8 us
    pallas_call x1, Pallas kernels, plane_swap(): pl.pallas_call(functools.partial(swap_kernel, spread), out_shape=jax.Shap...  29.1 us
    scatter-add x1, other arithmetic, give_back(): return g_look.at[row_id].add(rows_in, mode='drop')  24.9 us
  transfers between devices with their start and end apart: 1, of which 0 were waited for; matrix products, arithmetic and copies ran while one was open for 6% of the time, Pallas kernels for 32%

profile of v3, /device:TPU:0, one launch (start us, length us, event | category | flops | bytes accessed | tf_op | source)
XLA Modules:
  0.0 799.1 jit_solution(14099385853347084987)
XLA Ops:
  7.3 0.7 reshape.702
  8.0 0.3 fusion.32
  8.3 0.4 select_reduce_fusion.5
  8.9 6.2 all-gather.1
  15.2 0.7 multiply_subtract_fusion
  15.8 0.6 copy-done.3
  16.5 0.6 convert_reduce_fusion
  17.1 0.6 reduce_max.9
  18.4 1.6 copy.53
  20.0 2.5 pad_maximum_fusion
  22.5 89.3 %weight_gather.1 = f32[8,2,448,512]{3,2,1,0:T(8,128)} custom-call(f32[2,448,512]{2,1,0:T(8,128)} %bitcast.100), custom_call_target="tpu_custom_call" | custom-call | tf_op jit(solution)/shard_map/weight_gather/pallas_call | solution.py:169
  111.8 9.2 %convert_element_type.71 = bf16[8,2,448,512]{3,2,1,0:T(8,128)(2,1)} convert(f32[8,2,448,512]{3,2,1,0:T(8,128)} %weight_gather.1) | non-fusion elementwise | flops 3670016 | bytes 22020096 | tf_op jit(solution)/shard_map/convert_element_type | solution.py:1039
  121.0 2.3 fusion.65
  123.3 5.8 fusion.64
  129.0 0.6 sub.73.lab_ref
  129.8 0.7 convert_element_type.73
  130.5 8.2 %convert.11 = bf16[6288,512]{1,0:T(8,128)(2,1)} convert(f32[6288,512]{1,0:T(8,128)} %e_ref.1) | non-fusion elementwise | flops 3219456 | bytes 19316736
  138.7 7.4 gather_fusion.2
  146.3 1.4 convert.2.x_ref
  147.7 29.1 %plane_swap.2 = f32[8,96,512]{2,1,0:T(8,128)} custom-call(f32[8,96,512]{2,1,0:T(8,128)} %convert.2.x_ref), custom_call_target="tpu_custom_call" | custom-call | tf_op jit(solution)/shard_map/plane_swap/pallas_call | solution.py:383
  176.8 2.0 fusion.26
  178.9 0.5 while.22
  179.4 1.0 multiply_sine_fusion
  180.4 23.3 %layer_fwd.1 = (f32[512,512]{1,0:T(8,128)}, f32[512,512]{1,0:T(8,128)}, bf16[512,512]{1,0:T(8,128)(2,1)}, bf16[1024,128]{1,0:T(8,128)(2,1)}, bf16[128,1024]{1,0:...) custom-call(f32[512,512]{1,0:T(8,128)S(1)} %get-tuple-element.153.x0_ref, f32[2,512]{1,0:T(2,128)} %ln_ref.3, ...), custom_call_target="tpu_custom_call" | custom-call | tf_op jit(solution)/shard_map/layer_fwd/pallas_call | solution.py:818
  203.7 244.3 %head.1 = (f32[512,512]{1,0:T(8,128)}, f32[6288,512]{1,0:T(8,128)}, f32[8,512]{1,0:T(8,128)}, f32[8,512]{1,0:T(8,128)}) custom-call(f32[512,512]{1,0:T(8,128)} %get-tuple-element.154.f_ref, s32[8,512]{1,0:T(8,128)} %sub.73.lab_ref, f32[6288,512]{1,0:T(8,128)} %e_ref.1), custom_call_target="tpu_custom_call" | custom-call | flops 105495134208 | bytes 38633472 | tf_op jit(solution)/shard_map/head/pallas_call | solution.py:713
  448.1 0.3 select_reduce_fusion.4
  448.6 0.3 copy-done.11
  448.9 0.4 fusion.30
  449.4 1.0 fusion.22
  450.4 1.5 select_reduce_fusion.3
  452.0 1.3 fusion.54.loss_ref
  453.3 38.8 %layer_bwd.1 = (f32[8,928,512]{2,1,0:T(8,128)}, f32[512,512]{1,0:T(8,128)S(1)}) custom-call(f32[512,512]{1,0:T(8,128)} %get-tuple-element.156.dfin_ref, f32[512,512]{1,0:T(8,128)S(1)} %copy-done.2, f32[512,512]{1,0:T(8,128)} %get-tuple-element.157.x1_ref, f32[1,512]{1,0:T(1,128)} %fusion.54.loss_ref, f32[2,512]{1,0:T(2,128)} %ln_ref.3, ...), custom_call_target="tpu_custom_call" | custom-call | tf_op jit(solution)/shard_map/layer_bwd/pallas_call | solution.py:938
  492.1 2.4 gather_fusion.3
  494.5 1.3 broadcast_select_fusion.3.x_ref
  495.8 81.4 %row_return.2 = f32[4,8,96,512]{3,2,1,0:T(8,128)} custom-call(f32[8,96,512]{2,1,0:T(8,128)} %broadcast_select_fusion.3.x_ref), custom_call_target="tpu_custom_call" | custom-call | tf_op jit(solution)/shard_map/row_return/pallas_call | solution.py:438
  577.2 24.9 %scatter_custom_fusion.1 = f32[6288,512]{1,0:T(8,128)} fusion(s32[3072]{0:T(1024)S(1)} %bitcast.124, f32[3072,512]{1,0:T(8,128)} %bitcast.101, f32[]{:T(128)} %constant.86.clone.1), kind=kCustom, calls=%fused_computation.46 | custom fusion | flops 1572864 | bytes 12878336 | tf_op jit(solution)/shard_map/scatter-add | solution.py:1070
  602.4 137.9 %weight_scatter.1 = (f32[2,464,512]{2,1,0:T(8,128)}, f32[8,24,512]{2,1,0:T(8,128)}) custom-call(f32[8,2,464,512]{3,2,1,0:T(8,128)} %bitcast.99), custom_call_target="tpu_custom_call" | custom-call | tf_op jit(solution)/shard_map/weight_scatter/pallas_call | solution.py:340
  740.3 1.8 slice.43
  742.0 1.3 slice.63
  743.3 0.3 copy.54
  743.7 1.5 slice_reduce_fusion
  745.2 1.3 divide_subtract_fusion.6
  746.5 1.8 divide_subtract_fusion.4
  748.3 1.9 divide_subtract_fusion.5
  750.2 2.1 divide_subtract_fusion.3
  752.3 2.9 divide_subtract_fusion.2
  755.1 2.0 divide_subtract_fusion.1
  757.2 34.6 %divide_subtract_fusion = (f32[6288,512]{1,0:T(8,128)}, f32[6288,512]{1,0:T(8,128)}, f32[6288,512]{1,0:T(8,128)}) fusion(f32[6288,512]{1,0:T(8,128)} %e_ref.1, f32[6288,512]{1,0:T(8,128)} %all-reduce.2.cloned.1.call-done, f32[6288,512]{1,0:T(8,128)} %get-tuple-element.166, f32[6288,512]{1,0:T(8,128)} %param.36, f32[6288,512]{1,0:T(8,128)} %param.43), kind=kLoop, calls=%fused_computation.44 | loop fusion | flops 38633472 | bytes 103022592 | tf_op jit(solution)/shard_map/sub | solution.py:982
  (67 shorter events, 1.3 us)
Async XLA Ops:
  7.2 750.0 %all-reduce.2.cloned.1.call-start = ((), (), s32[]{:S(2)}) async-start(), calls=%async_computation | async-start | bytes 25755648 | tf_op jit(solution)/shard_map/psum | solution.py:1058
  15.1 3.3 copy-start.10
  15.8 0.6 copy-start.3
  123.3 5.8 copy-start.15
  123.3 6.5 copy-start.8
  179.4 1.0 copy-start.1
  448.0 0.8 copy-start.11
  448.0 0.9 copy-start.4
  448.0 2.4 copy-start.5
  448.0 3.9 copy-start.14
  448.1 5.3 copy-start.2
  602.3 142.8 %copy-start.13 = (f32[2,512]{1,0:T(2,128)S(1)}, f32[2,512]{1,0:T(2,128)}, u32[]{:S(2)}) copy-start(f32[2,512]{1,0:T(2,128)} %ln_ref.3) | copy-start | bytes 12292
  602.3 142.8 %copy-start.16 = (f32[2,512]{1,0:T(2,128)S(1)}, f32[2,512]{1,0:T(2,128)}, u32[]{:S(2)}) copy-start(f32[2,512]{1,0:T(2,128)} %param.37) | copy-start | bytes 12292
  602.4 142.8 %copy-start.17 = (f32[2,512]{1,0:T(2,128)S(1)}, f32[2,512]{1,0:T(2,128)}, u32[]{:S(2)}) copy-start(f32[2,512]{1,0:T(2,128)} %param.44) | copy-start | bytes 12292
  602.4 144.2 %copy-start.12 = (f32[64,512]{1,0:T(8,128)S(1)}, f32[64,512]{1,0:T(8,128)}, u32[]{:S(2)}) copy-start(f32[64,512]{1,0:T(8,128)} %param.33) | copy-start | bytes 393220
  740.2 10.0 %copy-start.9 = (f32[2,512,64]{1,2,0:T(8,128)S(1)}, f32[2,512,64]{1,2,0:T(8,128)}, u32[]{:S(2)}) copy-start(f32[2,512,64]{1,2,0:T(8,128)} %param.32) | copy-start | bytes 786436
  740.2 14.9 %copy-start = (f32[2,512,256]{2,1,0:T(8,128)S(1)}, f32[2,512,256]{2,1,0:T(8,128)}, u32[]{:S(2)}) copy-start(f32[2,512,256]{2,1,0:T(8,128)} %param.34) | copy-start | bytes 3145732
  743.7 11.5 %copy-start.6 = (f32[2,512,256]{2,1,0:T(8,128)S(1)}, f32[2,512,256]{2,1,0:T(8,128)}, u32[]{:S(2)}) copy-start(f32[2,512,256]{2,1,0:T(8,128)} %param.41) | copy-start | bytes 3145732
  743.7 11.5 %copy-start.7 = (f32[2,512,256]{2,1,0:T(8,128)S(1)}, f32[2,512,256]{2,1,0:T(8,128)}, u32[]{:S(2)}) copy-start(f32[2,512,256]{2,1,0:T(8,128)} %param.48) | copy-start | bytes 3145732
Sparse Core Ops, SparseCore 0:
  448.2 269.3 all-reduce.1

commit v4 on v3

--- a/solution.py
+++ b/solution.py
@@ -54,59 +54,6 @@
     for peer in peers:
         signal(*peer)
     pl.semaphore_wait(pltpu.get_barrier_semaphore(), len(peers))
-
-
-def gather_kernel(x_ref, out_ref, own_sem, send_y, send_l, send_r, recv):
-    tp, dp, z, y = place()
-    partner = tp + 1 - 2 * y
-
-    def program(k):
-        line_barrier(k, tp, dp, [])
-
-        def send(src, slot, sems, to):
-            copy = remote(src, out_ref.at[slot], sems.at[slot], recv.at[slot], to, dp)
-            copy.start()
-            return copy
-
-        def arrived(slot):
-            remote(x_ref, out_ref.at[slot], send_y.at[slot], recv.at[slot], partner, dp).wait_recv()
-
-        sends = []
-        if k > 0:
-            sends.append(send(x_ref, tp, send_l, tp - 2))
-        if k < NZ - 1:
-            sends.append(send(x_ref, tp, send_r, tp + 2))
-        sends.append(send(x_ref, tp, send_y, partner))
-        own = pltpu.make_async_copy(x_ref, out_ref.at[tp], own_sem)
-        own.start()
-        for side, zz in ARRIVALS[k]:
-            slot = 2 * zz + y
-            arrived(slot)
-            if side == "L" and k < NZ - 1:
-                sends.append(send(out_ref.at[slot], slot, send_r, tp + 2))
-            if side == "R" and k > 0:
-                sends.append(send(out_ref.at[slot], slot, send_l, tp - 2))
-            sends.append(send(out_ref.at[slot], slot, send_y, partner))
-        for zz in range(NZ):
-            arrived(2 * zz + 1 - y)
-        own.wait()
-        for copy in sends:
-            copy.wait_send()
-
-    for k in range(NZ):
-        pl.when(z == k)(functools.partial(program, k))
-
-
-def plane_gather(x, collective_id):
-    return pl.pallas_call(
-        gather_kernel,
-        out_shape=jax.ShapeDtypeStruct((2 * NZ,) + x.shape, x.dtype),
-        in_specs=[ANY],
-        out_specs=ANY,
-        scratch_shapes=[pltpu.SemaphoreType.DMA] + [pltpu.SemaphoreType.DMA((2 * NZ,))] * 4,
-        compiler_params=pltpu.CompilerParams(collective_id=collective_id, has_side_effects=True),
-        name="plane_gather",
-    )(x)
 
 
 def weight_gather_kernel(x_ref, out_ref, own_sem, send_y, send_l, send_r, send_c, recv):
@@ -179,9 +126,9 @@
     return out.reshape(2 * NZ, rows, width)
 
 
-def add_into(acc, other):
+def add_into(acc, other, step=None):
     rows = acc.shape[0]
-    step = 64 if rows % 64 == 0 else rows
+    step = step or (64 if rows % 64 == 0 else 8)
 
     def body(n, carry):
         at = pl.ds(pl.multiple_of(n * step, step), step)
@@ -189,168 +136,6 @@
         return carry
 
     lax.fori_loop(0, rows // step, body, 0)
-
-
-def scatter_kernel(p_ref, out_ref, acc, from_y, from_l, from_r, load_sem, out_sem, send_y, send_l, send_r, recv_y, recv_l, recv_r):
-    tp, dp, z, y = place()
-    partner = tp + 1 - 2 * y
-
-    def program(k):
-        line_barrier(k, tp, dp, [])
-        sends = []
-        loads = []
-        for zz in REDUCE_ORDER[k]:
-            copy = remote(p_ref.at[2 * zz + 1 - y], from_y.at[zz], send_y.at[zz], recv_y.at[zz], partner, dp)
-            copy.start()
-            sends.append(copy)
-        for zz in REDUCE_ORDER[k]:
-            load = pltpu.make_async_copy(p_ref.at[2 * zz + y], acc.at[zz], load_sem.at[zz])
-            load.start()
-            loads.append(load)
-        for n, zz in enumerate(REDUCE_ORDER[k]):
-            loads[n].wait()
-            remote(acc.at[zz], from_y.at[zz], send_y.at[zz], recv_y.at[zz], partner, dp).wait_recv()
-            add_into(acc.at[zz], from_y.at[zz])
-            if zz >= k and k > 0:
-                remote(acc.at[zz], from_l.at[zz], send_l.at[zz], recv_l.at[zz], partner, dp).wait_recv()
-                add_into(acc.at[zz], from_l.at[zz])
-            if zz <= k and k < NZ - 1:
-                remote(acc.at[zz], from_r.at[zz], send_r.at[zz], recv_r.at[zz], partner, dp).wait_recv()
-                add_into(acc.at[zz], from_r.at[zz])
-            if zz > k:
-                copy = remote(acc.at[zz], from_l.at[zz], send_r.at[zz], recv_l.at[zz], tp + 2, dp)
-                copy.start()
-                sends.append(copy)
-            if zz < k:
-                copy = remote(acc.at[zz], from_r.at[zz], send_l.at[zz], recv_r.at[zz], tp - 2, dp)
-                copy.start()
-                sends.append(copy)
-        out = pltpu.make_async_copy(acc.at[k], out_ref, out_sem)
-        out.start()
-        out.wait()
-        for copy in sends:
-            copy.wait_send()
-
-    for k in range(NZ):
-        pl.when(z == k)(functools.partial(program, k))
-
-
-def plane_scatter(p, collective_id):
-    _, rows, width = p.shape
-    line = (NZ, rows, width)
-    return pl.pallas_call(
-        scatter_kernel,
-        out_shape=jax.ShapeDtypeStruct((rows, width), p.dtype),
-        in_specs=[ANY],
-        out_specs=ANY,
-        scratch_shapes=[pltpu.VMEM(line, p.dtype)] * 4
-        + [pltpu.SemaphoreType.DMA((NZ,)), pltpu.SemaphoreType.DMA]
-        + [pltpu.SemaphoreType.DMA((NZ,))] * 6,
-        compiler_params=pltpu.CompilerParams(collective_id=collective_id, has_side_effects=True),
-        name="plane_scatter",
-    )(p)
-
-
-def weight_scatter_kernel(p_ref, out_ref, small_ref, acc, from_c, from_y, from_l, from_r, from_x, load_sem, out_sem, send_c, send_y, send_l, send_r,
-                          last_send, recv_c, recv_y, recv_l, recv_r, last_recv, small_send, small_recv):
-    tp, dp, z, y = place()
-    partner = tp + 1 - 2 * y
-    core = dp % 2
-    twin = dp + 1 - 2 * core
-    facing = lax.rem(dp + 2, 4)
-
-    def program(k):
-        plane_barrier(tp, dp, [(tp, twin), (tp, facing)])
-        sends = []
-        for zz in REDUCE_ORDER[k]:
-            for slot in (2 * zz + 1 - y, 2 * zz + y):
-                copy = remote(p_ref.at[slot, 1 - core], from_c.at[slot], send_c.at[slot], recv_c.at[slot], tp, twin)
-                copy.start()
-                sends.append(copy)
-                pltpu.make_async_copy(p_ref.at[slot, core], acc.at[slot], load_sem.at[slot]).start()
-
-        def chip_sum(slot):
-            pltpu.make_async_copy(p_ref.at[slot, core], acc.at[slot], load_sem.at[slot]).wait()
-            remote(acc.at[slot], from_c.at[slot], send_c.at[slot], recv_c.at[slot], tp, twin).wait_recv()
-            add_into(acc.at[slot], from_c.at[slot])
-
-        for zz in REDUCE_ORDER[k]:
-            slot = 2 * zz + 1 - y
-            chip_sum(slot)
-            copy = remote(acc.at[slot], from_y.at[zz], send_y.at[zz], recv_y.at[zz], partner, dp)
-            copy.start()
-            sends.append(copy)
-        for zz in REDUCE_ORDER[k]:
-            chip_sum(2 * zz + y)
-        for zz in REDUCE_ORDER[k]:
-            slot = 2 * zz + y
-            line = acc.at[slot]
-            remote(line, from_y.at[zz], send_y.at[zz], recv_y.at[zz], partner, dp).wait_recv()
-            add_into(line, from_y.at[zz])
-            if zz >= k and k > 0:
-                remote(line, from_l.at[zz], send_l.at[zz], recv_l.at[zz], partner, dp).wait_recv()
-                add_into(line, from_l.at[zz])
-            if zz <= k and k < NZ - 1:
-                remote(line, from_r.at[zz], send_r.at[zz], recv_r.at[zz], partner, dp).wait_recv()
-                add_into(line, from_r.at[zz])
-            if zz > k:
-                copy = remote(line, from_l.at[zz], send_r.at[zz], recv_l.at[zz], tp + 2, dp)
-                copy.start()
-                sends.append(copy)
-            if zz < k:
-                copy = remote(line, from_r.at[zz], send_l.at[zz], recv_r.at[zz], tp - 2, dp)
-                copy.start()
-                sends.append(copy)
-        total = acc.at[2 * k + y]
-        copy = remote(total, from_x, last_send.at[0], last_recv.at[0], tp, facing)
-        copy.start()
-        copy.wait()
-        add_into(total, from_x)
-        copy = remote(total, out_ref.at[core], last_send.at[1], last_recv.at[1], tp, twin)
-        copy.start()
-        out = pltpu.make_async_copy(total, out_ref.at[core], out_sem)
-        out.start()
-        copy.wait_send()
-        remote(total, out_ref.at[1 - core], last_send.at[1], last_recv.at[1], tp, twin).wait_recv()
-        out.wait()
-
-        n_small, n_rows = small_ref.shape[1], out_ref.shape[1]
-        mine = out_ref.at[1, pl.ds(n_rows - 32, n_small), :]
-        for n in range(1, 2 * NZ):
-            to = lax.rem(tp + n, 2 * NZ)
-            copy = remote(mine, small_ref.at[tp], small_send.at[to], small_recv.at[tp], to, dp)
-            copy.start()
-            sends.append(copy)
-        here = pltpu.make_async_copy(mine, small_ref.at[tp], out_sem)
-        here.start()
-        for n in range(1, 2 * NZ):
-            source = lax.rem(tp + n, 2 * NZ)
-            remote(small_ref.at[source], small_ref.at[source], small_send.at[source], small_recv.at[source], source, dp).wait_recv()
-        here.wait()
-        for copy in sends:
-            copy.wait_send()
-
-    for k in range(NZ):
-        pl.when(z == k)(functools.partial(program, k))
-
-
-def weight_scatter(p, collective_id):
-    _, rows, width = p.shape
-    half = (rows // 2, width)
-    out, small = pl.pallas_call(
-        weight_scatter_kernel,
-        out_shape=(jax.ShapeDtypeStruct((2,) + half, p.dtype), jax.ShapeDtypeStruct((2 * NZ, 24, width), p.dtype)),
-        in_specs=[ANY],
-        out_specs=(ANY, ANY),
-        scratch_shapes=[pltpu.VMEM((2 * NZ,) + half, p.dtype)] * 2 + [pltpu.VMEM((NZ,) + half, p.dtype)] * 3
-        + [pltpu.VMEM(half, p.dtype)]
-        + [pltpu.SemaphoreType.DMA((2 * NZ,)), pltpu.SemaphoreType.DMA]
-        + ([pltpu.SemaphoreType.DMA((2 * NZ,))] + [pltpu.SemaphoreType.DMA((NZ,))] * 3 + [pltpu.SemaphoreType.DMA((2,))]) * 2
-        + [pltpu.SemaphoreType.DMA((2 * NZ,))] * 2,
-        compiler_params=pltpu.CompilerParams(collective_id=collective_id, has_side_effects=True),
-        name="weight_scatter",
-    )(p.reshape((2 * NZ, 2) + half))
-    return out.reshape(rows, width), small
 
 
 def plane_barrier(tp, dp, others):
@@ -388,84 +173,6 @@
         scratch_shapes=[pltpu.SemaphoreType.DMA] + [pltpu.SemaphoreType.DMA((2 * NZ,))] * 2,
         compiler_params=pltpu.CompilerParams(collective_id=collective_id, has_side_effects=True),
         name="plane_spread" if spread else "plane_swap",
-    )(x)
-
-
-def row_return_kernel(x_ref, out_ref, own_sem, send, send_c, send_x, recv):
-    tp, dp, _, _ = place()
-    core = dp % 2
-    twin = dp + 1 - 2 * core
-    facing = lax.rem(dp + 2, 4)
-    plane_barrier(tp, dp, [(tp, twin), (tp, facing)])
-    copies = []
-
-    def forward(group, source, sems, to_dp):
-        copy = remote(out_ref.at[group, source], out_ref.at[group, source], sems.at[source], recv.at[group, source], tp, to_dp)
-        copy.start()
-        copies.append(copy)
-
-    def arrived(group, source):
-        remote(out_ref.at[group, source], out_ref.at[group, source], send.at[source], recv.at[group, source], tp, twin).wait_recv()
-
-    for n in range(1, 2 * NZ):
-        to = lax.rem(tp + n, 2 * NZ)
-        copy = remote(x_ref.at[to], out_ref.at[dp, tp], send.at[to], recv.at[dp, tp], to, dp)
-        copy.start()
-        copies.append(copy)
-    own = pltpu.make_async_copy(x_ref.at[tp], out_ref.at[dp, tp], own_sem)
-    own.start()
-    own.wait()
-    forward(dp, tp, send_x, facing)
-    forward(dp, tp, send_c.at[0], twin)
-    for n in range(1, 2 * NZ):
-        source = lax.rem(tp + 2 * NZ - n, 2 * NZ)
-        arrived(dp, source)
-        forward(dp, source, send_x, facing)
-        forward(dp, source, send_c.at[0], twin)
-    for n in range(2 * NZ):
-        source = lax.rem(tp + 2 * NZ - n, 2 * NZ)
-        arrived(facing, source)
-        forward(facing, source, send_c.at[1], twin)
-    for n in range(2 * NZ):
-        source = lax.rem(tp + 2 * NZ - n, 2 * NZ)
-        arrived(twin, source)
-        arrived(lax.rem(twin + 2, 4), source)
-    for copy in copies:
-        copy.wait_send()
-
-
-def row_return(x, collective_id):
-    return pl.pallas_call(
-        row_return_kernel,
-        out_shape=jax.ShapeDtypeStruct((4,) + x.shape, x.dtype),
-        in_specs=[ANY],
-        out_specs=ANY,
-        scratch_shapes=[pltpu.SemaphoreType.DMA, pltpu.SemaphoreType.DMA((2 * NZ,)), pltpu.SemaphoreType.DMA((2, 2 * NZ)),
-                        pltpu.SemaphoreType.DMA((2 * NZ,)), pltpu.SemaphoreType.DMA((4, 2 * NZ))],
-        compiler_params=pltpu.CompilerParams(collective_id=collective_id, has_side_effects=True),
-        name="row_return",
-    )(x)
-
-
-def pair_kernel(x_ref, out_ref, send, recv):
-    tp, dp, _, y = place()
-    partner = tp + 1 - 2 * y
-    signal(partner, dp)
-    pl.semaphore_wait(pltpu.get_barrier_semaphore(), 1)
-    copy = remote(x_ref, out_ref, send, recv, partner, dp)
-    copy.start()
-    copy.wait()
-
-
-def pair_swap(x, collective_id):
-    return pl.pallas_call(
-        pair_kernel,
-        out_shape=jax.ShapeDtypeStruct(x.shape, x.dtype),
-        in_specs=[VMEM],
-        out_specs=VMEM,
-        scratch_shapes=[pltpu.SemaphoreType.DMA, pltpu.SemaphoreType.DMA],
-        compiler_params=pltpu.CompilerParams(collective_id=collective_id, has_side_effects=True),
-        name="pair_swap",
     )(x)
 
 
@@ -949,6 +656,235 @@
     )(d_fin, x0, x1, loss_row, ln, cos_t, sin_t, *weights, *saved)
 
 
+N_BLOCK = 12
+EARLY = 9
+W_REDUCE = {
+    0: {0: (3,), 2: (2,), 4: (1,), 6: (0,)},
+    1: {2: (3,), 4: (2, 0), 6: (1,)},
+    2: {2: (0,), 4: (1, 3), 6: (2,)},
+    3: {0: (0,), 2: (1,), 4: (2,), 6: (3,)},
+}
+
+
+def tail_kernel(g_ref, p_ref, e_ref, m_ref, v_ref, e_new, m_new, v_new, w_out, small_ref,
+                s_buf, from_c, from_x, t_buf, state_in, state_out, acc, w_c, w_y, w_l, w_r, w_x,
+                g_load, g_send_c, g_recv_c, g_send_x, g_recv_x, g_send_t, g_recv_t, in_sem, out_sem,
+                w_load, w_out_sem, send_c, send_y, send_l, send_r, recv_c, recv_y, recv_l, recv_r, last_send, last_recv, small_send, small_recv):
+    tp, dp, z, y = place()
+    partner = tp + 1 - 2 * y
+    core = dp % 2
+    twin = dp + 1 - 2 * core
+    facing = lax.rem(dp + 2, 4)
+    half = g_ref.shape[0] // 2
+    size = s_buf.shape[1]
+    sizes = [min(size, half - b * size) for b in range(N_BLOCK)]
+
+    def rows(which, b):
+        return pl.ds(pl.multiple_of(which * half + b * size, 8), sizes[b])
+
+    def part(buf, b):
+        return buf.at[b, pl.ds(0, sizes[b]), :]
+
+    todo = [(0, 0)] + [pair for b in range(1, N_BLOCK) for pair in ((0, b), (1, b - 1))] + [(1, N_BLOCK - 1)]
+
+    def state_loads(q):
+        other, b = todo[q]
+        at = rows(core + other - 2 * core * other, b)
+        return [pltpu.make_async_copy(ref.at[at, :], state_in.at[q % 2, n, pl.ds(0, sizes[b]), :], in_sem.at[q % 2, n])
+                for n, ref in enumerate((e_ref, m_ref, v_ref))]
+
+    def state_stores(q):
+        other, b = todo[q]
+        at = rows(core + other - 2 * core * other, b)
+        return [pltpu.make_async_copy(state_out.at[q % 2, n, pl.ds(0, sizes[b]), :], ref.at[at, :], out_sem.at[q % 2, n])
+                for n, ref in enumerate((e_new, m_new, v_new))]
+
+    def update(q):
+        other, b = todo[q]
+        grad = from_x if other == 0 else t_buf
+        for c in state_loads(q):
+            c.wait()
+        if q >= 2:
+            for c in state_stores(q - 2):
+                c.wait()
+
+        def body(n, carry):
+            at = pl.ds(pl.multiple_of(n * 24, 8), 24)
+            new = adam_update(state_in[q % 2, 0, at, :], grad[b, at, :], state_in[q % 2, 1, at, :], state_in[q % 2, 2, at, :])
+            for i in range(3):
+                state_out[q % 2, i, at, :] = new[i]
+            return carry
+
+        lax.fori_loop(0, sizes[b] // 24, body, 0)
+        for c in state_stores(q):
+            c.start()
+        if q + 2 < len(todo):
+            for c in state_loads(q + 2):
+                c.start()
+
+    plane_barrier(tp, dp, [(tp, twin), (tp, facing)])
+    for q in range(2):
+        for c in state_loads(q):
+            c.start()
+
+    def g_first(b):
+        remote(g_ref.at[rows(1 - core, b), :], part(from_c, b), g_send_c.at[b], g_recv_c.at[b], tp, twin).start()
+        pltpu.make_async_copy(g_ref.at[rows(core, b), :], part(s_buf, b), g_load.at[b]).start()
+
+    def g_chip_sum(b):
+        pltpu.make_async_copy(g_ref.at[rows(core, b), :], part(s_buf, b), g_load.at[b]).wait()
+        remote(part(s_buf, b), part(from_c, b), g_send_c.at[b], g_recv_c.at[b], tp, twin).wait_recv()
+        add_into(part(s_buf, b), part(from_c, b), 24)
+
+    def g_copy_x(b):
+        return remote(part(s_buf, b), part(from_x, b), g_send_x.at[b], g_recv_x.at[b], tp, facing)
+
+    def g_copy_t(b):
+        return remote(part(from_x, b), part(t_buf, b), g_send_t.at[b], g_recv_t.at[b], tp, twin)
+
+    def w_first(k):
+        for zz in REDUCE_ORDER[k]:
+            for slot in (2 * zz + 1 - y, 2 * zz + y):
+                remote(p_ref.at[slot, 1 - core], w_c.at[slot], send_c.at[slot], recv_c.at[slot], tp, twin).start()
+                pltpu.make_async_copy(p_ref.at[slot, core], acc.at[slot], w_load.at[slot]).start()
+
+    def w_chip_sum(slot):
+        pltpu.make_async_copy(p_ref.at[slot, core], acc.at[slot], w_load.at[slot]).wait()
+        remote(acc.at[slot], w_c.at[slot], send_c.at[slot], recv_c.at[slot], tp, twin).wait_recv()
+        add_into(acc.at[slot], w_c.at[slot])
+
+    def w_second(k):
+        for zz in REDUCE_ORDER[k]:
+            slot = 2 * zz + 1 - y
+            w_chip_sum(slot)
+            remote(acc.at[slot], w_y.at[zz], send_y.at[zz], recv_y.at[zz], partner, dp).start()
+        for zz in REDUCE_ORDER[k]:
+            w_chip_sum(2 * zz + y)
+
+    def w_reduce(k, shards):
+        for zz in shards:
+            line = acc.at[2 * zz + y]
+            remote(line, w_y.at[zz], send_y.at[zz], recv_y.at[zz], partner, dp).wait_recv()
+            add_into(line, w_y.at[zz])
+            if zz >= k and k > 0:
+                remote(line, w_l.at[zz - 1], send_l.at[zz], recv_l.at[zz], partner, dp).wait_recv()
+                add_into(line, w_l.at[zz - 1])
+            if zz <= k and k < NZ - 1:
+                remote(line, w_r.at[zz], send_r.at[zz], recv_r.at[zz], partner, dp).wait_recv()
+                add_into(line, w_r.at[zz])
+            if zz > k:
+                remote(line, w_l.at[zz - 1], send_r.at[zz], recv_l.at[zz], tp + 2, dp).start()
+            if zz < k:
+                remote(line, w_r.at[zz], send_l.at[zz], recv_r.at[zz], tp - 2, dp).start()
+
+    def on_position(f):
+        for k in range(NZ):
+            pl.when(z == k)(functools.partial(f, k))
+
+    g_first(0)
+    g_first(1)
+    on_position(w_first)
+    for b in range(2, N_BLOCK):
+        g_first(b)
+    for b in range(2):
+        g_chip_sum(b)
+        g_copy_x(b).start()
+    on_position(w_second)
+    for b in range(2, EARLY):
+        g_chip_sum(b)
+        g_copy_x(b).start()
+
+    total = acc.at[tp]
+    w_copy_x = remote(total, w_x, last_send.at[0], last_recv.at[0], tp, facing)
+    w_copy_c = remote(total, w_out.at[core], last_send.at[1], last_recv.at[1], tp, twin)
+    w_store = pltpu.make_async_copy(total, w_out.at[core], w_out_sem)
+    n_small, n_rows = small_ref.shape[1], w_out.shape[1]
+    mine = w_out.at[1, pl.ds(n_rows - 32, n_small), :]
+    small_here = pltpu.make_async_copy(mine, small_ref.at[tp], w_out_sem)
+    peers = [lax.rem(tp + n, 2 * NZ) for n in range(1, 2 * NZ)]
+    q = 0
+    for b in range(N_BLOCK):
+        g_copy_x(b).wait_recv()
+        add_into(part(from_x, b), part(s_buf, b), 24)
+        g_copy_t(b).start()
+        update(q)
+        q += 1
+        if b > 0:
+            g_copy_t(b - 1).wait_recv()
+            update(q)
+            q += 1
+        for k in range(NZ):
+            if b in W_REDUCE[k]:
+                pl.when(z == k)(functools.partial(w_reduce, k, W_REDUCE[k][b]))
+        if b == 6:
+            w_copy_x.start()
+            for late in range(EARLY, N_BLOCK):
+                g_chip_sum(late)
+                g_copy_x(late).start()
+        if b == 8:
+            w_copy_x.wait()
+            add_into(total, w_x)
+            w_copy_c.start()
+            w_store.start()
+        if b == 9:
+            w_copy_c.wait_send()
+            remote(total, w_out.at[1 - core], last_send.at[1], last_recv.at[1], tp, twin).wait_recv()
+            w_store.wait()
+            for to in peers:
+                remote(mine, small_ref.at[tp], small_send.at[to], small_recv.at[tp], to, dp).start()
+            small_here.start()
+    g_copy_t(N_BLOCK - 1).wait_recv()
+    update(q)
+    for source in peers:
+        remote(small_ref.at[source], small_ref.at[source], small_send.at[source], small_recv.at[source], source, dp).wait_recv()
+        remote(mine, small_ref.at[tp], small_send.at[source], small_recv.at[tp], source, dp).wait_send()
+    small_here.wait()
+    for b in range(N_BLOCK):
+        remote(g_ref.at[rows(1 - core, b), :], part(from_c, b), g_send_c.at[b], g_recv_c.at[b], tp, twin).wait_send()
+        g_copy_x(b).wait_send()
+        g_copy_t(b).wait_send()
+
+    def w_done(k):
+        for zz in range(NZ):
+            line = acc.at[2 * zz + y]
+            for slot in (2 * zz + 1 - y, 2 * zz + y):
+                remote(p_ref.at[slot, 1 - core], w_c.at[slot], send_c.at[slot], recv_c.at[slot], tp, twin).wait_send()
+            remote(line, w_y.at[zz], send_y.at[zz], recv_y.at[zz], partner, dp).wait_send()
+            if zz > k:
+                remote(line, w_l.at[zz - 1], send_r.at[zz], recv_l.at[zz], tp + 2, dp).wait_send()
+            if zz < k:
+                remote(line, w_r.at[zz], send_l.at[zz], recv_r.at[zz], tp - 2, dp).wait_send()
+
+    on_position(w_done)
+    for last in (len(todo) - 2, len(todo) - 1):
+        for c in state_stores(last):
+            c.wait()
+
+
+def tail(g_table, g_rows, embed, m_embed, v_embed, collective_id):
+    vocab, width = embed.shape
+    rows = g_rows.shape[1]
+    half = (rows // 2, width)
+    size = -(-vocab // (2 * N_BLOCK * 24)) * 24
+    blocks = pltpu.VMEM((N_BLOCK, size, width), F32)
+    dma = lambda *n: pltpu.SemaphoreType.DMA(n)
+    table = jax.ShapeDtypeStruct((vocab, width), F32)
+    *new, w_sum, small = pl.pallas_call(
+        tail_kernel,
+        out_shape=(table, table, table, jax.ShapeDtypeStruct((2,) + half, F32), jax.ShapeDtypeStruct((2 * NZ, 24, width), F32)),
+        in_specs=[ANY] * 5,
+        out_specs=(ANY,) * 5,
+        scratch_shapes=[blocks] * 4 + [pltpu.VMEM((2, 3, size, width), F32)] * 2
+        + [pltpu.VMEM((2 * NZ,) + half, F32)] * 2 + [pltpu.VMEM((NZ,) + half, F32)] + [pltpu.VMEM((NZ - 1,) + half, F32)] * 2
+        + [pltpu.VMEM(half, F32)]
+        + [dma(N_BLOCK)] * 7 + [dma(2, 3)] * 2
+        + [dma(2 * NZ), pltpu.SemaphoreType.DMA] + [dma(2 * NZ), dma(NZ), dma(NZ), dma(NZ)] * 2 + [dma(2)] * 2 + [dma(2 * NZ)] * 2,
+        compiler_params=pltpu.CompilerParams(collective_id=collective_id, has_side_effects=True, vmem_limit_bytes=67000000),
+        name="tail",
+    )(g_table, g_rows.reshape((2 * NZ, 2) + half), embed, m_embed, v_embed)
+    return new, w_sum.reshape(rows, width), small
+
+
 def norm_fwd(x_f32, scale):
     centered = x_f32 - jnp.mean(x_f32, axis=-1, keepdims=True)
     inv_std = lax.rsqrt(jnp.mean(centered * centered, axis=-1, keepdims=True) + LN_EPS)
@@ -1019,7 +955,7 @@
 
         chunks = tokens.reshape(n_tp, own)
         shard, row, rank, _ = routing(chunks)
-        shard_all, row_all, rank_all, rounds_all = routing(all_tokens)
+        rounds_all = routing(all_tokens)[3]
         slots = jnp.arange(CAP)
         my_shard = lax.dynamic_index_in_dim(shard, tp_rank, 0, keepdims=False)
         my_rank = lax.dynamic_index_in_dim(rank, tp_rank, 0, keepdims=False)
@@ -1055,34 +991,29 @@
         d_fin, g_head_part, log_norm, lab_sum = head(f_own, lab_loc, embed, logit_scale, logit_scale / tok_total, 4)
         log_norm = lax.dynamic_index_in_dim(log_norm, tp_rank, 0, keepdims=False)
         loss_row = (log_norm + LOGIT_ZLOSS * log_norm * log_norm - jnp.sum(lab_sum, axis=0) * logit_scale) / tok_total
-        g_head = lax.psum(g_head_part, 'dp')
         g_rows, d_zero = layer_bwd(d_fin, x_zero, x_one, loss_row[None, :], ln_scales, cos_t, sin_t, weights, saved, 7)
 
-        my_row_shard = my_shard
-
-        def give_back(step, g_look, collective_id):
-            mine = (my_row_shard[None, None, :] == jnp.arange(n_tp)[:, None, None]) & (my_rank[None, None, :] == slots[None, :, None] + step * CAP)
+        def give_back(step, g_sum, collective_id):
+            mine = (my_shard[None, None, :] == jnp.arange(n_tp)[:, None, None]) & (my_rank[None, None, :] == slots[None, :, None] + step * CAP)
             ids = jnp.sum(jnp.where(mine, jnp.arange(own)[None, None, :], 0), axis=-1).reshape(-1)
             rows_out = jnp.take(d_zero, ids, axis=0).reshape(n_tp, CAP, d_model)
-            rows_in = row_return(rows_out, collective_id).reshape(-1, d_model)
-            here = (shard_all[:, None, :] == tp_rank) & (rank_all[:, None, :] == slots[None, :, None] + step * CAP)
-            row_id = jnp.where(jnp.any(here, axis=-1), jnp.sum(jnp.where(here, row_all[:, None, :], 0), axis=-1), vocab_loc).reshape(-1)
-            return g_look.at[row_id].add(rows_in, mode='drop')
-
-        g_look = give_back(0, jnp.zeros((vocab_loc, d_model), F32), 8)
-        g_look = lax.while_loop(lambda s: s[0] < rounds_all, lambda s: (s[0] + 1, give_back(s[0], s[1], 9)), (jnp.int32(1), g_look))[1]
-
-        g_shard, g_small = weight_scatter(g_rows, 10)
+            rows_in = plane_swap(rows_out, False, collective_id).reshape(-1, d_model)
+            here = (shard[:, None, :] == tp_rank) & (rank[:, None, :] == slots[None, :, None] + step * CAP)
+            row_id = jnp.where(jnp.any(here, axis=-1), jnp.sum(jnp.where(here, row[:, None, :], 0), axis=-1), vocab_loc).reshape(-1)
+            return g_sum.at[row_id].add(rows_in, mode='drop')
+
+        g_table = give_back(0, g_head_part, 8)
+        g_table = lax.while_loop(lambda s: s[0] < rounds_all, lambda s: (s[0] + 1, give_back(s[0], s[1], 9)), (jnp.int32(1), g_table))[1]
+
+        new_table, g_shard, g_small = tail(g_table, g_rows, embed, state_arrays[7], state_arrays[14], 10)
         n_kv = 2 * head_dim // n_tp
         g_kv = g_small[:, :n_kv].reshape(2, head_dim, d_model).transpose(0, 2, 1)
         loss = jnp.sum(g_small[0, n_kv + 2])
-        gradients = (g_head + g_look, g_small[0, n_kv:n_kv + 2], g_shard[:cuts[0]].T, g_kv, g_shard[cuts[0]:cuts[1]],
+        gradients = (None, g_small[0, n_kv:n_kv + 2], g_shard[:cuts[0]].T, g_kv, g_shard[cuts[0]:cuts[1]],
                      g_shard[cuts[1]:cuts[3]].reshape(2, f_loc, d_model).transpose(0, 2, 1), g_shard[cuts[3]:cuts[3] + f_loc])
 
-        outs_p = []
-        outs_m = []
-        outs_v = []
-        for index in range(7):
+        outs_p, outs_m, outs_v = ([array] for array in new_table)
+        for index in range(1, 7):
             new_p, new_m, new_v = adam_update(state_arrays[index], gradients[index], state_arrays[7 + index], state_arrays[14 + index])
             outs_p.append(new_p)
             outs_m.append(new_m)

time: 808 us -> 773 us (0.957)
  other arithmetic: 104 us -> 60.6 us
  local copies, waits for them, and re-layouts: 25.4 us -> 56.4 us
  between operations: 15.7 us -> 1.99 us
    pallas_call x2 -> x1, Pallas kernels: 219 us -> 181 us  [tail(): pl.pallas_call(tail_kernel, out_shape=(table, table, table, jax.ShapeDtyp...]
    sub x7 -> x6, other arithmetic: 46.5 us -> 10.9 us  [adam_update(): param_in - LEARN_RATE * mom_new / (jnp.sqrt(vel_new) + ADAM_EPS)]
    unnamed x37 -> x52, local copies, waits for them, and re-layouts: 2.55 us -> 35.8 us
    pallas_call x1 -> x2, Pallas kernels: 29.1 us -> 56.6 us  [plane_swap(): pl.pallas_call(functools.partial(swap_kernel, spread), out_shape=jax.Shap...]
    pallas_call x1, Pallas kernels: 89.3 us -> 98.4 us  [weight_gather(): pl.pallas_call(weight_gather_kernel, out_shape=jax.ShapeDtypeStruct((2 *...]
    scatter-add x1, other arithmetic: 24.9 us -> 16.6 us  [give_back(): return g_sum.at[row_id].add(rows_in, mode='drop')]
  transfers between devices with their start and end apart: 1 -> 0, of which waited for: 0 -> 0; matrix products, arithmetic and copies ran while one was open for 6% -> 0% of each run, Pallas kernels for 32% -> 0%
where the time goes in v4:
time: 773 us; the launch traced here: 765 us
  Pallas kernels  637 us (82%)
  other arithmetic  60.6 us (8%)
  local copies, waits for them, and re-layouts  56.4 us (7%)
    pallas_call x1, Pallas kernels, head(): pl.pallas_call(functools.partial(head_kernel, scale, token_scale), out_sh...  239 us
    pallas_call x1, Pallas kernels, tail(): pl.pallas_call(tail_kernel, out_shape=(table, table, table, jax.ShapeDtyp...  181 us
    pallas_call x1, Pallas kernels, weight_gather(): pl.pallas_call(weight_gather_kernel, out_shape=jax.ShapeDtypeStruct((2 *...  98.4 us
    pallas_call x2, Pallas kernels, plane_swap(): pl.pallas_call(functools.partial(swap_kernel, spread), out_shape=jax.Shap...  56.6 us
    pallas_call x1, Pallas kernels, layer_bwd(): pl.pallas_call(layer_bwd_kernel, out_shape=(jax.ShapeDtypeStruct((2 * NZ,...  39.4 us
    unnamed x52, local copies, waits for them, and re-layouts  35.8 us
    pallas_call x1, Pallas kernels, layer_fwd(): pl.pallas_call(layer_fwd_kernel, out_shape=(jax.ShapeDtypeStruct((own, wi...  22.9 us
    scatter-add x1, other arithmetic, give_back(): return g_sum.at[row_id].add(rows_in, mode='drop')  16.6 us

profile of v4, /device:TPU:0, one launch (start us, length us, event | category | flops | bytes accessed | tf_op | source)
XLA Modules:
  0.0 765.0 jit_solution(8175384836902004967)
XLA Ops:
  0.7 0.8 broadcast_subtract_fusion
  1.5 0.6 sub.63.lab_ref
  2.1 0.7 reshape.673
  3.5 0.4 select_reduce_fusion.4
  4.1 0.6 fusion.45
  4.8 0.3 select_reduce_fusion.3
  5.2 0.6 compare_and_fusion.3
  5.8 0.6 pad_clamp_fusion.2
  6.5 6.2 all-gather.1
  12.9 0.6 convert_reduce_fusion
  13.5 0.6 reduce_max.9
  14.9 1.0 multiply_sine_fusion
  15.8 0.7 convert_element_type.65
  16.5 7.4 gather_fusion.2
  24.1 1.4 convert.2.x_ref
  25.5 31.8 %plane_swap.4 = f32[8,96,512]{2,1,0:T(8,128)} custom-call(f32[8,96,512]{2,1,0:T(8,128)} %convert.2.x_ref), custom_call_target="tpu_custom_call" | custom-call | tf_op jit(solution)/shard_map/plane_swap/pallas_call | solution.py:168
  57.3 2.1 fusion.23
  59.5 0.3 copy.51
  59.8 0.5 copy-done.11
  60.4 2.4 pad_maximum_fusion
  62.9 8.2 %convert.10 = bf16[6288,512]{1,0:T(8,128)(2,1)} convert(f32[6288,512]{1,0:T(8,128)} %e_ref.3) | non-fusion elementwise | flops 3219456 | bytes 19316736
  71.1 98.4 %weight_gather.1 = f32[8,2,448,512]{3,2,1,0:T(8,128)} custom-call(f32[2,448,512]{2,1,0:T(8,128)} %bitcast.89), custom_call_target="tpu_custom_call" | custom-call | tf_op jit(solution)/shard_map/weight_gather/pallas_call | solution.py:116
  169.5 9.2 %convert_element_type.63 = bf16[8,2,448,512]{3,2,1,0:T(8,128)(2,1)} convert(f32[8,2,448,512]{3,2,1,0:T(8,128)} %weight_gather.1) | non-fusion elementwise | flops 3670016 | bytes 22020096 | tf_op jit(solution)/shard_map/convert_element_type | solution.py:975
  178.7 2.3 fusion.58
  181.0 5.8 fusion.57
  186.7 22.9 %layer_fwd.1 = (f32[512,512]{1,0:T(8,128)}, f32[512,512]{1,0:T(8,128)}, bf16[512,512]{1,0:T(8,128)(2,1)}, bf16[1024,128]{1,0:T(8,128)(2,1)}, bf16[128,1024]{1,0:...) custom-call(f32[512,512]{1,0:T(8,128)S(1)} %get-tuple-element.156.x0_ref, f32[2,512]{1,0:T(2,128)} %ln_ref.3, ...), custom_call_target="tpu_custom_call" | custom-call | tf_op jit(solution)/shard_map/layer_fwd/pallas_call | solution.py:525
  209.7 238.9 %head.1 = (f32[512,512]{1,0:T(8,128)}, f32[6288,512]{1,0:T(8,128)}, f32[8,512]{1,0:T(8,128)}, f32[8,512]{1,0:T(8,128)}) custom-call(f32[512,512]{1,0:T(8,128)} %get-tuple-element.157.f_ref, s32[8,512]{1,0:T(8,128)} %sub.63.lab_ref, f32[6288,512]{1,0:T(8,128)} %e_ref.3), custom_call_target="tpu_custom_call" | custom-call | flops 105495134208 | bytes 38633472 | tf_op jit(solution)/shard_map/head/pallas_call | solution.py:420
  448.6 0.7 reduce_sum.89
  449.3 1.3 fusion.48.loss_ref
  450.6 39.4 %layer_bwd.1 = (f32[8,928,512]{2,1,0:T(8,128)}, f32[512,512]{1,0:T(8,128)S(1)}) custom-call(f32[512,512]{1,0:T(8,128)} %get-tuple-element.159.dfin_ref, f32[512,512]{1,0:T(8,128)} %copy-done.2, f32[512,512]{1,0:T(8,128)} %get-tuple-element.160.x1_ref, f32[1,512]{1,0:T(1,128)} %fusion.48.loss_ref, f32[2,512]{1,0:T(2,128)} %ln_ref.3, ...), custom_call_target="tpu_custom_call" | custom-call | tf_op jit(solution)/shard_map/layer_bwd/pallas_call | solution.py:645
  490.1 2.2 gather_fusion.3
  492.3 1.3 broadcast_select_fusion.3.x_ref
  493.6 24.8 %plane_swap.5 = f32[8,96,512]{2,1,0:T(8,128)} custom-call(f32[8,96,512]{2,1,0:T(8,128)} %broadcast_select_fusion.3.x_ref), custom_call_target="tpu_custom_call" | custom-call | tf_op jit(solution)/shard_map/plane_swap/pallas_call | solution.py:168
  518.4 16.6 %scatter_fusion.1 = f32[6288,512]{1,0:T(8,128)} fusion(f32[6288,512]{1,0:T(8,128)} %get-tuple-element.158, s32[768]{0:T(1024)S(1)} %copy-done.19, f32[768,512]{1,0:T(8,128)} %bitcast.90), kind=kCustom, calls=%fused_computation.5 | custom fusion | flops 393216 | bytes 4721664 | tf_op jit(solution)/shard_map/scatter-add | solution.py:1003
  535.2 181.1 %tail.1 = (f32[6288,512]{1,0:T(8,128)}, f32[6288,512]{1,0:T(8,128)}, f32[6288,512]{1,0:T(8,128)}, f32[2,464,512]{2,1,0:T(8,128)}, f32[8,24,512]{2,1,0:T(8,128)}) custom-call(f32[6288,512]{1,0:T(8,128)} %get-tuple-element.169.g_ref, f32[8,2,464,512]{3,2,1,0:T(8,128)} %bitcast.88, f32[6288,512]{1,0:T(8,128)} %e_ref.3, f32[6288,512]{1,0:T(8,128)} %m_ref.1, ...), custom_call_target="tpu_custom_call" | custom-call | tf_op jit(solution)/shard_map/tail/pallas_call | solution.py:872
  716.3 1.4 slice_reduce_fusion
  717.8 1.3 divide_subtract_fusion.5
  719.1 1.0 slice.43
  720.1 1.9 divide_subtract_fusion.3
  722.0 1.8 divide_subtract_fusion.4
  723.8 1.0 divide_subtract_fusion.2
  725.5 1.3 divide_subtract_fusion.1
  726.8 0.3 copy.52
  727.1 0.9 copy-done.1
  728.0 3.5 divide_subtract_fusion
  731.6 11.1 %copy.71 = f32[6288,512]{1,0:T(8,128)} copy(f32[6288,512]{1,0:T(8,128)} %get-tuple-element.517) | data formatting | bytes 25755648
  742.7 11.1 %copy.72 = f32[6288,512]{1,0:T(8,128)} copy(f32[6288,512]{1,0:T(8,128)} %get-tuple-element.524) | data formatting | bytes 25755648
  753.7 11.1 %copy.73 = f32[6288,512]{1,0:T(8,128)} copy(f32[6288,512]{1,0:T(8,128)} %get-tuple-element.531) | data formatting | bytes 25755648
  (75 shorter events, 2.5 us)
Async XLA Ops:
  0.7 15.2 %copy-start.7 = (f32[2,512,64]{1,2,0:T(8,128)S(1)}, f32[2,512,64]{1,2,0:T(8,128)}, u32[]{:S(2)}) copy-start(f32[2,512,64]{1,2,0:T(8,128)} %param.32) | copy-start | bytes 786436
  57.3 2.1 copy-start
  59.5 0.9 copy-start.11
  59.5 1.0 copy-start.12
  71.1 98.4 %copy-start.4 = (s32[8,512]{1,0:T(8,128)}, s32[8,512]{1,0:T(8,128)S(1)}, u32[]{:S(2)}) copy-start(s32[8,512]{1,0:T(8,128)S(1)} %get-tuple-element.541) | copy-start | bytes 49156
  71.1 115.7 %copy-start.2 = (f32[512,512]{1,0:T(8,128)}, f32[512,512]{1,0:T(8,128)S(1)}, u32[]{:S(2)}) copy-start(f32[512,512]{1,0:T(8,128)S(1)} %get-tuple-element.156.x0_ref) | copy-start | bytes 3145732
  450.6 39.5 %copy-start.20 = (s32[1024]{0:T(1024)S(1)}, s32[1024]{0:T(1024)}, u32[]{:S(2)}) copy-start(s32[1024]{0:T(1024)} %pad_clamp_fusion.2) | copy-start | bytes 12292
  490.1 2.2 copy-start.21
  493.6 24.8 %copy-start.19 = (s32[768]{0:T(1024)S(1)}, s32[768]{0:T(1024)}, u32[]{:S(2)}) copy-start(s32[768]{0:T(1024)} %get-tuple-element.222) | copy-start | bytes 9220
  518.4 16.6 %copy-start.5 = (s32[8,512]{1,0:T(8,128)S(1)}, s32[8,512]{1,0:T(8,128)}, u32[]{:S(2)}) copy-start(s32[8,512]{1,0:T(8,128)} %copy-done.4) | copy-start | bytes 49156
  535.1 182.6 %copy-start.18 = (f32[2,512]{1,0:T(2,128)S(1)}, f32[2,512]{1,0:T(2,128)}, u32[]{:S(2)}) copy-start(f32[2,512]{1,0:T(2,128)} %ln_ref.3) | copy-start | bytes 12292
  535.2 182.6 %copy-start.22 = (f32[2,512]{1,0:T(2,128)S(1)}, f32[2,512]{1,0:T(2,128)}, u32[]{:S(2)}) copy-start(f32[2,512]{1,0:T(2,128)} %param.37) | copy-start | bytes 12292
  535.2 182.6 %copy-start.23 = (f32[2,512]{1,0:T(2,128)S(1)}, f32[2,512]{1,0:T(2,128)}, u32[]{:S(2)}) copy-start(f32[2,512]{1,0:T(2,128)} %param.44) | copy-start | bytes 12292
  716.3 5.7 copy-start.13
  716.3 5.7 copy-start.16
  716.3 5.7 copy-start.17
  716.3 7.5 copy-start.8
  716.3 7.5 copy-start.14
  716.3 7.5 copy-start.15
  722.0 2.9 copy-start.6
  723.8 1.2 copy-start.3
  723.8 1.5 copy-start.9
  723.8 1.6 copy-start.10
  726.8 1.2 copy-start.1

commit v5 on v4

--- a/solution.py
+++ b/solution.py
@@ -45,87 +45,6 @@
     pl.semaphore_signal(pltpu.get_barrier_semaphore(), inc=1, device_id=(tp, dp), device_id_type=pl.DeviceIdType.MESH)
 
 
-def line_barrier(k, tp, dp, others):
-    peers = [(tp + 1 - 2 * (tp % 2), dp)] + others
-    if k > 0:
-        peers.append((tp - 2, dp))
-    if k < NZ - 1:
-        peers.append((tp + 2, dp))
-    for peer in peers:
-        signal(*peer)
-    pl.semaphore_wait(pltpu.get_barrier_semaphore(), len(peers))
-
-
-def weight_gather_kernel(x_ref, out_ref, own_sem, send_y, send_l, send_r, send_c, recv):
-    tp, dp, z, y = place()
-    partner = tp + 1 - 2 * y
-    core = dp % 2
-    twin = dp + 1 - 2 * core
-
-    def program(k):
-        line_barrier(k, tp, dp, [(tp, twin)])
-
-        def send(src, slot, sems, to, to_dp):
-            copy = remote(src, out_ref.at[slot, core], sems.at[slot], recv.at[slot, core], to, to_dp)
-            copy.start()
-            return copy
-
-        def arrived(slot, half):
-            remote(x_ref.at[0], out_ref.at[slot, half], send_y.at[slot], recv.at[slot, half], partner, dp).wait_recv()
-
-        mine = x_ref.at[core]
-        sends = []
-        if k > 0:
-            sends.append(send(mine, tp, send_l, tp - 2, dp))
-        if k < NZ - 1:
-            sends.append(send(mine, tp, send_r, tp + 2, dp))
-        sends.append(send(mine, tp, send_y, partner, dp))
-        own = pltpu.make_async_copy(x_ref, out_ref.at[tp], own_sem)
-        own.start()
-        across = [k] + [zz for _, zz in ARRIVALS[k]]
-        for n, (side, zz) in enumerate(ARRIVALS[k]):
-            slot = 2 * zz + y
-            arrived(slot, core)
-            if side == "L" and k < NZ - 1:
-                sends.append(send(out_ref.at[slot, core], slot, send_r, tp + 2, dp))
-            if side == "R" and k > 0:
-                sends.append(send(out_ref.at[slot, core], slot, send_l, tp - 2, dp))
-            sends.append(send(out_ref.at[slot, core], slot, send_y, partner, dp))
-            sends.append(send(out_ref.at[slot, core], slot, send_c, tp, twin))
-            slot = 2 * across[n] + 1 - y
-            arrived(slot, core)
-            sends.append(send(out_ref.at[slot, core], slot, send_c, tp, twin))
-        slot = 2 * across[-1] + 1 - y
-        arrived(slot, core)
-        sends.append(send(out_ref.at[slot, core], slot, send_c, tp, twin))
-        for zz in range(NZ):
-            if zz != k:
-                arrived(2 * zz + y, 1 - core)
-            arrived(2 * zz + 1 - y, 1 - core)
-        own.wait()
-        for copy in sends:
-            copy.wait_send()
-
-    for k in range(NZ):
-        pl.when(z == k)(functools.partial(program, k))
-
-
-def weight_gather(x, collective_id):
-    rows, width = x.shape
-    halves = x.reshape(2, rows // 2, width)
-    out = pl.pallas_call(
-        weight_gather_kernel,
-        out_shape=jax.ShapeDtypeStruct((2 * NZ,) + halves.shape, x.dtype),
-        in_specs=[ANY],
-        out_specs=ANY,
-        scratch_shapes=[pltpu.SemaphoreType.DMA] + [pltpu.SemaphoreType.DMA((2 * NZ,))] * 4
-        + [pltpu.SemaphoreType.DMA((2 * NZ, 2))],
-        compiler_params=pltpu.CompilerParams(collective_id=collective_id, has_side_effects=True),
-        name="weight_gather",
-    )(halves)
-    return out.reshape(2 * NZ, rows, width)
-
-
 def add_into(acc, other, step=None):
     rows = acc.shape[0]
     step = step or (64 if rows % 64 == 0 else 8)
@@ -145,16 +64,16 @@
     pl.semaphore_wait(pltpu.get_barrier_semaphore(), len(peers))
 
 
-def swap_kernel(spread, x_ref, out_ref, own_sem, send, recv):
+def swap_kernel(x_ref, out_ref, own_sem, send, recv):
     tp, dp, _, _ = place()
     plane_barrier(tp, dp, [])
     copies = []
     for n in range(1, 2 * NZ):
         to = lax.rem(tp + n, 2 * NZ)
-        copy = remote(x_ref if spread else x_ref.at[to], out_ref.at[tp], send.at[to], recv.at[tp], to, dp)
+        copy = remote(x_ref.at[to], out_ref.at[tp], send.at[to], recv.at[tp], to, dp)
         copy.start()
         copies.append(copy)
-    own = pltpu.make_async_copy(x_ref if spread else x_ref.at[tp], out_ref.at[tp], own_sem)
+    own = pltpu.make_async_copy(x_ref.at[tp], out_ref.at[tp], own_sem)
     own.start()
     for n in range(1, 2 * NZ):
         source = lax.rem(tp + n, 2 * NZ)
@@ -164,15 +83,15 @@
         copy.wait_send()
 
 
-def plane_swap(x, spread, collective_id):
+def plane_swap(x, collective_id):
     return pl.pallas_call(
-        functools.partial(swap_kernel, spread),
-        out_shape=jax.ShapeDtypeStruct((2 * NZ,) + x.shape if spread else x.shape, x.dtype),
+        swap_kernel,
+        out_shape=jax.ShapeDtypeStruct(x.shape, x.dtype),
         in_specs=[ANY],
         out_specs=ANY,
         scratch_shapes=[pltpu.SemaphoreType.DMA] + [pltpu.SemaphoreType.DMA((2 * NZ,))] * 2,
         compiler_params=pltpu.CompilerParams(collective_id=collective_id, has_side_effects=True),
-        name="plane_spread" if spread else "plane_swap",
+        name="plane_swap",
     )(x)
 
 
@@ -447,48 +366,158 @@
     return lo * cos_t - hi * sin_t, hi * cos_t + lo * sin_t
 
 
-def layer_fwd_kernel(x0_ref, ln_ref, cos_ref, sin_ref, wq_ref, wkv_ref, wo_ref, wg_ref, wu_ref, wd_ref,
-                     f_ref, x1_ref, q_ref, kv_ref, kvt_ref, lse_ref, ctx_ref, u_b, kv_out, kv_in, send_sem, recv_sem):
-    tp, dp, _, y = place()
+EVENTS = {
+    0: (((("R", 1),), (0,)), ((("R", 2),), (1,)), ((("R", 3),), (2,)), ((), (3,))),
+    1: (((("L", 0), ("R", 2)), (1,)), ((("R", 3),), (0,)), ((), (2,)), ((), (3,))),
+    2: (((("R", 3), ("L", 1)), (2,)), ((("L", 0),), (3,)), ((), (1,)), ((), (0,))),
+    3: (((("L", 2),), (3,)), ((("L", 1),), (2,)), ((("L", 0),), (1,)), ((), (0,))),
+}
+MLP_ORDER = {k: [2 * k] + [code for line, other in EVENTS[k] for code in [2 * zz for _, zz in line] + [2 * zz + 1 for zz in other]] for k in range(NZ)}
+
+
+def front_kernel(rows_ref, pick_ref, extra_ref, w_ref, wkv_ref, ln_ref, cos_ref, sin_ref,
+                 f_ref, x1_ref, x0_ref, q_ref, kv_ref, kvt_ref, lse_ref, ctx_ref, wq_ref, wo_ref, wg_ref, wu_ref, wd_ref,
+                 wl, rows_in, u_b, kv_out, kv_in, own_sem, r_send, r_recv, a_y, a_l, a_r, a_c, a_recv,
+                 b_y, b_l, b_r, b_x, b_c, b_recv, kv_send, kv_recv):
+    tp, dp, z, y = place()
     partner = tp + 1 - 2 * y
+    core = dp % 2
+    twin = dp + 1 - 2 * core
+    facing = lax.rem(dp + 2, 4)
     own, width = x0_ref.shape
+    shards, w_rows = wl.shape[0], wl.shape[1]
+    nq = q_ref.shape[0]
+    ff = wg_ref.shape[0]
+    n_a = nq // shards
+    n_f = ff // shards
+    n_b = 3 * n_f // 4
     hd = kv_out.shape[0] // 2
     quarter = hd // 2
-    heads = q_ref.shape[0] // hd
-    signal(partner, dp)
+    heads = nq // hd
+
+    def a_rows(c):
+        return pl.ds(pl.multiple_of(c * n_a, 8), n_a)
+
+    def b_rows(d):
+        return pl.ds(pl.multiple_of(2 * n_a + d * n_b, 8), n_b)
+
+    def a_copy(slot, sems, to, to_dp, first=False):
+        src = w_ref.at[a_rows(core), :] if first else wl.at[slot, a_rows(core), :]
+        return remote(src, wl.at[slot, a_rows(core), :], sems.at[slot], a_recv.at[slot, core], to, to_dp)
+
+    def b_copy(slot, piece, sems, to, to_dp, first=False):
+        src = w_ref.at[b_rows(piece), :] if first else wl.at[slot, b_rows(piece), :]
+        return remote(src, wl.at[slot, b_rows(piece), :], sems.at[slot], b_recv.at[slot, piece], to, to_dp)
+
+    def a_wait(slot, c):
+        remote(w_ref.at[a_rows(c), :], wl.at[slot, a_rows(c), :], a_y.at[slot], a_recv.at[slot, c], partner, dp).wait_recv()
+
+    def b_wait(slot, piece):
+        remote(w_ref.at[b_rows(piece), :], wl.at[slot, b_rows(piece), :], b_y.at[slot], b_recv.at[slot, piece], partner, dp).wait_recv()
+
+    def on_position(f):
+        for k in range(NZ):
+            pl.when(z == k)(functools.partial(f, k))
+
+    def line_sends(k, make, y_sems, l_sems, r_sems, slot, side, first=False):
+        sends = [make(slot, y_sems, partner, dp, first)]
+        if k > 0 and side != "L":
+            sends.append(make(slot, l_sems, tp - 2, dp, first))
+        if k < NZ - 1 and side != "R":
+            sends.append(make(slot, r_sems, tp + 2, dp, first))
+        return sends
+
+    def b_own(slot, sems, to, to_dp, first=False):
+        return b_copy(slot, dp, sems, to, to_dp, first)
+
+    def a_sends(k, slot, side, first=False):
+        return line_sends(k, a_copy, a_y, a_l, a_r, slot, side, first)
+
+    def b_sends(k, slot, side, first=False):
+        return line_sends(k, b_own, b_y, b_l, b_r, slot, side, first)
+
+    def start(copies):
+        for c in copies:
+            c.start()
+
+    plane_barrier(tp, dp, [(tp, twin), (tp, facing)])
+    peers = [lax.rem(tp + n, shards) for n in range(1, shards)]
+
+    def row_copy(to):
+        return remote(rows_ref.at[to], rows_in.at[tp], r_send.at[to], r_recv.at[tp], to, dp)
+
+    on_position(lambda k: start(b_sends(k, tp, "", True)))
+    start([row_copy(to) for to in peers])
+    on_position(lambda k: start(a_sends(k, tp, "", True)))
+    own_rows = pltpu.make_async_copy(rows_ref.at[tp], rows_in.at[tp], own_sem.at[0])
+    own_rows.start()
+    own_w = pltpu.make_async_copy(w_ref, wl.at[tp], own_sem.at[1])
+    own_w.start()
+
+    def a_event(t, k):
+        line, other = EVENTS[k][t]
+        for side, zz in line:
+            slot = 2 * zz + y
+            a_wait(slot, core)
+            start(a_sends(k, slot, side))
+            a_copy(slot, a_c, tp, twin).start()
+        for zz in other:
+            slot = 2 * zz + 1 - y
+            a_wait(slot, core)
+            a_copy(slot, a_c, tp, twin).start()
+
+    def b_event(t, k):
+        line, other = EVENTS[k][t]
+        for side, zz in line:
+            slot = 2 * zz + y
+            b_wait(slot, dp)
+            start(b_sends(k, slot, side))
+            b_copy(slot, dp, b_x, tp, facing).start()
+            b_copy(slot, dp, b_c.at[0], tp, twin).start()
+        for zz in other:
+            slot = 2 * zz + 1 - y
+            b_wait(slot, dp)
+            b_copy(slot, dp, b_x, tp, facing).start()
+            b_copy(slot, dp, b_c.at[0], tp, twin).start()
+
+    on_position(functools.partial(b_event, 0))
+
+    own_rows.wait()
+    for source in peers:
+        remote(rows_ref.at[source], rows_in.at[source], r_send.at[source], r_recv.at[source], source, dp).wait_recv()
+    x0_ref[...] = extra_ref[...] + mm(pick_ref[...], rows_in[...].reshape(pick_ref.shape[1], width).astype(BF16))
     u_b[...] = norm_fwd(x0_ref[...], ln_ref[0:1, :])[0]
-    u = u_b[...]
+    x1_ref[...] = x0_ref[...]
     cos_t = cos_ref[...]
     sin_t = sin_ref[...]
-    kv = mm(wkv_ref[...], u, TB)
+    kv = mm(wkv_ref[...], u_b[...], TB)
     lo, hi = turn(kv[:quarter], kv[quarter:hd], cos_t, sin_t)
     kv_out[0:quarter, :] = lo
     kv_out[quarter:hd, :] = hi
     kv_out[hd:, :] = kv[hd:]
-    pl.semaphore_wait(pltpu.get_barrier_semaphore(), 1)
-    copy = remote(kv_out, kv_in, send_sem, recv_sem, partner, dp)
-    copy.start()
-
-    q_all = mm(wq_ref[...], u, TB)
+    kv_copy = remote(kv_out, kv_in, kv_send, kv_recv, partner, dp)
+    kv_copy.start()
+
+    on_position(functools.partial(a_event, 0))
+    on_position(functools.partial(b_event, 1))
+    on_position(functools.partial(a_event, 1))
+    on_position(functools.partial(b_event, 2))
+    on_position(functools.partial(a_event, 2))
+    on_position(functools.partial(a_event, 3))
+    on_position(functools.partial(b_event, 3))
+    own_w.wait()
+    for source in peers:
+        a_wait(source, 1 - core)
+    for s in range(shards):
+        wq_ref[s * n_a:(s + 1) * n_a, :] = wl[s, 0:n_a, :].astype(BF16)
+        wo_ref[s * n_a:(s + 1) * n_a, :] = wl[s, n_a:2 * n_a, :].astype(BF16)
+
+    q_all = mm(wq_ref[...], u_b[...], TB)
     for h in range(heads):
         lo, hi = turn(q_all[h * hd:h * hd + quarter], q_all[h * hd + quarter:(h + 1) * hd], cos_t, sin_t)
         q_ref[h * hd:h * hd + quarter, :] = lo.astype(BF16)
         q_ref[h * hd + quarter:(h + 1) * hd, :] = hi.astype(BF16)
-
-    x1_ref[...] = x0_ref[...]
-    step = min(512, wg_ref.shape[0])
-
-    def mlp(n, carry):
-        at = pl.ds(pl.multiple_of(n * step, step), step)
-        gate = mm(u_b[...], wg_ref[at, :], TB)
-        up = mm(u_b[...], wu_ref[at, :], TB)
-        hidden = (gate * jax.nn.sigmoid(gate) * up).astype(BF16)
-        x1_ref[...] += mm(hidden, wd_ref[at, :])
-        return carry
-
-    lax.fori_loop(0, wg_ref.shape[0] // step, mlp, 0)
-
-    copy.wait()
+    kv_copy.wait()
 
     def fill(mine, other):
         kv_ref[mine * own:(mine + 1) * own, :] = kv_out[...].T.astype(BF16)
@@ -515,26 +544,74 @@
 
     lax.fori_loop(0, heads, attend, 0)
     x1_ref[...] += mm(ctx_ref[...], wo_ref[...], TA)
+
+    def slot_of(step):
+        code = lookup(MLP_ORDER, z, step)
+        other = code % 2
+        return code // 2 * 2 + y + other - 2 * y * other
+
+    def mlp(step, carry):
+        def pass_on():
+            slot = slot_of(step + 1)
+            b_wait(slot, facing)
+            b_copy(slot, facing, b_c.at[1], tp, twin).start()
+        pl.when(step < shards - 1)(pass_on)
+        slot = slot_of(step)
+
+        def rest():
+            b_wait(slot, twin)
+            b_wait(slot, lax.rem(twin + 2, 4))
+        pl.when(step > 0)(rest)
+        at = pl.ds(pl.multiple_of(slot * n_f, n_f), n_f)
+        wg_ref[at, :] = wl[slot, 2 * n_a:2 * n_a + n_f, :].astype(BF16)
+        wu_ref[at, :] = wl[slot, 2 * n_a + n_f:2 * n_a + 2 * n_f, :].astype(BF16)
+        wd_ref[at, :] = wl[slot, 2 * n_a + 2 * n_f:2 * n_a + 3 * n_f, :].astype(BF16)
+        gate = mm(u_b[...], wg_ref[at, :], TB)
+        up = mm(u_b[...], wu_ref[at, :], TB)
+        x1_ref[...] += mm((gate * jax.nn.sigmoid(gate) * up).astype(BF16), wd_ref[at, :])
+        return carry
+
+    lax.fori_loop(0, shards, mlp, 0)
     f_ref[...] = norm_fwd(x1_ref[...], ln_ref[1:2, :])[0].astype(F32)
 
-
-def layer_fwd(x0, ln, cos_t, sin_t, weights, collective_id):
-    own, width = x0.shape
-    two_hd = weights[1].shape[0]
-    nq = weights[0].shape[0]
+    def finish(k):
+        done = a_sends(k, tp, "", True) + b_sends(k, tp, "", True)
+        for line, other in EVENTS[k]:
+            for side, zz in line:
+                done += a_sends(k, 2 * zz + y, side) + b_sends(k, 2 * zz + y, side)
+        for c in done:
+            c.wait_send()
+
+    on_position(finish)
+    for to in peers:
+        row_copy(to).wait_send()
+        a_copy(to, a_c, tp, twin).wait_send()
+        b_copy(to, dp, b_x, tp, facing).wait_send()
+        b_copy(to, dp, b_c.at[0], tp, twin).wait_send()
+        b_copy(to, facing, b_c.at[1], tp, twin).wait_send()
+
+
+def front(rows, pick, extra, w_rows, wkv_t, ln, cos_t, sin_t, n_q, collective_id):
+    own, width = extra.shape
+    two_hd = wkv_t.shape[0]
+    shards = 2 * NZ
+    ff = (w_rows.shape[0] * shards - 2 * n_q) // 3
+    dma = lambda *n: pltpu.SemaphoreType.DMA(n)
+    s = jax.ShapeDtypeStruct
     return pl.pallas_call(
-        layer_fwd_kernel,
-        out_shape=(jax.ShapeDtypeStruct((own, width), F32), jax.ShapeDtypeStruct((own, width), F32),
-                   jax.ShapeDtypeStruct((nq, own), BF16), jax.ShapeDtypeStruct((2 * own, two_hd), BF16),
-                   jax.ShapeDtypeStruct((two_hd, 2 * own), BF16), jax.ShapeDtypeStruct((2 * nq // two_hd, own), F32),
-                   jax.ShapeDtypeStruct((nq, own), BF16)),
-        in_specs=[VMEM] * 10,
-        out_specs=(VMEM,) * 7,
-        scratch_shapes=[pltpu.VMEM((own, width), BF16), pltpu.VMEM((two_hd, own), F32), pltpu.VMEM((two_hd, own), F32),
-                        pltpu.SemaphoreType.DMA, pltpu.SemaphoreType.DMA],
+        front_kernel,
+        out_shape=(s((own, width), F32),) * 3 + (s((n_q, own), BF16), s((2 * own, two_hd), BF16), s((two_hd, 2 * own), BF16),
+                   s((2 * n_q // two_hd, own), F32), s((n_q, own), BF16), s((n_q, width), BF16), s((n_q, width), BF16))
+        + (s((ff, width), BF16),) * 3,
+        in_specs=[VMEM] * 3 + [ANY] + [VMEM] * 4,
+        out_specs=(VMEM,) * 13,
+        scratch_shapes=[pltpu.VMEM((shards,) + w_rows.shape, F32), pltpu.VMEM(rows.shape, F32), pltpu.VMEM((own, width), BF16),
+                        pltpu.VMEM((two_hd, own), F32), pltpu.VMEM((two_hd, own), F32),
+                        dma(2), dma(shards), dma(shards)] + [dma(shards)] * 4 + [dma(shards, 2)]
+        + [dma(shards)] * 4 + [dma(2, shards), dma(shards, 4), pltpu.SemaphoreType.DMA, pltpu.SemaphoreType.DMA],
         compiler_params=pltpu.CompilerParams(collective_id=collective_id, has_side_effects=True, vmem_limit_bytes=60000000),
-        name="layer_fwd",
-    )(x0, ln, cos_t, sin_t, *weights)
+        name="front",
+    )(rows, pick, extra, w_rows, wkv_t, ln, cos_t, sin_t)
 
 
 def layer_bwd_kernel(dfin_ref, x0_ref, x1_ref, loss_ref, ln_ref, cos_ref, sin_ref, wq_ref, wkv_ref, wo_ref, wg_ref, wu_ref, wd_ref,
@@ -899,19 +976,6 @@
     return d_in, d_scale
 
 
-def rope_tables(positions, head_dim):
-    inv_freq = ROPE_BASE ** (-jnp.arange(0, head_dim, 2).astype(F32) / head_dim)
-    angles = positions.astype(F32)[:, None] * inv_freq[None, :]
-    return jnp.cos(angles), jnp.sin(angles)
-
-
-def rotate(x_in, cos_t, sin_t):
-    half_dim = x_in.shape[-1] // 2
-    x_lo = x_in[..., :half_dim]
-    x_hi = x_in[..., half_dim:]
-    return jnp.concatenate([x_lo * cos_t - x_hi * sin_t, x_hi * cos_t + x_lo * sin_t], axis=-1)
-
-
 def adam_update(param_in, grad_in, mom_in, vel_in):
     mom_new = BETA_ONE * mom_in + (1.0 - BETA_ONE) * grad_in
     vel_new = BETA_TWO * vel_in + (1.0 - BETA_TWO) * grad_in * grad_in
@@ -934,14 +998,12 @@
         head_dim = w_kv.shape[2]
         q_loc = w_q.shape[1]
         f_loc = w_down.shape[0]
-        heads = n_tp * q_loc // head_dim
         tok_loc = batch_loc * seq_len
         tok_total = tok_loc * n_dp
         own = tok_loc // n_tp
         tp_rank = lax.axis_index('tp')
         half = tp_rank % 2
 
-        all_tokens = lax.all_gather(tokens, 'dp').reshape(n_dp * n_tp, own)
         strict = (jnp.arange(own)[:, None] > jnp.arange(own)[None, :]).astype(BF16)
 
         def routing(chunks):
@@ -954,37 +1016,34 @@
             return shard, row, rank, (most + CAP - 1) // CAP
 
         chunks = tokens.reshape(n_tp, own)
-        shard, row, rank, _ = routing(chunks)
-        rounds_all = routing(all_tokens)[3]
+        shard, row, rank, rounds = routing(chunks)
         slots = jnp.arange(CAP)
         my_shard = lax.dynamic_index_in_dim(shard, tp_rank, 0, keepdims=False)
         my_rank = lax.dynamic_index_in_dim(rank, tp_rank, 0, keepdims=False)
 
-        def fetch(step, x_sum, collective_id):
+        def fetch(step):
             here = (shard[:, None, :] == tp_rank) & (rank[:, None, :] == slots[None, :, None] + step * CAP)
             ids = jnp.sum(jnp.where(here, row[:, None, :], 0), axis=-1).reshape(-1)
-            rows_out = lax.optimization_barrier(jnp.take(embed, ids, axis=0)).astype(BF16).astype(F32).reshape(n_tp, CAP, d_model)
-            rows_in = plane_swap(rows_out, False, collective_id).reshape(n_tp * CAP, d_model).astype(BF16)
             pick = (my_shard[:, None, None] == jnp.arange(n_tp)[None, :, None]) & (my_rank[:, None, None] == slots[None, None, :] + step * CAP)
-            return x_sum + dot('rc,cd->rd', pick.reshape(own, n_tp * CAP).astype(BF16), rows_in)
-
-        x_zero = fetch(0, jnp.zeros((own, d_model), F32), 0)
-        x_zero = lax.while_loop(lambda s: s[0] < rounds_all, lambda s: (s[0] + 1, fetch(s[0], s[1], 1)), (jnp.int32(1), x_zero))[1]
+            return jnp.take(embed, ids, axis=0).reshape(n_tp, CAP, d_model), pick.reshape(own, n_tp * CAP).astype(BF16)
+
+        def fetch_more(state):
+            rows_out, pick = fetch(state[0])
+            rows_in = plane_swap(rows_out, 1).reshape(n_tp * CAP, d_model).astype(BF16)
+            return state[0] + 1, state[1] + dot('rc,cd->rd', pick, rows_in)
+
+        more_rows = lax.while_loop(lambda state: state[0] < rounds, fetch_more, (jnp.int32(1), jnp.zeros((own, d_model), F32)))[1]
+        rows_first, pick_first = fetch(0)
 
         w_rows = jnp.concatenate([w_q.T, w_o, w_gu.transpose(0, 2, 1).reshape(2 * f_loc, d_model), w_down], axis=0)
-        w_all = weight_gather(w_rows, 2).astype(BF16)
         cuts = (q_loc, 2 * q_loc, 2 * q_loc + f_loc, 2 * q_loc + 2 * f_loc)
-        wq_t = w_all[:, :cuts[0]].reshape(-1, d_model)
-        wo_b = w_all[:, cuts[0]:cuts[1]].reshape(-1, d_model)
-        wg_t = w_all[:, cuts[1]:cuts[2]].reshape(-1, d_model)
-        wu_t = w_all[:, cuts[2]:cuts[3]].reshape(-1, d_model)
-        wd_b = w_all[:, cuts[3]:].reshape(-1, d_model)
         wkv_t = w_kv.transpose(0, 2, 1).reshape(2 * head_dim, d_model).astype(BF16)
-        weights = (wq_t, wkv_t, wo_b, wg_t, wu_t, wd_b)
         inv_freq = ROPE_BASE ** (-jnp.arange(0, head_dim, 2).astype(F32) / head_dim)
         angles = inv_freq[:, None] * (half * own + jnp.arange(own)).astype(F32)[None, :]
         cos_t, sin_t = jnp.cos(angles), jnp.sin(angles)
-        f_own, x_one, *saved = layer_fwd(x_zero, ln_scales, cos_t, sin_t, weights, 3)
+        f_own, x_one, x_zero, *saved = front(rows_first, pick_first, more_rows, w_rows, wkv_t, ln_scales, cos_t, sin_t, n_tp * q_loc, 0)
+        saved, (wq_t, wo_b, wg_t, wu_t, wd_b) = saved[:5], saved[5:]
+        weights = (wq_t, wkv_t, wo_b, wg_t, wu_t, wd_b)
 
         logit_scale = d_model ** -0.5
         lab_loc = labels.reshape(n_tp, own) - tp_rank * vocab_loc
@@ -997,13 +1056,13 @@
             mine = (my_shard[None, None, :] == jnp.arange(n_tp)[:, None, None]) & (my_rank[None, None, :] == slots[None, :, None] + step * CAP)
             ids = jnp.sum(jnp.where(mine, jnp.arange(own)[None, None, :], 0), axis=-1).reshape(-1)
             rows_out = jnp.take(d_zero, ids, axis=0).reshape(n_tp, CAP, d_model)
-            rows_in = plane_swap(rows_out, False, collective_id).reshape(-1, d_model)
+            rows_in = plane_swap(rows_out, collective_id).reshape(-1, d_model)
             here = (shard[:, None, :] == tp_rank) & (rank[:, None, :] == slots[None, :, None] + step * CAP)
             row_id = jnp.where(jnp.any(here, axis=-1), jnp.sum(jnp.where(here, row[:, None, :], 0), axis=-1), vocab_loc).reshape(-1)
             return g_sum.at[row_id].add(rows_in, mode='drop')
 
         g_table = give_back(0, g_head_part, 8)
-        g_table = lax.while_loop(lambda s: s[0] < rounds_all, lambda s: (s[0] + 1, give_back(s[0], s[1], 9)), (jnp.int32(1), g_table))[1]
+        g_table = lax.while_loop(lambda s: s[0] < rounds, lambda s: (s[0] + 1, give_back(s[0], s[1], 9)), (jnp.int32(1), g_table))[1]
 
         new_table, g_shard, g_small = tail(g_table, g_rows, embed, state_arrays[7], state_arrays[14], 10)
         n_kv = 2 * head_dim // n_tp

time: 773 us -> 701 us (0.907)
  Pallas kernels: 637 us -> 600 us
  other arithmetic: 60.6 us -> 42.3 us
    pallas_call x4 -> x2, Pallas kernels: 178 us -> 132 us  [the longest x1 106 us: front(): pl.pallas_call(front_kernel, out_shape=(s((own, width), F32),) * 3 + (s((...]
    convert_element_type x1, other arithmetic: 9.24 us -> 0.15 us  [fetch(): pick.reshape(own, n_tp * CAP).astype(BF16)]
    unnamed x1 -> x0, other arithmetic: 8.24 us -> none
    pallas_call x1, Pallas kernels: 239 us -> 247 us  [head(): pl.pallas_call(functools.partial(head_kernel, scale, token_scale), out_sh...]
    slice x2 -> x0, local copies, waits for them, and re-layouts: 8.04 us -> none  [the longest x1 5.78 us: local_step(): wd_b = w_all[:, cuts[3]:].reshape(-1, d_model)]
    unnamed x52 -> x49, local copies, waits for them, and re-layouts: 35.8 us -> 34.8 us
where the time goes in v5:
time: 701 us; the launch traced here: 694 us
  Pallas kernels  600 us (86%)
  local copies, waits for them, and re-layouts  49 us (7%)
  other arithmetic  42.3 us (6%)
    pallas_call x1, Pallas kernels, head(): pl.pallas_call(functools.partial(head_kernel, scale, token_scale), out_sh...  247 us
    pallas_call x1, Pallas kernels, tail(): pl.pallas_call(tail_kernel, out_shape=(table, table, table, jax.ShapeDtyp...  181 us
    pallas_call x1, Pallas kernels, front(): pl.pallas_call(front_kernel, out_shape=(s((own, width), F32),) * 3 + (s((...  106 us
    pallas_call x1, Pallas kernels, layer_bwd(): pl.pallas_call(layer_bwd_kernel, out_shape=(jax.ShapeDtypeStruct((2 * NZ,...  39.3 us
    unnamed x49, local copies, waits for them, and re-layouts  34.8 us
    pallas_call x1, Pallas kernels, plane_swap(): pl.pallas_call(swap_kernel, out_shape=jax.ShapeDtypeStruct(x.shape, x.dty...  26.2 us
    scatter-add x1, other arithmetic, give_back(): return g_sum.at[row_id].add(rows_in, mode='drop')  16.6 us

profile of v5, /device:TPU:0, one launch (start us, length us, event | category | flops | bytes accessed | tf_op | source)
XLA Modules:
  0.0 693.7 jit_solution(5199895505891219254)
XLA Ops:
  0.7 0.7 broadcast_subtract_fusion
  1.4 0.6 sub.56.lab_ref
  2.0 0.7 reshape.622
  2.8 0.2 convert_reduce_fusion
  3.0 0.6 reduce_max.9
  4.3 0.3 fusion.22
  4.7 0.3 fusion.20
  5.0 0.4 select_reduce_fusion.4
  5.5 0.1 reduce_or.21
  5.6 0.6 fusion.36
  6.3 0.3 select_reduce_fusion.3
  6.6 0.6 compare_and_fusion.3
  7.3 0.6 pad_clamp_fusion.2
  7.9 1.0 multiply_sine_fusion
  8.9 1.6 convert_element_type.47
  10.5 0.1 and_convert_fusion
  10.7 1.2 copy.51.pick_ref
  11.8 0.3 copy.50
  12.2 1.4 pad_maximum_fusion.w_ref
  13.6 0.1 broadcast_in_dim.157
  13.7 7.4 %gather_fusion.2 = f32[768,512]{1,0:T(8,128)S(1)} fusion(f32[6288,512]{1,0:T(8,128)} %get-tuple-element.546, s32[1024]{0:T(1024)S(1)} %pad_clamp_fusion.3), kind=kCustom, calls=%fused_computation.2 | custom fusion | bytes 3148800 | tf_op jit(solution)/shard_map/jit(_take)/gather | solution.py:1028
  21.2 1.3 broadcast_select_fusion.4.rows_ref
  22.5 106.1 %front.1 = (f32[512,512]{1,0:T(8,128)}, f32[512,512]{1,0:T(8,128)}, f32[512,512]{1,0:T(8,128)}, bf16[512,512]{1,0:T(8,128)(2,1)}, bf16[1024,128]{1,0:T(8,128)(2,...) custom-call(f32[8,96,512]{2,1,0:T(8,128)} %broadcast_select_fusion.4, ...), custom_call_target="tpu_custom_call" | custom-call | tf_op jit(solution)/shard_map/front/pallas_call | solution.py:601
  128.7 247.1 %head.1 = (f32[512,512]{1,0:T(8,128)}, f32[6288,512]{1,0:T(8,128)}, f32[8,512]{1,0:T(8,128)}, f32[8,512]{1,0:T(8,128)}) custom-call(f32[512,512]{1,0:T(8,128)} %get-tuple-element.163.f_ref, s32[8,512]{1,0:T(8,128)} %sub.56.lab_ref, f32[6288,512]{1,0:T(8,128)} %get-tuple-element.546), custom_call_target="tpu_custom_call" | custom-call | flops 105495134208 | bytes 38633472 | tf_op jit(solution)/shard_map/head/pallas_call | solution.py:339
  375.8 0.7 reduce_sum.89
  376.5 1.3 fusion.39.loss_ref
  377.8 39.3 %layer_bwd.1 = (f32[8,928,512]{2,1,0:T(8,128)}, f32[512,512]{1,0:T(8,128)S(1)}) custom-call(f32[512,512]{1,0:T(8,128)} %get-tuple-element.165.dfin_ref, f32[512,512]{1,0:T(8,128)} %get-tuple-element.166.x0_ref, f32[512,512]{1,0:T(8,128)} %get-tuple-element.167.x1_ref, f32[1,512]{1,0:T(1,128)} %fusion.39.loss_ref, f32[2,512]{1,0:T(2,128)} %ln_ref.3, ...), custom_call_target="tpu_custom_call" | custom-call | tf_op jit(solution)/shard_map/layer_bwd/pallas_call | solution.py:722
  417.1 2.2 gather_fusion.3
  419.3 1.3 broadcast_select_fusion.3.x_ref
  420.6 26.2 %plane_swap.3 = f32[8,96,512]{2,1,0:T(8,128)} custom-call(f32[8,96,512]{2,1,0:T(8,128)} %broadcast_select_fusion.3.x_ref), custom_call_target="tpu_custom_call" | custom-call | tf_op jit(solution)/shard_map/plane_swap/pallas_call | solution.py:87
  446.8 16.6 %scatter_fusion.1 = f32[6288,512]{1,0:T(8,128)} fusion(f32[6288,512]{1,0:T(8,128)} %get-tuple-element.164, s32[768]{0:T(1024)S(1)} %copy-done.18, f32[768,512]{1,0:T(8,128)} %bitcast.69), kind=kCustom, calls=%fused_computation.5 | custom fusion | flops 393216 | bytes 4721664 | tf_op jit(solution)/shard_map/scatter-add | solution.py:1062
  463.4 0.2 while.23
  463.7 181.0 %tail.1 = (f32[6288,512]{1,0:T(8,128)}, f32[6288,512]{1,0:T(8,128)}, f32[6288,512]{1,0:T(8,128)}, f32[2,464,512]{2,1,0:T(8,128)}, f32[8,24,512]{2,1,0:T(8,128)}) custom-call(f32[6288,512]{1,0:T(8,128)} %get-tuple-element.181.g_ref, f32[8,2,464,512]{3,2,1,0:T(8,128)} %bitcast.68, f32[6288,512]{1,0:T(8,128)} %get-tuple-element.546, f32[6288,512]{1,0:T(8,128)} %m_ref.1, ...), custom_call_target="tpu_custom_call" | custom-call | tf_op jit(solution)/shard_map/tail/pallas_call | solution.py:949
  644.7 1.4 slice_reduce_fusion
  646.2 1.3 divide_subtract_fusion.5
  647.5 1.0 slice.23
  648.5 1.9 divide_subtract_fusion.3
  650.4 1.8 divide_subtract_fusion.4
  652.2 1.0 divide_subtract_fusion.2
  653.4 0.3 copy-done.8
  653.7 0.2 copy-done.9
  653.9 1.3 divide_subtract_fusion.1
  655.2 0.3 copy.52
  655.5 0.9 copy-done.1
  656.4 3.5 divide_subtract_fusion
  660.0 11.1 %copy.70 = f32[6288,512]{1,0:T(8,128)} copy(f32[6288,512]{1,0:T(8,128)} %get-tuple-element.524) | data formatting | bytes 25755648
  671.1 11.1 %copy.71 = f32[6288,512]{1,0:T(8,128)} copy(f32[6288,512]{1,0:T(8,128)} %get-tuple-element.531) | data formatting | bytes 25755648
  682.1 11.1 %copy.72 = f32[6288,512]{1,0:T(8,128)} copy(f32[6288,512]{1,0:T(8,128)} %get-tuple-element.538) | data formatting | bytes 25755648
  (61 shorter events, 0.6 us)
Async XLA Ops:
  6.2 5.7 copy-start
  10.7 1.5 copy-start.4
  10.7 1.5 copy-start.10
  10.7 1.5 copy-start.11
  13.7 7.5 %copy-start.2 = (s32[8,512]{1,0:T(8,128)}, s32[8,512]{1,0:T(8,128)S(1)}, u32[]{:S(2)}) copy-start(s32[8,512]{1,0:T(8,128)S(1)} %get-tuple-element.549) | copy-start | bytes 49156
  377.8 39.3 %copy-start.19 = (s32[1024]{0:T(1024)S(1)}, s32[1024]{0:T(1024)}, u32[]{:S(2)}) copy-start(s32[1024]{0:T(1024)} %pad_clamp_fusion.2) | copy-start | bytes 12292
  417.1 2.2 copy-start.20
  420.6 26.2 %copy-start.18 = (s32[768]{0:T(1024)S(1)}, s32[768]{0:T(1024)}, u32[]{:S(2)}) copy-start(s32[768]{0:T(1024)} %get-tuple-element.234) | copy-start | bytes 9220
  446.8 16.6 %copy-start.3 = (s32[8,512]{1,0:T(8,128)S(1)}, s32[8,512]{1,0:T(8,128)}, u32[]{:S(2)}) copy-start(s32[8,512]{1,0:T(8,128)} %copy-done.2) | copy-start | bytes 49156
  463.7 182.5 %copy-start.17 = (f32[2,512]{1,0:T(2,128)S(1)}, f32[2,512]{1,0:T(2,128)}, u32[]{:S(2)}) copy-start(f32[2,512]{1,0:T(2,128)} %ln_ref.3) | copy-start | bytes 12292
  463.7 182.5 %copy-start.21 = (f32[2,512]{1,0:T(2,128)S(1)}, f32[2,512]{1,0:T(2,128)}, u32[]{:S(2)}) copy-start(f32[2,512]{1,0:T(2,128)} %param.37) | copy-start | bytes 12292
  463.7 182.5 %copy-start.22 = (f32[2,512]{1,0:T(2,128)S(1)}, f32[2,512]{1,0:T(2,128)}, u32[]{:S(2)}) copy-start(f32[2,512]{1,0:T(2,128)} %param.44) | copy-start | bytes 12292
  644.7 5.7 copy-start.12
  644.7 5.7 copy-start.15
  644.7 5.7 copy-start.16
  644.7 7.5 %copy-start.7 = (f32[2,512,64]{1,2,0:T(8,128)S(1)}, f32[2,512,64]{1,2,0:T(8,128)}, u32[]{:S(2)}) copy-start(f32[2,512,64]{1,2,0:T(8,128)} %param.32) | copy-start | bytes 786436
  644.7 7.5 %copy-start.13 = (f32[2,512,64]{1,2,0:T(8,128)S(1)}, f32[2,512,64]{1,2,0:T(8,128)}, u32[]{:S(2)}) copy-start(f32[2,512,64]{1,2,0:T(8,128)} %param.39) | copy-start | bytes 786436
  644.7 7.5 %copy-start.14 = (f32[2,512,64]{1,2,0:T(8,128)S(1)}, f32[2,512,64]{1,2,0:T(8,128)}, u32[]{:S(2)}) copy-start(f32[2,512,64]{1,2,0:T(8,128)} %param.46) | copy-start | bytes 786436
  650.4 2.9 copy-start.6
  652.2 1.2 copy-start.5
  652.2 1.5 copy-start.8
  652.2 1.6 copy-start.9
  655.2 1.2 copy-start.1

commit v6 on v5

--- a/solution.py
+++ b/solution.py
@@ -615,8 +615,8 @@
 
 
 def layer_bwd_kernel(dfin_ref, x0_ref, x1_ref, loss_ref, ln_ref, cos_ref, sin_ref, wq_ref, wkv_ref, wo_ref, wg_ref, wu_ref, wd_ref,
-                     q_ref, kv_ref, kvt_ref, lse_ref, ctx_ref, rows_ref, d0_ref, d_one, d_b, u_b, dctx, dq, dkv, dkv_in,
-                     g_q, g_o, g_g, g_u, g_d, small, out_sem, send_sem, recv_sem):
+                     q_ref, kv_ref, kvt_ref, lse_ref, ctx_ref, pick_ref, rows_ref, d0_ref, back_ref, d_one, d_b, u_b, dctx, dq, dkv, dkv_in,
+                     hid, d_gate, d_up, rows_out, g_q, g_o, g_g, g_u, g_d, small, out_sem, send_sem, recv_sem, r_send, r_recv):
     tp, dp, _, y = place()
     partner = tp + 1 - 2 * y
     own, width = x0_ref.shape
@@ -625,14 +625,14 @@
     nq = q_ref.shape[0]
     heads = nq // hd
     ff = wg_ref.shape[0]
-    signal(partner, dp)
+    shards = rows_ref.shape[0]
+    plane_barrier(tp, dp, [])
     _, f_hat, f_inv = norm_fwd(x1_ref[...], ln_ref[1:2, :])
     d_in, g_fin = norm_bwd(dfin_ref[...], f_hat, f_inv, ln_ref[1:2, :])
     d_one[...] = d_in
     d_b[...] = d_in.astype(BF16)
     u_b[...] = norm_fwd(x0_ref[...], ln_ref[0:1, :])[0]
     dctx[...] = mm(wo_ref[...], d_b[...], TB).astype(BF16)
-    g_o[...] = mm(ctx_ref[...], d_b[...])
     cos_t = cos_ref[...]
     sin_t = sin_ref[...]
     blank = jnp.zeros((hd, own), BF16)
@@ -656,12 +656,10 @@
         return carry
 
     lax.fori_loop(0, heads, attend, 0)
-    pl.semaphore_wait(pltpu.get_barrier_semaphore(), 1)
     copy = remote(dkv.at[pl.ds(pl.multiple_of((1 - y) * own, own), own), :], dkv_in, send_sem, recv_sem, partner, dp)
     copy.start()
 
     d0_ref[...] = mm(dq[...], wq_ref[...], TA)
-    g_q[...] = mm(dq[...], u_b[...])
     step = min(512, ff)
 
     def mlp(n, carry):
@@ -670,12 +668,10 @@
         up = mm(wu_ref[at, :], u_b[...], TB)
         d_hidden = mm(wd_ref[at, :], d_b[...], TB)
         sig = jax.nn.sigmoid(gate)
-        g_d[at, :] = mm((gate * sig * up).astype(BF16), d_b[...])
-        d_gate = (d_hidden * up * sig * (1.0 + gate * (1.0 - sig))).astype(BF16)
-        d_up = (d_hidden * gate * sig).astype(BF16)
-        g_g[at, :] = mm(d_gate, u_b[...])
-        g_u[at, :] = mm(d_up, u_b[...])
-        d0_ref[...] += mm(d_gate, wg_ref[at, :], TA) + mm(d_up, wu_ref[at, :], TA)
+        hid[at, :] = (gate * sig * up).astype(BF16)
+        d_gate[at, :] = (d_hidden * up * sig * (1.0 + gate * (1.0 - sig))).astype(BF16)
+        d_up[at, :] = (d_hidden * gate * sig).astype(BF16)
+        d0_ref[...] += mm(d_gate[at, :], wg_ref[at, :], TA) + mm(d_up[at, :], wu_ref[at, :], TA)
         return carry
 
     lax.fori_loop(0, ff // step, mlp, 0)
@@ -687,12 +683,38 @@
     d_u = d0_ref[...] + mm(d_kv, wkv_ref[...], TA)
     _, u_hat, u_inv = norm_fwd(x0_ref[...], ln_ref[0:1, :])
     d_in, g_in = norm_bwd(d_u, u_hat, u_inv, ln_ref[0:1, :])
-    d0_ref[...] = d_one[...] + d_in
+    d_zero = d_one[...] + d_in
+    d0_ref[...] = d_zero
+    high = d_zero.astype(BF16)
+    left = d_zero - high.astype(F32)
+    middle = left.astype(BF16)
+    low = (left - middle.astype(F32)).astype(BF16)
+    rows_out[...] = (mm(pick_ref[...], high, TA) + mm(pick_ref[...], middle, TA) + mm(pick_ref[...], low, TA)).reshape(rows_out.shape)
+
+    def row_copy(to):
+        return remote(rows_out.at[to], back_ref.at[tp], r_send.at[to], r_recv.at[tp], to, dp)
+
+    peers = [lax.rem(tp + n, shards) for n in range(1, shards)]
+    for to in peers:
+        row_copy(to).start()
+    own_rows = pltpu.make_async_copy(rows_out.at[tp], back_ref.at[tp], out_sem.at[7 * 2 * NZ])
+    own_rows.start()
+
+    g_o[...] = mm(ctx_ref[...], d_b[...])
+    g_q[...] = mm(dq[...], u_b[...])
+
+    def weight_grads(n, carry):
+        at = pl.ds(pl.multiple_of(n * step, step), step)
+        g_d[at, :] = mm(hid[at, :], d_b[...])
+        g_g[at, :] = mm(d_gate[at, :], u_b[...])
+        g_u[at, :] = mm(d_up[at, :], u_b[...])
+        return carry
+
+    lax.fori_loop(0, ff // step, weight_grads, 0)
     small[2 * hd:, :] = jnp.zeros_like(small[2 * hd:, :])
     small[2 * hd:2 * hd + 1, :] = g_in.reshape(1, width)
     small[2 * hd + 1:2 * hd + 2, :] = g_fin.reshape(1, width)
     small[2 * hd + 2:2 * hd + 3, :] = loss_ref[...]
-    shards = rows_ref.shape[0]
     copies = []
 
     def put(src, first, size, s):
@@ -710,42 +732,48 @@
         c.start()
     for c in copies:
         c.wait()
-
-
-def layer_bwd(d_fin, x0, x1, loss_row, ln, cos_t, sin_t, weights, saved, collective_id):
+    own_rows.wait()
+    for source in peers:
+        remote(rows_out.at[source], back_ref.at[source], r_send.at[source], r_recv.at[source], source, dp).wait_recv()
+        row_copy(source).wait_send()
+
+
+def layer_bwd(d_fin, x0, x1, loss_row, ln, cos_t, sin_t, weights, saved, pick, collective_id):
     own, width = x0.shape
     nq = weights[0].shape[0]
     two_hd = weights[1].shape[0]
     ff = weights[3].shape[0]
     rows = (2 * nq + 3 * ff + two_hd) // (2 * NZ) + 16
     chunk = (own, width)
+    back = (2 * NZ, pick.shape[1] // (2 * NZ), width)
     return pl.pallas_call(
         layer_bwd_kernel,
-        out_shape=(jax.ShapeDtypeStruct((2 * NZ, rows, width), F32), jax.ShapeDtypeStruct(chunk, F32)),
-        in_specs=[VMEM] * 18,
-        out_specs=(ANY, VMEM),
+        out_shape=(jax.ShapeDtypeStruct((2 * NZ, rows, width), F32), jax.ShapeDtypeStruct(chunk, F32), jax.ShapeDtypeStruct(back, F32)),
+        in_specs=[VMEM] * 19,
+        out_specs=(ANY, VMEM, ANY),
         scratch_shapes=[pltpu.VMEM(chunk, F32), pltpu.VMEM(chunk, BF16), pltpu.VMEM(chunk, BF16), pltpu.VMEM((nq, own), BF16),
-                        pltpu.VMEM((nq, own), BF16), pltpu.VMEM((2 * own, two_hd), F32), pltpu.VMEM((own, two_hd), F32),
-                        pltpu.VMEM((nq, width), F32), pltpu.VMEM((nq, width), F32)] + [pltpu.VMEM((ff, width), F32)] * 3
-        + [pltpu.VMEM((two_hd + 32, width), F32), pltpu.SemaphoreType.DMA((14 * NZ,)), pltpu.SemaphoreType.DMA, pltpu.SemaphoreType.DMA],
+                        pltpu.VMEM((nq, own), BF16), pltpu.VMEM((2 * own, two_hd), F32), pltpu.VMEM((own, two_hd), F32)]
+        + [pltpu.VMEM((ff, own), BF16)] * 3 + [pltpu.VMEM(back, F32), pltpu.VMEM((nq, width), F32), pltpu.VMEM((nq, width), F32)] + [pltpu.VMEM((ff, width), F32)] * 3
+        + [pltpu.VMEM((two_hd + 32, width), F32), pltpu.SemaphoreType.DMA((14 * NZ + 1,)), pltpu.SemaphoreType.DMA, pltpu.SemaphoreType.DMA,
+           pltpu.SemaphoreType.DMA((2 * NZ,)), pltpu.SemaphoreType.DMA((2 * NZ,))],
         compiler_params=pltpu.CompilerParams(collective_id=collective_id, has_side_effects=True, vmem_limit_bytes=60000000),
         name="layer_bwd",
-    )(d_fin, x0, x1, loss_row, ln, cos_t, sin_t, *weights, *saved)
+    )(d_fin, x0, x1, loss_row, ln, cos_t, sin_t, *weights, *saved, pick)
 
 
 N_BLOCK = 12
 EARLY = 9
 W_REDUCE = {
-    0: {0: (3,), 2: (2,), 4: (1,), 6: (0,)},
-    1: {2: (3,), 4: (2, 0), 6: (1,)},
-    2: {2: (0,), 4: (1, 3), 6: (2,)},
-    3: {0: (0,), 2: (1,), 4: (2,), 6: (3,)},
+    0: {1: (3,), 3: (2,), 5: (1,), 7: (0,)},
+    1: {3: (3,), 5: (2, 0), 7: (1,)},
+    2: {3: (0,), 5: (1, 3), 7: (2,)},
+    3: {1: (0,), 3: (1,), 5: (2,), 7: (3,)},
 }
 
 
-def tail_kernel(g_ref, p_ref, e_ref, m_ref, v_ref, e_new, m_new, v_new, w_out, small_ref,
-                s_buf, from_c, from_x, t_buf, state_in, state_out, acc, w_c, w_y, w_l, w_r, w_x,
-                g_load, g_send_c, g_recv_c, g_send_x, g_recv_x, g_send_t, g_recv_t, in_sem, out_sem,
+def tail_kernel(g_ref, p_ref, rows_ref, ids_ref, t_ref, w_out, small_ref,
+                s_buf, from_c, from_x, rows_c, ids_c, parts, acc, w_c, w_y, w_l, w_r, w_x,
+                g_load, g_send_c, g_recv_c, g_send_x, g_recv_x, g_send_t, g_recv_t, g_store, l_send, l_recv,
                 w_load, w_out_sem, send_c, send_y, send_l, send_r, recv_c, recv_y, recv_l, recv_r, last_send, last_recv, small_send, small_recv):
     tp, dp, z, y = place()
     partner = tp + 1 - 2 * y
@@ -754,70 +782,52 @@
     facing = lax.rem(dp + 2, 4)
     half = g_ref.shape[0] // 2
     size = s_buf.shape[1]
-    sizes = [min(size, half - b * size) for b in range(N_BLOCK)]
-
-    def rows(which, b):
-        return pl.ds(pl.multiple_of(which * half + b * size, 8), sizes[b])
-
-    def part(buf, b):
-        return buf.at[b, pl.ds(0, sizes[b]), :]
-
-    todo = [(0, 0)] + [pair for b in range(1, N_BLOCK) for pair in ((0, b), (1, b - 1))] + [(1, N_BLOCK - 1)]
-
-    def state_loads(q):
-        other, b = todo[q]
-        at = rows(core + other - 2 * core * other, b)
-        return [pltpu.make_async_copy(ref.at[at, :], state_in.at[q % 2, n, pl.ds(0, sizes[b]), :], in_sem.at[q % 2, n])
-                for n, ref in enumerate((e_ref, m_ref, v_ref))]
-
-    def state_stores(q):
-        other, b = todo[q]
-        at = rows(core + other - 2 * core * other, b)
-        return [pltpu.make_async_copy(state_out.at[q % 2, n, pl.ds(0, sizes[b]), :], ref.at[at, :], out_sem.at[q % 2, n])
-                for n, ref in enumerate((e_new, m_new, v_new))]
-
-    def update(q):
-        other, b = todo[q]
-        grad = from_x if other == 0 else t_buf
-        for c in state_loads(q):
-            c.wait()
-        if q >= 2:
-            for c in state_stores(q - 2):
-                c.wait()
-
-        def body(n, carry):
-            at = pl.ds(pl.multiple_of(n * 24, 8), 24)
-            new = adam_update(state_in[q % 2, 0, at, :], grad[b, at, :], state_in[q % 2, 1, at, :], state_in[q % 2, 2, at, :])
-            for i in range(3):
-                state_out[q % 2, i, at, :] = new[i]
+    last = half - (N_BLOCK - 1) * size
+    n_look = rows_ref.shape[0]
+
+    def rows(which, b, n):
+        return pl.ds(pl.multiple_of(which * half + b * size, 8), n)
+
+    def part(buf, b, n):
+        return buf.at[b, pl.ds(0, n), :]
+
+    plane_barrier(tp, dp, [(tp, twin), (tp, facing)])
+
+    look_copies = [remote(rows_ref, rows_c, l_send.at[0], l_recv.at[0], tp, twin), remote(ids_ref, ids_c, l_send.at[1], l_recv.at[1], tp, twin)]
+    for c in look_copies:
+        c.start()
+
+    def c_copy(b, n):
+        return remote(g_ref.at[rows(1 - core, b, n), :], part(from_c, b, n), g_send_c.at[b], g_recv_c.at[b], tp, twin)
+
+    def own_load(b, n):
+        return pltpu.make_async_copy(g_ref.at[rows(core, b, n), :], part(s_buf, b, n), g_load.at[b])
+
+    def x_copy(b, n):
+        return remote(part(s_buf, b, n), part(from_x, b, n), g_send_x.at[b], g_recv_x.at[b], tp, facing)
+
+    def t_copy(b, n):
+        return remote(part(from_x, b, n), t_ref.at[rows(core, b, n), :], g_send_t.at[b], g_recv_t.at[b], tp, twin)
+
+    def t_store(b, n):
+        return pltpu.make_async_copy(part(from_x, b, n), t_ref.at[rows(core, b, n), :], g_store.at[b])
+
+    def every(f, first, end):
+        def body(b, carry):
+            f(b, size)
             return carry
-
-        lax.fori_loop(0, sizes[b] // 24, body, 0)
-        for c in state_stores(q):
-            c.start()
-        if q + 2 < len(todo):
-            for c in state_loads(q + 2):
-                c.start()
-
-    plane_barrier(tp, dp, [(tp, twin), (tp, facing)])
-    for q in range(2):
-        for c in state_loads(q):
-            c.start()
-
-    def g_first(b):
-        remote(g_ref.at[rows(1 - core, b), :], part(from_c, b), g_send_c.at[b], g_recv_c.at[b], tp, twin).start()
-        pltpu.make_async_copy(g_ref.at[rows(core, b), :], part(s_buf, b), g_load.at[b]).start()
-
-    def g_chip_sum(b):
-        pltpu.make_async_copy(g_ref.at[rows(core, b), :], part(s_buf, b), g_load.at[b]).wait()
-        remote(part(s_buf, b), part(from_c, b), g_send_c.at[b], g_recv_c.at[b], tp, twin).wait_recv()
-        add_into(part(s_buf, b), part(from_c, b), 24)
-
-    def g_copy_x(b):
-        return remote(part(s_buf, b), part(from_x, b), g_send_x.at[b], g_recv_x.at[b], tp, facing)
-
-    def g_copy_t(b):
-        return remote(part(from_x, b), part(t_buf, b), g_send_t.at[b], g_recv_t.at[b], tp, twin)
+        lax.fori_loop(first, min(end, N_BLOCK - 1), body, 0)
+        if end == N_BLOCK:
+            f(N_BLOCK - 1, last)
+
+    def chip_sum(b, n):
+        own_load(b, n).wait()
+        c_copy(b, n).wait_recv()
+        ids = jnp.concatenate([ids_ref[...], ids_c[...]], axis=1) - (core * half + b * size)
+        hit = (lax.broadcasted_iota(jnp.int32, (n, 2 * n_look), 0) == ids).astype(F32).astype(BF16)
+        look = mm(hit, parts[0]) + mm(hit, parts[1]) + mm(hit, parts[2])
+        s_buf[b, 0:n, :] = s_buf[b, 0:n, :] + from_c[b, 0:n, :] + look
+        x_copy(b, n).start()
 
     def w_first(k):
         for zz in REDUCE_ORDER[k]:
@@ -858,18 +868,28 @@
         for k in range(NZ):
             pl.when(z == k)(functools.partial(f, k))
 
-    g_first(0)
-    g_first(1)
+    def first(b, n):
+        c_copy(b, n).start()
+        own_load(b, n).start()
+
+    every(first, 0, 4)
     on_position(w_first)
-    for b in range(2, N_BLOCK):
-        g_first(b)
-    for b in range(2):
-        g_chip_sum(b)
-        g_copy_x(b).start()
+    every(first, 4, N_BLOCK)
+
+    def split(at, value):
+        high = value.astype(BF16)
+        left = value - high.astype(F32)
+        middle = left.astype(BF16)
+        parts[0, at, :] = high
+        parts[1, at, :] = middle
+        parts[2, at, :] = (left - middle.astype(F32)).astype(BF16)
+
+    split(pl.ds(0, n_look), rows_ref[...])
+    for c in look_copies:
+        c.wait()
+    split(pl.ds(n_look, n_look), rows_c[...])
+    every(chip_sum, 0, EARLY)
     on_position(w_second)
-    for b in range(2, EARLY):
-        g_chip_sum(b)
-        g_copy_x(b).start()
 
     total = acc.at[tp]
     w_copy_x = remote(total, w_x, last_send.at[0], last_recv.at[0], tp, facing)
@@ -879,25 +899,18 @@
     mine = w_out.at[1, pl.ds(n_rows - 32, n_small), :]
     small_here = pltpu.make_async_copy(mine, small_ref.at[tp], w_out_sem)
     peers = [lax.rem(tp + n, 2 * NZ) for n in range(1, 2 * NZ)]
-    q = 0
     for b in range(N_BLOCK):
-        g_copy_x(b).wait_recv()
-        add_into(part(from_x, b), part(s_buf, b), 24)
-        g_copy_t(b).start()
-        update(q)
-        q += 1
-        if b > 0:
-            g_copy_t(b - 1).wait_recv()
-            update(q)
-            q += 1
+        n = last if b == N_BLOCK - 1 else size
+        x_copy(b, n).wait_recv()
+        add_into(part(from_x, b, n), part(s_buf, b, n), 24)
+        t_copy(b, n).start()
+        t_store(b, n).start()
         for k in range(NZ):
             if b in W_REDUCE[k]:
                 pl.when(z == k)(functools.partial(w_reduce, k, W_REDUCE[k][b]))
-        if b == 6:
+        if b == 7:
             w_copy_x.start()
-            for late in range(EARLY, N_BLOCK):
-                g_chip_sum(late)
-                g_copy_x(late).start()
+            every(chip_sum, EARLY, N_BLOCK)
         if b == 8:
             w_copy_x.wait()
             add_into(total, w_x)
@@ -910,16 +923,10 @@
             for to in peers:
                 remote(mine, small_ref.at[tp], small_send.at[to], small_recv.at[tp], to, dp).start()
             small_here.start()
-    g_copy_t(N_BLOCK - 1).wait_recv()
-    update(q)
     for source in peers:
         remote(small_ref.at[source], small_ref.at[source], small_send.at[source], small_recv.at[source], source, dp).wait_recv()
         remote(mine, small_ref.at[tp], small_send.at[source], small_recv.at[tp], source, dp).wait_send()
     small_here.wait()
-    for b in range(N_BLOCK):
-        remote(g_ref.at[rows(1 - core, b), :], part(from_c, b), g_send_c.at[b], g_recv_c.at[b], tp, twin).wait_send()
-        g_copy_x(b).wait_send()
-        g_copy_t(b).wait_send()
 
     def w_done(k):
         for zz in range(NZ):
@@ -933,33 +940,122 @@
                 remote(line, w_r.at[zz], send_l.at[zz], recv_r.at[zz], tp - 2, dp).wait_send()
 
     on_position(w_done)
-    for last in (len(todo) - 2, len(todo) - 1):
-        for c in state_stores(last):
-            c.wait()
-
-
-def tail(g_table, g_rows, embed, m_embed, v_embed, collective_id):
-    vocab, width = embed.shape
+
+    def drain(b, n):
+        c_copy(b, n).wait_send()
+        x_copy(b, n).wait_send()
+        t_copy(b, n).wait_send()
+        t_store(b, n).wait()
+        remote(part(from_x, b, n), t_ref.at[rows(1 - core, b, n), :], g_send_t.at[b], g_recv_t.at[b], tp, twin).wait_recv()
+
+    every(drain, 0, N_BLOCK)
+
+
+def tail(g_table, g_rows, look_rows, look_ids, collective_id):
+    vocab, width = g_table.shape
     rows = g_rows.shape[1]
     half = (rows // 2, width)
+    n_look = look_ids.shape[1]
     size = -(-vocab // (2 * N_BLOCK * 24)) * 24
     blocks = pltpu.VMEM((N_BLOCK, size, width), F32)
     dma = lambda *n: pltpu.SemaphoreType.DMA(n)
-    table = jax.ShapeDtypeStruct((vocab, width), F32)
-    *new, w_sum, small = pl.pallas_call(
+    t, w_sum, small = pl.pallas_call(
         tail_kernel,
-        out_shape=(table, table, table, jax.ShapeDtypeStruct((2,) + half, F32), jax.ShapeDtypeStruct((2 * NZ, 24, width), F32)),
-        in_specs=[ANY] * 5,
-        out_specs=(ANY,) * 5,
-        scratch_shapes=[blocks] * 4 + [pltpu.VMEM((2, 3, size, width), F32)] * 2
+        out_shape=(jax.ShapeDtypeStruct((vocab, width), F32), jax.ShapeDtypeStruct((2,) + half, F32), jax.ShapeDtypeStruct((2 * NZ, 24, width), F32)),
+        in_specs=[ANY, ANY, VMEM, VMEM],
+        out_specs=(ANY,) * 3,
+        scratch_shapes=[blocks] * 3 + [pltpu.VMEM((n_look, width), F32), pltpu.VMEM((1, n_look), jnp.int32), pltpu.VMEM((3, 2 * n_look, width), BF16)]
         + [pltpu.VMEM((2 * NZ,) + half, F32)] * 2 + [pltpu.VMEM((NZ,) + half, F32)] + [pltpu.VMEM((NZ - 1,) + half, F32)] * 2
         + [pltpu.VMEM(half, F32)]
-        + [dma(N_BLOCK)] * 7 + [dma(2, 3)] * 2
+        + [dma(N_BLOCK)] * 8 + [dma(2)] * 2
         + [dma(2 * NZ), pltpu.SemaphoreType.DMA] + [dma(2 * NZ), dma(NZ), dma(NZ), dma(NZ)] * 2 + [dma(2)] * 2 + [dma(2 * NZ)] * 2,
         compiler_params=pltpu.CompilerParams(collective_id=collective_id, has_side_effects=True, vmem_limit_bytes=67000000),
         name="tail",
-    )(g_table, g_rows.reshape((2 * NZ, 2) + half), embed, m_embed, v_embed)
-    return new, w_sum.reshape(rows, width), small
+    )(g_table, g_rows.reshape((2 * NZ, 2) + half), look_rows.reshape(n_look, width), look_ids)
+    return t, w_sum.reshape(rows, width), small
+
+
+UPDATE_ROWS = 512
+
+
+def update_kernel(t_ref, w_ref, small_ref, *refs):
+    state = [refs[7 * i:7 * i + 7] for i in range(3)]
+    new = [refs[21 + 7 * i:28 + 7 * i] for i in range(3)]
+    loss_ref = refs[42]
+    held, made, in_sem, out_sem = refs[43:]
+    vocab = t_ref.shape[0]
+    n_kv, hd = 2 * state[0][3].shape[2] // small_ref.shape[0], state[0][3].shape[2]
+    blocks = [(at, min(UPDATE_ROWS, vocab - at)) for at in range(0, vocab, UPDATE_ROWS)]
+
+    def loads(q):
+        at, n = blocks[q]
+        return [pltpu.make_async_copy(ref.at[pl.ds(at, n), :], held.at[q % 3, i, pl.ds(0, n), :], in_sem.at[q % 3, i])
+                for i, ref in enumerate((t_ref, state[0][0], state[1][0], state[2][0]))]
+
+    def stores(q):
+        at, n = blocks[q]
+        return [pltpu.make_async_copy(made.at[q % 2, i, pl.ds(0, n), :], new[i][0].at[pl.ds(at, n), :], out_sem.at[q % 2, i]) for i in range(3)]
+
+    for q in range(3):
+        for c in loads(q):
+            c.start()
+
+    def small_update(index, grad, *where):
+        got = adam_update(state[0][index][where], grad, state[1][index][where], state[2][index][where])
+        for i in range(3):
+            new[i][index][where] = got[i]
+
+    n_q, n_f = state[0][2].shape[1], state[0][6].shape[0]
+    small_update(1, small_ref[0, n_kv:n_kv + 2, :], Ellipsis)
+    small_update(2, w_ref[0:n_q, :].T, Ellipsis)
+    kv = small_ref[:, 0:n_kv, :].reshape(2 * hd, small_ref.shape[2]).T
+    for i in range(2):
+        small_update(3, kv[:, i * hd:(i + 1) * hd], i)
+    small_update(4, w_ref[n_q:2 * n_q, :], Ellipsis)
+    for i in range(2):
+        small_update(5, w_ref[2 * n_q + i * n_f:2 * n_q + (i + 1) * n_f, :].T, i)
+    small_update(6, w_ref[2 * n_q + 2 * n_f:2 * n_q + 3 * n_f, :], Ellipsis)
+    loss_ref[...] = jnp.sum(small_ref[0, n_kv + 2:n_kv + 3, :], axis=1, keepdims=True)
+
+    for q, (at, n) in enumerate(blocks):
+        for c in loads(q):
+            c.wait()
+        if q >= 2:
+            for c in stores(q - 2):
+                c.wait()
+        step = 32 if n % 32 == 0 else 16
+
+        def body(j, carry):
+            rows = pl.ds(pl.multiple_of(j * step, step), step)
+            got = adam_update(held[q % 3, 1, rows, :], held[q % 3, 0, rows, :], held[q % 3, 2, rows, :], held[q % 3, 3, rows, :])
+            for i in range(3):
+                made[q % 2, i, rows, :] = got[i]
+            return carry
+
+        lax.fori_loop(0, n // step, body, 0)
+        for c in stores(q):
+            c.start()
+        if q + 3 < len(blocks):
+            for c in loads(q + 3):
+                c.start()
+    for q in range(len(blocks) - 2, len(blocks)):
+        for c in stores(q):
+            c.wait()
+
+
+def update(g_table, g_shard, g_small, state_arrays):
+    specs = [ANY] + [VMEM] * 6
+    width = g_table.shape[1]
+    return pl.pallas_call(
+        update_kernel,
+        out_shape=tuple(jax.ShapeDtypeStruct(a.shape, F32) for a in state_arrays) + (jax.ShapeDtypeStruct((1, 1), F32),),
+        in_specs=[ANY, VMEM, VMEM] + specs * 3,
+        out_specs=tuple(specs * 3) + (VMEM,),
+        scratch_shapes=[pltpu.VMEM((3, 4, UPDATE_ROWS, width), F32), pltpu.VMEM((2, 3, UPDATE_ROWS, width), F32),
+                        pltpu.SemaphoreType.DMA((3, 4)), pltpu.SemaphoreType.DMA((2, 3))],
+        compiler_params=pltpu.CompilerParams(vmem_limit_bytes=60000000),
+        name="update",
+    )(g_table, g_shard, g_small, *state_arrays)
 
 
 def norm_fwd(x_f32, scale):
@@ -1050,34 +1146,22 @@
         d_fin, g_head_part, log_norm, lab_sum = head(f_own, lab_loc, embed, logit_scale, logit_scale / tok_total, 4)
         log_norm = lax.dynamic_index_in_dim(log_norm, tp_rank, 0, keepdims=False)
         loss_row = (log_norm + LOGIT_ZLOSS * log_norm * log_norm - jnp.sum(lab_sum, axis=0) * logit_scale) / tok_total
-        g_rows, d_zero = layer_bwd(d_fin, x_zero, x_one, loss_row[None, :], ln_scales, cos_t, sin_t, weights, saved, 7)
-
-        def give_back(step, g_sum, collective_id):
-            mine = (my_shard[None, None, :] == jnp.arange(n_tp)[:, None, None]) & (my_rank[None, None, :] == slots[None, :, None] + step * CAP)
+        g_rows, d_zero, rows_back = layer_bwd(d_fin, x_zero, x_one, loss_row[None, :], ln_scales, cos_t, sin_t, weights, saved, pick_first, 7)
+
+        def row_ids(step):
+            here = (shard[:, None, :] == tp_rank) & (rank[:, None, :] == slots[None, :, None] + step * CAP)
+            return jnp.where(jnp.any(here, axis=-1), jnp.sum(jnp.where(here, row[:, None, :], 0), axis=-1), vocab_loc).reshape(-1)
+
+        def give_back(state):
+            mine = (my_shard[None, None, :] == jnp.arange(n_tp)[:, None, None]) & (my_rank[None, None, :] == slots[None, :, None] + state[0] * CAP)
             ids = jnp.sum(jnp.where(mine, jnp.arange(own)[None, None, :], 0), axis=-1).reshape(-1)
-            rows_out = jnp.take(d_zero, ids, axis=0).reshape(n_tp, CAP, d_model)
-            rows_in = plane_swap(rows_out, collective_id).reshape(-1, d_model)
-            here = (shard[:, None, :] == tp_rank) & (rank[:, None, :] == slots[None, :, None] + step * CAP)
-            row_id = jnp.where(jnp.any(here, axis=-1), jnp.sum(jnp.where(here, row[:, None, :], 0), axis=-1), vocab_loc).reshape(-1)
-            return g_sum.at[row_id].add(rows_in, mode='drop')
-
-        g_table = give_back(0, g_head_part, 8)
-        g_table = lax.while_loop(lambda s: s[0] < rounds, lambda s: (s[0] + 1, give_back(s[0], s[1], 9)), (jnp.int32(1), g_table))[1]
-
-        new_table, g_shard, g_small = tail(g_table, g_rows, embed, state_arrays[7], state_arrays[14], 10)
-        n_kv = 2 * head_dim // n_tp
-        g_kv = g_small[:, :n_kv].reshape(2, head_dim, d_model).transpose(0, 2, 1)
-        loss = jnp.sum(g_small[0, n_kv + 2])
-        gradients = (None, g_small[0, n_kv:n_kv + 2], g_shard[:cuts[0]].T, g_kv, g_shard[cuts[0]:cuts[1]],
-                     g_shard[cuts[1]:cuts[3]].reshape(2, f_loc, d_model).transpose(0, 2, 1), g_shard[cuts[3]:cuts[3] + f_loc])
-
-        outs_p, outs_m, outs_v = ([array] for array in new_table)
-        for index in range(1, 7):
-            new_p, new_m, new_v = adam_update(state_arrays[index], gradients[index], state_arrays[7 + index], state_arrays[14 + index])
-            outs_p.append(new_p)
-            outs_m.append(new_m)
-            outs_v.append(new_v)
-        return tuple(outs_p) + tuple(outs_m) + tuple(outs_v) + (loss,)
+            rows_in = plane_swap(jnp.take(d_zero, ids, axis=0).reshape(n_tp, CAP, d_model), 9).reshape(-1, d_model)
+            return state[0] + 1, state[1].at[row_ids(state[0])].add(rows_in, mode='drop')
+
+        g_table = lax.while_loop(lambda state: state[0] < rounds, give_back, (jnp.int32(1), g_head_part))[1]
+        g_table, g_shard, g_small = tail(g_table, g_rows, rows_back, row_ids(0)[None, :], 10)
+        *new, loss = update(g_table, g_shard, g_small, state_arrays)
+        return tuple(new) + (loss.reshape(()),)
 
     return jax.shard_map(local_step, mesh=mesh, in_specs=(P('dp', None), P('dp', None)) + param_specs * 3,
                          out_specs=param_specs * 3 + (P(),), check_vma=False)

time: 701 us -> 680 us (0.970)
  Pallas kernels: 600 us -> 633 us
  other arithmetic: 42.3 us -> 10.1 us
  local copies, waits for them, and re-layouts: 49 us -> 25.6 us
    unnamed x49 -> x38, local copies, waits for them, and re-layouts: 34.8 us -> 14.5 us
    pallas_call x1, Pallas kernels: 39.3 us -> 59.1 us  [layer_bwd(): pl.pallas_call(layer_bwd_kernel, out_shape=(jax.ShapeDtypeStruct((2 * NZ,...]
    scatter-add x1 -> x0, other arithmetic: 16.6 us -> none  [give_back(): return g_sum.at[row_id].add(rows_in, mode='drop')]
    pallas_call x2, Pallas kernels: 207 us -> 221 us  [the longest x1 184 us: tail(): pl.pallas_call(tail_kernel, out_shape=(jax.ShapeDtypeStruct((vocab, width...]
    sub x7 -> x0, other arithmetic: 10.9 us -> none  [the longest x6 10.9 us: adam_update(): param_in - LEARN_RATE * mom_new / (jnp.sqrt(vel_new) + ADAM_EPS)]
where the time goes in v6:
time: 680 us; the launch traced here: 671 us
  Pallas kernels  633 us (93%)
  local copies, waits for them, and re-layouts  25.6 us (4%)
  other arithmetic  10.1 us (1%)
    pallas_call x1, Pallas kernels, head(): pl.pallas_call(functools.partial(head_kernel, scale, token_scale), out_sh...  247 us
    pallas_call x1, Pallas kernels, tail(): pl.pallas_call(tail_kernel, out_shape=(jax.ShapeDtypeStruct((vocab, width...  184 us
    pallas_call x1, Pallas kernels, front(): pl.pallas_call(front_kernel, out_shape=(s((own, width), F32),) * 3 + (s((...  106 us
    pallas_call x1, Pallas kernels, layer_bwd(): pl.pallas_call(layer_bwd_kernel, out_shape=(jax.ShapeDtypeStruct((2 * NZ,...  59.1 us
    pallas_call x1, Pallas kernels, update(): pl.pallas_call(update_kernel, out_shape=tuple((jax.ShapeDtypeStruct(a.sha...  36.8 us
    unnamed x38, local copies, waits for them, and re-layouts  14.5 us

profile of v6, /device:TPU:0, one launch (start us, length us, event | category | flops | bytes accessed | tf_op | source)
XLA Modules:
  0.0 671.1 jit_solution(1923458828443891165)
XLA Ops:
  0.7 0.0 copy-start.6
  0.7 0.0 copy-start.12
  0.7 0.8 broadcast_subtract_fusion
  1.5 0.6 sub.38.lab_ref
  2.2 0.7 reshape.517
  2.9 0.2 convert_reduce_fusion
  3.2 0.6 reduce_max.9
  4.5 0.0 copy-start.10
  4.5 0.3 fusion.22
  4.8 0.3 fusion.20
  5.1 0.4 select_reduce_fusion.3
  5.5 0.1 reshape.518
  5.6 0.7 select_n.168.ids_ref
  6.4 1.0 multiply_sine_fusion
  7.3 1.7 convert_element_type.47
  9.0 0.0 copy-done.11
  9.0 0.8 copy.78.refs_9_
  9.9 0.8 copy.80.refs_16_
  10.7 0.8 copy.76.refs_2_
  11.5 1.0 copy.79.refs_10_
  12.5 1.0 copy.81.refs_17_
  13.6 1.0 copy.77.refs_3_
  14.6 0.1 and_convert_fusion
  14.7 0.0 copy-start.3
  14.7 0.0 copy-start.5
  14.7 1.2 copy.74.pick_ref
  15.9 0.0 copy-done
  15.9 0.3 copy.73
  16.3 1.4 pad_maximum_fusion.w_ref
  17.6 0.1 broadcast_in_dim.133
  17.8 0.0 copy-start.1
  17.8 7.4 %gather_fusion.2 = f32[768,512]{1,0:T(8,128)S(1)} fusion(f32[6288,512]{1,0:T(8,128)} %get-tuple-element.590, s32[1024]{0:T(1024)S(1)} %pad_clamp_fusion.2), kind=kCustom, calls=%fused_computation.2 | custom fusion | bytes 3148800 | tf_op jit(solution)/shard_map/jit(_take)/gather | solution.py:1124
  25.2 1.3 broadcast_select_fusion.3.rows_ref
  26.6 106.1 %front.1 = (f32[512,512]{1,0:T(8,128)}, f32[512,512]{1,0:T(8,128)}, f32[512,512]{1,0:T(8,128)}, bf16[512,512]{1,0:T(8,128)(2,1)}, bf16[1024,128]{1,0:T(8,128)(2,...) custom-call(f32[8,96,512]{2,1,0:T(8,128)} %broadcast_select_fusion.3, ...), custom_call_target="tpu_custom_call" | custom-call | tf_op jit(solution)/shard_map/front/pallas_call | solution.py:601
  132.7 247.1 %head.1 = (f32[512,512]{1,0:T(8,128)}, f32[6288,512]{1,0:T(8,128)}, f32[8,512]{1,0:T(8,128)}, f32[8,512]{1,0:T(8,128)}) custom-call(f32[512,512]{1,0:T(8,128)} %get-tuple-element.184.f_ref, s32[8,512]{1,0:T(8,128)} %sub.38.lab_ref, f32[6288,512]{1,0:T(8,128)} %get-tuple-element.590), custom_call_target="tpu_custom_call" | custom-call | flops 105495134208 | bytes 38633472 | tf_op jit(solution)/shard_map/head/pallas_call | solution.py:339
  379.8 0.7 reduce_sum.70
  380.5 1.3 fusion.29.loss_ref
  381.9 59.1 %layer_bwd.1 = (f32[8,928,512]{2,1,0:T(8,128)}, f32[512,512]{1,0:T(8,128)S(1)}, f32[8,96,512]{2,1,0:T(8,128)}) custom-call(f32[512,512]{1,0:T(8,128)} %get-tuple-element.186.dfin_ref, f32[512,512]{1,0:T(8,128)} %get-tuple-element.187.x0_ref, f32[512,512]{1,0:T(8,128)} %get-tuple-element.188.x1_ref, f32[1,512]{1,0:T(1,128)} %fusion.29.loss_ref, ...), custom_call_target="tpu_custom_call" | custom-call | tf_op jit(solution)/shard_map/layer_bwd/pallas_call | solution.py:749
  441.0 183.8 %tail.1 = (f32[6288,512]{1,0:T(8,128)}, f32[2,464,512]{2,1,0:T(8,128)}, f32[8,24,512]{2,1,0:T(8,128)}) custom-call(f32[6288,512]{1,0:T(8,128)} %get-tuple-element.202.g_ref, f32[8,2,464,512]{3,2,1,0:T(8,128)} %bitcast.42, f32[768,512]{1,0:T(8,128)} %bitcast.48, s32[1,768]{1,0:T(1,128)} %select_n.168.ids_ref), custom_call_target="tpu_custom_call" | custom-call | tf_op jit(solution)/shard_map/tail/pallas_call | solution.py:962
  624.9 36.8 %update.1 = (f32[6288,512]{1,0:T(8,128)}, f32[2,512]{1,0:T(2,128)}, f32[512,64]{1,0:T(8,128)}, f32[2,512,64]{2,1,0:T(8,128)}, f32[64,512]{1,0:T(8,128)}, /*index...) custom-call(f32[6288,512]{1,0:T(8,128)} %get-tuple-element.205.t_ref, ...), custom_call_target="tpu_custom_call" | custom-call | tf_op jit(solution)/shard_map/update/pallas_call | solution.py:1049
  661.7 0.0 copy-start.8
  661.7 0.0 copy-start.7
  661.7 1.8 copy.82
  663.5 1.7 copy.84
  665.3 1.7 copy.86
  667.0 1.9 copy.83
  668.9 0.9 copy.85
  669.8 0.9 copy.87
  (31 shorter events, 0.2 us)
Async XLA Ops:
  0.7 10.0 %copy-start.6 = (f32[512,64]{0,1:T(8,128)S(1)}, f32[512,64]{0,1:T(8,128)}, u32[]{:S(2)}) copy-start(f32[512,64]{0,1:T(8,128)} %param.31) | copy-start | bytes 393220
  0.7 9.2 %copy-start.12 = (f32[512,64]{0,1:T(8,128)S(1)}, f32[512,64]{0,1:T(8,128)}, u32[]{:S(2)}) copy-start(f32[512,64]{0,1:T(8,128)} %param.45) | copy-start | bytes 393220
  0.7 10.9 %copy-start.9 = (f32[2,512,64]{1,2,0:T(8,128)S(1)}, f32[2,512,64]{1,2,0:T(8,128)}, u32[]{:S(2)}) copy-start(f32[2,512,64]{1,2,0:T(8,128)} %param.39) | copy-start | bytes 786436
  0.7 8.3 %copy-start.11 = (f32[512,64]{0,1:T(8,128)S(1)}, f32[512,64]{0,1:T(8,128)}, u32[]{:S(2)}) copy-start(f32[512,64]{0,1:T(8,128)} %param.38) | copy-start | bytes 393220
  4.5 8.1 %copy-start.10 = (f32[2,512,64]{1,2,0:T(8,128)S(1)}, f32[2,512,64]{1,2,0:T(8,128)}, u32[]{:S(2)}) copy-start(f32[2,512,64]{1,2,0:T(8,128)} %param.46) | copy-start | bytes 786436
  7.3 6.2 copy-start.4
  13.6 2.3 copy-start
  14.7 1.5 copy-start.3
  14.7 1.5 copy-start.5
  17.8 7.5 %copy-start.1 = (s32[8,512]{1,0:T(8,128)}, s32[8,512]{1,0:T(8,128)S(1)}, u32[]{:S(2)}) copy-start(s32[8,512]{1,0:T(8,128)S(1)} %get-tuple-element.593) | copy-start | bytes 49156
  381.9 59.2 %copy-start.2 = (s32[8,512]{1,0:T(8,128)S(1)}, s32[8,512]{1,0:T(8,128)}, u32[]{:S(2)}) copy-start(s32[8,512]{1,0:T(8,128)} %copy-done.1) | copy-start | bytes 49156
  661.7 7.2 %copy-start.8 = (f32[2,512,64]{2,1,0:T(8,128)S(1)}, f32[2,512,64]{2,1,0:T(8,128)}, u32[]{:S(2)}) copy-start(f32[2,512,64]{2,1,0:T(8,128)} %get-tuple-element.330) | copy-start | bytes 786436
  661.7 8.1 %copy-start.7 = (f32[2,512,64]{2,1,0:T(8,128)S(1)}, f32[2,512,64]{2,1,0:T(8,128)}, u32[]{:S(2)}) copy-start(f32[2,512,64]{2,1,0:T(8,128)} %get-tuple-element.337) | copy-start | bytes 786436

commit v7 on v6

--- a/solution.py
+++ b/solution.py
@@ -375,9 +375,9 @@
 MLP_ORDER = {k: [2 * k] + [code for line, other in EVENTS[k] for code in [2 * zz for _, zz in line] + [2 * zz + 1 for zz in other]] for k in range(NZ)}
 
 
-def front_kernel(rows_ref, pick_ref, extra_ref, w_ref, wkv_ref, ln_ref, cos_ref, sin_ref,
+def front_kernel(ids_ref, e_ref, pick_ref, extra_ref, w_ref, wkv_ref, ln_ref, cos_ref, sin_ref,
                  f_ref, x1_ref, x0_ref, q_ref, kv_ref, kvt_ref, lse_ref, ctx_ref, wq_ref, wo_ref, wg_ref, wu_ref, wd_ref,
-                 wl, rows_in, u_b, kv_out, kv_in, own_sem, r_send, r_recv, a_y, a_l, a_r, a_c, a_recv,
+                 table, rows_ref, wl, rows_in, u_b, kv_out, kv_in, own_sem, r_send, r_recv, a_y, a_l, a_r, a_c, a_recv,
                  b_y, b_l, b_r, b_x, b_c, b_recv, kv_send, kv_recv):
     tp, dp, z, y = place()
     partner = tp + 1 - 2 * y
@@ -440,6 +440,8 @@
         for c in copies:
             c.start()
 
+    load = pltpu.make_async_copy(e_ref, table, own_sem.at[2])
+    load.start()
     plane_barrier(tp, dp, [(tp, twin), (tp, facing)])
     peers = [lax.rem(tp + n, shards) for n in range(1, shards)]
 
@@ -447,10 +449,7 @@
         return remote(rows_ref.at[to], rows_in.at[tp], r_send.at[to], r_recv.at[tp], to, dp)
 
     on_position(lambda k: start(b_sends(k, tp, "", True)))
-    start([row_copy(to) for to in peers])
     on_position(lambda k: start(a_sends(k, tp, "", True)))
-    own_rows = pltpu.make_async_copy(rows_ref.at[tp], rows_in.at[tp], own_sem.at[0])
-    own_rows.start()
     own_w = pltpu.make_async_copy(w_ref, wl.at[tp], own_sem.at[1])
     own_w.start()
 
@@ -480,8 +479,22 @@
             b_copy(slot, dp, b_x, tp, facing).start()
             b_copy(slot, dp, b_c.at[0], tp, twin).start()
 
+    load.wait()
+    cap = rows_ref.shape[1]
+
+    def pick_rows(n, carry):
+        for i in range(8):
+            rows_ref[n // (cap // 8), pl.ds(lax.rem(n, cap // 8) * 8 + i, 1), :] = table[pl.ds(ids_ref[n * 8 + i], 1), :]
+        return carry
+
+    lax.fori_loop(0, shards * cap // 8, pick_rows, 0)
     on_position(functools.partial(b_event, 0))
-
+    on_position(functools.partial(a_event, 0))
+    start([row_copy(to) for to in peers])
+    own_rows = pltpu.make_async_copy(rows_ref.at[tp], rows_in.at[tp], own_sem.at[0])
+    own_rows.start()
+    on_position(functools.partial(b_event, 1))
+    on_position(functools.partial(a_event, 1))
     own_rows.wait()
     for source in peers:
         remote(rows_ref.at[source], rows_in.at[source], r_send.at[source], r_recv.at[source], source, dp).wait_recv()
@@ -498,53 +511,6 @@
     kv_copy = remote(kv_out, kv_in, kv_send, kv_recv, partner, dp)
     kv_copy.start()
 
-    on_position(functools.partial(a_event, 0))
-    on_position(functools.partial(b_event, 1))
-    on_position(functools.partial(a_event, 1))
-    on_position(functools.partial(b_event, 2))
-    on_position(functools.partial(a_event, 2))
-    on_position(functools.partial(a_event, 3))
-    on_position(functools.partial(b_event, 3))
-    own_w.wait()
-    for source in peers:
-        a_wait(source, 1 - core)
-    for s in range(shards):
-        wq_ref[s * n_a:(s + 1) * n_a, :] = wl[s, 0:n_a, :].astype(BF16)
-        wo_ref[s * n_a:(s + 1) * n_a, :] = wl[s, n_a:2 * n_a, :].astype(BF16)
-
-    q_all = mm(wq_ref[...], u_b[...], TB)
-    for h in range(heads):
-        lo, hi = turn(q_all[h * hd:h * hd + quarter], q_all[h * hd + quarter:(h + 1) * hd], cos_t, sin_t)
-        q_ref[h * hd:h * hd + quarter, :] = lo.astype(BF16)
-        q_ref[h * hd + quarter:(h + 1) * hd, :] = hi.astype(BF16)
-    kv_copy.wait()
-
-    def fill(mine, other):
-        kv_ref[mine * own:(mine + 1) * own, :] = kv_out[...].T.astype(BF16)
-        kv_ref[other * own:(other + 1) * own, :] = kv_in[...].T.astype(BF16)
-        kvt_ref[:, mine * own:(mine + 1) * own] = kv_out[...].astype(BF16)
-        kvt_ref[:, other * own:(other + 1) * own] = kv_in[...].astype(BF16)
-
-    pl.when(y == 0)(lambda: fill(0, 1))
-    pl.when(y == 1)(lambda: fill(1, 0))
-    blank = jnp.zeros((hd, own), BF16)
-    slope = hd ** -0.5 * LOG2E
-
-    def attend(h, carry):
-        at = pl.ds(pl.multiple_of(h * hd, hd), hd)
-        scores = mm(kv_ref[...], jnp.concatenate([q_ref[at, :], blank], axis=0))
-        allowed = lax.broadcasted_iota(jnp.int32, scores.shape, 0) <= lax.broadcasted_iota(jnp.int32, scores.shape, 1) + y * own
-        scores = jnp.where(allowed, scores * slope, -1e30)
-        top = jnp.max(scores, axis=0, keepdims=True)
-        prob = jnp.exp2(scores - top)
-        total = jnp.sum(prob, axis=0, keepdims=True)
-        lse_ref[pl.ds(h, 1), :] = top + jnp.log2(total)
-        ctx_ref[at, :] = mm(kvt_ref[hd:, :], (prob * (1.0 / total)).astype(BF16)).astype(BF16)
-        return carry
-
-    lax.fori_loop(0, heads, attend, 0)
-    x1_ref[...] += mm(ctx_ref[...], wo_ref[...], TA)
-
     def slot_of(step):
         code = lookup(MLP_ORDER, z, step)
         other = code % 2
@@ -571,7 +537,53 @@
         x1_ref[...] += mm((gate * jax.nn.sigmoid(gate) * up).astype(BF16), wd_ref[at, :])
         return carry
 
-    lax.fori_loop(0, shards, mlp, 0)
+    own_w.wait()
+    lax.fori_loop(0, 3, mlp, 0)
+    on_position(functools.partial(b_event, 2))
+    on_position(functools.partial(a_event, 2))
+    lax.fori_loop(3, 4, mlp, 0)
+    on_position(functools.partial(a_event, 3))
+    on_position(functools.partial(b_event, 3))
+    for source in peers:
+        a_wait(source, 1 - core)
+    for s in range(shards):
+        wq_ref[s * n_a:(s + 1) * n_a, :] = wl[s, 0:n_a, :].astype(BF16)
+        wo_ref[s * n_a:(s + 1) * n_a, :] = wl[s, n_a:2 * n_a, :].astype(BF16)
+
+    q_all = mm(wq_ref[...], u_b[...], TB)
+    for h in range(heads):
+        lo, hi = turn(q_all[h * hd:h * hd + quarter], q_all[h * hd + quarter:(h + 1) * hd], cos_t, sin_t)
+        q_ref[h * hd:h * hd + quarter, :] = lo.astype(BF16)
+        q_ref[h * hd + quarter:(h + 1) * hd, :] = hi.astype(BF16)
+    kv_copy.wait()
+
+    def fill(mine, other):
+        kv_ref[mine * own:(mine + 1) * own, :] = kv_out[...].T.astype(BF16)
+        kv_ref[other * own:(other + 1) * own, :] = kv_in[...].T.astype(BF16)
+        kvt_ref[:, mine * own:(mine + 1) * own] = kv_out[...].astype(BF16)
+        kvt_ref[:, other * own:(other + 1) * own] = kv_in[...].astype(BF16)
+
+    pl.when(y == 0)(lambda: fill(0, 1))
+    pl.when(y == 1)(lambda: fill(1, 0))
+    blank = jnp.zeros((hd, own), BF16)
+    slope = hd ** -0.5 * LOG2E
+
+    def attend(h, carry):
+        at = pl.ds(pl.multiple_of(h * hd, hd), hd)
+        scores = mm(kv_ref[...], jnp.concatenate([q_ref[at, :], blank], axis=0))
+        allowed = lax.broadcasted_iota(jnp.int32, scores.shape, 0) <= lax.broadcasted_iota(jnp.int32, scores.shape, 1) + y * own
+        scores = jnp.where(allowed, scores * slope, -1e30)
+        top = jnp.max(scores, axis=0, keepdims=True)
+        prob = jnp.exp2(scores - top)
+        total = jnp.sum(prob, axis=0, keepdims=True)
+        lse_ref[pl.ds(h, 1), :] = top + jnp.log2(total)
+        ctx_ref[at, :] = mm(kvt_ref[hd:, :], (prob * (1.0 / total)).astype(BF16)).astype(BF16)
+        return carry
+
+    lax.fori_loop(0, heads, attend, 0)
+    x1_ref[...] += mm(ctx_ref[...], wo_ref[...], TA)
+
+    lax.fori_loop(4, shards, mlp, 0)
     f_ref[...] = norm_fwd(x1_ref[...], ln_ref[1:2, :])[0].astype(F32)
 
     def finish(k):
@@ -591,27 +603,28 @@
         b_copy(to, facing, b_c.at[1], tp, twin).wait_send()
 
 
-def front(rows, pick, extra, w_rows, wkv_t, ln, cos_t, sin_t, n_q, collective_id):
+def front(ids, embed, pick, extra, w_rows, wkv_t, ln, cos_t, sin_t, n_q, collective_id):
     own, width = extra.shape
     two_hd = wkv_t.shape[0]
     shards = 2 * NZ
     ff = (w_rows.shape[0] * shards - 2 * n_q) // 3
     dma = lambda *n: pltpu.SemaphoreType.DMA(n)
     s = jax.ShapeDtypeStruct
+    rows = (shards, ids.shape[0] // shards, width)
     return pl.pallas_call(
         front_kernel,
         out_shape=(s((own, width), F32),) * 3 + (s((n_q, own), BF16), s((2 * own, two_hd), BF16), s((two_hd, 2 * own), BF16),
                    s((2 * n_q // two_hd, own), F32), s((n_q, own), BF16), s((n_q, width), BF16), s((n_q, width), BF16))
         + (s((ff, width), BF16),) * 3,
-        in_specs=[VMEM] * 3 + [ANY] + [VMEM] * 4,
+        in_specs=[pl.BlockSpec(memory_space=pltpu.SMEM), ANY, VMEM, VMEM, ANY] + [VMEM] * 4,
         out_specs=(VMEM,) * 13,
-        scratch_shapes=[pltpu.VMEM((shards,) + w_rows.shape, F32), pltpu.VMEM(rows.shape, F32), pltpu.VMEM((own, width), BF16),
+        scratch_shapes=[pltpu.VMEM(embed.shape, F32), pltpu.VMEM(rows, F32), pltpu.VMEM((shards,) + w_rows.shape, F32), pltpu.VMEM(rows, F32), pltpu.VMEM((own, width), BF16),
                         pltpu.VMEM((two_hd, own), F32), pltpu.VMEM((two_hd, own), F32),
-                        dma(2), dma(shards), dma(shards)] + [dma(shards)] * 4 + [dma(shards, 2)]
+                        dma(3), dma(shards), dma(shards)] + [dma(shards)] * 4 + [dma(shards, 2)]
         + [dma(shards)] * 4 + [dma(2, shards), dma(shards, 4), pltpu.SemaphoreType.DMA, pltpu.SemaphoreType.DMA],
         compiler_params=pltpu.CompilerParams(collective_id=collective_id, has_side_effects=True, vmem_limit_bytes=60000000),
         name="front",
-    )(rows, pick, extra, w_rows, wkv_t, ln, cos_t, sin_t)
+    )(ids, embed, pick, extra, w_rows, wkv_t, ln, cos_t, sin_t)
 
 
 def layer_bwd_kernel(dfin_ref, x0_ref, x1_ref, loss_ref, ln_ref, cos_ref, sin_ref, wq_ref, wkv_ref, wo_ref, wg_ref, wu_ref, wd_ref,
@@ -984,7 +997,7 @@
     loss_ref = refs[42]
     held, made, in_sem, out_sem = refs[43:]
     vocab = t_ref.shape[0]
-    n_kv, hd = 2 * state[0][3].shape[2] // small_ref.shape[0], state[0][3].shape[2]
+    n_kv, hd = 2 * state[0][3].shape[1] // small_ref.shape[0], state[0][3].shape[1]
     blocks = [(at, min(UPDATE_ROWS, vocab - at)) for at in range(0, vocab, UPDATE_ROWS)]
 
     def loads(q):
@@ -1005,12 +1018,12 @@
         for i in range(3):
             new[i][index][where] = got[i]
 
-    n_q, n_f = state[0][2].shape[1], state[0][6].shape[0]
+    n_q, n_f = state[0][2].shape[0], state[0][6].shape[0]
     small_update(1, small_ref[0, n_kv:n_kv + 2, :], Ellipsis)
-    small_update(2, w_ref[0:n_q, :].T, Ellipsis)
-    kv = small_ref[:, 0:n_kv, :].reshape(2 * hd, small_ref.shape[2]).T
+    small_update(2, w_ref[0:n_q, :], Ellipsis)
+    kv = small_ref[:, 0:n_kv, :].reshape(2 * hd, small_ref.shape[2])
     for i in range(2):
-        small_update(3, kv[:, i * hd:(i + 1) * hd], i)
+        small_update(3, kv[i * hd:(i + 1) * hd], i)
     small_update(4, w_ref[n_q:2 * n_q, :], Ellipsis)
     for i in range(2):
         small_update(5, w_ref[2 * n_q + i * n_f:2 * n_q + (i + 1) * n_f, :].T, i)
@@ -1046,16 +1059,22 @@
 def update(g_table, g_shard, g_small, state_arrays):
     specs = [ANY] + [VMEM] * 6
     width = g_table.shape[1]
-    return pl.pallas_call(
+
+    def flip(arrays):
+        return [a.swapaxes(-1, -2) if i % 7 in (2, 3) else a for i, a in enumerate(arrays)]
+
+    given = flip(state_arrays)
+    *new, loss = pl.pallas_call(
         update_kernel,
-        out_shape=tuple(jax.ShapeDtypeStruct(a.shape, F32) for a in state_arrays) + (jax.ShapeDtypeStruct((1, 1), F32),),
+        out_shape=tuple(jax.ShapeDtypeStruct(a.shape, F32) for a in given) + (jax.ShapeDtypeStruct((1, 1), F32),),
         in_specs=[ANY, VMEM, VMEM] + specs * 3,
         out_specs=tuple(specs * 3) + (VMEM,),
         scratch_shapes=[pltpu.VMEM((3, 4, UPDATE_ROWS, width), F32), pltpu.VMEM((2, 3, UPDATE_ROWS, width), F32),
                         pltpu.SemaphoreType.DMA((3, 4)), pltpu.SemaphoreType.DMA((2, 3))],
         compiler_params=pltpu.CompilerParams(vmem_limit_bytes=60000000),
         name="update",
-    )(g_table, g_shard, g_small, *state_arrays)
+    )(g_table, g_shard, g_small, *given)
+    return flip(new) + [loss]
 
 
 def norm_fwd(x_f32, scale):
@@ -1121,15 +1140,15 @@
             here = (shard[:, None, :] == tp_rank) & (rank[:, None, :] == slots[None, :, None] + step * CAP)
             ids = jnp.sum(jnp.where(here, row[:, None, :], 0), axis=-1).reshape(-1)
             pick = (my_shard[:, None, None] == jnp.arange(n_tp)[None, :, None]) & (my_rank[:, None, None] == slots[None, None, :] + step * CAP)
-            return jnp.take(embed, ids, axis=0).reshape(n_tp, CAP, d_model), pick.reshape(own, n_tp * CAP).astype(BF16)
+            return ids, pick.reshape(own, n_tp * CAP).astype(BF16)
 
         def fetch_more(state):
-            rows_out, pick = fetch(state[0])
-            rows_in = plane_swap(rows_out, 1).reshape(n_tp * CAP, d_model).astype(BF16)
+            ids, pick = fetch(state[0])
+            rows_in = plane_swap(jnp.take(embed, ids, axis=0).reshape(n_tp, CAP, d_model), 1).reshape(n_tp * CAP, d_model).astype(BF16)
             return state[0] + 1, state[1] + dot('rc,cd->rd', pick, rows_in)
 
         more_rows = lax.while_loop(lambda state: state[0] < rounds, fetch_more, (jnp.int32(1), jnp.zeros((own, d_model), F32)))[1]
-        rows_first, pick_first = fetch(0)
+        ids_first, pick_first = fetch(0)
 
         w_rows = jnp.concatenate([w_q.T, w_o, w_gu.transpose(0, 2, 1).reshape(2 * f_loc, d_model), w_down], axis=0)
         cuts = (q_loc, 2 * q_loc, 2 * q_loc + f_loc, 2 * q_loc + 2 * f_loc)
@@ -1137,7 +1156,7 @@
         inv_freq = ROPE_BASE ** (-jnp.arange(0, head_dim, 2).astype(F32) / head_dim)
         angles = inv_freq[:, None] * (half * own + jnp.arange(own)).astype(F32)[None, :]
         cos_t, sin_t = jnp.cos(angles), jnp.sin(angles)
-        f_own, x_one, x_zero, *saved = front(rows_first, pick_first, more_rows, w_rows, wkv_t, ln_scales, cos_t, sin_t, n_tp * q_loc, 0)
+        f_own, x_one, x_zero, *saved = front(ids_first, embed, pick_first, more_rows, w_rows, wkv_t, ln_scales, cos_t, sin_t, n_tp * q_loc, 0)
         saved, (wq_t, wo_b, wg_t, wu_t, wd_b) = saved[:5], saved[5:]
         weights = (wq_t, wkv_t, wo_b, wg_t, wu_t, wd_b)
 

time: 680 us -> 650 us (0.956)
  local copies, waits for them, and re-layouts: 25.6 us -> 4.31 us
    unnamed x38 -> x12, local copies, waits for them, and re-layouts: 14.5 us -> 0.04 us
    pallas_call x1, Pallas kernels: 106 us -> 98.2 us  [front(): pl.pallas_call(front_kernel, out_shape=(s((own, width), F32),) * 3 + (s((...]
    gather x1 -> x0, local copies, waits for them, and re-layouts: 7.43 us -> none  [fetch(): jnp.take(embed, ids, axis=0).reshape(n_tp, CAP, d_model)]
where the time goes in v7:
time: 650 us; the launch traced here: 643 us
  Pallas kernels  627 us (96%)
  other arithmetic  8.56 us (1%)
    pallas_call x1, Pallas kernels, head(): pl.pallas_call(functools.partial(head_kernel, scale, token_scale), out_sh...  250 us
    pallas_call x1, Pallas kernels, tail(): pl.pallas_call(tail_kernel, out_shape=(jax.ShapeDtypeStruct((vocab, width...  183 us
    pallas_call x1, Pallas kernels, front(): pl.pallas_call(front_kernel, out_shape=(s((own, width), F32),) * 3 + (s((...  98.2 us
    pallas_call x1, Pallas kernels, layer_bwd(): pl.pallas_call(layer_bwd_kernel, out_shape=(jax.ShapeDtypeStruct((2 * NZ,...  59.1 us
    pallas_call x1, Pallas kernels, update(): pl.pallas_call(update_kernel, out_shape=tuple((jax.ShapeDtypeStruct(a.sha...  36.6 us

profile of v7, /device:TPU:0, one launch (start us, length us, event | category | flops | bytes accessed | tf_op | source)
XLA Modules:
  0.0 642.6 jit_solution(3986688994789021052)
XLA Ops:
  0.7 0.7 broadcast_subtract_fusion
  1.4 0.6 sub.38.lab_ref
  2.0 0.7 reshape.477
  2.8 0.2 convert_reduce_fusion
  3.0 0.6 reduce_max.9
  4.3 0.3 fusion.22
  4.6 0.0 copy-start
  4.7 0.3 fusion.20
  5.0 0.4 select_reduce_fusion.3
  5.4 0.7 select_n.143.ids_ref
  6.1 0.7 reshape.478.ids_ref
  6.8 1.0 multiply_sine_fusion
  7.7 1.6 bitcast_convert_fusion
  9.4 0.1 and_convert_fusion
  9.5 0.0 copy-start.3
  9.5 0.0 copy-start.4
  9.6 0.0 copy-start.5
  9.6 1.2 copy.50.pick_ref
  10.7 0.0 copy-done
  10.7 0.3 copy.49
  11.1 0.0 copy-done.3
  11.1 0.0 copy-done.4
  11.1 0.0 copy-done.5
  11.1 1.4 pad_maximum_fusion.w_ref
  12.5 0.1 broadcast_in_dim.123
  12.6 0.0 copy-start.1
  12.6 98.2 %front.1 = (f32[512,512]{1,0:T(8,128)}, f32[512,512]{1,0:T(8,128)}, f32[512,512]{1,0:T(8,128)}, bf16[512,512]{1,0:T(8,128)(2,1)}, bf16[1024,128]{1,0:T(8,128)(2,...) custom-call(s32[768]{0:T(1024)} %reshape.478.ids_ref, ...), custom_call_target="tpu_custom_call" | custom-call | tf_op jit(solution)/shard_map/front/pallas_call | solution.py:614
  110.8 0.0 copy-done.1
  110.8 250.1 %head.1 = (f32[512,512]{1,0:T(8,128)}, f32[6288,512]{1,0:T(8,128)}, f32[8,512]{1,0:T(8,128)}, f32[8,512]{1,0:T(8,128)}) custom-call(f32[512,512]{1,0:T(8,128)} %get-tuple-element.184.f_ref, s32[8,512]{1,0:T(8,128)} %sub.38.lab_ref, f32[6288,512]{1,0:T(8,128)} %get-tuple-element.524), custom_call_target="tpu_custom_call" | custom-call | flops 105495134208 | bytes 38633472 | tf_op jit(solution)/shard_map/head/pallas_call | solution.py:339
  360.9 0.7 reduce_sum.70
  361.6 1.3 fusion.28.loss_ref
  362.9 0.0 copy-start.2
  362.9 59.1 %layer_bwd.1 = (f32[8,928,512]{2,1,0:T(8,128)}, f32[512,512]{1,0:T(8,128)S(1)}, f32[8,96,512]{2,1,0:T(8,128)}) custom-call(f32[512,512]{1,0:T(8,128)} %get-tuple-element.186.dfin_ref, f32[512,512]{1,0:T(8,128)} %get-tuple-element.187.x0_ref, f32[512,512]{1,0:T(8,128)} %get-tuple-element.188.x1_ref, f32[1,512]{1,0:T(1,128)} %fusion.28.loss_ref, ...), custom_call_target="tpu_custom_call" | custom-call | tf_op jit(solution)/shard_map/layer_bwd/pallas_call | solution.py:762
  422.1 0.0 copy-done.2
  422.1 183.5 %tail.1 = (f32[6288,512]{1,0:T(8,128)}, f32[2,464,512]{2,1,0:T(8,128)}, f32[8,24,512]{2,1,0:T(8,128)}) custom-call(f32[6288,512]{1,0:T(8,128)} %get-tuple-element.202.g_ref, f32[8,2,464,512]{3,2,1,0:T(8,128)} %bitcast.51, f32[768,512]{1,0:T(8,128)} %bitcast.56, s32[1,768]{1,0:T(1,128)} %select_n.143.ids_ref), custom_call_target="tpu_custom_call" | custom-call | tf_op jit(solution)/shard_map/tail/pallas_call | solution.py:975
  605.6 36.6 %update.1 = (f32[6288,512]{1,0:T(8,128)}, f32[2,512]{1,0:T(2,128)}, f32[64,512]{1,0:T(8,128)}, f32[2,64,512]{2,1,0:T(8,128)}, f32[64,512]{1,0:T(8,128)}, /*index...) custom-call(f32[6288,512]{1,0:T(8,128)} %get-tuple-element.205.t_ref, ...), custom_call_target="tpu_custom_call" | custom-call | tf_op jit(solution)/shard_map/update/pallas_call | solution.py:1067
  (12 shorter events, 0.1 us)
Async XLA Ops:
  4.6 6.1 copy-start
  9.5 1.5 copy-start.3
  9.5 1.5 copy-start.4
  9.6 1.5 copy-start.5
  12.6 98.2 %copy-start.1 = (s32[8,512]{1,0:T(8,128)}, s32[8,512]{1,0:T(8,128)S(1)}, u32[]{:S(2)}) copy-start(s32[8,512]{1,0:T(8,128)S(1)} %get-tuple-element.527) | copy-start | bytes 49156
  362.9 59.1 %copy-start.2 = (s32[8,512]{1,0:T(8,128)S(1)}, s32[8,512]{1,0:T(8,128)}, u32[]{:S(2)}) copy-start(s32[8,512]{1,0:T(8,128)} %copy-done.1) | copy-start | bytes 49156

commit v8 on v7

--- a/solution.py
+++ b/solution.py
@@ -95,18 +95,17 @@
     )(x)
 
 
-FORWARD = {
-    0: {1: (("R", 1),), 3: (("R", 2),), 5: (("R", 3),)},
-    1: {1: (("L", 0), ("R", 2)), 3: (("R", 3),)},
-    2: {1: (("R", 3), ("L", 1)), 3: (("L", 0),)},
-    3: {1: (("L", 2),), 3: (("L", 1),), 5: (("L", 0),)},
+GATHER_ORDER = ((0, 0), (0, -1), (0, 1), (1, 0), (1, -1), (1, 1), (0, 2), (1, 2))
+GATHER_EVENTS = {
+    0: ((1, 0, 2, "lr"), (0, -1, 0, "ry"), (0, 1, 0, "y")),
+    1: ((1, 0, 3, "lr"), (0, -1, 1, "y"), (0, 1, 1, "ly"), (0, -1, 2, "r"), (0, 1, 2, ""), (0, 1, 3, "l"), (0, -1, 3, "")),
+    3: ((1, -1, 2, "r"), (1, 0, 0, ""), (1, 0, 1, "")),
+    4: ((0, 2, 0, "y"), (0, 2, 1, "y"), (1, 1, 3, "l"), (1, -1, 0, ""), (1, -1, 1, ""), (1, -1, 3, "")),
+    5: ((1, 1, 0, ""), (1, 1, 1, ""), (1, 1, 2, "")),
+    6: ((0, 2, 2, ""), (0, 2, 3, "")),
+    7: ((1, 2, 0, ""), (1, 2, 1, ""), (1, 2, 2, ""), (1, 2, 3, "")),
 }
-REDUCE = {
-    0: {2: (3,), 4: (2,), 6: (1,), 7: (0,)},
-    1: {4: (3,), 6: (2, 0), 7: (1,)},
-    2: {4: (0,), 6: (1, 3), 7: (2,)},
-    3: {2: (0,), 4: (1,), 6: (2,), 7: (3,)},
-}
+SCATTER_ORDER = ((1, 2), (1, -1), (1, 1), (0, 2), (1, 0), (0, -1), (0, 1), (0, 0))
 SUB = 256
 GROUP = 6
 
@@ -120,36 +119,51 @@
 
 
 def head_kernel(scale, token_scale, f_ref, lab_ref, e_ref, dfin_ref, ghead_ref, norm_ref, labsum_ref,
-                e_b, e_t, fbuf, f_b, g_acc, from_y, from_l, from_r, dl, lse_all, load_sem, ag_y, ag_l, ag_r, ag_recv,
-                rs_y, rs_l, rs_r, recv_y, recv_l, recv_r, st_send, st_recv):
+                e_b, e_t, fbuf, f_b, g_acc, from_y, from_l, from_r, dl, lse_all, load_sem, ag_send, ag_recv,
+                send_y, send_l, send_r, recv_y, recv_l, recv_r, st_send, st_recv):
     tp, dp, z, y = place()
     partner = tp + 1 - 2 * y
+    left = 2 * lax.rem(z + NZ - 1, NZ) + y
+    right = 2 * lax.rem(z + 1, NZ) + y
     vocab, width = e_ref.shape
     own = f_ref.shape[0]
+    quarter = own // 4
     whole = vocab // (SUB * GROUP)
     rest = vocab - whole * SUB * GROUP
-    log2e = 1.4426950408889634
-    slope = scale * log2e
+    slope = scale * LOG2E
     blocks = [(j * SUB, SUB) for j in range(GROUP)]
-    tail = [(n, min(SUB, rest - n)) for n in range(0, rest, SUB)]
+    tail_blocks = [(n, min(SUB, rest - n)) for n in range(0, rest, SUB)]
 
     plane_barrier(tp, dp, [])
 
-    def send(src, slot, sems, to):
-        remote(src, fbuf.at[slot], sems.at[slot], ag_recv.at[slot], to, dp).start()
-
-    def arrived(slot):
-        remote(f_ref, fbuf.at[slot], ag_y.at[slot], ag_recv.at[slot], partner, dp).wait_recv()
-
-    def first_sends(k):
-        if k > 0:
-            send(f_ref, tp, ag_l, tp - 2)
-        if k < NZ - 1:
-            send(f_ref, tp, ag_r, tp + 2)
-        send(f_ref, tp, ag_y, partner)
-
-    for k in range(NZ):
-        pl.when(z == k)(functools.partial(first_sends, k))
+    def slot_of(o, d):
+        return 2 * lax.rem(z + d + NZ, NZ) + y + o - 2 * y * o
+
+    def slot_at(order, step):
+        o = jnp.int32(0)
+        d = jnp.int32(0)
+        for s in range(2 * NZ):
+            o = o + jnp.where(step == s, order[s][0], 0)
+            d = d + jnp.where(step == s, order[s][1], 0)
+        return slot_of(o, d)
+
+    def piece(ref, q):
+        return ref.at[pl.ds(q * quarter, quarter), :]
+
+    def pass_on(o, d, q, to):
+        slot = slot_of(o, d)
+        src = piece(f_ref if (o, d) == (0, 0) else fbuf.at[slot], q)
+        return remote(src, piece(fbuf.at[slot], q), ag_send.at["lry".index(to), slot, q], ag_recv.at[slot, q],
+                      {"l": left, "r": right, "y": partner}[to], dp)
+
+    def arrived(o, d, q):
+        slot = slot_of(o, d)
+        remote(piece(f_ref, q), piece(fbuf.at[slot], q), ag_send.at[0, slot, q], ag_recv.at[slot, q], partner, dp).wait_recv()
+
+    for q in range(4):
+        pass_on(0, 0, q, "l").start()
+        pass_on(0, 0, q, "r").start()
+        pass_on(0, 0, (q + 2) % 4, "y").start()
     load = pltpu.make_async_copy(e_ref, g_acc, load_sem.at[0])
     load.start()
     own_copy = pltpu.make_async_copy(f_ref, fbuf.at[tp], load_sem.at[1])
@@ -174,31 +188,17 @@
         def body(n, c):
             return group(pl.multiple_of(n * SUB * GROUP, SUB * GROUP), blocks, c)
         carry = lax.fori_loop(0, whole, body, carry)
-        return group(whole * SUB * GROUP, tail, carry) if tail else carry
-
-    order1 = {k: (k,) + tuple(v for pair in zip([a[1] for a in ARRIVALS[k]], [k] + [a[1] for a in ARRIVALS[k]]) for v in pair) + (ARRIVALS[k][-1][1],) for k in range(NZ)}
-    order1 = {k: [2 * zz + (s % 2 == 0 and s > 0 or s == 7) for s, zz in enumerate(order1[k])] for k in range(NZ)}
-
-    def chunk_of(table, step):
-        code = lookup(table, z, step)
-        other = code % 2
-        return code // 2 * 2 + y + other - 2 * y * other
+        return group(whole * SUB * GROUP, tail_blocks, carry) if tail_blocks else carry
 
     def gather_step(step, carry):
-        slot = chunk_of(order1, step)
-        for k in range(NZ):
-            for s, shards in FORWARD[k].items():
-                def pass_on(k=k, shards=shards):
-                    for side, zz in shards:
-                        at = 2 * zz + y
-                        arrived(at)
-                        if side == "L" and k < NZ - 1:
-                            send(fbuf.at[at], at, ag_r, tp + 2)
-                        if side == "R" and k > 0:
-                            send(fbuf.at[at], at, ag_l, tp - 2)
-                        send(fbuf.at[at], at, ag_y, partner)
-                pl.when((z == k) & (step == s))(pass_on)
-        pl.when(slot % 2 != y)(lambda: arrived(slot))
+        for s, events in GATHER_EVENTS.items():
+            def serve(events=events):
+                for o, d, q, to in events:
+                    arrived(o, d, q)
+                    for t in to:
+                        pass_on(o, d, q, t).start()
+            pl.when(step == s)(serve)
+        slot = slot_at(GATHER_ORDER, step)
         f_b[slot] = fbuf[slot].astype(BF16)
         f_now = f_b[slot]
 
@@ -223,25 +223,13 @@
     for n in range(1, 2 * NZ):
         to = lax.rem(tp + n, 2 * NZ)
         remote(lse_all.at[tp], lse_all.at[tp], st_send.at[to], st_recv.at[tp], to, dp).start()
-
-    def gathers_done(k):
-        def done(sems, slot):
-            remote(f_ref, fbuf.at[slot], sems.at[slot], ag_recv.at[slot], partner, dp).wait_send()
-        if k > 0:
-            done(ag_l, tp)
-        if k < NZ - 1:
-            done(ag_r, tp)
-        done(ag_y, tp)
-        for side, zz in ARRIVALS[k]:
-            at = 2 * zz + y
-            if side == "L" and k < NZ - 1:
-                done(ag_r, at)
-            if side == "R" and k > 0:
-                done(ag_l, at)
-            done(ag_y, at)
-
-    for k in range(NZ):
-        pl.when(z == k)(functools.partial(gathers_done, k))
+    for q in range(4):
+        for to in "lry":
+            pass_on(0, 0, q, to).wait_send()
+    for events in GATHER_EVENTS.values():
+        for o, d, q, to in events:
+            for t in to:
+                pass_on(o, d, q, t).wait_send()
 
     def clear(n, carry):
         g_acc[pl.ds(pl.multiple_of(n * 16, 16), 16), :] = jnp.zeros((16, width), F32)
@@ -255,14 +243,61 @@
     log_norm = peak + jnp.log(jnp.sum(jnp.exp(lse_all[...] - peak[None]), axis=0))
     norm_ref[...] = log_norm
 
-    order2 = {k: [2 * zz + 1 - s for zz in REDUCE_ORDER[k] for s in range(2)] for k in range(NZ)}
+    def part(o, d, q):
+        return piece(fbuf.at[slot_of(o, d)], q)
+
+    def to_y(d, q):
+        return remote(part(1, d, q), from_y.at[d % 4, q], send_y.at[d % 4, q], recv_y.at[d % 4, q], partner, dp)
+
+    def to_left(o, d, q):
+        rel = 1 if d == 2 else 0
+        return remote(part(o, d, q), from_r.at[o, rel, q], send_l.at[o, rel, q], recv_r.at[o, rel, q], left, dp)
+
+    def to_right(o, d, q):
+        rel = 1 if d == 2 else 0
+        return remote(part(o, d, q), from_l.at[o, rel, q], send_r.at[o, rel, q], recv_l.at[o, rel, q], right, dp)
+
+    def add(o, d, q, buf, sem):
+        remote(part(o, d, q), buf, send_y.at[0, 0], sem, partner, dp).wait_recv()
+        add_into(part(o, d, q), buf)
+
+    def add_y(d, q):
+        add(0, d, q, from_y.at[d % 4, q], recv_y.at[d % 4, q])
+
+    def add_r(o, rel, q):
+        add(o, -rel, q, from_r.at[o, rel, q], recv_r.at[o, rel, q])
+
+    def add_l(o, rel, q):
+        add(o, rel, q, from_l.at[o, rel, q], recv_l.at[o, rel, q])
+
+    def needs(o, d):
+        if (o, d) == (0, 2):
+            return [(add_y, 2, 0), (add_y, 2, 1)]
+        if d == -1:
+            return ([(add_y, -1, 0), (add_y, -1, 1), (add_r, 0, 1, 0)] if o == 0 else []) + [(add_r, o, 1, 2)]
+        if d == 1:
+            return ([(add_y, 1, 0), (add_y, 1, 1), (add_l, 0, 1, 1)] if o == 0 else []) + [(add_l, o, 1, 3)]
+        if (o, d) == (1, 0):
+            return [(f, 1, 0, q) for q in (2, 3) for f in (add_r, add_l)]
+        if (o, d) == (0, 0):
+            return [(add_y, 0, q) for q in range(4)] + [(f, 0, 0, q) for f in (add_r, add_l) for q in range(4)]
+        return []
+
+    def leaves(o, d):
+        if d == 2:
+            first = [to_y(2, 0), to_y(2, 1)] if o == 1 else [to_left(0, 2, 0), to_right(0, 2, 1)]
+            return first + [to_left(o, 2, 2), to_right(o, 2, 3)]
+        if d in (-1, 1):
+            along = to_left if d == -1 else to_right
+            return [to_y(d, 0), to_y(d, 1)] + [along(1, d, 2), along(1, d, 3)] if o == 1 else [along(0, d, q) for q in range(4)]
+        return [to_y(0, q) for q in range(4)] if o == 1 else []
 
     def scatter_step(step, lab_sum):
-        slot = chunk_of(order2, step)
+        slot = slot_at(SCATTER_ORDER, step)
         f_now = f_b[slot]
         acc = fbuf.at[slot]
         norm = norm_ref[pl.ds(slot, 1), :]
-        shift = norm * log2e
+        shift = norm * LOG2E
         coef = (1.0 + 2.0 * LOGIT_ZLOSS * norm) * token_scale
         lab = lab_ref[pl.ds(slot, 1), :]
         acc[...] = jnp.zeros((width, own), F32)
@@ -282,29 +317,13 @@
             return hits
 
         lab_sum = over_blocks(group, lab_sum)
-
-        def hand_over():
-            remote(acc, from_y.at[slot // 2], rs_y.at[slot // 2], recv_y.at[slot // 2], partner, dp).start()
-        pl.when(slot % 2 != y)(hand_over)
-
-        for k in range(NZ):
-            for s, shards in REDUCE[k].items():
-                def reduce(k=k, shards=shards):
-                    for zz in shards:
-                        line = fbuf.at[2 * zz + y]
-                        remote(line, from_y.at[zz], rs_y.at[zz], recv_y.at[zz], partner, dp).wait_recv()
-                        add_into(line, from_y.at[zz])
-                        if zz >= k and k > 0:
-                            remote(line, from_l.at[zz - 1], rs_l.at[zz], recv_l.at[zz], partner, dp).wait_recv()
-                            add_into(line, from_l.at[zz - 1])
-                        if zz <= k and k < NZ - 1:
-                            remote(line, from_r.at[zz], rs_r.at[zz], recv_r.at[zz], partner, dp).wait_recv()
-                            add_into(line, from_r.at[zz])
-                        if zz > k:
-                            remote(line, from_l.at[zz - 1], rs_r.at[zz], recv_l.at[zz], tp + 2, dp).start()
-                        if zz < k:
-                            remote(line, from_r.at[zz], rs_l.at[zz], recv_r.at[zz], tp - 2, dp).start()
-                pl.when((z == k) & (step == s))(reduce)
+        for s, (o, d) in enumerate(SCATTER_ORDER):
+            def reduce(o=o, d=d):
+                for f, *args in needs(o, d):
+                    f(*args)
+                for c in leaves(o, d):
+                    c.start()
+            pl.when(step == s)(reduce)
         return lab_sum
 
     lab_sum = lax.fori_loop(0, 2 * NZ, scatter_step, jnp.zeros((8, own), F32))
@@ -312,18 +331,9 @@
     store = pltpu.make_async_copy(g_acc, ghead_ref, load_sem.at[0])
     store.start()
     dfin_ref[...] = fbuf[tp].T
-
-    def scatters_done(k):
-        for zz in range(NZ):
-            line = fbuf.at[2 * zz + y]
-            remote(line, from_y.at[zz], rs_y.at[zz], recv_y.at[zz], partner, dp).wait_send()
-            if zz > k:
-                remote(line, from_l.at[zz - 1], rs_r.at[zz], recv_l.at[zz], partner, dp).wait_send()
-            if zz < k:
-                remote(line, from_r.at[zz], rs_l.at[zz], recv_r.at[zz], partner, dp).wait_send()
-
-    for k in range(NZ):
-        pl.when(z == k)(functools.partial(scatters_done, k))
+    for o, d in SCATTER_ORDER:
+        for c in leaves(o, d):
+            c.wait_send()
     for n in range(1, 2 * NZ):
         to = lax.rem(tp + n, 2 * NZ)
         remote(lse_all.at[tp], lse_all.at[tp], st_send.at[to], st_recv.at[tp], to, dp).wait_send()
@@ -334,8 +344,8 @@
     own, width = f_own.shape
     vocab = embed.shape[0]
     chunk = (own, width)
-    dma8 = pltpu.SemaphoreType.DMA((2 * NZ,))
-    dma4 = pltpu.SemaphoreType.DMA((NZ,))
+    strip = (own // 4, width)
+    dma = lambda *n: pltpu.SemaphoreType.DMA(n)
     return pl.pallas_call(
         functools.partial(head_kernel, scale, token_scale),
         out_shape=(jax.ShapeDtypeStruct((own, width), F32), jax.ShapeDtypeStruct((vocab, width), F32),
@@ -344,9 +354,10 @@
         out_specs=(VMEM, ANY, VMEM, VMEM),
         scratch_shapes=[pltpu.VMEM((vocab, width), BF16), pltpu.VMEM((width, vocab), BF16),
                         pltpu.VMEM((2 * NZ,) + chunk, F32), pltpu.VMEM((2 * NZ,) + chunk, BF16), pltpu.VMEM((vocab, width), F32),
-                        pltpu.VMEM((NZ,) + chunk, F32), pltpu.VMEM((NZ - 1,) + chunk, F32), pltpu.VMEM((NZ - 1,) + chunk, F32),
+                        pltpu.VMEM((NZ, 4) + strip, F32), pltpu.VMEM((2, 2, 4) + strip, F32), pltpu.VMEM((2, 2, 4) + strip, F32),
                         pltpu.VMEM((SUB * GROUP, own), BF16), pltpu.VMEM((2 * NZ, 2 * NZ, own), F32),
-                        pltpu.SemaphoreType.DMA((2,)), dma8, dma8, dma8, dma8, dma4, dma4, dma4, dma4, dma4, dma4, dma8, dma8],
+                        dma(2), dma(3, 2 * NZ, 4), dma(2 * NZ, 4), dma(NZ, 4), dma(2, 2, 4), dma(2, 2, 4), dma(NZ, 4), dma(2, 2, 4), dma(2, 2, 4),
+                        dma(2 * NZ), dma(2 * NZ)],
         compiler_params=pltpu.CompilerParams(collective_id=collective_id, has_side_effects=True, vmem_limit_bytes=67000000),
         cost_estimate=pl.CostEstimate(flops=8 * vocab * width * own * 8, bytes_accessed=3 * 4 * vocab * width, transcendentals=2 * vocab * own * 8),
         name="head",

time: 650 us -> 673 us (1.035)
  Pallas kernels: 627 us -> 651 us
    pallas_call x1, Pallas kernels: 250 us -> 269 us  [head(): pl.pallas_call(functools.partial(head_kernel, scale, token_scale), out_sh...]
where the time goes in v8:
time: 673 us; the launch traced here: 666 us
  Pallas kernels  651 us (97%)
  other arithmetic  8.56 us (1%)
    pallas_call x1, Pallas kernels, head(): pl.pallas_call(functools.partial(head_kernel, scale, token_scale), out_sh...  269 us
    pallas_call x1, Pallas kernels, tail(): pl.pallas_call(tail_kernel, out_shape=(jax.ShapeDtypeStruct((vocab, width...  185 us
    pallas_call x1, Pallas kernels, front(): pl.pallas_call(front_kernel, out_shape=(s((own, width), F32),) * 3 + (s((...  98.2 us
    pallas_call x1, Pallas kernels, layer_bwd(): pl.pallas_call(layer_bwd_kernel, out_shape=(jax.ShapeDtypeStruct((2 * NZ,...  61.6 us
    pallas_call x1, Pallas kernels, update(): pl.pallas_call(update_kernel, out_shape=tuple((jax.ShapeDtypeStruct(a.sha...  36.6 us

profile of v8, /device:TPU:0, one launch (start us, length us, event | category | flops | bytes accessed | tf_op | source)
XLA Modules:
  0.0 666.1 jit_solution(3968961990509671469)
XLA Ops:
  0.7 0.7 broadcast_subtract_fusion
  1.4 0.6 sub.38.lab_ref
  2.0 0.7 reshape.477
  2.8 0.2 convert_reduce_fusion
  3.0 0.6 reduce_max.9
  4.3 0.3 fusion.22
  4.6 0.0 copy-start
  4.7 0.3 fusion.20
  5.0 0.4 select_reduce_fusion.3
  5.4 0.7 select_n.143.ids_ref
  6.1 0.7 reshape.478.ids_ref
  6.8 1.0 multiply_sine_fusion
  7.7 1.6 bitcast_convert_fusion
  9.4 0.1 and_convert_fusion
  9.5 0.0 copy-start.3
  9.5 0.0 copy-start.4
  9.6 0.0 copy-start.5
  9.6 1.2 copy.50.pick_ref
  10.7 0.0 copy-done
  10.7 0.3 copy.49
  11.1 0.0 copy-done.3
  11.1 0.0 copy-done.4
  11.1 0.0 copy-done.5
  11.1 1.4 pad_maximum_fusion.w_ref
  12.5 0.1 broadcast_in_dim.123
  12.6 0.0 copy-start.1
  12.6 98.2 %front.1 = (f32[512,512]{1,0:T(8,128)}, f32[512,512]{1,0:T(8,128)}, f32[512,512]{1,0:T(8,128)}, bf16[512,512]{1,0:T(8,128)(2,1)}, bf16[1024,128]{1,0:T(8,128)(2,...) custom-call(s32[768]{0:T(1024)} %reshape.478.ids_ref, ...), custom_call_target="tpu_custom_call" | custom-call | tf_op jit(solution)/shard_map/front/pallas_call | solution.py:625
  110.8 0.0 copy-done.1
  110.8 269.2 %head.1 = (f32[512,512]{1,0:T(8,128)}, f32[6288,512]{1,0:T(8,128)}, f32[8,512]{1,0:T(8,128)}, f32[8,512]{1,0:T(8,128)}) custom-call(f32[512,512]{1,0:T(8,128)} %get-tuple-element.184.f_ref, s32[8,512]{1,0:T(8,128)} %sub.38.lab_ref, f32[6288,512]{1,0:T(8,128)} %get-tuple-element.524), custom_call_target="tpu_custom_call" | custom-call | flops 105495134208 | bytes 38633472 | tf_op jit(solution)/shard_map/head/pallas_call | solution.py:349
  380.0 0.7 reduce_sum.70
  380.7 1.3 fusion.28.loss_ref
  382.0 0.0 copy-start.2
  382.0 61.6 %layer_bwd.1 = (f32[8,928,512]{2,1,0:T(8,128)}, f32[512,512]{1,0:T(8,128)S(1)}, f32[8,96,512]{2,1,0:T(8,128)}) custom-call(f32[512,512]{1,0:T(8,128)} %get-tuple-element.186.dfin_ref, f32[512,512]{1,0:T(8,128)} %get-tuple-element.187.x0_ref, f32[512,512]{1,0:T(8,128)} %get-tuple-element.188.x1_ref, f32[1,512]{1,0:T(1,128)} %fusion.28.loss_ref, ...), custom_call_target="tpu_custom_call" | custom-call | tf_op jit(solution)/shard_map/layer_bwd/pallas_call | solution.py:773
  443.7 0.0 copy-done.2
  443.7 0.3 while.23
  444.0 185.0 %tail.1 = (f32[6288,512]{1,0:T(8,128)}, f32[2,464,512]{2,1,0:T(8,128)}, f32[8,24,512]{2,1,0:T(8,128)}) custom-call(f32[6288,512]{1,0:T(8,128)} %get-tuple-element.202.g_ref, f32[8,2,464,512]{3,2,1,0:T(8,128)} %bitcast.51, f32[768,512]{1,0:T(8,128)} %bitcast.56, s32[1,768]{1,0:T(1,128)} %select_n.143.ids_ref), custom_call_target="tpu_custom_call" | custom-call | tf_op jit(solution)/shard_map/tail/pallas_call | solution.py:986
  629.0 36.6 %update.1 = (f32[6288,512]{1,0:T(8,128)}, f32[2,512]{1,0:T(2,128)}, f32[64,512]{1,0:T(8,128)}, f32[2,64,512]{2,1,0:T(8,128)}, f32[64,512]{1,0:T(8,128)}, /*index...) custom-call(f32[6288,512]{1,0:T(8,128)} %get-tuple-element.205.t_ref, ...), custom_call_target="tpu_custom_call" | custom-call | tf_op jit(solution)/shard_map/update/pallas_call | solution.py:1078
  (11 shorter events, 0.1 us)
Async XLA Ops:
  4.6 6.1 copy-start
  9.5 1.5 copy-start.3
  9.5 1.5 copy-start.4
  9.6 1.5 copy-start.5
  12.6 98.2 %copy-start.1 = (s32[8,512]{1,0:T(8,128)}, s32[8,512]{1,0:T(8,128)S(1)}, u32[]{:S(2)}) copy-start(s32[8,512]{1,0:T(8,128)S(1)} %get-tuple-element.527) | copy-start | bytes 49156
  382.0 61.6 %copy-start.2 = (s32[8,512]{1,0:T(8,128)S(1)}, s32[8,512]{1,0:T(8,128)}, u32[]{:S(2)}) copy-start(s32[8,512]{1,0:T(8,128)} %copy-done.1) | copy-start | bytes 49156

commit v9 on v7

--- a/solution.py
+++ b/solution.py
@@ -95,17 +95,83 @@
     )(x)
 
 
-FORWARD = {
-    0: {1: (("R", 1),), 3: (("R", 2),), 5: (("R", 3),)},
-    1: {1: (("L", 0), ("R", 2)), 3: (("R", 3),)},
-    2: {1: (("R", 3), ("L", 1)), 3: (("L", 0),)},
-    3: {1: (("L", 2),), 3: (("L", 1),), 5: (("L", 0),)},
+GATHER_ORDER = {
+    0: ((0, 0), (0, 1), (1, 0), (0, 2), (1, 1), (0, 3), (1, 2), (1, 3)),
+    1: ((0, 1), (0, 0), (0, 2), (1, 1), (1, 0), (0, 3), (1, 2), (1, 3)),
+    2: ((0, 2), (0, 1), (0, 3), (1, 2), (0, 0), (1, 3), (1, 1), (1, 0)),
+    3: ((0, 3), (0, 2), (1, 3), (0, 1), (1, 2), (0, 0), (1, 1), (1, 0)),
 }
-REDUCE = {
-    0: {2: (3,), 4: (2,), 6: (1,), 7: (0,)},
-    1: {4: (3,), 6: (2, 0), 7: (1,)},
-    2: {4: (0,), 6: (1, 3), 7: (2,)},
-    3: {2: (0,), 4: (1,), 6: (2,), 7: (3,)},
+GATHER_EVENTS = {
+    0: {
+        1: ((0, 1, 0, 'y'), (1, 0, 1, 'r'), (0, 1, 1, 'y'), (1, 0, 0, '')),
+        3: ((0, 2, 0, 'y'), (1, 1, 0, ''), (0, 2, 1, 'y'), (1, 1, 1, '')),
+        5: ((0, 3, 0, 'y'), (1, 2, 0, ''), (0, 3, 1, ''), (1, 2, 1, '')),
+        7: ((1, 3, 0, ''), (1, 3, 1, '')),
+    },
+    1: {
+        1: ((0, 0, 0, 'ry'), (0, 2, 0, 'ly'), (1, 1, 0, ''), (0, 0, 1, 'r'), (0, 2, 1, 'ly'), (1, 1, 1, '')),
+        4: ((0, 3, 0, 'ly'), (1, 0, 0, ''), (1, 0, 1, 'r')),
+        5: ((0, 3, 1, 'l'), (1, 2, 0, '')),
+        6: ((1, 2, 1, ''), (1, 3, 1, 'l')),
+        7: ((1, 3, 0, ''),),
+    },
+    2: {
+        1: ((0, 1, 0, 'ry'), (0, 3, 0, 'ly'), (1, 2, 0, ''), (0, 1, 1, 'ry'), (0, 3, 1, 'l'), (1, 2, 1, '')),
+        4: ((0, 0, 0, 'ry'), (1, 1, 0, ''), (1, 3, 1, 'l'), (0, 0, 1, 'r'), (1, 3, 0, '')),
+        6: ((1, 0, 1, 'r'), (1, 1, 1, '')),
+        7: ((1, 0, 0, ''),),
+    },
+    3: {
+        1: ((0, 2, 0, 'y'), (1, 3, 1, 'l'), (0, 2, 1, 'y'), (1, 3, 0, '')),
+        3: ((0, 1, 0, 'y'), (1, 2, 0, ''), (0, 1, 1, 'y'), (1, 2, 1, '')),
+        5: ((0, 0, 0, 'y'), (1, 1, 0, ''), (0, 0, 1, ''), (1, 1, 1, '')),
+        7: ((1, 0, 0, ''), (1, 0, 1, '')),
+    },
+}
+SCATTER_ORDER = {
+    0: ((1, 3), (1, 2), (0, 3), (1, 1), (0, 2), (1, 0), (0, 1), (0, 0)),
+    1: ((1, 3), (1, 2), (0, 3), (1, 0), (1, 1), (0, 2), (0, 0), (0, 1)),
+    2: ((1, 0), (1, 1), (1, 3), (0, 0), (1, 2), (0, 3), (0, 1), (0, 2)),
+    3: ((1, 0), (1, 1), (0, 0), (1, 2), (0, 1), (1, 3), (0, 2), (0, 3)),
+}
+SCATTER_EVENTS = {
+    0: {
+        0: ((1, 3, 0, '', 'y'), (1, 3, 1, '', 'r')),
+        1: ((1, 2, 0, '', 'y'), (1, 2, 1, '', 'y')),
+        2: ((0, 3, 1, '', 'r'), (0, 3, 0, 'y', 'r')),
+        3: ((1, 1, 0, '', 'y'), (1, 1, 1, '', 'y')),
+        4: ((0, 2, 0, 'y', 'r'),),
+        5: ((0, 2, 1, 'y', 'r'), (1, 0, 0, '', 'y')),
+        6: ((1, 0, 1, 'r', 'y'), (0, 1, 0, 'y', 'r')),
+        7: ((0, 1, 1, 'y', 'r'), (0, 0, 0, 'ry', ''), (0, 0, 1, 'ry', '')),
+    },
+    1: {
+        0: ((1, 3, 0, '', 'y'),),
+        1: ((1, 2, 0, '', 'y'), (1, 2, 1, '', 'y')),
+        2: ((1, 3, 1, 'l', 'r'),),
+        3: ((1, 0, 0, '', 'y'),),
+        4: ((0, 3, 1, 'l', 'r'), (1, 0, 1, 'r', 'l'), (1, 1, 0, '', 'y'), (1, 1, 1, '', 'y')),
+        6: ((0, 3, 0, 'ly', 'r'), (0, 0, 1, 'r', 'l')),
+        7: ((0, 2, 0, 'ly', 'r'), (0, 0, 0, 'ry', 'l'), (0, 2, 1, 'ly', 'r'), (0, 1, 0, 'lry', ''), (0, 1, 1, 'lry', '')),
+    },
+    2: {
+        0: ((1, 0, 0, '', 'y'),),
+        1: ((1, 1, 0, '', 'y'), (1, 1, 1, '', 'y')),
+        2: ((1, 0, 1, 'r', 'l'), (1, 3, 0, '', 'y')),
+        4: ((1, 3, 1, 'l', 'r'), (0, 0, 1, 'r', 'l'), (1, 2, 0, '', 'y'), (1, 2, 1, '', 'y')),
+        6: ((0, 0, 0, 'ry', 'l'), (0, 3, 1, 'l', 'r')),
+        7: ((0, 1, 0, 'ry', 'l'), (0, 3, 0, 'ly', 'r'), (0, 1, 1, 'ry', 'l'), (0, 2, 0, 'lry', ''), (0, 2, 1, 'lry', '')),
+    },
+    3: {
+        0: ((1, 0, 0, '', 'y'), (1, 0, 1, '', 'l')),
+        1: ((1, 1, 0, '', 'y'), (1, 1, 1, '', 'y')),
+        2: ((0, 0, 1, '', 'l'), (0, 0, 0, 'y', 'l')),
+        3: ((1, 2, 0, '', 'y'), (1, 2, 1, '', 'y')),
+        4: ((0, 1, 0, 'y', 'l'),),
+        5: ((0, 1, 1, 'y', 'l'), (1, 3, 0, '', 'y')),
+        6: ((1, 3, 1, 'l', 'y'), (0, 2, 0, 'y', 'l')),
+        7: ((0, 2, 1, 'y', 'l'), (0, 3, 0, 'ly', ''), (0, 3, 1, 'ly', '')),
+    },
 }
 SUB = 256
 GROUP = 6
@@ -119,9 +185,9 @@
     return value
 
 
-def head_kernel(scale, token_scale, f_ref, lab_ref, e_ref, dfin_ref, ghead_ref, norm_ref, labsum_ref,
-                e_b, e_t, fbuf, f_b, g_acc, from_y, from_l, from_r, dl, lse_all, load_sem, ag_y, ag_l, ag_r, ag_recv,
-                rs_y, rs_l, rs_r, recv_y, recv_l, recv_r, st_send, st_recv):
+def head_kernel(scale, token_scale, f_ref, lab_ref, e_ref, dfin_ref, ghead_ref, norm_ref, labsum_ref, z_ref,
+                e_b, e_t, fbuf, f_b, g_acc, from_y, from_l, from_r, dl, z_buf, z_rest, lse_all, z_sem, load_sem, ag_send, ag_recv,
+                send_y, send_l, send_r, recv_y, recv_l, recv_r, st_send, st_recv):
     tp, dp, z, y = place()
     partner = tp + 1 - 2 * y
     vocab, width = e_ref.shape
@@ -135,21 +201,38 @@
 
     plane_barrier(tp, dp, [])
 
-    def send(src, slot, sems, to):
-        remote(src, fbuf.at[slot], sems.at[slot], ag_recv.at[slot], to, dp).start()
-
-    def arrived(slot):
-        remote(f_ref, fbuf.at[slot], ag_y.at[slot], ag_recv.at[slot], partner, dp).wait_recv()
+    half = own // 2
+    to_tp = {"l": tp - 2, "r": tp + 2, "y": partner}
+
+    def slot_of(o, zz):
+        return 2 * zz + (1 - y if o else y)
+
+    def piece(ref, h):
+        return ref.at[pl.ds(h * half, half), :]
+
+    def pass_on(o, zz, h, to, own_chunk=False):
+        slot = slot_of(o, zz)
+        return remote(piece(f_ref if own_chunk else fbuf.at[slot], h), piece(fbuf.at[slot], h), ag_send.at["lry".index(to), slot, h],
+                      ag_recv.at[slot, h], to_tp[to], dp)
+
+    def arrived(o, zz, h):
+        slot = slot_of(o, zz)
+        remote(piece(f_ref, h), piece(fbuf.at[slot], h), ag_send.at[0, slot, h], ag_recv.at[slot, h], partner, dp).wait_recv()
+
+    def own_sends(k):
+        first = (1, 0) if k in (0, NZ - 1) else (0, 1)
+        return [pass_on(0, k, h, "y", True) for h in first] + [
+            pass_on(0, k, h, to, True) for h in range(2) for to in ("l" if k > 0 else "") + ("r" if k < NZ - 1 else "")]
+
+    def on_position(f):
+        for k in range(NZ):
+            pl.when(z == k)(functools.partial(f, k))
 
     def first_sends(k):
-        if k > 0:
-            send(f_ref, tp, ag_l, tp - 2)
-        if k < NZ - 1:
-            send(f_ref, tp, ag_r, tp + 2)
-        send(f_ref, tp, ag_y, partner)
-
-    for k in range(NZ):
-        pl.when(z == k)(functools.partial(first_sends, k))
+        for c in own_sends(k):
+            c.start()
+
+    on_position(first_sends)
     load = pltpu.make_async_copy(e_ref, g_acc, load_sem.at[0])
     load.start()
     own_copy = pltpu.make_async_copy(f_ref, fbuf.at[tp], load_sem.at[1])
@@ -170,78 +253,90 @@
         prepare(pl.ds(vocab // SUB * SUB, vocab % SUB), vocab % SUB)
     own_copy.wait()
 
-    def over_blocks(group, carry):
-        def body(n, c):
-            return group(pl.multiple_of(n * SUB * GROUP, SUB * GROUP), blocks, c)
-        carry = lax.fori_loop(0, whole, body, carry)
-        return group(whole * SUB * GROUP, tail, carry) if tail else carry
-
-    order1 = {k: (k,) + tuple(v for pair in zip([a[1] for a in ARRIVALS[k]], [k] + [a[1] for a in ARRIVALS[k]]) for v in pair) + (ARRIVALS[k][-1][1],) for k in range(NZ)}
-    order1 = {k: [2 * zz + (s % 2 == 0 and s > 0 or s == 7) for s, zz in enumerate(order1[k])] for k in range(NZ)}
-
-    def chunk_of(table, step):
-        code = lookup(table, z, step)
+    big = SUB * GROUP
+
+    def z_copies(slot, n, out):
+        if n is None:
+            pair = (z_rest, z_ref.at[slot, pl.ds(whole * big, rest), :])
+            sem = z_sem.at[2]
+        else:
+            pair = (z_buf.at[lax.rem(n, 2)], z_ref.at[slot, pl.ds(pl.multiple_of(n * big, big), big), :])
+            sem = z_sem.at[lax.rem(n, 2)]
+        return pltpu.make_async_copy(*(pair if out else pair[::-1]), sem)
+
+    def slot_at(order, step):
+        code = lookup({k: [2 * zz + o for o, zz in order[k]] for k in range(NZ)}, z, step)
         other = code % 2
         return code // 2 * 2 + y + other - 2 * y * other
 
     def gather_step(step, carry):
-        slot = chunk_of(order1, step)
         for k in range(NZ):
-            for s, shards in FORWARD[k].items():
-                def pass_on(k=k, shards=shards):
-                    for side, zz in shards:
-                        at = 2 * zz + y
-                        arrived(at)
-                        if side == "L" and k < NZ - 1:
-                            send(fbuf.at[at], at, ag_r, tp + 2)
-                        if side == "R" and k > 0:
-                            send(fbuf.at[at], at, ag_l, tp - 2)
-                        send(fbuf.at[at], at, ag_y, partner)
-                pl.when((z == k) & (step == s))(pass_on)
-        pl.when(slot % 2 != y)(lambda: arrived(slot))
+            for at, events in GATHER_EVENTS[k].items():
+                def serve(events=events):
+                    for o, zz, h, to in events:
+                        arrived(o, zz, h)
+                        for t in to:
+                            pass_on(o, zz, h, t).start()
+                pl.when((z == k) & (step == at))(serve)
+        slot = slot_at(GATHER_ORDER, step)
         f_b[slot] = fbuf[slot].astype(BF16)
         f_now = f_b[slot]
 
-        def group(base, parts, c):
+        def group(base, parts, kept, c):
             top, total = c
             for first, size in parts:
                 logit = lax.dot_general(e_b[pl.ds(base + first, size), :], f_now, (((1,), (1,)), ((), ())), preferred_element_type=F32)
+                kept[pl.ds(first, size), :] = logit
                 logit = logit.reshape(size // 8, 8, own)
                 new = jnp.maximum(top, jnp.max(logit, axis=0))
                 total = total * jnp.exp2((top - new) * slope) + jnp.sum(jnp.exp2((logit - new[None]) * slope), axis=0)
                 top = new
             return top, total
 
-        top, total = over_blocks(group, (jnp.full((8, own), -3e38, F32), jnp.zeros((8, own), F32)))
+        def body(n, c):
+            @pl.when(step * whole + n >= 2)
+            def _():
+                z_copies(slot, n, True).wait()
+            c = group(pl.multiple_of(n * big, big), blocks, z_buf.at[lax.rem(n, 2)], c)
+            z_copies(slot, n, True).start()
+            return c
+
+        top, total = lax.fori_loop(0, whole, body, (jnp.full((8, own), -3e38, F32), jnp.zeros((8, own), F32)))
+        if tail:
+            @pl.when(step > 0)
+            def _():
+                z_copies(slot, None, True).wait()
+            top, total = group(whole * big, tail, z_rest, (top, total))
+            z_copies(slot, None, True).start()
         most = jnp.max(top, axis=0, keepdims=True)
         total = jnp.sum(total * jnp.exp2((top - most) * slope), axis=0, keepdims=True)
         lse_all[tp, pl.ds(slot, 1), :] = most * scale + jnp.log(total)
         return carry
 
     lax.fori_loop(0, 2 * NZ, gather_step, 0)
+    for n in range(2):
+        z_copies(0, jnp.int32(n), True).wait()
+    if tail:
+        z_copies(0, None, True).wait()
 
     for n in range(1, 2 * NZ):
         to = lax.rem(tp + n, 2 * NZ)
         remote(lse_all.at[tp], lse_all.at[tp], st_send.at[to], st_recv.at[tp], to, dp).start()
 
     def gathers_done(k):
-        def done(sems, slot):
-            remote(f_ref, fbuf.at[slot], sems.at[slot], ag_recv.at[slot], partner, dp).wait_send()
-        if k > 0:
-            done(ag_l, tp)
-        if k < NZ - 1:
-            done(ag_r, tp)
-        done(ag_y, tp)
-        for side, zz in ARRIVALS[k]:
-            at = 2 * zz + y
-            if side == "L" and k < NZ - 1:
-                done(ag_r, at)
-            if side == "R" and k > 0:
-                done(ag_l, at)
-            done(ag_y, at)
-
-    for k in range(NZ):
-        pl.when(z == k)(functools.partial(gathers_done, k))
+        for c in own_sends(k):
+            c.wait_send()
+        for events in GATHER_EVENTS[k].values():
+            for o, zz, h, to in events:
+                for t in to:
+                    pass_on(o, zz, h, t).wait_send()
+
+    on_position(gathers_done)
+    start_slot = slot_at(SCATTER_ORDER, 0)
+    for n in range(2):
+        z_copies(start_slot, jnp.int32(n), False).start()
+    if tail:
+        z_copies(start_slot, None, False).start()
 
     def clear(n, carry):
         g_acc[pl.ds(pl.multiple_of(n * 16, 16), 16), :] = jnp.zeros((16, width), F32)
@@ -255,10 +350,29 @@
     log_norm = peak + jnp.log(jnp.sum(jnp.exp(lse_all[...] - peak[None]), axis=0))
     norm_ref[...] = log_norm
 
-    order2 = {k: [2 * zz + 1 - s for zz in REDUCE_ORDER[k] for s in range(2)] for k in range(NZ)}
+    def leave(o, zz, h, to):
+        src = piece(fbuf.at[slot_of(o, zz)], h)
+        if to == "y":
+            at = 2 * zz + h
+            return remote(src, from_y.at[at], send_y.at[at], recv_y.at[at], partner, dp)
+        if to == "l":
+            at = 6 if o else 2 * zz + h
+            return remote(src, from_r.at[at], send_l.at[at], recv_r.at[at], tp - 2, dp)
+        at = 6 if o else 2 * zz - 2 + h
+        return remote(src, from_l.at[at], send_r.at[at], recv_l.at[at], tp + 2, dp)
+
+    def collect(o, zz, h, sums, to):
+        here = piece(fbuf.at[slot_of(o, zz)], h)
+        for d in sums:
+            at, buf, sem = {"y": (2 * zz + h, from_y, recv_y), "l": (6 if o else 2 * zz - 2 + h, from_l, recv_l),
+                            "r": (6 if o else 2 * zz + h, from_r, recv_r)}[d]
+            remote(here, buf.at[at], send_y.at[0], sem.at[at], partner, dp).wait_recv()
+            add_into(here, buf.at[at])
+        if to:
+            leave(o, zz, h, to).start()
 
     def scatter_step(step, lab_sum):
-        slot = chunk_of(order2, step)
+        slot = slot_at(SCATTER_ORDER, step)
         f_now = f_b[slot]
         acc = fbuf.at[slot]
         norm = norm_ref[pl.ds(slot, 1), :]
@@ -267,10 +381,10 @@
         lab = lab_ref[pl.ds(slot, 1), :]
         acc[...] = jnp.zeros((width, own), F32)
 
-        def group(base, parts, hits):
+        def group(base, parts, kept, hits):
             for first, size in parts:
                 at = pl.ds(base + first, size)
-                logit = lax.dot_general(e_b[at, :], f_now, (((1,), (1,)), ((), ())), preferred_element_type=F32)
+                logit = kept[pl.ds(first, size), :]
                 hit = lax.broadcasted_iota(jnp.int32, (size, own), 0) == lab - (base + first)
                 prob = jnp.exp2(logit * slope - shift) * coef
                 grad = jnp.where(hit, prob - token_scale, prob).astype(BF16)
@@ -281,30 +395,36 @@
             acc[...] += jnp.dot(e_t[:, pl.ds(base, size)], dl[pl.ds(0, size), :], preferred_element_type=F32)
             return hits
 
-        lab_sum = over_blocks(group, lab_sum)
-
-        def hand_over():
-            remote(acc, from_y.at[slot // 2], rs_y.at[slot // 2], recv_y.at[slot // 2], partner, dp).start()
-        pl.when(slot % 2 != y)(hand_over)
+        following = slot_at(SCATTER_ORDER, jnp.minimum(step + 1, 2 * NZ - 1))
+
+        def body(n, hits):
+            z_copies(slot, n, False).wait()
+            hits = group(pl.multiple_of(n * big, big), blocks, z_buf.at[lax.rem(n, 2)], hits)
+
+            @pl.when(n + 2 < whole)
+            def _():
+                z_copies(slot, n + 2, False).start()
+
+            @pl.when((n + 2 >= whole) & (step + 1 < 2 * NZ))
+            def _():
+                z_copies(following, n + 2 - whole, False).start()
+            return hits
+
+        lab_sum = lax.fori_loop(0, whole, body, lab_sum)
+        if tail:
+            z_copies(slot, None, False).wait()
+            lab_sum = group(whole * big, tail, z_rest, lab_sum)
+
+            @pl.when(step + 1 < 2 * NZ)
+            def _():
+                z_copies(following, None, False).start()
 
         for k in range(NZ):
-            for s, shards in REDUCE[k].items():
-                def reduce(k=k, shards=shards):
-                    for zz in shards:
-                        line = fbuf.at[2 * zz + y]
-                        remote(line, from_y.at[zz], rs_y.at[zz], recv_y.at[zz], partner, dp).wait_recv()
-                        add_into(line, from_y.at[zz])
-                        if zz >= k and k > 0:
-                            remote(line, from_l.at[zz - 1], rs_l.at[zz], recv_l.at[zz], partner, dp).wait_recv()
-                            add_into(line, from_l.at[zz - 1])
-                        if zz <= k and k < NZ - 1:
-                            remote(line, from_r.at[zz], rs_r.at[zz], recv_r.at[zz], partner, dp).wait_recv()
-                            add_into(line, from_r.at[zz])
-                        if zz > k:
-                            remote(line, from_l.at[zz - 1], rs_r.at[zz], recv_l.at[zz], tp + 2, dp).start()
-                        if zz < k:
-                            remote(line, from_r.at[zz], rs_l.at[zz], recv_r.at[zz], tp - 2, dp).start()
-                pl.when((z == k) & (step == s))(reduce)
+            for at, events in SCATTER_EVENTS[k].items():
+                def reduce(events=events):
+                    for event in events:
+                        collect(*event)
+                pl.when((z == k) & (step == at))(reduce)
         return lab_sum
 
     lab_sum = lax.fori_loop(0, 2 * NZ, scatter_step, jnp.zeros((8, own), F32))
@@ -314,16 +434,12 @@
     dfin_ref[...] = fbuf[tp].T
 
     def scatters_done(k):
-        for zz in range(NZ):
-            line = fbuf.at[2 * zz + y]
-            remote(line, from_y.at[zz], rs_y.at[zz], recv_y.at[zz], partner, dp).wait_send()
-            if zz > k:
-                remote(line, from_l.at[zz - 1], rs_r.at[zz], recv_l.at[zz], partner, dp).wait_send()
-            if zz < k:
-                remote(line, from_r.at[zz], rs_l.at[zz], recv_r.at[zz], partner, dp).wait_send()
-
-    for k in range(NZ):
-        pl.when(z == k)(functools.partial(scatters_done, k))
+        for events in SCATTER_EVENTS[k].values():
+            for o, zz, h, _, to in events:
+                if to:
+                    leave(o, zz, h, to).wait_send()
+
+    on_position(scatters_done)
     for n in range(1, 2 * NZ):
         to = lax.rem(tp + n, 2 * NZ)
         remote(lse_all.at[tp], lse_all.at[tp], st_send.at[to], st_recv.at[tp], to, dp).wait_send()
@@ -334,19 +450,21 @@
     own, width = f_own.shape
     vocab = embed.shape[0]
     chunk = (own, width)
-    dma8 = pltpu.SemaphoreType.DMA((2 * NZ,))
-    dma4 = pltpu.SemaphoreType.DMA((NZ,))
+    strips = lambda n: pltpu.VMEM((n, own // 2, width), F32)
+    dma = lambda *n: pltpu.SemaphoreType.DMA(n)
     return pl.pallas_call(
         functools.partial(head_kernel, scale, token_scale),
         out_shape=(jax.ShapeDtypeStruct((own, width), F32), jax.ShapeDtypeStruct((vocab, width), F32),
-                   jax.ShapeDtypeStruct((2 * NZ, own), F32), jax.ShapeDtypeStruct((8, own), F32)),
+                   jax.ShapeDtypeStruct((2 * NZ, own), F32), jax.ShapeDtypeStruct((8, own), F32),
+                   jax.ShapeDtypeStruct((2 * NZ, vocab, own), F32)),
         in_specs=[VMEM, VMEM, ANY],
-        out_specs=(VMEM, ANY, VMEM, VMEM),
+        out_specs=(VMEM, ANY, VMEM, VMEM, ANY),
         scratch_shapes=[pltpu.VMEM((vocab, width), BF16), pltpu.VMEM((width, vocab), BF16),
                         pltpu.VMEM((2 * NZ,) + chunk, F32), pltpu.VMEM((2 * NZ,) + chunk, BF16), pltpu.VMEM((vocab, width), F32),
-                        pltpu.VMEM((NZ,) + chunk, F32), pltpu.VMEM((NZ - 1,) + chunk, F32), pltpu.VMEM((NZ - 1,) + chunk, F32),
-                        pltpu.VMEM((SUB * GROUP, own), BF16), pltpu.VMEM((2 * NZ, 2 * NZ, own), F32),
-                        pltpu.SemaphoreType.DMA((2,)), dma8, dma8, dma8, dma8, dma4, dma4, dma4, dma4, dma4, dma4, dma8, dma8],
+                        strips(8), strips(7), strips(7),
+                        pltpu.VMEM((SUB * GROUP, own), BF16), pltpu.VMEM((2, SUB * GROUP, own), F32),
+                        pltpu.VMEM((max(vocab % (SUB * GROUP), 8), own), F32), pltpu.VMEM((2 * NZ, 2 * NZ, own), F32),
+                        dma(3), dma(2), dma(3, 2 * NZ, 2), dma(2 * NZ, 2), dma(8), dma(7), dma(7), dma(8), dma(7), dma(7), dma(2 * NZ), dma(2 * NZ)],
         compiler_params=pltpu.CompilerParams(collective_id=collective_id, has_side_effects=True, vmem_limit_bytes=67000000),
         cost_estimate=pl.CostEstimate(flops=8 * vocab * width * own * 8, bytes_accessed=3 * 4 * vocab * width, transcendentals=2 * vocab * own * 8),
         name="head",
@@ -1162,7 +1280,7 @@
 
         logit_scale = d_model ** -0.5
         lab_loc = labels.reshape(n_tp, own) - tp_rank * vocab_loc
-        d_fin, g_head_part, log_norm, lab_sum = head(f_own, lab_loc, embed, logit_scale, logit_scale / tok_total, 4)
+        d_fin, g_head_part, log_norm, lab_sum, _ = head(f_own, lab_loc, embed, logit_scale, logit_scale / tok_total, 4)
         log_norm = lax.dynamic_index_in_dim(log_norm, tp_rank, 0, keepdims=False)
         loss_row = (log_norm + LOGIT_ZLOSS * log_norm * log_norm - jnp.sum(lab_sum, axis=0) * logit_scale) / tok_total
         g_rows, d_zero, rows_back = layer_bwd(d_fin, x_zero, x_one, loss_row[None, :], ln_scales, cos_t, sin_t, weights, saved, pick_first, 7)

time: 650 us -> 616 us (0.948)
  Pallas kernels: 627 us -> 594 us
    pallas_call x1, Pallas kernels: 250 us -> 201 us  [head(): pl.pallas_call(functools.partial(head_kernel, scale, token_scale), out_sh...]
    pallas_call x1, Pallas kernels: 59.1 us -> 69.9 us  [layer_bwd(): pl.pallas_call(layer_bwd_kernel, out_shape=(jax.ShapeDtypeStruct((2 * NZ,...]
where the time goes in v9:
time: 616 us; the launch traced here: 609 us
  Pallas kernels  594 us (96%)
  other arithmetic  8.56 us (1%)
    pallas_call x1, Pallas kernels, head(): pl.pallas_call(functools.partial(head_kernel, scale, token_scale), out_sh...  201 us
    pallas_call x1, Pallas kernels, tail(): pl.pallas_call(tail_kernel, out_shape=(jax.ShapeDtypeStruct((vocab, width...  188 us
    pallas_call x1, Pallas kernels, front(): pl.pallas_call(front_kernel, out_shape=(s((own, width), F32),) * 3 + (s((...  98.1 us
    pallas_call x1, Pallas kernels, layer_bwd(): pl.pallas_call(layer_bwd_kernel, out_shape=(jax.ShapeDtypeStruct((2 * NZ,...  69.9 us
    pallas_call x1, Pallas kernels, update(): pl.pallas_call(update_kernel, out_shape=tuple((jax.ShapeDtypeStruct(a.sha...  36.6 us

profile of v9, /device:TPU:0, one launch (start us, length us, event | category | flops | bytes accessed | tf_op | source)
XLA Modules:
  0.0 609.5 jit_solution(11491977465044952182)
XLA Ops:
  0.7 0.7 broadcast_subtract_fusion
  1.4 0.6 sub.38.lab_ref
  2.0 0.7 reshape.477
  2.8 0.2 convert_reduce_fusion
  3.0 0.6 reduce_max.9
  4.3 0.3 fusion.22
  4.6 0.0 copy-start
  4.7 0.3 fusion.20
  5.0 0.4 select_reduce_fusion.3
  5.4 0.7 select_n.143.ids_ref
  6.1 0.7 reshape.478.ids_ref
  6.8 1.0 multiply_sine_fusion
  7.7 1.6 bitcast_convert_fusion
  9.4 0.1 and_convert_fusion
  9.5 0.0 copy-start.3
  9.5 0.0 copy-start.4
  9.6 0.0 copy-start.5
  9.6 1.2 copy.50.pick_ref
  10.7 0.0 copy-done
  10.7 0.3 copy.49
  11.1 0.0 copy-done.3
  11.1 0.0 copy-done.4
  11.1 0.0 copy-done.5
  11.1 1.4 pad_maximum_fusion.w_ref
  12.5 0.1 broadcast_in_dim.123
  12.6 0.0 copy-start.1
  12.6 98.1 %front.1 = (f32[512,512]{1,0:T(8,128)}, f32[512,512]{1,0:T(8,128)}, f32[512,512]{1,0:T(8,128)}, bf16[512,512]{1,0:T(8,128)(2,1)}, bf16[1024,128]{1,0:T(8,128)(2,...) custom-call(s32[768]{0:T(1024)} %reshape.478.ids_ref, ...), custom_call_target="tpu_custom_call" | custom-call | tf_op jit(solution)/shard_map/front/pallas_call | solution.py:732
  110.7 0.0 copy-done.1
  110.7 201.5 %head.1 = (f32[512,512]{1,0:T(8,128)}, f32[6288,512]{1,0:T(8,128)}, f32[8,512]{1,0:T(8,128)}, f32[8,512]{1,0:T(8,128)}, f32[8,6288,512]{2,1,0:T(8,128)}) custom-call(f32[512,512]{1,0:T(8,128)} %get-tuple-element.184.f_ref, s32[8,512]{1,0:T(8,128)} %sub.38.lab_ref, f32[6288,512]{1,0:T(8,128)} %get-tuple-element.524), custom_call_target="tpu_custom_call" | custom-call | flops 105495134208 | bytes 38633472 | tf_op jit(solution)/shard_map/head/pallas_call | solution.py:455
  312.2 0.7 reduce_sum.70
  312.9 1.3 fusion.28.loss_ref
  314.3 0.0 copy-start.2
  314.3 69.9 %layer_bwd.1 = (f32[8,928,512]{2,1,0:T(8,128)}, f32[512,512]{1,0:T(8,128)S(1)}, f32[8,96,512]{2,1,0:T(8,128)}) custom-call(f32[512,512]{1,0:T(8,128)} %get-tuple-element.186.dfin_ref, f32[512,512]{1,0:T(8,128)} %get-tuple-element.187.x0_ref, f32[512,512]{1,0:T(8,128)} %get-tuple-element.188.x1_ref, f32[1,512]{1,0:T(1,128)} %fusion.28.loss_ref, ...), custom_call_target="tpu_custom_call" | custom-call | tf_op jit(solution)/shard_map/layer_bwd/pallas_call | solution.py:880
  384.1 0.0 copy-done.2
  384.2 188.2 %tail.1 = (f32[6288,512]{1,0:T(8,128)}, f32[2,464,512]{2,1,0:T(8,128)}, f32[8,24,512]{2,1,0:T(8,128)}) custom-call(f32[6288,512]{1,0:T(8,128)} %get-tuple-element.202.g_ref, f32[8,2,464,512]{3,2,1,0:T(8,128)} %bitcast.51, f32[768,512]{1,0:T(8,128)} %bitcast.56, s32[1,768]{1,0:T(1,128)} %select_n.143.ids_ref), custom_call_target="tpu_custom_call" | custom-call | tf_op jit(solution)/shard_map/tail/pallas_call | solution.py:1093
  572.4 36.6 %update.1 = (f32[6288,512]{1,0:T(8,128)}, f32[2,512]{1,0:T(2,128)}, f32[64,512]{1,0:T(8,128)}, f32[2,64,512]{2,1,0:T(8,128)}, f32[64,512]{1,0:T(8,128)}, /*index...) custom-call(f32[6288,512]{1,0:T(8,128)} %get-tuple-element.205.t_ref, ...), custom_call_target="tpu_custom_call" | custom-call | tf_op jit(solution)/shard_map/update/pallas_call | solution.py:1185
  (12 shorter events, 0.1 us)
Async XLA Ops:
  4.6 6.1 copy-start
  9.5 1.5 copy-start.3
  9.5 1.5 copy-start.4
  9.6 1.5 copy-start.5
  12.6 98.1 %copy-start.1 = (s32[8,512]{1,0:T(8,128)}, s32[8,512]{1,0:T(8,128)S(1)}, u32[]{:S(2)}) copy-start(s32[8,512]{1,0:T(8,128)S(1)} %get-tuple-element.527) | copy-start | bytes 49156
  314.3 69.9 %copy-start.2 = (s32[8,512]{1,0:T(8,128)S(1)}, s32[8,512]{1,0:T(8,128)}, u32[]{:S(2)}) copy-start(s32[8,512]{1,0:T(8,128)} %copy-done.1) | copy-start | bytes 49156

commit v10 on v9

--- a/solution.py
+++ b/solution.py
@@ -92,6 +92,34 @@
         scratch_shapes=[pltpu.SemaphoreType.DMA] + [pltpu.SemaphoreType.DMA((2 * NZ,))] * 2,
         compiler_params=pltpu.CompilerParams(collective_id=collective_id, has_side_effects=True),
         name="plane_swap",
+    )(x)
+
+
+def group_kernel(x_ref, out_ref, own_sem, send, recv):
+    tp, dp, _, _ = place()
+    group = [lax.rem(dp + n, 4) for n in range(1, 4)]
+    for to in group:
+        signal(tp, to)
+    pl.semaphore_wait(pltpu.get_barrier_semaphore(), 3)
+    own = pltpu.make_async_copy(x_ref, out_ref.at[dp], own_sem)
+    own.start()
+    for n, to in enumerate(group):
+        remote(x_ref, out_ref.at[dp], send.at[n], recv.at[dp], tp, to).start()
+    own.wait()
+    for n, to in enumerate(group):
+        remote(x_ref, out_ref.at[to], send.at[n], recv.at[to], tp, to).wait_recv()
+        remote(x_ref, out_ref.at[dp], send.at[n], recv.at[dp], tp, to).wait_send()
+
+
+def group_gather(x, collective_id):
+    return pl.pallas_call(
+        group_kernel,
+        out_shape=jax.ShapeDtypeStruct((4,) + x.shape, x.dtype),
+        in_specs=[ANY],
+        out_specs=ANY,
+        scratch_shapes=[pltpu.SemaphoreType.DMA, pltpu.SemaphoreType.DMA((3,)), pltpu.SemaphoreType.DMA((4,))],
+        compiler_params=pltpu.CompilerParams(collective_id=collective_id, has_side_effects=True),
+        name="group_gather",
     )(x)
 
 
@@ -493,10 +521,10 @@
 MLP_ORDER = {k: [2 * k] + [code for line, other in EVENTS[k] for code in [2 * zz for _, zz in line] + [2 * zz + 1 for zz in other]] for k in range(NZ)}
 
 
-def front_kernel(ids_ref, e_ref, pick_ref, extra_ref, w_ref, wkv_ref, ln_ref, cos_ref, sin_ref,
-                 f_ref, x1_ref, x0_ref, q_ref, kv_ref, kvt_ref, lse_ref, ctx_ref, wq_ref, wo_ref, wg_ref, wu_ref, wd_ref,
+def front_kernel(ids_ref, e_ref, rounds_ref, pick_ref, extra_ref, w_ref, wkv_ref, ln_ref, cos_ref, sin_ref,
+                 f_ref, x1_ref, x0_ref, q_ref, kv_ref, kvt_ref, lse_ref, ctx_ref, wq_ref, wo_ref, wg_ref, wu_ref, wd_ref, rounds_all,
                  table, rows_ref, wl, rows_in, u_b, kv_out, kv_in, own_sem, r_send, r_recv, a_y, a_l, a_r, a_c, a_recv,
-                 b_y, b_l, b_r, b_x, b_c, b_recv, kv_send, kv_recv):
+                 b_y, b_l, b_r, b_x, b_c, b_recv, kv_send, kv_recv, n_send, n_recv):
     tp, dp, z, y = place()
     partner = tp + 1 - 2 * y
     core = dp % 2
@@ -560,8 +588,16 @@
 
     load = pltpu.make_async_copy(e_ref, table, own_sem.at[2])
     load.start()
-    plane_barrier(tp, dp, [(tp, twin), (tp, facing)])
+    group = [twin, facing, lax.rem(twin + 2, 4)]
+    plane_barrier(tp, dp, [(tp, d) for d in group])
     peers = [lax.rem(tp + n, shards) for n in range(1, shards)]
+
+    def rounds_copy(n):
+        return remote(rounds_ref, rounds_all.at[dp], n_send.at[n], n_recv.at[dp], tp, group[n])
+
+    for n in range(3):
+        rounds_copy(n).start()
+    rounds_all[dp] = rounds_ref[...]
 
     def row_copy(to):
         return remote(rows_ref.at[to], rows_in.at[tp], r_send.at[to], r_recv.at[tp], to, dp)
@@ -713,6 +749,9 @@
             c.wait_send()
 
     on_position(finish)
+    for n in range(3):
+        rounds_copy(n).wait_send()
+        remote(rounds_ref, rounds_all.at[group[n]], n_send.at[n], n_recv.at[group[n]], tp, twin).wait_recv()
     for to in peers:
         row_copy(to).wait_send()
         a_copy(to, a_c, tp, twin).wait_send()
@@ -721,7 +760,7 @@
         b_copy(to, facing, b_c.at[1], tp, twin).wait_send()
 
 
-def front(ids, embed, pick, extra, w_rows, wkv_t, ln, cos_t, sin_t, n_q, collective_id):
+def front(ids, embed, rounds, pick, extra, w_rows, wkv_t, ln, cos_t, sin_t, n_q, collective_id):
     own, width = extra.shape
     two_hd = wkv_t.shape[0]
     shards = 2 * NZ
@@ -733,23 +772,28 @@
         front_kernel,
         out_shape=(s((own, width), F32),) * 3 + (s((n_q, own), BF16), s((2 * own, two_hd), BF16), s((two_hd, 2 * own), BF16),
                    s((2 * n_q // two_hd, own), F32), s((n_q, own), BF16), s((n_q, width), BF16), s((n_q, width), BF16))
-        + (s((ff, width), BF16),) * 3,
-        in_specs=[pl.BlockSpec(memory_space=pltpu.SMEM), ANY, VMEM, VMEM, ANY] + [VMEM] * 4,
-        out_specs=(VMEM,) * 13,
+        + (s((ff, width), BF16),) * 3 + (s((4, 1, 128), jnp.int32),),
+        in_specs=[pl.BlockSpec(memory_space=pltpu.SMEM), ANY, VMEM, VMEM, VMEM, ANY] + [VMEM] * 4,
+        out_specs=(VMEM,) * 14,
         scratch_shapes=[pltpu.VMEM(embed.shape, F32), pltpu.VMEM(rows, F32), pltpu.VMEM((shards,) + w_rows.shape, F32), pltpu.VMEM(rows, F32), pltpu.VMEM((own, width), BF16),
                         pltpu.VMEM((two_hd, own), F32), pltpu.VMEM((two_hd, own), F32),
                         dma(3), dma(shards), dma(shards)] + [dma(shards)] * 4 + [dma(shards, 2)]
-        + [dma(shards)] * 4 + [dma(2, shards), dma(shards, 4), pltpu.SemaphoreType.DMA, pltpu.SemaphoreType.DMA],
+        + [dma(shards)] * 4 + [dma(2, shards), dma(shards, 4), pltpu.SemaphoreType.DMA, pltpu.SemaphoreType.DMA, dma(3), dma(4)],
         compiler_params=pltpu.CompilerParams(collective_id=collective_id, has_side_effects=True, vmem_limit_bytes=60000000),
         name="front",
-    )(ids, embed, pick, extra, w_rows, wkv_t, ln, cos_t, sin_t)
+    )(ids, embed, rounds, pick, extra, w_rows, wkv_t, ln, cos_t, sin_t)
 
 
 def layer_bwd_kernel(dfin_ref, x0_ref, x1_ref, loss_ref, ln_ref, cos_ref, sin_ref, wq_ref, wkv_ref, wo_ref, wg_ref, wu_ref, wd_ref,
-                     q_ref, kv_ref, kvt_ref, lse_ref, ctx_ref, pick_ref, rows_ref, d0_ref, back_ref, d_one, d_b, u_b, dctx, dq, dkv, dkv_in,
-                     hid, d_gate, d_up, rows_out, g_q, g_o, g_g, g_u, g_d, small, out_sem, send_sem, recv_sem, r_send, r_recv):
-    tp, dp, _, y = place()
+                     q_ref, kv_ref, kvt_ref, lse_ref, ctx_ref, pick_ref, g_ref, ids_ref, rows_ref, d0_ref, back_ref, early_ref, ids_all, d_one, d_b, u_b, dctx, dq, dkv, dkv_in,
+                     hid, d_gate, d_up, rows_out, g_q, g_o, g_g, g_u, g_d, small, s_early, c_early, out_sem, send_sem, recv_sem,
+                     r_send, x_send, c_send, r_recv, g_load, g_send, g_recv, id_send, id_recv):
+    tp, dp, z, y = place()
     partner = tp + 1 - 2 * y
+    core = dp % 2
+    twin = dp + 1 - 2 * core
+    facing = lax.rem(dp + 2, 4)
+    across = lax.rem(twin + 2, 4)
     own, width = x0_ref.shape
     hd = kv_ref.shape[1] // 2
     quarter = hd // 2
@@ -757,13 +801,43 @@
     heads = nq // hd
     ff = wg_ref.shape[0]
     shards = rows_ref.shape[0]
-    plane_barrier(tp, dp, [])
+    plane_barrier(tp, dp, [(tp, twin), (tp, facing), (tp, across)])
+
+    n_early, g_size = s_early.shape[0], s_early.shape[1]
+
+    def g_rows(which, b):
+        return g_ref.at[pl.ds(pl.multiple_of(which * (g_ref.shape[0] // 2) + b * g_size, 8), g_size), :]
+
+    def g_load_copy(b):
+        return pltpu.make_async_copy(g_rows(core, b), s_early.at[b], g_load.at[b])
+
+    def g_chip_copy(b):
+        return remote(g_rows(1 - core, b), c_early.at[b], g_send.at[0, b], g_recv.at[0, b], tp, twin)
+
+    def g_x_copy(b):
+        return remote(s_early.at[b], early_ref.at[b], g_send.at[1, b], g_recv.at[1, b], tp, facing)
+
+    for b in range(n_early):
+        g_chip_copy(b).start()
+        g_load_copy(b).start()
+
+    def ids_copy(n, to):
+        return remote(ids_ref, ids_all.at[dp], id_send.at[n], id_recv.at[dp], tp, to)
+
+    for n, to in enumerate((twin, facing, across)):
+        ids_copy(n, to).start()
+    ids_all[dp] = ids_ref[...]
     _, f_hat, f_inv = norm_fwd(x1_ref[...], ln_ref[1:2, :])
     d_in, g_fin = norm_bwd(dfin_ref[...], f_hat, f_inv, ln_ref[1:2, :])
     d_one[...] = d_in
     d_b[...] = d_in.astype(BF16)
     u_b[...] = norm_fwd(x0_ref[...], ln_ref[0:1, :])[0]
     dctx[...] = mm(wo_ref[...], d_b[...], TB).astype(BF16)
+    for b in range(n_early):
+        g_load_copy(b).wait()
+        g_chip_copy(b).wait_recv()
+        add_into(s_early.at[b], c_early.at[b], 24)
+        g_x_copy(b).start()
     cos_t = cos_ref[...]
     sin_t = sin_ref[...]
     blank = jnp.zeros((hd, own), BF16)
@@ -823,13 +897,37 @@
     rows_out[...] = (mm(pick_ref[...], high, TA) + mm(pick_ref[...], middle, TA) + mm(pick_ref[...], low, TA)).reshape(rows_out.shape)
 
     def row_copy(to):
-        return remote(rows_out.at[to], back_ref.at[tp], r_send.at[to], r_recv.at[tp], to, dp)
-
-    peers = [lax.rem(tp + n, shards) for n in range(1, shards)]
-    for to in peers:
-        row_copy(to).start()
-    own_rows = pltpu.make_async_copy(rows_out.at[tp], back_ref.at[tp], out_sem.at[7 * 2 * NZ])
+        return remote(rows_out.at[to], back_ref.at[dp, tp], r_send.at[to], r_recv.at[dp, tp], to, dp)
+
+    def x_copy(slot):
+        return remote(back_ref.at[dp, slot], back_ref.at[dp, slot], x_send.at[slot], r_recv.at[dp, slot], tp, facing)
+
+    def c_copy(group, n, slot):
+        return remote(back_ref.at[group, slot], back_ref.at[group, slot], c_send.at[n, slot], r_recv.at[group, slot], tp, twin)
+
+    def back(group, slot):
+        remote(rows_out.at[slot], back_ref.at[group, slot], r_send.at[slot], r_recv.at[group, slot], tp, twin).wait_recv()
+
+    def near_first(k):
+        return sorted(((o, zz) for o in range(2) for zz in range(NZ)), key=lambda c: (abs(c[1] - k), c[0]))
+
+    def slot_of(o, zz):
+        return 2 * zz + (1 - y if o else y)
+
+    def on_position(f):
+        for k in range(NZ):
+            pl.when(z == k)(functools.partial(f, k))
+
+    def rows_leave(k):
+        for c in near_first(k)[:0:-1]:
+            row_copy(slot_of(*c)).start()
+
+    on_position(rows_leave)
+    own_rows = pltpu.make_async_copy(rows_out.at[tp], back_ref.at[dp, tp], out_sem.at[7 * 2 * NZ])
     own_rows.start()
+    own_rows.wait()
+    x_copy(tp).start()
+    c_copy(dp, 0, tp).start()
 
     g_o[...] = mm(ctx_ref[...], d_b[...])
     g_q[...] = mm(dq[...], u_b[...])
@@ -863,13 +961,39 @@
         c.start()
     for c in copies:
         c.wait()
-    own_rows.wait()
-    for source in peers:
-        remote(rows_out.at[source], back_ref.at[source], r_send.at[source], r_recv.at[source], source, dp).wait_recv()
-        row_copy(source).wait_send()
-
-
-def layer_bwd(d_fin, x0, x1, loss_row, ln, cos_t, sin_t, weights, saved, pick, collective_id):
+
+    def relay(k):
+        order = near_first(k)
+        for c in order[1:]:
+            back(dp, slot_of(*c))
+            x_copy(slot_of(*c)).start()
+            c_copy(dp, 0, slot_of(*c)).start()
+        for c in order:
+            back(facing, slot_of(*c))
+            c_copy(facing, 1, slot_of(*c)).start()
+
+    on_position(relay)
+    for b in range(n_early):
+        g_x_copy(b).wait_recv()
+        add_into(early_ref.at[b], s_early.at[b], 24)
+    for slot in range(shards):
+        back(twin, slot)
+        back(across, slot)
+    for n, to in enumerate((twin, facing, across)):
+        remote(ids_ref, ids_all.at[to], id_send.at[n], id_recv.at[to], tp, to).wait_recv()
+        ids_copy(n, to).wait_send()
+    for n in range(1, shards):
+        row_copy(lax.rem(tp + n, shards)).wait_send()
+    for slot in range(shards):
+        x_copy(slot).wait_send()
+        c_copy(dp, 0, slot).wait_send()
+        c_copy(facing, 1, slot).wait_send()
+    for b in range(n_early):
+        g_chip_copy(b).wait_send()
+        g_x_copy(b).wait_send()
+
+
+def layer_bwd(d_fin, x0, x1, loss_row, ln, cos_t, sin_t, weights, saved, pick, g_table, ids, collective_id):
     own, width = x0.shape
     nq = weights[0].shape[0]
     two_hd = weights[1].shape[0]
@@ -877,34 +1001,45 @@
     rows = (2 * nq + 3 * ff + two_hd) // (2 * NZ) + 16
     chunk = (own, width)
     back = (2 * NZ, pick.shape[1] // (2 * NZ), width)
+    blocks = (N_EARLY, table_block(g_table.shape[0]), width)
+    dma = lambda *n: pltpu.SemaphoreType.DMA(n)
     return pl.pallas_call(
         layer_bwd_kernel,
-        out_shape=(jax.ShapeDtypeStruct((2 * NZ, rows, width), F32), jax.ShapeDtypeStruct(chunk, F32), jax.ShapeDtypeStruct(back, F32)),
-        in_specs=[VMEM] * 19,
-        out_specs=(ANY, VMEM, ANY),
+        out_shape=(jax.ShapeDtypeStruct((2 * NZ, rows, width), F32), jax.ShapeDtypeStruct(chunk, F32), jax.ShapeDtypeStruct((4,) + back, F32),
+                   jax.ShapeDtypeStruct(blocks, F32), jax.ShapeDtypeStruct((4,) + ids.shape, jnp.int32)),
+        in_specs=[VMEM] * 19 + [ANY, VMEM],
+        out_specs=(ANY, VMEM, ANY, VMEM, VMEM),
         scratch_shapes=[pltpu.VMEM(chunk, F32), pltpu.VMEM(chunk, BF16), pltpu.VMEM(chunk, BF16), pltpu.VMEM((nq, own), BF16),
                         pltpu.VMEM((nq, own), BF16), pltpu.VMEM((2 * own, two_hd), F32), pltpu.VMEM((own, two_hd), F32)]
         + [pltpu.VMEM((ff, own), BF16)] * 3 + [pltpu.VMEM(back, F32), pltpu.VMEM((nq, width), F32), pltpu.VMEM((nq, width), F32)] + [pltpu.VMEM((ff, width), F32)] * 3
-        + [pltpu.VMEM((two_hd + 32, width), F32), pltpu.SemaphoreType.DMA((14 * NZ + 1,)), pltpu.SemaphoreType.DMA, pltpu.SemaphoreType.DMA,
-           pltpu.SemaphoreType.DMA((2 * NZ,)), pltpu.SemaphoreType.DMA((2 * NZ,))],
-        compiler_params=pltpu.CompilerParams(collective_id=collective_id, has_side_effects=True, vmem_limit_bytes=60000000),
+        + [pltpu.VMEM((two_hd + 32, width), F32), pltpu.VMEM(blocks, F32), pltpu.VMEM(blocks, F32), dma(14 * NZ + 1),
+           pltpu.SemaphoreType.DMA, pltpu.SemaphoreType.DMA, dma(2 * NZ), dma(2 * NZ), dma(2, 2 * NZ), dma(4, 2 * NZ),
+           dma(N_EARLY), dma(2, N_EARLY), dma(2, N_EARLY), dma(3), dma(4)],
+        compiler_params=pltpu.CompilerParams(collective_id=collective_id, has_side_effects=True, vmem_limit_bytes=66000000),
         name="layer_bwd",
-    )(d_fin, x0, x1, loss_row, ln, cos_t, sin_t, *weights, *saved, pick)
+    )(d_fin, x0, x1, loss_row, ln, cos_t, sin_t, *weights, *saved, pick, g_table, ids)
 
 
 N_BLOCK = 12
-EARLY = 9
+N_EARLY = 3
+AHEAD = 11
+
+
+def table_block(vocab):
+    return -(-vocab // (2 * N_BLOCK * 24)) * 24
+
+
 W_REDUCE = {
-    0: {1: (3,), 3: (2,), 5: (1,), 7: (0,)},
-    1: {3: (3,), 5: (2, 0), 7: (1,)},
-    2: {3: (0,), 5: (1, 3), 7: (2,)},
-    3: {1: (0,), 3: (1,), 5: (2,), 7: (3,)},
+    0: {4: (3,), 6: (2,), 8: (1,), 9: (0,)},
+    1: {6: (3,), 8: (2, 0), 9: (1,)},
+    2: {6: (0,), 8: (1, 3), 9: (2,)},
+    3: {4: (0,), 6: (1,), 8: (2,), 9: (3,)},
 }
 
 
-def tail_kernel(g_ref, p_ref, rows_ref, ids_ref, t_ref, w_out, small_ref,
-                s_buf, from_c, from_x, rows_c, ids_c, parts, acc, w_c, w_y, w_l, w_r, w_x,
-                g_load, g_send_c, g_recv_c, g_send_x, g_recv_x, g_send_t, g_recv_t, g_store, l_send, l_recv,
+def tail_kernel(g_ref, p_ref, rows_ref, ids_ref, early_ref, t_ref, w_out, small_ref,
+                s_buf, from_c, from_x, look_in, parts, acc, w_c, w_y, w_l, w_r, w_x,
+                g_load, g_send_c, g_recv_c, g_send_x, g_recv_x, g_send_t, g_recv_t, g_store, l_sem,
                 w_load, w_out_sem, send_c, send_y, send_l, send_r, recv_c, recv_y, recv_l, recv_r, last_send, last_recv, small_send, small_recv):
     tp, dp, z, y = place()
     partner = tp + 1 - 2 * y
@@ -914,19 +1049,27 @@
     half = g_ref.shape[0] // 2
     size = s_buf.shape[1]
     last = half - (N_BLOCK - 1) * size
-    n_look = rows_ref.shape[0]
+    n_look = rows_ref.shape[1]
 
     def rows(which, b, n):
         return pl.ds(pl.multiple_of(which * half + b * size, 8), n)
 
     def part(buf, b, n):
-        return buf.at[b, pl.ds(0, n), :]
+        return buf.at[b - N_EARLY if buf is not from_x else b, pl.ds(0, n), :]
 
     plane_barrier(tp, dp, [(tp, twin), (tp, facing)])
 
-    look_copies = [remote(rows_ref, rows_c, l_send.at[0], l_recv.at[0], tp, twin), remote(ids_ref, ids_c, l_send.at[1], l_recv.at[1], tp, twin)]
-    for c in look_copies:
-        c.start()
+    chip = dp // 2
+    groups = (2 * chip, 2 * chip + 1, 2 - 2 * chip, 3 - 2 * chip)
+
+    def look_load(n):
+        return pltpu.make_async_copy(rows_ref.at[groups[n]], look_in.at[n % 2], l_sem.at[n % 2])
+
+    def early_load(b):
+        return pltpu.make_async_copy(early_ref.at[b], from_x.at[b], g_load.at[b])
+
+    for n in range(2):
+        look_load(n).start()
 
     def c_copy(b, n):
         return remote(g_ref.at[rows(1 - core, b, n), :], part(from_c, b, n), g_send_c.at[b], g_recv_c.at[b], tp, twin)
@@ -951,14 +1094,24 @@
         if end == N_BLOCK:
             f(N_BLOCK - 1, last)
 
+    def looked_up(b, n, first, count):
+        ids = jnp.concatenate([ids_ref[first + g] for g in range(count)], axis=1) - (core * half + b * size)
+        hit = (lax.broadcasted_iota(jnp.int32, (n, count * n_look), 0) == ids).astype(F32).astype(BF16)
+        span = pl.ds(pl.multiple_of(first * n_look, n_look), count * n_look)
+        return mm(hit, parts[0, span, :]) + mm(hit, parts[1, span, :]) + mm(hit, parts[2, span, :])
+
     def chip_sum(b, n):
         own_load(b, n).wait()
         c_copy(b, n).wait_recv()
-        ids = jnp.concatenate([ids_ref[...], ids_c[...]], axis=1) - (core * half + b * size)
-        hit = (lax.broadcasted_iota(jnp.int32, (n, 2 * n_look), 0) == ids).astype(F32).astype(BF16)
-        look = mm(hit, parts[0]) + mm(hit, parts[1]) + mm(hit, parts[2])
-        s_buf[b, 0:n, :] = s_buf[b, 0:n, :] + from_c[b, 0:n, :] + look
+        at = b - N_EARLY
+        s_buf[at, 0:n, :] = s_buf[at, 0:n, :] + from_c[at, 0:n, :] + looked_up(b, n, 2 * chip, 2)
         x_copy(b, n).start()
+
+    def early_sum(b, n):
+        early_load(b).wait()
+        from_x[b] = from_x[b] + looked_up(b, n, 0, 4)
+        t_copy(b, n).start()
+        t_store(b, n).start()
 
     def w_first(k):
         for zz in REDUCE_ORDER[k]:
@@ -1003,24 +1156,33 @@
         c_copy(b, n).start()
         own_load(b, n).start()
 
-    every(first, 0, 4)
+    every(first, N_EARLY, N_EARLY + 2)
     on_position(w_first)
-    every(first, 4, N_BLOCK)
-
-    def split(at, value):
+    every(first, N_EARLY + 2, N_BLOCK)
+    for b in range(N_EARLY):
+        early_load(b).start()
+
+    def split(n):
+        look_load(n).wait()
+        value = look_in[n % 2]
         high = value.astype(BF16)
         left = value - high.astype(F32)
         middle = left.astype(BF16)
+        at = pl.ds(pl.multiple_of(groups[n] * n_look, n_look), n_look)
         parts[0, at, :] = high
         parts[1, at, :] = middle
         parts[2, at, :] = (left - middle.astype(F32)).astype(BF16)
-
-    split(pl.ds(0, n_look), rows_ref[...])
-    for c in look_copies:
-        c.wait()
-    split(pl.ds(n_look, n_look), rows_c[...])
-    every(chip_sum, 0, EARLY)
+        if n + 2 < 4:
+            look_load(n + 2).start()
+
+    split(0)
+    split(1)
+    every(chip_sum, N_EARLY, N_EARLY + 3)
     on_position(w_second)
+    every(chip_sum, N_EARLY + 3, AHEAD)
+    split(2)
+    split(3)
+    every(early_sum, 0, N_EARLY)
 
     total = acc.at[tp]
     w_copy_x = remote(total, w_x, last_send.at[0], last_recv.at[0], tp, facing)
@@ -1030,7 +1192,7 @@
     mine = w_out.at[1, pl.ds(n_rows - 32, n_small), :]
     small_here = pltpu.make_async_copy(mine, small_ref.at[tp], w_out_sem)
     peers = [lax.rem(tp + n, 2 * NZ) for n in range(1, 2 * NZ)]
-    for b in range(N_BLOCK):
+    for b in range(N_EARLY, N_BLOCK):
         n = last if b == N_BLOCK - 1 else size
         x_copy(b, n).wait_recv()
         add_into(part(from_x, b, n), part(s_buf, b, n), 24)
@@ -1039,15 +1201,14 @@
         for k in range(NZ):
             if b in W_REDUCE[k]:
                 pl.when(z == k)(functools.partial(w_reduce, k, W_REDUCE[k][b]))
-        if b == 7:
+        if b == 9:
             w_copy_x.start()
-            every(chip_sum, EARLY, N_BLOCK)
-        if b == 8:
+            every(chip_sum, AHEAD, N_BLOCK)
+        if b == 10:
             w_copy_x.wait()
             add_into(total, w_x)
             w_copy_c.start()
             w_store.start()
-        if b == 9:
             w_copy_c.wait_send()
             remote(total, w_out.at[1 - core], last_send.at[1], last_recv.at[1], tp, twin).wait_recv()
             w_store.wait()
@@ -1073,36 +1234,39 @@
     on_position(w_done)
 
     def drain(b, n):
-        c_copy(b, n).wait_send()
-        x_copy(b, n).wait_send()
         t_copy(b, n).wait_send()
         t_store(b, n).wait()
         remote(part(from_x, b, n), t_ref.at[rows(1 - core, b, n), :], g_send_t.at[b], g_recv_t.at[b], tp, twin).wait_recv()
 
+    def sent(b, n):
+        c_copy(b, n).wait_send()
+        x_copy(b, n).wait_send()
+
     every(drain, 0, N_BLOCK)
-
-
-def tail(g_table, g_rows, look_rows, look_ids, collective_id):
+    every(sent, N_EARLY, N_BLOCK)
+
+
+def tail(g_table, g_rows, look_rows, look_ids, early, collective_id):
     vocab, width = g_table.shape
     rows = g_rows.shape[1]
     half = (rows // 2, width)
-    n_look = look_ids.shape[1]
-    size = -(-vocab // (2 * N_BLOCK * 24)) * 24
-    blocks = pltpu.VMEM((N_BLOCK, size, width), F32)
+    n_look = look_ids.shape[2]
+    size = table_block(vocab)
+    blocks = lambda n: pltpu.VMEM((n, size, width), F32)
     dma = lambda *n: pltpu.SemaphoreType.DMA(n)
     t, w_sum, small = pl.pallas_call(
         tail_kernel,
         out_shape=(jax.ShapeDtypeStruct((vocab, width), F32), jax.ShapeDtypeStruct((2,) + half, F32), jax.ShapeDtypeStruct((2 * NZ, 24, width), F32)),
-        in_specs=[ANY, ANY, VMEM, VMEM],
+        in_specs=[ANY, ANY, ANY, VMEM, ANY],
         out_specs=(ANY,) * 3,
-        scratch_shapes=[blocks] * 3 + [pltpu.VMEM((n_look, width), F32), pltpu.VMEM((1, n_look), jnp.int32), pltpu.VMEM((3, 2 * n_look, width), BF16)]
+        scratch_shapes=[blocks(N_BLOCK - N_EARLY)] * 2 + [blocks(N_BLOCK), pltpu.VMEM((2, n_look, width), F32), pltpu.VMEM((3, 4 * n_look, width), BF16)]
         + [pltpu.VMEM((2 * NZ,) + half, F32)] * 2 + [pltpu.VMEM((NZ,) + half, F32)] + [pltpu.VMEM((NZ - 1,) + half, F32)] * 2
         + [pltpu.VMEM(half, F32)]
-        + [dma(N_BLOCK)] * 8 + [dma(2)] * 2
+        + [dma(N_BLOCK)] * 8 + [dma(2)]
         + [dma(2 * NZ), pltpu.SemaphoreType.DMA] + [dma(2 * NZ), dma(NZ), dma(NZ), dma(NZ)] * 2 + [dma(2)] * 2 + [dma(2 * NZ)] * 2,
         compiler_params=pltpu.CompilerParams(collective_id=collective_id, has_side_effects=True, vmem_limit_bytes=67000000),
         name="tail",
-    )(g_table, g_rows.reshape((2 * NZ, 2) + half), look_rows.reshape(n_look, width), look_ids)
+    )(g_table, g_rows.reshape((2 * NZ, 2) + half), look_rows.reshape(4, n_look, width), look_ids, early)
     return t, w_sum.reshape(rows, width), small
 
 
@@ -1274,8 +1438,8 @@
         inv_freq = ROPE_BASE ** (-jnp.arange(0, head_dim, 2).astype(F32) / head_dim)
         angles = inv_freq[:, None] * (half * own + jnp.arange(own)).astype(F32)[None, :]
         cos_t, sin_t = jnp.cos(angles), jnp.sin(angles)
-        f_own, x_one, x_zero, *saved = front(ids_first, embed, pick_first, more_rows, w_rows, wkv_t, ln_scales, cos_t, sin_t, n_tp * q_loc, 0)
-        saved, (wq_t, wo_b, wg_t, wu_t, wd_b) = saved[:5], saved[5:]
+        f_own, x_one, x_zero, *saved = front(ids_first, embed, jnp.broadcast_to(rounds, (1, 128)), pick_first, more_rows, w_rows, wkv_t, ln_scales, cos_t, sin_t, n_tp * q_loc, 0)
+        saved, (wq_t, wo_b, wg_t, wu_t, wd_b), rounds_all = saved[:5], saved[5:10], jnp.max(saved[10])
         weights = (wq_t, wkv_t, wo_b, wg_t, wu_t, wd_b)
 
         logit_scale = d_model ** -0.5
@@ -1283,20 +1447,25 @@
         d_fin, g_head_part, log_norm, lab_sum, _ = head(f_own, lab_loc, embed, logit_scale, logit_scale / tok_total, 4)
         log_norm = lax.dynamic_index_in_dim(log_norm, tp_rank, 0, keepdims=False)
         loss_row = (log_norm + LOGIT_ZLOSS * log_norm * log_norm - jnp.sum(lab_sum, axis=0) * logit_scale) / tok_total
-        g_rows, d_zero, rows_back = layer_bwd(d_fin, x_zero, x_one, loss_row[None, :], ln_scales, cos_t, sin_t, weights, saved, pick_first, 7)
-
         def row_ids(step):
             here = (shard[:, None, :] == tp_rank) & (rank[:, None, :] == slots[None, :, None] + step * CAP)
             return jnp.where(jnp.any(here, axis=-1), jnp.sum(jnp.where(here, row[:, None, :], 0), axis=-1), vocab_loc).reshape(-1)
+
+        g_rows, d_zero, rows_back, early, ids_back = layer_bwd(d_fin, x_zero, x_one, loss_row[None, :], ln_scales, cos_t, sin_t, weights, saved,
+                                                               pick_first, g_head_part, row_ids(0)[None, :], 7)
+        g_table, g_shard, g_small = tail(g_head_part, g_rows, rows_back, ids_back, early, 10)
 
         def give_back(state):
             mine = (my_shard[None, None, :] == jnp.arange(n_tp)[:, None, None]) & (my_rank[None, None, :] == slots[None, :, None] + state[0] * CAP)
             ids = jnp.sum(jnp.where(mine, jnp.arange(own)[None, None, :], 0), axis=-1).reshape(-1)
             rows_in = plane_swap(jnp.take(d_zero, ids, axis=0).reshape(n_tp, CAP, d_model), 9).reshape(-1, d_model)
-            return state[0] + 1, state[1].at[row_ids(state[0])].add(rows_in, mode='drop')
-
-        g_table = lax.while_loop(lambda state: state[0] < rounds, give_back, (jnp.int32(1), g_head_part))[1]
-        g_table, g_shard, g_small = tail(g_table, g_rows, rows_back, row_ids(0)[None, :], 10)
+            n_rows = n_tp * CAP
+            id_rows = jnp.pad(row_ids(state[0]).astype(F32), (0, -n_rows % (8 * d_model))).reshape(-1, d_model)
+            both = group_gather(jnp.concatenate([rows_in, id_rows], axis=0), 11)
+            ids = both[:, n_rows:].reshape(n_dp, -1)[:, :n_rows].astype(jnp.int32)
+            return state[0] + 1, state[1].at[ids.reshape(-1)].add(both[:, :n_rows].reshape(-1, d_model), mode='drop')
+
+        g_table = lax.while_loop(lambda state: state[0] < rounds_all, give_back, (jnp.int32(1), g_table))[1]
         *new, loss = update(g_table, g_shard, g_small, state_arrays)
         return tuple(new) + (loss.reshape(()),)
 

time: 616 us -> 616 us (level)
    pallas_call x1, Pallas kernels: 188 us -> 155 us  [tail(): pl.pallas_call(tail_kernel, out_shape=(jax.ShapeDtypeStruct((vocab, width...]
    pallas_call x1, Pallas kernels: 69.9 us -> 99 us  [layer_bwd(): pl.pallas_call(layer_bwd_kernel, out_shape=(jax.ShapeDtypeStruct((2 * NZ,...]
where the time goes in v10:
time: 616 us; the launch traced here: 608 us
  Pallas kernels  590 us (96%)
  other arithmetic  9.89 us (2%)
    pallas_call x1, Pallas kernels, head(): pl.pallas_call(functools.partial(head_kernel, scale, token_scale), out_sh...  201 us
    pallas_call x1, Pallas kernels, tail(): pl.pallas_call(tail_kernel, out_shape=(jax.ShapeDtypeStruct((vocab, width...  155 us
    pallas_call x1, Pallas kernels, layer_bwd(): pl.pallas_call(layer_bwd_kernel, out_shape=(jax.ShapeDtypeStruct((2 * NZ,...  99 us
    pallas_call x1, Pallas kernels, front(): pl.pallas_call(front_kernel, out_shape=(s((own, width), F32),) * 3 + (s((...  98.2 us
    pallas_call x1, Pallas kernels, update(): pl.pallas_call(update_kernel, out_shape=tuple((jax.ShapeDtypeStruct(a.sha...  36.6 us

profile of v10, /device:TPU:0, one launch (start us, length us, event | category | flops | bytes accessed | tf_op | source)
XLA Modules:
  0.0 608.2 jit_solution(4480817760014275745)
XLA Ops:
  0.7 0.7 broadcast_subtract_fusion
  1.4 0.6 sub.38.lab_ref
  2.0 0.7 reshape.530
  2.8 0.2 convert_reduce_fusion
  3.0 0.6 reduce_max.18
  4.3 0.5 broadcast_in_dim.130.rounds_ref
  4.9 0.3 fusion.22
  5.1 0.0 copy-start
  5.2 0.3 fusion.20
  5.5 0.4 select_reduce_fusion.3
  5.9 0.7 select_n.155.ids_ref
  6.6 0.7 reshape.531.ids_ref
  7.3 1.0 multiply_sine_fusion
  8.3 1.6 bitcast_convert_fusion
  9.9 0.1 and_convert_fusion
  10.0 0.0 copy-start.2
  10.1 0.0 copy-start.3
  10.1 0.0 copy-start.4
  10.1 1.2 copy.50.pick_ref
  11.2 0.0 copy-done
  11.2 0.3 copy.49
  11.6 0.0 copy-done.2
  11.6 0.0 copy-done.3
  11.6 0.0 copy-done.4
  11.6 1.4 pad_maximum_fusion.1.w_ref
  13.0 0.1 broadcast_in_dim.131
  13.1 0.0 copy-start.1
  13.1 98.2 %front.1 = (f32[512,512]{1,0:T(8,128)}, f32[512,512]{1,0:T(8,128)}, f32[512,512]{1,0:T(8,128)}, bf16[512,512]{1,0:T(8,128)(2,1)}, bf16[1024,128]{1,0:T(8,128)(2,...) custom-call(s32[768]{0:T(1024)} %reshape.531.ids_ref, ...), custom_call_target="tpu_custom_call" | custom-call | tf_op jit(solution)/shard_map/front/pallas_call | solution.py:771
  111.3 0.0 copy-done.1
  111.3 1.3 reduce_max.19
  112.7 201.4 %head.1 = (f32[512,512]{1,0:T(8,128)}, f32[6288,512]{1,0:T(8,128)}, f32[8,512]{1,0:T(8,128)}, f32[8,512]{1,0:T(8,128)}, f32[8,6288,512]{2,1,0:T(8,128)}) custom-call(f32[512,512]{1,0:T(8,128)} %get-tuple-element.269.f_ref, s32[8,512]{1,0:T(8,128)} %sub.38.lab_ref, f32[6288,512]{1,0:T(8,128)} %get-tuple-element.615), custom_call_target="tpu_custom_call" | custom-call | flops 105495134208 | bytes 38633472 | tf_op jit(solution)/shard_map/head/pallas_call | solution.py:483
  314.0 0.7 reduce_sum.76
  314.8 1.3 fusion.28.loss_ref
  316.1 99.0 %layer_bwd.1 = (f32[8,928,512]{2,1,0:T(8,128)}, f32[512,512]{1,0:T(8,128)}, f32[4,8,96,512]{3,2,1,0:T(8,128)}, f32[3,264,512]{2,1,0:T(8,128)}, s32[4,1,768]{2,1,0:T(1,128)}) custom-call(f32[512,512]{1,0:T(8,128)} %get-tuple-element.271.dfin_ref, f32[512,512]{1,0:T(8,128)} %get-tuple-element.272.x0_ref, f32[512,512]{1,0:T(8,128)} %get-tuple-element.273.x1_ref, ...), custom_call_target="tpu_custom_call" | custom-call | tf_op jit(solution)/shard_map/layer_bwd/pallas_call | solution.py:1006
  415.1 155.0 %tail.1 = (f32[6288,512]{1,0:T(8,128)}, f32[2,464,512]{2,1,0:T(8,128)}, f32[8,24,512]{2,1,0:T(8,128)}) custom-call(f32[6288,512]{1,0:T(8,128)} %get-tuple-element.270.g_ref, f32[8,2,464,512]{3,2,1,0:T(8,128)} %bitcast.74, f32[4,768,512]{2,1,0:T(8,128)} %bitcast.75, s32[4,1,768]{2,1,0:T(1,128)} %get-tuple-element.288.ids_ref, ...), custom_call_target="tpu_custom_call" | custom-call | tf_op jit(solution)/shard_map/tail/pallas_call | solution.py:1257
  570.1 0.9 while.25
  571.1 36.6 %update.1 = (f32[6288,512]{1,0:T(8,128)}, f32[2,512]{1,0:T(2,128)}, f32[64,512]{1,0:T(8,128)}, f32[2,64,512]{2,1,0:T(8,128)}, f32[64,512]{1,0:T(8,128)}, /*index...) custom-call(f32[6288,512]{1,0:T(8,128)} %get-tuple-element.293.t_ref, ...), custom_call_target="tpu_custom_call" | custom-call | tf_op jit(solution)/shard_map/update/pallas_call | solution.py:1349
  (11 shorter events, 0.1 us)
Async XLA Ops:
  5.1 6.1 %copy-start = (f32[2,512,256]{2,1,0:T(8,128)S(1)}, f32[2,512,256]{2,1,0:T(8,128)}, u32[]{:S(2)}) copy-start(f32[2,512,256]{2,1,0:T(8,128)} %refs_5_.1) | copy-start | bytes 3145732
  10.0 1.5 copy-start.2
  10.1 1.5 copy-start.3
  10.1 1.5 copy-start.4
  13.1 98.2 %copy-start.1 = (s32[8,512]{1,0:T(8,128)}, s32[8,512]{1,0:T(8,128)S(1)}, u32[]{:S(2)}) copy-start(s32[8,512]{1,0:T(8,128)S(1)} %get-tuple-element.618) | copy-start | bytes 49156

commit v11 on v10

--- a/solution.py
+++ b/solution.py
@@ -406,7 +406,7 @@
         norm = norm_ref[pl.ds(slot, 1), :]
         shift = norm * log2e
         coef = (1.0 + 2.0 * LOGIT_ZLOSS * norm) * token_scale
-        lab = lab_ref[pl.ds(slot, 1), :]
+        lab = lab_ref[pl.ds(slot, 1), :] - tp * vocab
         acc[...] = jnp.zeros((width, own), F32)
 
         def group(base, parts, kept, hits):
@@ -508,6 +508,10 @@
     return lax.dot_general(a, b, dims, preferred_element_type=F32)
 
 
+def picks(code, n_slots):
+    return (lax.broadcasted_iota(jnp.int32, (n_slots, code.shape[1]), 0) == code).astype(F32).astype(BF16)
+
+
 def turn(lo, hi, cos_t, sin_t):
     return lo * cos_t - hi * sin_t, hi * cos_t + lo * sin_t
 
@@ -521,7 +525,7 @@
 MLP_ORDER = {k: [2 * k] + [code for line, other in EVENTS[k] for code in [2 * zz for _, zz in line] + [2 * zz + 1 for zz in other]] for k in range(NZ)}
 
 
-def front_kernel(ids_ref, e_ref, rounds_ref, pick_ref, extra_ref, w_ref, wkv_ref, ln_ref, cos_ref, sin_ref,
+def front_kernel(ids_ref, e_ref, rounds_ref, code_ref, extra_ref, w_ref, wkv_ref, ln_ref, cos_ref, sin_ref,
                  f_ref, x1_ref, x0_ref, q_ref, kv_ref, kvt_ref, lse_ref, ctx_ref, wq_ref, wo_ref, wg_ref, wu_ref, wd_ref, rounds_all,
                  table, rows_ref, wl, rows_in, u_b, kv_out, kv_in, own_sem, r_send, r_recv, a_y, a_l, a_r, a_c, a_recv,
                  b_y, b_l, b_r, b_x, b_c, b_recv, kv_send, kv_recv, n_send, n_recv):
@@ -642,17 +646,18 @@
         return carry
 
     lax.fori_loop(0, shards * cap // 8, pick_rows, 0)
-    on_position(functools.partial(b_event, 0))
-    on_position(functools.partial(a_event, 0))
     start([row_copy(to) for to in peers])
     own_rows = pltpu.make_async_copy(rows_ref.at[tp], rows_in.at[tp], own_sem.at[0])
     own_rows.start()
+    on_position(functools.partial(b_event, 0))
+    on_position(functools.partial(a_event, 0))
     on_position(functools.partial(b_event, 1))
     on_position(functools.partial(a_event, 1))
     own_rows.wait()
     for source in peers:
         remote(rows_ref.at[source], rows_in.at[source], r_send.at[source], r_recv.at[source], source, dp).wait_recv()
-    x0_ref[...] = extra_ref[...] + mm(pick_ref[...], rows_in[...].reshape(pick_ref.shape[1], width).astype(BF16))
+    n_slots = shards * cap
+    x0_ref[...] = extra_ref[...] + mm(picks(code_ref[...], n_slots), rows_in[...].reshape(n_slots, width).astype(BF16), TA)
     u_b[...] = norm_fwd(x0_ref[...], ln_ref[0:1, :])[0]
     x1_ref[...] = x0_ref[...]
     cos_t = cos_ref[...]
@@ -760,7 +765,7 @@
         b_copy(to, facing, b_c.at[1], tp, twin).wait_send()
 
 
-def front(ids, embed, rounds, pick, extra, w_rows, wkv_t, ln, cos_t, sin_t, n_q, collective_id):
+def front(ids, embed, rounds, code, extra, w_rows, wkv_t, ln, cos_t, sin_t, n_q, collective_id):
     own, width = extra.shape
     two_hd = wkv_t.shape[0]
     shards = 2 * NZ
@@ -781,11 +786,11 @@
         + [dma(shards)] * 4 + [dma(2, shards), dma(shards, 4), pltpu.SemaphoreType.DMA, pltpu.SemaphoreType.DMA, dma(3), dma(4)],
         compiler_params=pltpu.CompilerParams(collective_id=collective_id, has_side_effects=True, vmem_limit_bytes=60000000),
         name="front",
-    )(ids, embed, rounds, pick, extra, w_rows, wkv_t, ln, cos_t, sin_t)
+    )(ids, embed, rounds, code, extra, w_rows, wkv_t, ln, cos_t, sin_t)
 
 
 def layer_bwd_kernel(dfin_ref, x0_ref, x1_ref, loss_ref, ln_ref, cos_ref, sin_ref, wq_ref, wkv_ref, wo_ref, wg_ref, wu_ref, wd_ref,
-                     q_ref, kv_ref, kvt_ref, lse_ref, ctx_ref, pick_ref, g_ref, ids_ref, rows_ref, d0_ref, back_ref, early_ref, ids_all, d_one, d_b, u_b, dctx, dq, dkv, dkv_in,
+                     q_ref, kv_ref, kvt_ref, lse_ref, ctx_ref, code_ref, g_ref, ids_ref, rows_ref, d0_ref, back_ref, early_ref, ids_all, d_one, d_b, u_b, dctx, dq, dkv, dkv_in,
                      hid, d_gate, d_up, rows_out, g_q, g_o, g_g, g_u, g_d, small, s_early, c_early, out_sem, send_sem, recv_sem,
                      r_send, x_send, c_send, r_recv, g_load, g_send, g_recv, id_send, id_recv):
     tp, dp, z, y = place()
@@ -894,7 +899,8 @@
     left = d_zero - high.astype(F32)
     middle = left.astype(BF16)
     low = (left - middle.astype(F32)).astype(BF16)
-    rows_out[...] = (mm(pick_ref[...], high, TA) + mm(pick_ref[...], middle, TA) + mm(pick_ref[...], low, TA)).reshape(rows_out.shape)
+    pick = picks(code_ref[...], rows_out.shape[0] * rows_out.shape[1])
+    rows_out[...] = (mm(pick, high) + mm(pick, middle) + mm(pick, low)).reshape(rows_out.shape)
 
     def row_copy(to):
         return remote(rows_out.at[to], back_ref.at[dp, tp], r_send.at[to], r_recv.at[dp, tp], to, dp)
@@ -919,7 +925,7 @@
             pl.when(z == k)(functools.partial(f, k))
 
     def rows_leave(k):
-        for c in near_first(k)[:0:-1]:
+        for c in near_first(k)[1:]:
             row_copy(slot_of(*c)).start()
 
     on_position(rows_leave)
@@ -993,14 +999,14 @@
         g_x_copy(b).wait_send()
 
 
-def layer_bwd(d_fin, x0, x1, loss_row, ln, cos_t, sin_t, weights, saved, pick, g_table, ids, collective_id):
+def layer_bwd(d_fin, x0, x1, loss_row, ln, cos_t, sin_t, weights, saved, code, g_table, ids, collective_id):
     own, width = x0.shape
     nq = weights[0].shape[0]
     two_hd = weights[1].shape[0]
     ff = weights[3].shape[0]
     rows = (2 * nq + 3 * ff + two_hd) // (2 * NZ) + 16
     chunk = (own, width)
-    back = (2 * NZ, pick.shape[1] // (2 * NZ), width)
+    back = (2 * NZ, ids.shape[1] // (2 * NZ), width)
     blocks = (N_EARLY, table_block(g_table.shape[0]), width)
     dma = lambda *n: pltpu.SemaphoreType.DMA(n)
     return pl.pallas_call(
@@ -1017,7 +1023,7 @@
            dma(N_EARLY), dma(2, N_EARLY), dma(2, N_EARLY), dma(3), dma(4)],
         compiler_params=pltpu.CompilerParams(collective_id=collective_id, has_side_effects=True, vmem_limit_bytes=66000000),
         name="layer_bwd",
-    )(d_fin, x0, x1, loss_row, ln, cos_t, sin_t, *weights, *saved, pick, g_table, ids)
+    )(d_fin, x0, x1, loss_row, ln, cos_t, sin_t, *weights, *saved, code, g_table, ids)
 
 
 N_BLOCK = 12
@@ -1273,13 +1279,14 @@
 UPDATE_ROWS = 512
 
 
-def update_kernel(t_ref, w_ref, small_ref, *refs):
+def update_kernel(t_ref, w_any, small_any, *refs):
     state = [refs[7 * i:7 * i + 7] for i in range(3)]
     new = [refs[21 + 7 * i:28 + 7 * i] for i in range(3)]
-    loss_ref = refs[42]
-    held, made, in_sem, out_sem = refs[43:]
+    loss_ref, held, made, w_ref, small_ref = refs[42:47]
+    old_small = [refs[47 + 6 * i:53 + 6 * i] for i in range(3)]
+    new_small = [refs[65 + 6 * i:71 + 6 * i] for i in range(3)]
+    in_sem, out_sem, g_sem, small_in, small_out = refs[83:]
     vocab = t_ref.shape[0]
-    n_kv, hd = 2 * state[0][3].shape[1] // small_ref.shape[0], state[0][3].shape[1]
     blocks = [(at, min(UPDATE_ROWS, vocab - at)) for at in range(0, vocab, UPDATE_ROWS)]
 
     def loads(q):
@@ -1294,23 +1301,32 @@
     for q in range(3):
         for c in loads(q):
             c.start()
+    grads = [pltpu.make_async_copy(w_any, w_ref, g_sem.at[0]), pltpu.make_async_copy(small_any, small_ref, g_sem.at[1])]
+    pairs = [(i, j) for i in range(3) for j in range(6)]
+    small_loads = grads + [pltpu.make_async_copy(state[i][j + 1], old_small[i][j], small_in.at[i, j]) for i, j in pairs]
+    small_stores = [pltpu.make_async_copy(new_small[i][j], new[i][j + 1], small_out.at[i, j]) for i, j in pairs]
+    for c in small_loads:
+        c.start()
 
     def small_update(index, grad, *where):
-        got = adam_update(state[0][index][where], grad, state[1][index][where], state[2][index][where])
+        got = adam_update(old_small[0][index - 1][where], grad, old_small[1][index - 1][where], old_small[2][index - 1][where])
         for i in range(3):
-            new[i][index][where] = got[i]
-
-    n_q, n_f = state[0][2].shape[0], state[0][6].shape[0]
-    small_update(1, small_ref[0, n_kv:n_kv + 2, :], Ellipsis)
-    small_update(2, w_ref[0:n_q, :], Ellipsis)
-    kv = small_ref[:, 0:n_kv, :].reshape(2 * hd, small_ref.shape[2])
-    for i in range(2):
-        small_update(3, kv[i * hd:(i + 1) * hd], i)
-    small_update(4, w_ref[n_q:2 * n_q, :], Ellipsis)
-    for i in range(2):
-        small_update(5, w_ref[2 * n_q + i * n_f:2 * n_q + (i + 1) * n_f, :].T, i)
-    small_update(6, w_ref[2 * n_q + 2 * n_f:2 * n_q + 3 * n_f, :], Ellipsis)
-    loss_ref[...] = jnp.sum(small_ref[0, n_kv + 2:n_kv + 3, :], axis=1, keepdims=True)
+            new_small[i][index - 1][where] = got[i]
+
+    def small_updates():
+        hd = old_small[0][2].shape[1]
+        n_kv = 2 * hd // small_ref.shape[0]
+        n_q, n_f = old_small[0][1].shape[0], old_small[0][5].shape[0]
+        small_update(1, small_ref[0, n_kv:n_kv + 2, :], Ellipsis)
+        small_update(2, w_ref[0:n_q, :], Ellipsis)
+        kv = small_ref[:, 0:n_kv, :].reshape(2 * hd, small_ref.shape[2])
+        for i in range(2):
+            small_update(3, kv[i * hd:(i + 1) * hd], i)
+        small_update(4, w_ref[n_q:2 * n_q, :], Ellipsis)
+        for i in range(2):
+            small_update(5, w_ref[2 * n_q + i * n_f:2 * n_q + (i + 1) * n_f, :].T, i)
+        small_update(6, w_ref[2 * n_q + 2 * n_f:2 * n_q + 3 * n_f, :], Ellipsis)
+        loss_ref[...] = jnp.sum(small_ref[0, n_kv + 2:n_kv + 3, :], axis=1, keepdims=True)
 
     for q, (at, n) in enumerate(blocks):
         for c in loads(q):
@@ -1333,26 +1349,36 @@
         if q + 3 < len(blocks):
             for c in loads(q + 3):
                 c.start()
+        if q == min(3, len(blocks) - 1):
+            for c in small_loads:
+                c.wait()
+            small_updates()
+            for c in small_stores:
+                c.start()
     for q in range(len(blocks) - 2, len(blocks)):
         for c in stores(q):
             c.wait()
+    for c in small_stores:
+        c.wait()
 
 
 def update(g_table, g_shard, g_small, state_arrays):
-    specs = [ANY] + [VMEM] * 6
     width = g_table.shape[1]
+    dma = lambda *n: pltpu.SemaphoreType.DMA(n)
 
     def flip(arrays):
         return [a.swapaxes(-1, -2) if i % 7 in (2, 3) else a for i, a in enumerate(arrays)]
 
     given = flip(state_arrays)
+    small = [pltpu.VMEM(a.shape, F32) for i, a in enumerate(given) if i % 7]
     *new, loss = pl.pallas_call(
         update_kernel,
         out_shape=tuple(jax.ShapeDtypeStruct(a.shape, F32) for a in given) + (jax.ShapeDtypeStruct((1, 1), F32),),
-        in_specs=[ANY, VMEM, VMEM] + specs * 3,
-        out_specs=tuple(specs * 3) + (VMEM,),
+        in_specs=[ANY] * 24,
+        out_specs=(ANY,) * 21 + (VMEM,),
         scratch_shapes=[pltpu.VMEM((3, 4, UPDATE_ROWS, width), F32), pltpu.VMEM((2, 3, UPDATE_ROWS, width), F32),
-                        pltpu.SemaphoreType.DMA((3, 4)), pltpu.SemaphoreType.DMA((2, 3))],
+                        pltpu.VMEM(g_shard.shape, F32), pltpu.VMEM(g_small.shape, F32)] + small * 2
+        + [dma(3, 4), dma(2, 3), dma(2), dma(3, 6), dma(3, 6)],
         compiler_params=pltpu.CompilerParams(vmem_limit_bytes=60000000),
         name="update",
     )(g_table, g_shard, g_small, *given)
@@ -1421,16 +1447,18 @@
         def fetch(step):
             here = (shard[:, None, :] == tp_rank) & (rank[:, None, :] == slots[None, :, None] + step * CAP)
             ids = jnp.sum(jnp.where(here, row[:, None, :], 0), axis=-1).reshape(-1)
-            pick = (my_shard[:, None, None] == jnp.arange(n_tp)[None, :, None]) & (my_rank[:, None, None] == slots[None, None, :] + step * CAP)
-            return ids, pick.reshape(own, n_tp * CAP).astype(BF16)
+            place = my_rank - step * CAP
+            return ids, jnp.where((place >= 0) & (place < CAP), my_shard * CAP + place, -1)
 
         def fetch_more(state):
-            ids, pick = fetch(state[0])
+            ids, code = fetch(state[0])
+            pick = (code[:, None] == jnp.arange(n_tp * CAP)[None, :]).astype(BF16)
             rows_in = plane_swap(jnp.take(embed, ids, axis=0).reshape(n_tp, CAP, d_model), 1).reshape(n_tp * CAP, d_model).astype(BF16)
             return state[0] + 1, state[1] + dot('rc,cd->rd', pick, rows_in)
 
         more_rows = lax.while_loop(lambda state: state[0] < rounds, fetch_more, (jnp.int32(1), jnp.zeros((own, d_model), F32)))[1]
-        ids_first, pick_first = fetch(0)
+        ids_first, code_first = fetch(0)
+        code_first = code_first[None, :]
 
         w_rows = jnp.concatenate([w_q.T, w_o, w_gu.transpose(0, 2, 1).reshape(2 * f_loc, d_model), w_down], axis=0)
         cuts = (q_loc, 2 * q_loc, 2 * q_loc + f_loc, 2 * q_loc + 2 * f_loc)
@@ -1438,13 +1466,12 @@
         inv_freq = ROPE_BASE ** (-jnp.arange(0, head_dim, 2).astype(F32) / head_dim)
         angles = inv_freq[:, None] * (half * own + jnp.arange(own)).astype(F32)[None, :]
         cos_t, sin_t = jnp.cos(angles), jnp.sin(angles)
-        f_own, x_one, x_zero, *saved = front(ids_first, embed, jnp.broadcast_to(rounds, (1, 128)), pick_first, more_rows, w_rows, wkv_t, ln_scales, cos_t, sin_t, n_tp * q_loc, 0)
+        f_own, x_one, x_zero, *saved = front(ids_first, embed, jnp.broadcast_to(rounds, (1, 128)), code_first, more_rows, w_rows, wkv_t, ln_scales, cos_t, sin_t, n_tp * q_loc, 0)
         saved, (wq_t, wo_b, wg_t, wu_t, wd_b), rounds_all = saved[:5], saved[5:10], jnp.max(saved[10])
         weights = (wq_t, wkv_t, wo_b, wg_t, wu_t, wd_b)
 
         logit_scale = d_model ** -0.5
-        lab_loc = labels.reshape(n_tp, own) - tp_rank * vocab_loc
-        d_fin, g_head_part, log_norm, lab_sum, _ = head(f_own, lab_loc, embed, logit_scale, logit_scale / tok_total, 4)
+        d_fin, g_head_part, log_norm, lab_sum, _ = head(f_own, labels.reshape(n_tp, own), embed, logit_scale, logit_scale / tok_total, 4)
         log_norm = lax.dynamic_index_in_dim(log_norm, tp_rank, 0, keepdims=False)
         loss_row = (log_norm + LOGIT_ZLOSS * log_norm * log_norm - jnp.sum(lab_sum, axis=0) * logit_scale) / tok_total
         def row_ids(step):
@@ -1452,7 +1479,7 @@
             return jnp.where(jnp.any(here, axis=-1), jnp.sum(jnp.where(here, row[:, None, :], 0), axis=-1), vocab_loc).reshape(-1)
 
         g_rows, d_zero, rows_back, early, ids_back = layer_bwd(d_fin, x_zero, x_one, loss_row[None, :], ln_scales, cos_t, sin_t, weights, saved,
-                                                               pick_first, g_head_part, row_ids(0)[None, :], 7)
+                                                               code_first, g_head_part, row_ids(0)[None, :], 7)
         g_table, g_shard, g_small = tail(g_head_part, g_rows, rows_back, ids_back, early, 10)
 
         def give_back(state):

time: 616 us -> 603 us (0.979)
  Pallas kernels: 590 us -> 579 us
    pallas_call x1, Pallas kernels: 155 us -> 141 us  [tail(): pl.pallas_call(tail_kernel, out_shape=(jax.ShapeDtypeStruct((vocab, width...]
    pallas_call x1, Pallas kernels: 201 us -> 195 us  [head(): pl.pallas_call(functools.partial(head_kernel, scale, token_scale), out_sh...]
where the time goes in v11:
time: 603 us; the launch traced here: 596 us
  Pallas kernels  579 us (96%)
  other arithmetic  9.56 us (2%)
    pallas_call x1, Pallas kernels, head(): pl.pallas_call(functools.partial(head_kernel, scale, token_scale), out_sh...  195 us
    pallas_call x1, Pallas kernels, tail(): pl.pallas_call(tail_kernel, out_shape=(jax.ShapeDtypeStruct((vocab, width...  141 us
    pallas_call x1, Pallas kernels, layer_bwd(): pl.pallas_call(layer_bwd_kernel, out_shape=(jax.ShapeDtypeStruct((2 * NZ,...  104 us
    pallas_call x1, Pallas kernels, front(): pl.pallas_call(front_kernel, out_shape=(s((own, width), F32),) * 3 + (s((...  104 us
    pallas_call x1, Pallas kernels, update(): pl.pallas_call(update_kernel, out_shape=tuple((jax.ShapeDtypeStruct(a.sha...  35.2 us

profile of v11, /device:TPU:0, one launch (start us, length us, event | category | flops | bytes accessed | tf_op | source)
XLA Modules:
  0.0 595.9 jit_solution(9657713523697920956)
XLA Ops:
  0.7 0.0 copy-start
  0.7 0.8 reshape.419
  1.5 1.3 reshape.422.lab_ref
  2.9 0.2 convert_reduce_fusion
  3.1 0.6 reduce_max.18
  4.4 0.5 broadcast_in_dim.133.rounds_ref
  4.9 0.0 copy-start.2
  4.9 0.0 copy-start.3
  4.9 0.0 copy-start.4
  4.9 0.3 fusion.14
  5.2 0.3 fusion.12
  5.6 0.4 select_reduce_fusion.3
  6.0 0.7 select_n.169.ids_ref
  6.6 0.7 reshape.420.ids_ref
  7.3 0.6 and_select_fusion
  7.9 1.0 multiply_sine_fusion
  8.9 1.6 bitcast_convert_fusion
  10.5 0.0 copy-done
  10.5 0.3 copy.46
  10.8 0.0 copy-done.2
  10.8 0.0 copy-done.3
  10.8 0.0 copy-done.4
  10.8 1.4 pad_maximum_fusion.1.w_ref
  12.2 0.1 broadcast_in_dim.135
  12.4 0.0 copy-start.1
  12.4 103.9 %front.1 = (f32[512,512]{1,0:T(8,128)}, f32[512,512]{1,0:T(8,128)}, f32[512,512]{1,0:T(8,128)}, bf16[512,512]{1,0:T(8,128)(2,1)}, bf16[1024,128]{1,0:T(8,128)(2,...) custom-call(s32[768]{0:T(1024)} %reshape.420.ids_ref, ...), custom_call_target="tpu_custom_call" | custom-call | tf_op jit(solution)/shard_map/front/pallas_call | solution.py:776
  116.3 0.0 copy-done.1
  116.3 1.3 reduce_max.19
  117.6 194.7 %head.1 = (f32[512,512]{1,0:T(8,128)}, f32[6288,512]{1,0:T(8,128)}, f32[8,512]{1,0:T(8,128)}, f32[8,512]{1,0:T(8,128)}, f32[8,6288,512]{2,1,0:T(8,128)}) custom-call(f32[512,512]{1,0:T(8,128)} %get-tuple-element.269.f_ref, s32[8,512]{1,0:T(8,128)} %reshape.422.lab_ref, f32[6288,512]{1,0:T(8,128)} %get-tuple-element.616), custom_call_target="tpu_custom_call" | custom-call | flops 105495134208 | bytes 38633472 | tf_op jit(solution)/shard_map/head/pallas_call | solution.py:483
  312.3 0.7 reduce_sum.76
  313.1 1.3 fusion.20.loss_ref
  314.4 104.2 %layer_bwd.1 = (f32[8,928,512]{2,1,0:T(8,128)}, f32[512,512]{1,0:T(8,128)}, f32[4,8,96,512]{3,2,1,0:T(8,128)}, f32[3,264,512]{2,1,0:T(8,128)}, s32[4,1,768]{2,1,0:T(1,128)}) custom-call(f32[512,512]{1,0:T(8,128)} %get-tuple-element.271.dfin_ref, f32[512,512]{1,0:T(8,128)} %get-tuple-element.272.x0_ref, f32[512,512]{1,0:T(8,128)} %get-tuple-element.273.x1_ref, ...), custom_call_target="tpu_custom_call" | custom-call | tf_op jit(solution)/shard_map/layer_bwd/pallas_call | solution.py:1012
  418.6 141.0 %tail.1 = (f32[6288,512]{1,0:T(8,128)}, f32[2,464,512]{2,1,0:T(8,128)}, f32[8,24,512]{2,1,0:T(8,128)}) custom-call(f32[6288,512]{1,0:T(8,128)} %get-tuple-element.270.g_ref, f32[8,2,464,512]{3,2,1,0:T(8,128)} %bitcast.74, f32[4,768,512]{2,1,0:T(8,128)} %bitcast.75, s32[4,1,768]{2,1,0:T(1,128)} %get-tuple-element.288.ids_ref, ...), custom_call_target="tpu_custom_call" | custom-call | tf_op jit(solution)/shard_map/tail/pallas_call | solution.py:1263
  559.6 0.7 while.25
  560.2 35.2 %update.1 = (f32[6288,512]{1,0:T(8,128)}, f32[2,512]{1,0:T(2,128)}, f32[64,512]{1,0:T(8,128)}, f32[2,64,512]{2,1,0:T(8,128)}, f32[64,512]{1,0:T(8,128)}, /*index...) custom-call(f32[6288,512]{1,0:T(8,128)} %get-tuple-element.293.t_ref, ...), custom_call_target="tpu_custom_call" | custom-call | tf_op jit(solution)/shard_map/update/pallas_call | solution.py:1374
  (8 shorter events, 0.1 us)
Async XLA Ops:
  0.7 9.8 %copy-start = (f32[2,512,256]{2,1,0:T(8,128)S(1)}, f32[2,512,256]{2,1,0:T(8,128)}, u32[]{:S(2)}) copy-start(f32[2,512,256]{2,1,0:T(8,128)} %refs_5_.1) | copy-start | bytes 3145732
  4.9 5.9 copy-start.2
  4.9 5.9 copy-start.3
  4.9 5.9 copy-start.4
  12.4 103.9 %copy-start.1 = (s32[8,512]{1,0:T(8,128)}, s32[8,512]{1,0:T(8,128)S(1)}, u32[]{:S(2)}) copy-start(s32[8,512]{1,0:T(8,128)S(1)} %get-tuple-element.619) | copy-start | bytes 49156

commit v12 on v11

--- a/solution.py
+++ b/solution.py
@@ -406,7 +406,7 @@
         norm = norm_ref[pl.ds(slot, 1), :]
         shift = norm * log2e
         coef = (1.0 + 2.0 * LOGIT_ZLOSS * norm) * token_scale
-        lab = lab_ref[pl.ds(slot, 1), :] - tp * vocab
+        lab = lab_ref[pl.ds(slot // 2, 1), pl.ds(pl.multiple_of(lax.rem(slot, 2) * own, own), own)] - tp * vocab
         acc[...] = jnp.zeros((width, own), F32)
 
         def group(base, parts, kept, hits):
@@ -662,7 +662,7 @@
     x1_ref[...] = x0_ref[...]
     cos_t = cos_ref[...]
     sin_t = sin_ref[...]
-    kv = mm(wkv_ref[...], u_b[...], TB)
+    kv = mm(wkv_ref[...].astype(BF16), u_b[...], TB)
     lo, hi = turn(kv[:quarter], kv[quarter:hd], cos_t, sin_t)
     kv_out[0:quarter, :] = lo
     kv_out[quarter:hd, :] = hi
@@ -789,7 +789,7 @@
     )(ids, embed, rounds, code, extra, w_rows, wkv_t, ln, cos_t, sin_t)
 
 
-def layer_bwd_kernel(dfin_ref, x0_ref, x1_ref, loss_ref, ln_ref, cos_ref, sin_ref, wq_ref, wkv_ref, wo_ref, wg_ref, wu_ref, wd_ref,
+def layer_bwd_kernel(scale, tok_total, dfin_ref, x0_ref, x1_ref, norm_ref, hits_ref, ln_ref, cos_ref, sin_ref, wq_ref, wkv_ref, wo_ref, wg_ref, wu_ref, wd_ref,
                      q_ref, kv_ref, kvt_ref, lse_ref, ctx_ref, code_ref, g_ref, ids_ref, rows_ref, d0_ref, back_ref, early_ref, ids_all, d_one, d_b, u_b, dctx, dq, dkv, dkv_in,
                      hid, d_gate, d_up, rows_out, g_q, g_o, g_g, g_u, g_d, small, s_early, c_early, out_sem, send_sem, recv_sem,
                      r_send, x_send, c_send, r_recv, g_load, g_send, g_recv, id_send, id_recv):
@@ -890,7 +890,7 @@
     lo, hi = turn(d_kv[:quarter], d_kv[quarter:hd], cos_t, -sin_t)
     d_kv = jnp.concatenate([lo, hi, d_kv[hd:]], axis=0).astype(BF16)
     small[0:2 * hd, :] = mm(d_kv, u_b[...])
-    d_u = d0_ref[...] + mm(d_kv, wkv_ref[...], TA)
+    d_u = d0_ref[...] + mm(d_kv, wkv_ref[...].astype(BF16), TA)
     _, u_hat, u_inv = norm_fwd(x0_ref[...], ln_ref[0:1, :])
     d_in, g_in = norm_bwd(d_u, u_hat, u_inv, ln_ref[0:1, :])
     d_zero = d_one[...] + d_in
@@ -949,7 +949,9 @@
     small[2 * hd:, :] = jnp.zeros_like(small[2 * hd:, :])
     small[2 * hd:2 * hd + 1, :] = g_in.reshape(1, width)
     small[2 * hd + 1:2 * hd + 2, :] = g_fin.reshape(1, width)
-    small[2 * hd + 2:2 * hd + 3, :] = loss_ref[...]
+    norm = norm_ref[pl.ds(tp, 1), :]
+    hits = jnp.sum(hits_ref[...], axis=0, keepdims=True)
+    small[2 * hd + 2:2 * hd + 3, :] = (norm + LOGIT_ZLOSS * norm * norm - hits * scale) / tok_total
     copies = []
 
     def put(src, first, size, s):
@@ -999,7 +1001,7 @@
         g_x_copy(b).wait_send()
 
 
-def layer_bwd(d_fin, x0, x1, loss_row, ln, cos_t, sin_t, weights, saved, code, g_table, ids, collective_id):
+def layer_bwd(scale, tok_total, d_fin, x0, x1, norms, hits, ln, cos_t, sin_t, weights, saved, code, g_table, ids, collective_id):
     own, width = x0.shape
     nq = weights[0].shape[0]
     two_hd = weights[1].shape[0]
@@ -1010,10 +1012,10 @@
     blocks = (N_EARLY, table_block(g_table.shape[0]), width)
     dma = lambda *n: pltpu.SemaphoreType.DMA(n)
     return pl.pallas_call(
-        layer_bwd_kernel,
+        functools.partial(layer_bwd_kernel, scale, tok_total),
         out_shape=(jax.ShapeDtypeStruct((2 * NZ, rows, width), F32), jax.ShapeDtypeStruct(chunk, F32), jax.ShapeDtypeStruct((4,) + back, F32),
                    jax.ShapeDtypeStruct(blocks, F32), jax.ShapeDtypeStruct((4,) + ids.shape, jnp.int32)),
-        in_specs=[VMEM] * 19 + [ANY, VMEM],
+        in_specs=[VMEM] * 20 + [ANY, VMEM],
         out_specs=(ANY, VMEM, ANY, VMEM, VMEM),
         scratch_shapes=[pltpu.VMEM(chunk, F32), pltpu.VMEM(chunk, BF16), pltpu.VMEM(chunk, BF16), pltpu.VMEM((nq, own), BF16),
                         pltpu.VMEM((nq, own), BF16), pltpu.VMEM((2 * own, two_hd), F32), pltpu.VMEM((own, two_hd), F32)]
@@ -1023,11 +1025,11 @@
            dma(N_EARLY), dma(2, N_EARLY), dma(2, N_EARLY), dma(3), dma(4)],
         compiler_params=pltpu.CompilerParams(collective_id=collective_id, has_side_effects=True, vmem_limit_bytes=66000000),
         name="layer_bwd",
-    )(d_fin, x0, x1, loss_row, ln, cos_t, sin_t, *weights, *saved, code, g_table, ids)
+    )(d_fin, x0, x1, norms, hits, ln, cos_t, sin_t, *weights, *saved, code, g_table, ids)
 
 
 N_BLOCK = 12
-N_EARLY = 3
+N_EARLY = 4
 AHEAD = 11
 
 
@@ -1036,10 +1038,10 @@
 
 
 W_REDUCE = {
-    0: {4: (3,), 6: (2,), 8: (1,), 9: (0,)},
-    1: {6: (3,), 8: (2, 0), 9: (1,)},
-    2: {6: (0,), 8: (1, 3), 9: (2,)},
-    3: {4: (0,), 6: (1,), 8: (2,), 9: (3,)},
+    0: {5: (3,), 7: (2,), 9: (1,), 10: (0,)},
+    1: {7: (3,), 9: (2, 0), 10: (1,)},
+    2: {7: (0,), 9: (1, 3), 10: (2,)},
+    3: {5: (0,), 7: (1,), 9: (2,), 10: (3,)},
 }
 
 
@@ -1200,17 +1202,7 @@
     peers = [lax.rem(tp + n, 2 * NZ) for n in range(1, 2 * NZ)]
     for b in range(N_EARLY, N_BLOCK):
         n = last if b == N_BLOCK - 1 else size
-        x_copy(b, n).wait_recv()
-        add_into(part(from_x, b, n), part(s_buf, b, n), 24)
-        t_copy(b, n).start()
-        t_store(b, n).start()
-        for k in range(NZ):
-            if b in W_REDUCE[k]:
-                pl.when(z == k)(functools.partial(w_reduce, k, W_REDUCE[k][b]))
-        if b == 9:
-            w_copy_x.start()
-            every(chip_sum, AHEAD, N_BLOCK)
-        if b == 10:
+        if b == N_BLOCK - 1:
             w_copy_x.wait()
             add_into(total, w_x)
             w_copy_c.start()
@@ -1221,6 +1213,16 @@
             for to in peers:
                 remote(mine, small_ref.at[tp], small_send.at[to], small_recv.at[tp], to, dp).start()
             small_here.start()
+        x_copy(b, n).wait_recv()
+        add_into(part(from_x, b, n), part(s_buf, b, n), 24)
+        t_copy(b, n).start()
+        t_store(b, n).start()
+        for k in range(NZ):
+            if b in W_REDUCE[k]:
+                pl.when(z == k)(functools.partial(w_reduce, k, W_REDUCE[k][b]))
+        if b == N_BLOCK - 2:
+            w_copy_x.start()
+            every(chip_sum, AHEAD, N_BLOCK)
     for source in peers:
         remote(small_ref.at[source], small_ref.at[source], small_send.at[source], small_recv.at[source], source, dp).wait_recv()
         remote(mine, small_ref.at[tp], small_send.at[source], small_recv.at[tp], source, dp).wait_send()
@@ -1462,7 +1464,7 @@
 
         w_rows = jnp.concatenate([w_q.T, w_o, w_gu.transpose(0, 2, 1).reshape(2 * f_loc, d_model), w_down], axis=0)
         cuts = (q_loc, 2 * q_loc, 2 * q_loc + f_loc, 2 * q_loc + 2 * f_loc)
-        wkv_t = w_kv.transpose(0, 2, 1).reshape(2 * head_dim, d_model).astype(BF16)
+        wkv_t = w_kv.transpose(0, 2, 1).reshape(2 * head_dim, d_model)
         inv_freq = ROPE_BASE ** (-jnp.arange(0, head_dim, 2).astype(F32) / head_dim)
         angles = inv_freq[:, None] * (half * own + jnp.arange(own)).astype(F32)[None, :]
         cos_t, sin_t = jnp.cos(angles), jnp.sin(angles)
@@ -1471,14 +1473,13 @@
         weights = (wq_t, wkv_t, wo_b, wg_t, wu_t, wd_b)
 
         logit_scale = d_model ** -0.5
-        d_fin, g_head_part, log_norm, lab_sum, _ = head(f_own, labels.reshape(n_tp, own), embed, logit_scale, logit_scale / tok_total, 4)
-        log_norm = lax.dynamic_index_in_dim(log_norm, tp_rank, 0, keepdims=False)
-        loss_row = (log_norm + LOGIT_ZLOSS * log_norm * log_norm - jnp.sum(lab_sum, axis=0) * logit_scale) / tok_total
+        d_fin, g_head_part, log_norm, lab_sum, _ = head(f_own, labels, embed, logit_scale, logit_scale / tok_total, 4)
+
         def row_ids(step):
             here = (shard[:, None, :] == tp_rank) & (rank[:, None, :] == slots[None, :, None] + step * CAP)
             return jnp.where(jnp.any(here, axis=-1), jnp.sum(jnp.where(here, row[:, None, :], 0), axis=-1), vocab_loc).reshape(-1)
 
-        g_rows, d_zero, rows_back, early, ids_back = layer_bwd(d_fin, x_zero, x_one, loss_row[None, :], ln_scales, cos_t, sin_t, weights, saved,
+        g_rows, d_zero, rows_back, early, ids_back = layer_bwd(logit_scale, tok_total, d_fin, x_zero, x_one, log_norm, lab_sum, ln_scales, cos_t, sin_t, weights, saved,
                                                                code_first, g_head_part, row_ids(0)[None, :], 7)
         g_table, g_shard, g_small = tail(g_head_part, g_rows, rows_back, ids_back, early, 10)
 

time: 603 us -> 601 us (level)
  no operation moved by 1% of the time
where the time goes in v12:
time: 601 us; the launch traced here: 594 us
  Pallas kernels  581 us (97%)
    pallas_call x1, Pallas kernels, head(): pl.pallas_call(functools.partial(head_kernel, scale, token_scale), out_sh...  195 us
    pallas_call x1, Pallas kernels, tail(): pl.pallas_call(tail_kernel, out_shape=(jax.ShapeDtypeStruct((vocab, width...  142 us
    pallas_call x1, Pallas kernels, layer_bwd(): pl.pallas_call(functools.partial(layer_bwd_kernel, scale, tok_total), out...  106 us
    pallas_call x1, Pallas kernels, front(): pl.pallas_call(front_kernel, out_shape=(s((own, width), F32),) * 3 + (s((...  104 us
    pallas_call x1, Pallas kernels, update(): pl.pallas_call(update_kernel, out_shape=tuple((jax.ShapeDtypeStruct(a.sha...  35.2 us

profile of v12, /device:TPU:0, one launch (start us, length us, event | category | flops | bytes accessed | tf_op | source)
XLA Modules:
  0.0 594.3 jit_solution(12581436421284117170)
XLA Ops:
  0.7 0.0 copy-start.1
  0.7 0.0 copy-start.2
  0.7 0.0 copy-start.3
  0.7 0.8 reshape.408
  1.6 0.2 convert_reduce_fusion
  1.8 0.6 reduce_max.18
  3.1 0.5 broadcast_in_dim.132.rounds_ref
  3.6 0.3 fusion.14
  3.9 0.3 fusion.12
  4.2 0.4 select_reduce_fusion.3
  4.6 0.7 select_n.167.ids_ref
  5.3 0.7 reshape.409.ids_ref
  6.0 0.6 and_select_fusion
  6.6 1.0 multiply_sine_fusion
  7.5 1.6 copy.46
  9.1 0.0 copy-done.1
  9.1 0.0 copy-done.2
  9.1 0.0 copy-done.3
  9.1 1.4 pad_maximum_fusion.1.w_ref
  10.5 0.1 broadcast_in_dim.134
  10.6 0.0 copy-start
  10.6 104.0 %front.1 = (f32[512,512]{1,0:T(8,128)}, f32[512,512]{1,0:T(8,128)}, f32[512,512]{1,0:T(8,128)}, bf16[512,512]{1,0:T(8,128)(2,1)}, bf16[1024,128]{1,0:T(8,128)(2,...) custom-call(s32[768]{0:T(1024)} %reshape.409.ids_ref, ...), custom_call_target="tpu_custom_call" | custom-call | tf_op jit(solution)/shard_map/front/pallas_call | solution.py:776
  114.6 0.0 copy-done
  114.6 1.3 reduce_max.19
  115.9 194.8 %head.1 = (f32[512,512]{1,0:T(8,128)}, f32[6288,512]{1,0:T(8,128)}, f32[8,512]{1,0:T(8,128)}, f32[8,512]{1,0:T(8,128)}, f32[8,6288,512]{2,1,0:T(8,128)}) custom-call(f32[512,512]{1,0:T(8,128)} %get-tuple-element.269.f_ref, s32[4,1024]{1,0:T(4,128)} %lab_ref.1, f32[6288,512]{1,0:T(8,128)} %get-tuple-element.616), custom_call_target="tpu_custom_call" | custom-call | flops 105495134208 | bytes 38633472 | tf_op jit(solution)/shard_map/head/pallas_call | solution.py:483
  310.7 105.6 %layer_bwd.1 = (f32[8,928,512]{2,1,0:T(8,128)}, f32[512,512]{1,0:T(8,128)}, f32[4,8,96,512]{3,2,1,0:T(8,128)}, f32[4,264,512]{2,1,0:T(8,128)}, s32[4,1,768]{2,1,0:T(1,128)}) custom-call(f32[512,512]{1,0:T(8,128)} %get-tuple-element.271.dfin_ref, f32[512,512]{1,0:T(8,128)} %get-tuple-element.272.x0_ref, f32[512,512]{1,0:T(8,128)} %get-tuple-element.273.x1_ref, ...), custom_call_target="tpu_custom_call" | custom-call | tf_op jit(solution)/shard_map/layer_bwd/pallas_call | solution.py:1014
  416.4 141.6 %tail.1 = (f32[6288,512]{1,0:T(8,128)}, f32[2,464,512]{2,1,0:T(8,128)}, f32[8,24,512]{2,1,0:T(8,128)}) custom-call(f32[6288,512]{1,0:T(8,128)} %get-tuple-element.270.g_ref, f32[8,2,464,512]{3,2,1,0:T(8,128)} %bitcast.73, f32[4,768,512]{2,1,0:T(8,128)} %bitcast.74, s32[4,1,768]{2,1,0:T(1,128)} %get-tuple-element.288.ids_ref, ...), custom_call_target="tpu_custom_call" | custom-call | tf_op jit(solution)/shard_map/tail/pallas_call | solution.py:1265
  558.0 0.7 while.25
  558.6 35.2 %update.1 = (f32[6288,512]{1,0:T(8,128)}, f32[2,512]{1,0:T(2,128)}, f32[64,512]{1,0:T(8,128)}, f32[2,64,512]{2,1,0:T(8,128)}, f32[64,512]{1,0:T(8,128)}, /*index...) custom-call(f32[6288,512]{1,0:T(8,128)} %get-tuple-element.293.t_ref, ...), custom_call_target="tpu_custom_call" | custom-call | tf_op jit(solution)/shard_map/update/pallas_call | solution.py:1376
  (7 shorter events, 0.1 us)
Async XLA Ops:
  0.7 8.4 %copy-start.1 = (f32[256,512]{1,0:T(8,128)S(1)}, f32[256,512]{1,0:T(8,128)}, u32[]{:S(2)}) copy-start(f32[256,512]{1,0:T(8,128)} %refs_6_.1) | copy-start | bytes 1572868
  0.7 8.4 %copy-start.2 = (f32[64,512]{1,0:T(8,128)S(1)}, f32[64,512]{1,0:T(8,128)}, u32[]{:S(2)}) copy-start(f32[64,512]{1,0:T(8,128)} %refs_4_.1) | copy-start | bytes 393220
  0.7 8.4 %copy-start.3 = (f32[512,64]{0,1:T(8,128)S(1)}, f32[512,64]{0,1:T(8,128)}, u32[]{:S(2)}) copy-start(f32[512,64]{0,1:T(8,128)} %param.31) | copy-start | bytes 393220
  10.6 104.0 %copy-start = (s32[8,512]{1,0:T(8,128)}, s32[8,512]{1,0:T(8,128)S(1)}, u32[]{:S(2)}) copy-start(s32[8,512]{1,0:T(8,128)S(1)} %get-tuple-element.619) | copy-start | bytes 49156

commit v13 on v12

--- a/solution.py
+++ b/solution.py
@@ -526,8 +526,8 @@
 
 
 def front_kernel(ids_ref, e_ref, rounds_ref, code_ref, extra_ref, w_ref, wkv_ref, ln_ref, cos_ref, sin_ref,
-                 f_ref, x1_ref, x0_ref, q_ref, kv_ref, kvt_ref, lse_ref, ctx_ref, wq_ref, wo_ref, wg_ref, wu_ref, wd_ref, rounds_all,
-                 table, rows_ref, wl, rows_in, u_b, kv_out, kv_in, own_sem, r_send, r_recv, a_y, a_l, a_r, a_c, a_recv,
+                 f_ref, x1_ref, x0_ref, q_ref, kv_ref, kvt_ref, lse_ref, ctx_ref, wq_ref, wo_ref, wg_out, wu_out, wd_out, rounds_all,
+                 wg_ref, wu_ref, wd_ref, w_sem, table, rows_ref, wl, rows_in, u_b, kv_out, kv_in, own_sem, r_send, r_recv, a_y, a_l, a_r, a_c, a_recv,
                  b_y, b_l, b_r, b_x, b_c, b_recv, kv_send, kv_recv, n_send, n_recv):
     tp, dp, z, y = place()
     partner = tp + 1 - 2 * y
@@ -537,7 +537,7 @@
     own, width = x0_ref.shape
     shards, w_rows = wl.shape[0], wl.shape[1]
     nq = q_ref.shape[0]
-    ff = wg_ref.shape[0]
+    ff = wg_out.shape[0]
     n_a = nq // shards
     n_f = ff // shards
     n_b = 3 * n_f // 4
@@ -662,7 +662,7 @@
     x1_ref[...] = x0_ref[...]
     cos_t = cos_ref[...]
     sin_t = sin_ref[...]
-    kv = mm(wkv_ref[...].astype(BF16), u_b[...], TB)
+    kv = mm(wkv_ref[...].reshape(2 * hd, width).astype(BF16), u_b[...], TB)
     lo, hi = turn(kv[:quarter], kv[quarter:hd], cos_t, sin_t)
     kv_out[0:quarter, :] = lo
     kv_out[quarter:hd, :] = hi
@@ -674,6 +674,11 @@
         code = lookup(MLP_ORDER, z, step)
         other = code % 2
         return code // 2 * 2 + y + other - 2 * y * other
+
+    def w_stores(slot):
+        at = pl.ds(pl.multiple_of(slot * n_f, n_f), n_f)
+        return [pltpu.make_async_copy(src.at[at, :], dst.at[at, :], w_sem.at[i, slot])
+                for i, (src, dst) in enumerate(((wg_ref, wg_out), (wu_ref, wu_out), (wd_ref, wd_out)))]
 
     def mlp(step, carry):
         def pass_on():
@@ -691,6 +696,8 @@
         wg_ref[at, :] = wl[slot, 2 * n_a:2 * n_a + n_f, :].astype(BF16)
         wu_ref[at, :] = wl[slot, 2 * n_a + n_f:2 * n_a + 2 * n_f, :].astype(BF16)
         wd_ref[at, :] = wl[slot, 2 * n_a + 2 * n_f:2 * n_a + 3 * n_f, :].astype(BF16)
+        for c in w_stores(slot):
+            c.start()
         gate = mm(u_b[...], wg_ref[at, :], TB)
         up = mm(u_b[...], wu_ref[at, :], TB)
         x1_ref[...] += mm((gate * jax.nn.sigmoid(gate) * up).astype(BF16), wd_ref[at, :])
@@ -754,6 +761,9 @@
             c.wait_send()
 
     on_position(finish)
+    for slot in range(shards):
+        for c in w_stores(slot):
+            c.wait()
     for n in range(3):
         rounds_copy(n).wait_send()
         remote(rounds_ref, rounds_all.at[group[n]], n_send.at[n], n_recv.at[group[n]], tp, twin).wait_recv()
@@ -767,7 +777,7 @@
 
 def front(ids, embed, rounds, code, extra, w_rows, wkv_t, ln, cos_t, sin_t, n_q, collective_id):
     own, width = extra.shape
-    two_hd = wkv_t.shape[0]
+    two_hd = 2 * wkv_t.shape[1]
     shards = 2 * NZ
     ff = (w_rows.shape[0] * shards - 2 * n_q) // 3
     dma = lambda *n: pltpu.SemaphoreType.DMA(n)
@@ -779,8 +789,8 @@
                    s((2 * n_q // two_hd, own), F32), s((n_q, own), BF16), s((n_q, width), BF16), s((n_q, width), BF16))
         + (s((ff, width), BF16),) * 3 + (s((4, 1, 128), jnp.int32),),
         in_specs=[pl.BlockSpec(memory_space=pltpu.SMEM), ANY, VMEM, VMEM, VMEM, ANY] + [VMEM] * 4,
-        out_specs=(VMEM,) * 14,
-        scratch_shapes=[pltpu.VMEM(embed.shape, F32), pltpu.VMEM(rows, F32), pltpu.VMEM((shards,) + w_rows.shape, F32), pltpu.VMEM(rows, F32), pltpu.VMEM((own, width), BF16),
+        out_specs=(VMEM,) * 10 + (ANY,) * 3 + (VMEM,),
+        scratch_shapes=[pltpu.VMEM((ff, width), BF16)] * 3 + [dma(3, shards), pltpu.VMEM(embed.shape, F32), pltpu.VMEM(rows, F32), pltpu.VMEM((shards,) + w_rows.shape, F32), pltpu.VMEM(rows, F32), pltpu.VMEM((own, width), BF16),
                         pltpu.VMEM((two_hd, own), F32), pltpu.VMEM((two_hd, own), F32),
                         dma(3), dma(shards), dma(shards)] + [dma(shards)] * 4 + [dma(shards, 2)]
         + [dma(shards)] * 4 + [dma(2, shards), dma(shards, 4), pltpu.SemaphoreType.DMA, pltpu.SemaphoreType.DMA, dma(3), dma(4)],
@@ -789,9 +799,9 @@
     )(ids, embed, rounds, code, extra, w_rows, wkv_t, ln, cos_t, sin_t)
 
 
-def layer_bwd_kernel(scale, tok_total, dfin_ref, x0_ref, x1_ref, norm_ref, hits_ref, ln_ref, cos_ref, sin_ref, wq_ref, wkv_ref, wo_ref, wg_ref, wu_ref, wd_ref,
+def layer_bwd_kernel(scale, tok_total, dfin_ref, x0_ref, x1_ref, norm_ref, hits_ref, ln_ref, cos_ref, sin_ref, wq_ref, wkv_ref, wo_ref, wg_any, wu_any, wd_any,
                      q_ref, kv_ref, kvt_ref, lse_ref, ctx_ref, code_ref, g_ref, ids_ref, rows_ref, d0_ref, back_ref, early_ref, ids_all, d_one, d_b, u_b, dctx, dq, dkv, dkv_in,
-                     hid, d_gate, d_up, rows_out, g_q, g_o, g_g, g_u, g_d, small, s_early, c_early, out_sem, send_sem, recv_sem,
+                     hid, d_gate, d_up, rows_out, g_q, g_o, g_g, g_u, g_d, small, s_early, c_early, wg_ref, wu_ref, wd_ref, w_sem, out_sem, send_sem, recv_sem,
                      r_send, x_send, c_send, r_recv, g_load, g_send, g_recv, id_send, id_recv):
     tp, dp, z, y = place()
     partner = tp + 1 - 2 * y
@@ -806,6 +816,9 @@
     heads = nq // hd
     ff = wg_ref.shape[0]
     shards = rows_ref.shape[0]
+    w_loads = [pltpu.make_async_copy(src, dst, w_sem.at[i]) for i, (src, dst) in enumerate(((wg_any, wg_ref), (wu_any, wu_ref), (wd_any, wd_ref)))]
+    for c in w_loads:
+        c.start()
     plane_barrier(tp, dp, [(tp, twin), (tp, facing), (tp, across)])
 
     n_early, g_size = s_early.shape[0], s_early.shape[1]
@@ -871,6 +884,8 @@
 
     d0_ref[...] = mm(dq[...], wq_ref[...], TA)
     step = min(512, ff)
+    for c in w_loads:
+        c.wait()
 
     def mlp(n, carry):
         at = pl.ds(pl.multiple_of(n * step, step), step)
@@ -890,7 +905,7 @@
     lo, hi = turn(d_kv[:quarter], d_kv[quarter:hd], cos_t, -sin_t)
     d_kv = jnp.concatenate([lo, hi, d_kv[hd:]], axis=0).astype(BF16)
     small[0:2 * hd, :] = mm(d_kv, u_b[...])
-    d_u = d0_ref[...] + mm(d_kv, wkv_ref[...].astype(BF16), TA)
+    d_u = d0_ref[...] + mm(d_kv, wkv_ref[...].reshape(2 * hd, width).astype(BF16), TA)
     _, u_hat, u_inv = norm_fwd(x0_ref[...], ln_ref[0:1, :])
     d_in, g_in = norm_bwd(d_u, u_hat, u_inv, ln_ref[0:1, :])
     d_zero = d_one[...] + d_in
@@ -1004,7 +1019,7 @@
 def layer_bwd(scale, tok_total, d_fin, x0, x1, norms, hits, ln, cos_t, sin_t, weights, saved, code, g_table, ids, collective_id):
     own, width = x0.shape
     nq = weights[0].shape[0]
-    two_hd = weights[1].shape[0]
+    two_hd = 2 * weights[1].shape[1]
     ff = weights[3].shape[0]
     rows = (2 * nq + 3 * ff + two_hd) // (2 * NZ) + 16
     chunk = (own, width)
@@ -1015,12 +1030,13 @@
         functools.partial(layer_bwd_kernel, scale, tok_total),
         out_shape=(jax.ShapeDtypeStruct((2 * NZ, rows, width), F32), jax.ShapeDtypeStruct(chunk, F32), jax.ShapeDtypeStruct((4,) + back, F32),
                    jax.ShapeDtypeStruct(blocks, F32), jax.ShapeDtypeStruct((4,) + ids.shape, jnp.int32)),
-        in_specs=[VMEM] * 20 + [ANY, VMEM],
+        in_specs=[VMEM] * 11 + [ANY] * 3 + [VMEM] * 6 + [ANY, VMEM],
         out_specs=(ANY, VMEM, ANY, VMEM, VMEM),
         scratch_shapes=[pltpu.VMEM(chunk, F32), pltpu.VMEM(chunk, BF16), pltpu.VMEM(chunk, BF16), pltpu.VMEM((nq, own), BF16),
                         pltpu.VMEM((nq, own), BF16), pltpu.VMEM((2 * own, two_hd), F32), pltpu.VMEM((own, two_hd), F32)]
         + [pltpu.VMEM((ff, own), BF16)] * 3 + [pltpu.VMEM(back, F32), pltpu.VMEM((nq, width), F32), pltpu.VMEM((nq, width), F32)] + [pltpu.VMEM((ff, width), F32)] * 3
-        + [pltpu.VMEM((two_hd + 32, width), F32), pltpu.VMEM(blocks, F32), pltpu.VMEM(blocks, F32), dma(14 * NZ + 1),
+        + [pltpu.VMEM((two_hd + 32, width), F32), pltpu.VMEM(blocks, F32), pltpu.VMEM(blocks, F32)]
+        + [pltpu.VMEM((ff, width), BF16)] * 3 + [dma(3), dma(14 * NZ + 1),
            pltpu.SemaphoreType.DMA, pltpu.SemaphoreType.DMA, dma(2 * NZ), dma(2 * NZ), dma(2, 2 * NZ), dma(4, 2 * NZ),
            dma(N_EARLY), dma(2, N_EARLY), dma(2, N_EARLY), dma(3), dma(4)],
         compiler_params=pltpu.CompilerParams(collective_id=collective_id, has_side_effects=True, vmem_limit_bytes=66000000),
@@ -1029,7 +1045,7 @@
 
 
 N_BLOCK = 12
-N_EARLY = 4
+N_EARLY = 3
 AHEAD = 11
 
 
@@ -1038,10 +1054,10 @@
 
 
 W_REDUCE = {
-    0: {5: (3,), 7: (2,), 9: (1,), 10: (0,)},
-    1: {7: (3,), 9: (2, 0), 10: (1,)},
-    2: {7: (0,), 9: (1, 3), 10: (2,)},
-    3: {5: (0,), 7: (1,), 9: (2,), 10: (3,)},
+    0: {4: (3,), 6: (2,), 8: (1,), 9: (0,)},
+    1: {6: (3,), 8: (2, 0), 9: (1,)},
+    2: {6: (0,), 8: (1, 3), 9: (2,)},
+    3: {4: (0,), 6: (1,), 8: (2,), 9: (3,)},
 }
 
 
@@ -1220,7 +1236,7 @@
         for k in range(NZ):
             if b in W_REDUCE[k]:
                 pl.when(z == k)(functools.partial(w_reduce, k, W_REDUCE[k][b]))
-        if b == N_BLOCK - 2:
+        if b == N_BLOCK - 3:
             w_copy_x.start()
             every(chip_sum, AHEAD, N_BLOCK)
     for source in peers:
@@ -1293,14 +1309,14 @@
 
     def loads(q):
         at, n = blocks[q]
-        return [pltpu.make_async_copy(ref.at[pl.ds(at, n), :], held.at[q % 3, i, pl.ds(0, n), :], in_sem.at[q % 3, i])
+        return [pltpu.make_async_copy(ref.at[pl.ds(at, n), :], held.at[q % 4, i, pl.ds(0, n), :], in_sem.at[q % 4, i])
                 for i, ref in enumerate((t_ref, state[0][0], state[1][0], state[2][0]))]
 
     def stores(q):
         at, n = blocks[q]
-        return [pltpu.make_async_copy(made.at[q % 2, i, pl.ds(0, n), :], new[i][0].at[pl.ds(at, n), :], out_sem.at[q % 2, i]) for i in range(3)]
-
-    for q in range(3):
+        return [pltpu.make_async_copy(made.at[q % 3, i, pl.ds(0, n), :], new[i][0].at[pl.ds(at, n), :], out_sem.at[q % 3, i]) for i in range(3)]
+
+    for q in range(4):
         for c in loads(q):
             c.start()
     grads = [pltpu.make_async_copy(w_any, w_ref, g_sem.at[0]), pltpu.make_async_copy(small_any, small_ref, g_sem.at[1])]
@@ -1333,23 +1349,23 @@
     for q, (at, n) in enumerate(blocks):
         for c in loads(q):
             c.wait()
-        if q >= 2:
-            for c in stores(q - 2):
+        if q >= 3:
+            for c in stores(q - 3):
                 c.wait()
         step = 32 if n % 32 == 0 else 16
 
         def body(j, carry):
             rows = pl.ds(pl.multiple_of(j * step, step), step)
-            got = adam_update(held[q % 3, 1, rows, :], held[q % 3, 0, rows, :], held[q % 3, 2, rows, :], held[q % 3, 3, rows, :])
+            got = adam_update(held[q % 4, 1, rows, :], held[q % 4, 0, rows, :], held[q % 4, 2, rows, :], held[q % 4, 3, rows, :])
             for i in range(3):
-                made[q % 2, i, rows, :] = got[i]
+                made[q % 3, i, rows, :] = got[i]
             return carry
 
         lax.fori_loop(0, n // step, body, 0)
         for c in stores(q):
             c.start()
-        if q + 3 < len(blocks):
-            for c in loads(q + 3):
+        if q + 4 < len(blocks):
+            for c in loads(q + 4):
                 c.start()
         if q == min(3, len(blocks) - 1):
             for c in small_loads:
@@ -1357,7 +1373,7 @@
             small_updates()
             for c in small_stores:
                 c.start()
-    for q in range(len(blocks) - 2, len(blocks)):
+    for q in range(len(blocks) - 3, len(blocks)):
         for c in stores(q):
             c.wait()
     for c in small_stores:
@@ -1378,9 +1394,9 @@
         out_shape=tuple(jax.ShapeDtypeStruct(a.shape, F32) for a in given) + (jax.ShapeDtypeStruct((1, 1), F32),),
         in_specs=[ANY] * 24,
         out_specs=(ANY,) * 21 + (VMEM,),
-        scratch_shapes=[pltpu.VMEM((3, 4, UPDATE_ROWS, width), F32), pltpu.VMEM((2, 3, UPDATE_ROWS, width), F32),
+        scratch_shapes=[pltpu.VMEM((4, 4, UPDATE_ROWS, width), F32), pltpu.VMEM((3, 3, UPDATE_ROWS, width), F32),
                         pltpu.VMEM(g_shard.shape, F32), pltpu.VMEM(g_small.shape, F32)] + small * 2
-        + [dma(3, 4), dma(2, 3), dma(2), dma(3, 6), dma(3, 6)],
+        + [dma(4, 4), dma(3, 3), dma(2), dma(3, 6), dma(3, 6)],
         compiler_params=pltpu.CompilerParams(vmem_limit_bytes=60000000),
         name="update",
     )(g_table, g_shard, g_small, *given)
@@ -1464,7 +1480,7 @@
 
         w_rows = jnp.concatenate([w_q.T, w_o, w_gu.transpose(0, 2, 1).reshape(2 * f_loc, d_model), w_down], axis=0)
         cuts = (q_loc, 2 * q_loc, 2 * q_loc + f_loc, 2 * q_loc + 2 * f_loc)
-        wkv_t = w_kv.transpose(0, 2, 1).reshape(2 * head_dim, d_model)
+        wkv_t = w_kv.transpose(0, 2, 1)
         inv_freq = ROPE_BASE ** (-jnp.arange(0, head_dim, 2).astype(F32) / head_dim)
         angles = inv_freq[:, None] * (half * own + jnp.arange(own)).astype(F32)[None, :]
         cos_t, sin_t = jnp.cos(angles), jnp.sin(angles)

time: 601 us -> 595 us (0.990)
  no operation moved by 1% of the time
where the time goes in v13:
time: 595 us; the launch traced here: 589 us
  Pallas kernels  575 us (97%)
    pallas_call x1, Pallas kernels, head(): pl.pallas_call(functools.partial(head_kernel, scale, token_scale), out_sh...  195 us
    pallas_call x1, Pallas kernels, tail(): pl.pallas_call(tail_kernel, out_shape=(jax.ShapeDtypeStruct((vocab, width...  141 us
    pallas_call x1, Pallas kernels, layer_bwd(): pl.pallas_call(functools.partial(layer_bwd_kernel, scale, tok_total), out...  102 us
    pallas_call x1, Pallas kernels, front(): pl.pallas_call(front_kernel, out_shape=(s((own, width), F32),) * 3 + (s((...  102 us
    pallas_call x1, Pallas kernels, update(): pl.pallas_call(update_kernel, out_shape=tuple((jax.ShapeDtypeStruct(a.sha...  35.2 us

profile of v13, /device:TPU:0, one launch (start us, length us, event | category | flops | bytes accessed | tf_op | source)
XLA Modules:
  0.0 588.6 jit_solution(7832756605696148413)
XLA Ops:
  0.7 0.0 copy-start.1
  0.7 0.0 copy-start.2
  0.7 0.0 copy-start.3
  0.7 0.8 reshape.405
  1.6 0.2 convert_reduce_fusion
  1.8 0.6 reduce_max.18
  3.1 0.5 broadcast_in_dim.132.rounds_ref
  3.6 0.3 fusion.14
  3.9 0.3 fusion.12
  4.2 0.4 select_reduce_fusion.3
  4.6 0.7 select_n.167.ids_ref
  5.3 0.7 reshape.406.ids_ref
  6.0 0.6 and_select_fusion
  6.6 1.0 multiply_sine_fusion
  7.5 1.6 copy.46
  9.1 0.0 copy-done.1
  9.1 0.0 copy-done.2
  9.1 0.0 copy-done.3
  9.1 1.4 pad_maximum_fusion.1.w_ref
  10.5 0.1 broadcast_in_dim.134
  10.6 0.0 copy-start
  10.6 102.3 %front.1 = (f32[512,512]{1,0:T(8,128)}, f32[512,512]{1,0:T(8,128)}, f32[512,512]{1,0:T(8,128)}, bf16[512,512]{1,0:T(8,128)(2,1)}, bf16[1024,128]{1,0:T(8,128)(2,...) custom-call(s32[768]{0:T(1024)} %reshape.406.ids_ref, ...), custom_call_target="tpu_custom_call" | custom-call | tf_op jit(solution)/shard_map/front/pallas_call | solution.py:786
  113.0 0.0 copy-done
  113.0 1.3 reduce_max.19
  114.3 194.8 %head.1 = (f32[512,512]{1,0:T(8,128)}, f32[6288,512]{1,0:T(8,128)}, f32[8,512]{1,0:T(8,128)}, f32[8,512]{1,0:T(8,128)}, f32[8,6288,512]{2,1,0:T(8,128)}) custom-call(f32[512,512]{1,0:T(8,128)} %get-tuple-element.269.f_ref, s32[4,1024]{1,0:T(4,128)} %lab_ref.1, f32[6288,512]{1,0:T(8,128)} %get-tuple-element.616), custom_call_target="tpu_custom_call" | custom-call | flops 105495134208 | bytes 38633472 | tf_op jit(solution)/shard_map/head/pallas_call | solution.py:483
  309.1 102.4 %layer_bwd.1 = (f32[8,928,512]{2,1,0:T(8,128)}, f32[512,512]{1,0:T(8,128)}, f32[4,8,96,512]{3,2,1,0:T(8,128)}, f32[3,264,512]{2,1,0:T(8,128)}, s32[4,1,768]{2,1,0:T(1,128)}) custom-call(f32[512,512]{1,0:T(8,128)} %get-tuple-element.271.dfin_ref, f32[512,512]{1,0:T(8,128)} %get-tuple-element.272.x0_ref, f32[512,512]{1,0:T(8,128)} %get-tuple-element.273.x1_ref, ...), custom_call_target="tpu_custom_call" | custom-call | tf_op jit(solution)/shard_map/layer_bwd/pallas_call | solution.py:1029
  411.5 140.7 %tail.1 = (f32[6288,512]{1,0:T(8,128)}, f32[2,464,512]{2,1,0:T(8,128)}, f32[8,24,512]{2,1,0:T(8,128)}) custom-call(f32[6288,512]{1,0:T(8,128)} %get-tuple-element.270.g_ref, f32[8,2,464,512]{3,2,1,0:T(8,128)} %bitcast.71, f32[4,768,512]{2,1,0:T(8,128)} %bitcast.72, s32[4,1,768]{2,1,0:T(1,128)} %get-tuple-element.288.ids_ref, ...), custom_call_target="tpu_custom_call" | custom-call | tf_op jit(solution)/shard_map/tail/pallas_call | solution.py:1281
  552.2 0.7 while.25
  552.9 35.2 %update.1 = (f32[6288,512]{1,0:T(8,128)}, f32[2,512]{1,0:T(2,128)}, f32[64,512]{1,0:T(8,128)}, f32[2,64,512]{2,1,0:T(8,128)}, f32[64,512]{1,0:T(8,128)}, /*index...) custom-call(f32[6288,512]{1,0:T(8,128)} %get-tuple-element.293.t_ref, ...), custom_call_target="tpu_custom_call" | custom-call | tf_op jit(solution)/shard_map/update/pallas_call | solution.py:1392
  (7 shorter events, 0.1 us)
Async XLA Ops:
  0.7 8.4 %copy-start.1 = (f32[256,512]{1,0:T(8,128)S(1)}, f32[256,512]{1,0:T(8,128)}, u32[]{:S(2)}) copy-start(f32[256,512]{1,0:T(8,128)} %refs_6_.1) | copy-start | bytes 1572868
  0.7 8.4 %copy-start.2 = (f32[64,512]{1,0:T(8,128)S(1)}, f32[64,512]{1,0:T(8,128)}, u32[]{:S(2)}) copy-start(f32[64,512]{1,0:T(8,128)} %refs_4_.1) | copy-start | bytes 393220
  0.7 8.4 %copy-start.3 = (f32[512,64]{0,1:T(8,128)S(1)}, f32[512,64]{0,1:T(8,128)}, u32[]{:S(2)}) copy-start(f32[512,64]{0,1:T(8,128)} %param.31) | copy-start | bytes 393220
  10.6 102.3 %copy-start = (s32[8,512]{1,0:T(8,128)}, s32[8,512]{1,0:T(8,128)S(1)}, u32[]{:S(2)}) copy-start(s32[8,512]{1,0:T(8,128)S(1)} %get-tuple-element.619) | copy-start | bytes 49156

commit v14 on v13

--- a/solution.py
+++ b/solution.py
@@ -55,6 +55,10 @@
         return carry
 
     lax.fori_loop(0, rows // step, body, 0)
+
+
+def near_first(k):
+    return sorted(((o, zz) for o in range(2) for zz in range(NZ)), key=lambda c: (abs(c[1] - k), c[0]))
 
 
 def plane_barrier(tp, dp, others):
@@ -646,11 +650,11 @@
         return carry
 
     lax.fori_loop(0, shards * cap // 8, pick_rows, 0)
-    start([row_copy(to) for to in peers])
+    on_position(functools.partial(b_event, 0))
+    on_position(functools.partial(a_event, 0))
+    on_position(lambda k: start([row_copy(2 * zz + (1 - y if o else y)) for o, zz in near_first(k)[1:]]))
     own_rows = pltpu.make_async_copy(rows_ref.at[tp], rows_in.at[tp], own_sem.at[0])
     own_rows.start()
-    on_position(functools.partial(b_event, 0))
-    on_position(functools.partial(a_event, 0))
     on_position(functools.partial(b_event, 1))
     on_position(functools.partial(a_event, 1))
     own_rows.wait()
@@ -928,9 +932,6 @@
 
     def back(group, slot):
         remote(rows_out.at[slot], back_ref.at[group, slot], r_send.at[slot], r_recv.at[group, slot], tp, twin).wait_recv()
-
-    def near_first(k):
-        return sorted(((o, zz) for o in range(2) for zz in range(NZ)), key=lambda c: (abs(c[1] - k), c[0]))
 
     def slot_of(o, zz):
         return 2 * zz + (1 - y if o else y)

time: 595 us -> 597 us (level)
  no operation moved by 1% of the time
where the time goes in v14:
time: 597 us; the launch traced here: 590 us
  Pallas kernels  577 us (97%)
    pallas_call x1, Pallas kernels, head(): pl.pallas_call(functools.partial(head_kernel, scale, token_scale), out_sh...  195 us
    pallas_call x1, Pallas kernels, tail(): pl.pallas_call(tail_kernel, out_shape=(jax.ShapeDtypeStruct((vocab, width...  141 us
    pallas_call x1, Pallas kernels, front(): pl.pallas_call(front_kernel, out_shape=(s((own, width), F32),) * 3 + (s((...  103 us
    pallas_call x1, Pallas kernels, layer_bwd(): pl.pallas_call(functools.partial(layer_bwd_kernel, scale, tok_total), out...  102 us
    pallas_call x1, Pallas kernels, update(): pl.pallas_call(update_kernel, out_shape=tuple((jax.ShapeDtypeStruct(a.sha...  35.2 us

profile of v14, /device:TPU:0, one launch (start us, length us, event | category | flops | bytes accessed | tf_op | source)
XLA Modules:
  0.0 590.0 jit_solution(523456603706397489)
XLA Ops:
  0.7 0.0 copy-start.1
  0.7 0.0 copy-start.2
  0.7 0.0 copy-start.3
  0.7 0.8 reshape.405
  1.6 0.2 convert_reduce_fusion
  1.8 0.6 reduce_max.18
  3.1 0.5 broadcast_in_dim.132.rounds_ref
  3.6 0.3 fusion.14
  3.9 0.3 fusion.12
  4.2 0.4 select_reduce_fusion.3
  4.6 0.7 select_n.167.ids_ref
  5.3 0.7 reshape.406.ids_ref
  6.0 0.6 and_select_fusion
  6.6 1.0 multiply_sine_fusion
  7.5 1.6 copy.46
  9.1 0.0 copy-done.1
  9.1 0.0 copy-done.2
  9.1 0.0 copy-done.3
  9.1 1.4 pad_maximum_fusion.1.w_ref
  10.5 0.1 broadcast_in_dim.134
  10.6 0.0 copy-start
  10.6 103.5 %front.1 = (f32[512,512]{1,0:T(8,128)}, f32[512,512]{1,0:T(8,128)}, f32[512,512]{1,0:T(8,128)}, bf16[512,512]{1,0:T(8,128)(2,1)}, bf16[1024,128]{1,0:T(8,128)(2,...) custom-call(s32[768]{0:T(1024)} %reshape.406.ids_ref, ...), custom_call_target="tpu_custom_call" | custom-call | tf_op jit(solution)/shard_map/front/pallas_call | solution.py:790
  114.1 0.0 copy-done
  114.1 1.3 reduce_max.19
  115.5 195.3 %head.1 = (f32[512,512]{1,0:T(8,128)}, f32[6288,512]{1,0:T(8,128)}, f32[8,512]{1,0:T(8,128)}, f32[8,512]{1,0:T(8,128)}, f32[8,6288,512]{2,1,0:T(8,128)}) custom-call(f32[512,512]{1,0:T(8,128)} %get-tuple-element.269.f_ref, s32[4,1024]{1,0:T(4,128)} %lab_ref.1, f32[6288,512]{1,0:T(8,128)} %get-tuple-element.616), custom_call_target="tpu_custom_call" | custom-call | flops 105495134208 | bytes 38633472 | tf_op jit(solution)/shard_map/head/pallas_call | solution.py:487
  310.8 101.6 %layer_bwd.1 = (f32[8,928,512]{2,1,0:T(8,128)}, f32[512,512]{1,0:T(8,128)}, f32[4,8,96,512]{3,2,1,0:T(8,128)}, f32[3,264,512]{2,1,0:T(8,128)}, s32[4,1,768]{2,1,0:T(1,128)}) custom-call(f32[512,512]{1,0:T(8,128)} %get-tuple-element.271.dfin_ref, f32[512,512]{1,0:T(8,128)} %get-tuple-element.272.x0_ref, f32[512,512]{1,0:T(8,128)} %get-tuple-element.273.x1_ref, ...), custom_call_target="tpu_custom_call" | custom-call | tf_op jit(solution)/shard_map/layer_bwd/pallas_call | solution.py:1030
  412.4 141.3 %tail.1 = (f32[6288,512]{1,0:T(8,128)}, f32[2,464,512]{2,1,0:T(8,128)}, f32[8,24,512]{2,1,0:T(8,128)}) custom-call(f32[6288,512]{1,0:T(8,128)} %get-tuple-element.270.g_ref, f32[8,2,464,512]{3,2,1,0:T(8,128)} %bitcast.71, f32[4,768,512]{2,1,0:T(8,128)} %bitcast.72, s32[4,1,768]{2,1,0:T(1,128)} %get-tuple-element.288.ids_ref, ...), custom_call_target="tpu_custom_call" | custom-call | tf_op jit(solution)/shard_map/tail/pallas_call | solution.py:1282
  553.6 0.7 while.25
  554.3 35.2 %update.1 = (f32[6288,512]{1,0:T(8,128)}, f32[2,512]{1,0:T(2,128)}, f32[64,512]{1,0:T(8,128)}, f32[2,64,512]{2,1,0:T(8,128)}, f32[64,512]{1,0:T(8,128)}, /*index...) custom-call(f32[6288,512]{1,0:T(8,128)} %get-tuple-element.293.t_ref, ...), custom_call_target="tpu_custom_call" | custom-call | tf_op jit(solution)/shard_map/update/pallas_call | solution.py:1393
  (7 shorter events, 0.1 us)
Async XLA Ops:
  0.7 8.4 %copy-start.1 = (f32[256,512]{1,0:T(8,128)S(1)}, f32[256,512]{1,0:T(8,128)}, u32[]{:S(2)}) copy-start(f32[256,512]{1,0:T(8,128)} %refs_6_.1) | copy-start | bytes 1572868
  0.7 8.4 %copy-start.2 = (f32[64,512]{1,0:T(8,128)S(1)}, f32[64,512]{1,0:T(8,128)}, u32[]{:S(2)}) copy-start(f32[64,512]{1,0:T(8,128)} %refs_4_.1) | copy-start | bytes 393220
  0.7 8.4 %copy-start.3 = (f32[512,64]{0,1:T(8,128)S(1)}, f32[512,64]{0,1:T(8,128)}, u32[]{:S(2)}) copy-start(f32[512,64]{0,1:T(8,128)} %param.31) | copy-start | bytes 393220
  10.6 103.5 %copy-start = (s32[8,512]{1,0:T(8,128)}, s32[8,512]{1,0:T(8,128)S(1)}, u32[]{:S(2)}) copy-start(s32[8,512]{1,0:T(8,128)S(1)} %get-tuple-element.619) | copy-start | bytes 49156

commit v15 on v14

--- a/solution.py
+++ b/solution.py
@@ -652,11 +652,11 @@
     lax.fori_loop(0, shards * cap // 8, pick_rows, 0)
     on_position(functools.partial(b_event, 0))
     on_position(functools.partial(a_event, 0))
+    on_position(functools.partial(b_event, 1))
+    on_position(functools.partial(a_event, 1))
     on_position(lambda k: start([row_copy(2 * zz + (1 - y if o else y)) for o, zz in near_first(k)[1:]]))
     own_rows = pltpu.make_async_copy(rows_ref.at[tp], rows_in.at[tp], own_sem.at[0])
     own_rows.start()
-    on_position(functools.partial(b_event, 1))
-    on_position(functools.partial(a_event, 1))
     own_rows.wait()
     for source in peers:
         remote(rows_ref.at[source], rows_in.at[source], r_send.at[source], r_recv.at[source], source, dp).wait_recv()

time: 597 us -> 608 us (1.018)
  Pallas kernels: 577 us -> 588 us
    pallas_call x1, Pallas kernels: 103 us -> 116 us  [front(): pl.pallas_call(front_kernel, out_shape=(s((own, width), F32),) * 3 + (s((...]
where the time goes in v15:
time: 608 us; the launch traced here: 602 us
  Pallas kernels  588 us (97%)
    pallas_call x1, Pallas kernels, head(): pl.pallas_call(functools.partial(head_kernel, scale, token_scale), out_sh...  195 us
    pallas_call x1, Pallas kernels, tail(): pl.pallas_call(tail_kernel, out_shape=(jax.ShapeDtypeStruct((vocab, width...  143 us
    pallas_call x1, Pallas kernels, front(): pl.pallas_call(front_kernel, out_shape=(s((own, width), F32),) * 3 + (s((...  116 us
    pallas_call x1, Pallas kernels, layer_bwd(): pl.pallas_call(functools.partial(layer_bwd_kernel, scale, tok_total), out...  100 us
    pallas_call x1, Pallas kernels, update(): pl.pallas_call(update_kernel, out_shape=tuple((jax.ShapeDtypeStruct(a.sha...  35.2 us

profile of v15, /device:TPU:0, one launch (start us, length us, event | category | flops | bytes accessed | tf_op | source)
XLA Modules:
  0.0 601.6 jit_solution(17843620921140678772)
XLA Ops:
  0.7 0.0 copy-start.1
  0.7 0.0 copy-start.2
  0.7 0.0 copy-start.3
  0.7 0.8 reshape.405
  1.6 0.2 convert_reduce_fusion
  1.8 0.6 reduce_max.18
  3.1 0.5 broadcast_in_dim.132.rounds_ref
  3.6 0.3 fusion.14
  3.9 0.3 fusion.12
  4.2 0.4 select_reduce_fusion.3
  4.6 0.7 select_n.167.ids_ref
  5.3 0.7 reshape.406.ids_ref
  6.0 0.6 and_select_fusion
  6.6 1.0 multiply_sine_fusion
  7.5 1.6 copy.46
  9.1 0.0 copy-done.1
  9.1 0.0 copy-done.2
  9.1 0.0 copy-done.3
  9.1 1.4 pad_maximum_fusion.1.w_ref
  10.5 0.1 broadcast_in_dim.134
  10.6 0.0 copy-start
  10.6 115.5 %front.1 = (f32[512,512]{1,0:T(8,128)}, f32[512,512]{1,0:T(8,128)}, f32[512,512]{1,0:T(8,128)}, bf16[512,512]{1,0:T(8,128)(2,1)}, bf16[1024,128]{1,0:T(8,128)(2,...) custom-call(s32[768]{0:T(1024)} %reshape.406.ids_ref, ...), custom_call_target="tpu_custom_call" | custom-call | tf_op jit(solution)/shard_map/front/pallas_call | solution.py:790
  126.2 0.0 copy-done
  126.2 1.3 reduce_max.19
  127.5 194.8 %head.1 = (f32[512,512]{1,0:T(8,128)}, f32[6288,512]{1,0:T(8,128)}, f32[8,512]{1,0:T(8,128)}, f32[8,512]{1,0:T(8,128)}, f32[8,6288,512]{2,1,0:T(8,128)}) custom-call(f32[512,512]{1,0:T(8,128)} %get-tuple-element.269.f_ref, s32[4,1024]{1,0:T(4,128)} %lab_ref.1, f32[6288,512]{1,0:T(8,128)} %get-tuple-element.616), custom_call_target="tpu_custom_call" | custom-call | flops 105495134208 | bytes 38633472 | tf_op jit(solution)/shard_map/head/pallas_call | solution.py:487
  322.3 100.1 %layer_bwd.1 = (f32[8,928,512]{2,1,0:T(8,128)}, f32[512,512]{1,0:T(8,128)}, f32[4,8,96,512]{3,2,1,0:T(8,128)}, f32[3,264,512]{2,1,0:T(8,128)}, s32[4,1,768]{2,1,0:T(1,128)}) custom-call(f32[512,512]{1,0:T(8,128)} %get-tuple-element.271.dfin_ref, f32[512,512]{1,0:T(8,128)} %get-tuple-element.272.x0_ref, f32[512,512]{1,0:T(8,128)} %get-tuple-element.273.x1_ref, ...), custom_call_target="tpu_custom_call" | custom-call | tf_op jit(solution)/shard_map/layer_bwd/pallas_call | solution.py:1030
  422.4 142.8 %tail.1 = (f32[6288,512]{1,0:T(8,128)}, f32[2,464,512]{2,1,0:T(8,128)}, f32[8,24,512]{2,1,0:T(8,128)}) custom-call(f32[6288,512]{1,0:T(8,128)} %get-tuple-element.270.g_ref, f32[8,2,464,512]{3,2,1,0:T(8,128)} %bitcast.71, f32[4,768,512]{2,1,0:T(8,128)} %bitcast.72, s32[4,1,768]{2,1,0:T(1,128)} %get-tuple-element.288.ids_ref, ...), custom_call_target="tpu_custom_call" | custom-call | tf_op jit(solution)/shard_map/tail/pallas_call | solution.py:1282
  565.2 0.7 while.25
  565.9 35.2 %update.1 = (f32[6288,512]{1,0:T(8,128)}, f32[2,512]{1,0:T(2,128)}, f32[64,512]{1,0:T(8,128)}, f32[2,64,512]{2,1,0:T(8,128)}, f32[64,512]{1,0:T(8,128)}, /*index...) custom-call(f32[6288,512]{1,0:T(8,128)} %get-tuple-element.293.t_ref, ...), custom_call_target="tpu_custom_call" | custom-call | tf_op jit(solution)/shard_map/update/pallas_call | solution.py:1393
  (7 shorter events, 0.1 us)
Async XLA Ops:
  0.7 8.4 %copy-start.1 = (f32[256,512]{1,0:T(8,128)S(1)}, f32[256,512]{1,0:T(8,128)}, u32[]{:S(2)}) copy-start(f32[256,512]{1,0:T(8,128)} %refs_6_.1) | copy-start | bytes 1572868
  0.7 8.4 %copy-start.2 = (f32[64,512]{1,0:T(8,128)S(1)}, f32[64,512]{1,0:T(8,128)}, u32[]{:S(2)}) copy-start(f32[64,512]{1,0:T(8,128)} %refs_4_.1) | copy-start | bytes 393220
  0.7 8.4 %copy-start.3 = (f32[512,64]{0,1:T(8,128)S(1)}, f32[512,64]{0,1:T(8,128)}, u32[]{:S(2)}) copy-start(f32[512,64]{0,1:T(8,128)} %param.31) | copy-start | bytes 393220
  10.6 115.5 %copy-start = (s32[8,512]{1,0:T(8,128)}, s32[8,512]{1,0:T(8,128)S(1)}, u32[]{:S(2)}) copy-start(s32[8,512]{1,0:T(8,128)S(1)} %get-tuple-element.619) | copy-start | bytes 49156
